TPU v7x, 8 devices: a whole 2x2x1 slice. The times are simulated.
8 devices in a mesh: sweep: 2 (over z, y), ent: 4 (over x, core).
Axes of the slice: x: 2, y: 2, z: 1, core: 2. Of those that a mesh axis runs over, the one named last changes fastest.
Arguments:
- ent_emb: float32 [65536, 400], P(('sweep', 'ent')), parts along dimension 0
- ent_ada: float32 [65536], P(('sweep', 'ent')), parts along dimension 0
- rel_emb: float32 [2690, 400], P('sweep'), parts along dimension 0
- rel_ada: float32 [2690], P('sweep'), parts along dimension 0
- head_idx: int32 [8, 3, 2048], P(('sweep', 'ent')), parts along dimension 0
- tail_idx: int32 [8, 3, 2048], P(('sweep', 'ent')), parts along dimension 0
- rel_idx: int32 [8, 3, 2048], P(('sweep', 'ent')), parts along dimension 0
- edge_mask: int32 [8, 3, 2048], P(('sweep', 'ent')), parts along dimension 0
- neg_idx: int32 [6, 1000], P('sweep'), parts along dimension 0
Outputs:
- output 1: float32 [65536, 400], P(('sweep', 'ent')), parts along dimension 0
- output 2: float32 [65536], P(('sweep', 'ent')), parts along dimension 0
- output 3: float32 [2690, 400], P('sweep'), parts along dimension 0
- output 4: float32 [2690], P('sweep'), parts along dimension 0
- output 5: float32 [8, 3], P(('sweep', 'ent')), parts along dimension 0
There are 2 independent parts. A program takes and returns all parts, laid end to end along the dimension named above; each array names one.
All inputs are finite; a program needn't handle non-finite values.
Results may differ from a plain program's by a relative error of at most 0.001.
Values are sent between devices in bfloat16 or wider.
A program may use at most 1 GiB of HBM per device.

v0:
```python
import jax
import jax.numpy as jnp
from jax import lax
from jax.sharding import PartitionSpec as P

LEARN_RATE = 0.05
ADA_EPS = 1e-10


def bucket_grads(head_rows, tail_rows, neg_rows, rel_rows, edge_w):
    half = head_rows.shape[-1] // 2
    head_f = head_rows.astype(jnp.float32)
    h_re = head_f[:, :half]
    h_im = head_f[:, half:]
    r_re = rel_rows[:, :half]
    r_im = rel_rows[:, half:]
    query = jnp.concatenate([h_re * r_re - h_im * r_im, h_re * r_im + h_im * r_re], axis=1)
    query_bf = query.astype(jnp.bfloat16)
    tail_f = tail_rows.astype(jnp.float32)
    pos_score = jnp.sum(query * tail_f, axis=1)
    neg_score = jnp.einsum('bd,nd->bn', query_bf, neg_rows, preferred_element_type=jnp.float32)
    top_score = jnp.maximum(pos_score, jnp.max(neg_score, axis=1))
    pos_exp = jnp.exp(pos_score - top_score)
    neg_exp = jnp.exp(neg_score - top_score[:, None])
    norm_sum = pos_exp + jnp.sum(neg_exp, axis=1)
    log_norm = top_score + jnp.log(norm_sum)
    loss = jnp.sum(edge_w * (log_norm - pos_score)) / edge_w.shape[0]
    pos_grad = edge_w * (pos_exp / norm_sum - 1.0)
    neg_grad = (edge_w[:, None] * neg_exp / norm_sum[:, None]).astype(jnp.bfloat16)
    query_grad = pos_grad[:, None] * tail_f + jnp.einsum('bn,nd->bd', neg_grad, neg_rows, preferred_element_type=jnp.float32)
    tail_grad = pos_grad[:, None] * query
    negrow_grad = jnp.einsum('bn,bd->nd', neg_grad, query_bf, preferred_element_type=jnp.float32)
    g_re = query_grad[:, :half]
    g_im = query_grad[:, half:]
    head_grad = jnp.concatenate([g_re * r_re + g_im * r_im, g_im * r_re - g_re * r_im], axis=1)
    relrow_grad = jnp.concatenate([g_re * h_re + g_im * h_im, g_im * h_re - g_re * h_im], axis=1)
    return loss, head_grad, tail_grad, negrow_grad, relrow_grad


def adagrad_rows(table, state, grad):
    new_state = state + jnp.mean(grad * grad, axis=1)
    return table - LEARN_RATE * grad / jnp.sqrt(new_state + ADA_EPS)[:, None], new_state


def solution(mesh):
    ent_size = mesh.shape['ent']
    row_spec = P(('sweep', 'ent'), None)
    flat_spec = P(('sweep', 'ent'))
    rel_spec = P('sweep', None)
    state_spec = P('sweep')
    edge_spec = P(('sweep', 'ent'), None, None)

    def device_fn(ent_emb, ent_ada, rel_emb, rel_ada, head_idx, tail_idx, rel_idx, edge_mask, neg_idx):
        part_rows = ent_emb.shape[0]
        num_rel = rel_emb.shape[0]
        rounds = head_idx.shape[1]
        my_dev = lax.axis_index('ent')
        table, state, rel_tab, rel_state = ent_emb, ent_ada, rel_emb, rel_ada
        losses = []
        for round_no in range(rounds):
            table_bf = table.astype(jnp.bfloat16)
            if round_no == 0:
                tail_tab = table_bf
            else:
                tail_tab = lax.ppermute(table_bf, 'ent', [(sender, (sender - round_no) % ent_size) for sender in range(ent_size)])
            neg_ids = neg_idx[round_no]
            neg_local = neg_ids % part_rows
            owned = (neg_ids // part_rows) == my_dev
            neg_mine = jnp.where(owned[:, None], jnp.take(table_bf, neg_local, axis=0), jnp.zeros((), jnp.bfloat16))
            neg_rows = lax.psum(neg_mine, 'ent')
            head_ids = head_idx[0, round_no]
            tail_ids = tail_idx[0, round_no]
            rel_ids = rel_idx[0, round_no]
            edge_w = edge_mask[0, round_no].astype(jnp.float32)
            loss, head_grad, tail_grad, negrow_grad, relrow_grad = bucket_grads(
                jnp.take(table_bf, head_ids, axis=0), jnp.take(tail_tab, tail_ids, axis=0),
                neg_rows, jnp.take(rel_tab, rel_ids, axis=0), edge_w)
            losses.append(loss)
            if round_no == 0:
                back_grad, back_ids = tail_grad, tail_ids
            else:
                back_grad, back_ids = lax.ppermute((tail_grad, tail_ids), 'ent', [(sender, (sender + round_no) % ent_size) for sender in range(ent_size)])
            neg_sum = lax.psum(negrow_grad, 'ent')
            rel_sum = lax.psum(jax.ops.segment_sum(relrow_grad, rel_ids, num_segments=num_rel), 'ent')
            row_grads = jnp.concatenate([head_grad, back_grad, jnp.where(owned[:, None], neg_sum, 0.0)], axis=0)
            row_ids = jnp.concatenate([head_ids, back_ids, neg_local], axis=0)
            grad_ent = jax.ops.segment_sum(row_grads, row_ids, num_segments=part_rows)
            table, state = adagrad_rows(table, state, grad_ent)
            rel_tab, rel_state = adagrad_rows(rel_tab, rel_state, rel_sum)
        return table, state, rel_tab, rel_state, jnp.stack(losses)[None, :]

    return jax.shard_map(device_fn, mesh=mesh,
                         in_specs=(row_spec, flat_spec, rel_spec, state_spec, edge_spec, edge_spec, edge_spec, edge_spec, rel_spec),
                         out_specs=(row_spec, flat_spec, rel_spec, state_spec, row_spec), check_vma=False)
```

profile of v0, /device:TPU:0, one launch (start us, length us, event | category | flops | bytes accessed | tf_op | source)
XLA Modules:
  0.0 1144.6 jit_solution(10664023479477630992)
XLA Ops:
  8.7 15.9 %copy.63 = f32[8192,400]{1,0:T(8,128)} copy(f32[8192,400]{0,1:T(8,128)} %param.15) | data formatting | bytes 26214400 | tf_op args[0]
  62.8 12.0 %gather_fusion.2 = bf16[2048,400]{1,0:T(8,128)(2,1)S(1)} fusion(bf16[8192,400]{1,0:T(8,128)(2,1)} %convert_element_type.86, s32[2048]{0:T(1024)S(1)} %fusion.41), kind=kCustom, calls=%fused_computation.3.clone | custom fusion | bytes 3284992 | tf_op jit(solution)/shard_map/jit(_take)/gather | solution.py:76
  74.8 13.7 %gather_fusion = bf16[2048,400]{1,0:T(8,128)(2,1)} fusion(bf16[8192,400]{1,0:T(8,128)(2,1)} %convert_element_type.86, s32[2048]{0:T(1024)S(1)} %fusion.39), kind=kCustom, calls=%fused_computation.clone | custom fusion | bytes 3284992 | tf_op jit(solution)/shard_map/jit(_take)/gather | solution.py:76
  121.4 15.1 %scatter_custom_fusion.1 = f32[1345,400]{1,0:T(8,128)} fusion(s32[2048]{0:T(1024)S(1)} %bitcast.58, f32[2048,400]{1,0:T(8,128)} %copy.65, f32[]{:T(128)} %constant.104.clone.1), kind=kCustom, calls=%fused_computation.103 | custom fusion | flops 819200 | bytes 2152512 | tf_op jit(solution)/shard_map/scatter-add | solution.py:84
  138.7 84.2 %all-reduce.20.cloned.1.call-done = (f32[1000,400]{0,1:T(8,128)}, f32[1345,400]{1,0:T(8,128)}) async-done(((f32[1000,400]{0,1:T(8,128)}, f32[1345,400]{1,0:T(8,128)}), (f32[1000,400]{0,1:T(8,128)}, f32[1345,400]{1,0:T(8,128)})) %all-reduce.20.cloned.1.call-update) | async-done | bytes 3752016 | tf_op jit(solution)/shard_map/psum | solution.py:83
  230.3 10.4 copy.62
  240.7 37.9 %scatter_custom_fusion = f32[8192,400]{1,0:T(8,128)} fusion(s32[5096]{0:T(1024)S(1)} %pad_add_fusion, f32[5096,400]{1,0:T(8,128)} %copy.62, f32[]{:T(128)} %constant.104.clone.1), kind=kCustom, calls=%fused_computation.28 | custom fusion | flops 2038400 | bytes 13107712 | tf_op jit(solution)/shard_map/scatter-add | solution.py:87
  285.8 15.2 %fusion.66 = bf16[8192,400]{1,0:T(8,128)(2,1)} fusion(f32[8192,400]{1,0:T(8,128)} %copy.63, f32[8192]{0:T(1024)S(1)} %add_sqrt_fusion.2, f32[8192,400]{1,0:T(8,128)} %scatter_custom_fusion), kind=kLoop, calls=%fused_computation.217 | loop fusion | flops 13107200 | bytes 32800768 | tf_op jit(solution)/shard_map/convert_element_type | solution.py:61
  301.0 10.8 copy.68
  344.0 13.9 %gather_fusion.4 = bf16[2048,400]{1,0:T(8,128)(2,1)} fusion(bf16[8192,400]{1,0:T(8,128)(2,1)} %fusion.66, s32[2048]{0:T(1024)S(1)} %fusion.42), kind=kCustom, calls=%fused_computation.4.clone | custom fusion | bytes 3284992 | tf_op jit(solution)/shard_map/jit(_take)/gather | solution.py:76
  384.5 11.7 %collective-permute-done.1 = bf16[8192,400]{0,1:T(8,128)(2,1)} collective-permute-done((bf16[8192,400]{0,1:T(8,128)(2,1)}, bf16[8192,400]{0,1:T(8,128)(2,1)}, u32[]{:S(2)}, u32[]{:S(2)}) %collective-permute-start.1) | collective-permute-done | bytes 6553632 | tf_op jit(solution)/shard_map/ppermute | solution.py:65
  396.3 10.7 copy.69
  406.9 13.7 %gather_fusion.6 = bf16[2048,400]{1,0:T(8,128)(2,1)} fusion(bf16[8192,400]{1,0:T(8,128)(2,1)} %copy.69, s32[2048]{0:T(1024)S(1)} %fusion.44), kind=kCustom, calls=%fused_computation.5.clone | custom fusion | bytes 3284992 | tf_op jit(solution)/shard_map/jit(_take)/gather | solution.py:76
  453.8 15.0 %scatter_custom_fusion.3 = f32[1345,400]{1,0:T(8,128)} fusion(s32[2048]{0:T(1024)S(1)} %bitcast.55, f32[2048,400]{1,0:T(8,128)} %copy.74, f32[]{:T(128)} %constant.104.clone.1), kind=kCustom, calls=%fused_computation.101 | custom fusion | flops 819200 | bytes 2152512 | tf_op jit(solution)/shard_map/scatter-add | solution.py:84
  478.4 81.6 %all-reduce.18.cloned.1.call-done = (f32[1000,400]{0,1:T(8,128)}, f32[1345,400]{1,0:T(8,128)}) async-done(((f32[1000,400]{0,1:T(8,128)}, f32[1345,400]{1,0:T(8,128)}), (f32[1000,400]{0,1:T(8,128)}, f32[1345,400]{1,0:T(8,128)})) %all-reduce.18.cloned.1.call-update) | async-done | bytes 3752016 | tf_op jit(solution)/shard_map/psum | solution.py:83
  568.8 10.4 copy.72
  579.2 37.9 %scatter_custom_fusion.2 = f32[8192,400]{1,0:T(8,128)} fusion(s32[5096]{0:T(1024)S(1)} %pad_add_fusion.1, f32[5096,400]{1,0:T(8,128)} %copy.72, f32[]{:T(128)} %constant.104.clone.1), kind=kCustom, calls=%fused_computation.26 | custom fusion | flops 2038400 | bytes 13107712 | tf_op jit(solution)/shard_map/scatter-add | solution.py:87
  624.2 26.2 %fusion.67 = (bf16[8192,400]{1,0:T(8,128)(2,1)}, f32[8192,400]{1,0:T(8,128)}) fusion(f32[8192]{0:T(1024)S(1)} %add_sqrt_fusion.1, f32[8192,400]{1,0:T(8,128)} %scatter_custom_fusion.2, f32[8192,400]{1,0:T(8,128)} %copy.63, f32[8192]{0:T(1024)S(1)} %add_sqrt_fusion.2, f32[8192,400]{1,0:T(8,128)} %scatter_custom_fusion), kind=kLoop, calls=%fused_computation.218 | loop fusion | flops 22937600 | bytes 59047936 | tf_op jit(solution)/shard_map/convert_element_type | solution.py:61
  650.5 10.7 copy.76
  666.2 11.3 gather_fusion.9
  684.9 9.6 gather_fusion.11
  698.9 13.9 %gather_fusion.8 = bf16[2048,400]{1,0:T(8,128)(2,1)} fusion(bf16[8192,400]{1,0:T(8,128)(2,1)} %get-tuple-element.35, s32[2048]{0:T(1024)S(1)} %fusion.45), kind=kCustom, calls=%fused_computation.6.clone | custom fusion | bytes 3284992 | tf_op jit(solution)/shard_map/jit(_take)/gather | solution.py:76
  722.3 16.3 %all-reduce.14.cloned.1.call-done = bf16[1000,400]{0,1:T(8,128)(2,1)} async-done(((bf16[1000,400]{0,1:T(8,128)(2,1)}), bf16[1000,400]{0,1:T(8,128)(2,1)}) %all-reduce.14.cloned.1.call-update) | async-done | bytes 800016 | tf_op jit(solution)/shard_map/psum | solution.py:70
  746.2 70.7 %collective-permute-done.4 = bf16[8192,400]{0,1:T(8,128)(2,1)} collective-permute-done((bf16[8192,400]{0,1:T(8,128)(2,1)}, bf16[8192,400]{0,1:T(8,128)(2,1)}, u32[]{:S(2)}, u32[]{:S(2)}) %collective-permute-start.4) | collective-permute-done | bytes 6553632 | tf_op jit(solution)/shard_map/ppermute | solution.py:65
  816.9 10.7 copy.77
  827.6 13.7 %gather_fusion.10 = bf16[2048,400]{1,0:T(8,128)(2,1)} fusion(bf16[8192,400]{1,0:T(8,128)(2,1)} %copy.77, s32[2048]{0:T(1024)S(1)} %fusion.47), kind=kCustom, calls=%fused_computation.7.clone | custom fusion | bytes 3284992 | tf_op jit(solution)/shard_map/jit(_take)/gather | solution.py:76
  869.4 14.9 %scatter_custom_fusion.5 = f32[1345,400]{1,0:T(8,128)} fusion(s32[2048]{0:T(1024)S(1)} %bitcast.49, f32[2048,400]{1,0:T(8,128)} %copy.81, f32[]{:T(128)} %constant.104.clone.1), kind=kCustom, calls=%fused_computation.99 | custom fusion | flops 819200 | bytes 2152512 | tf_op jit(solution)/shard_map/scatter-add | solution.py:84
  890.7 133.3 %collective-permute-done.3 = s32[2048]{0:T(1024)S(1)} collective-permute-done((s32[2048]{0:T(1024)S(1)}, s32[2048]{0:T(1024)S(1)}, u32[]{:S(2)}, u32[]{:S(2)}) %collective-permute-start.3) | collective-permute-done | bytes 8224 | tf_op jit(solution)/shard_map/ppermute | solution.py:82
  1047.2 10.4 copy.80
  1057.6 37.9 %scatter_custom_fusion.4 = f32[8192,400]{1,0:T(8,128)} fusion(s32[5096]{0:T(1024)S(1)} %pad_add_fusion.2, f32[5096,400]{1,0:T(8,128)} %copy.80, f32[]{:T(128)} %constant.104.clone.1), kind=kCustom, calls=%fused_computation.24 | custom fusion | flops 2038400 | bytes 13107712 | tf_op jit(solution)/shard_map/scatter-add | solution.py:87
  1103.2 17.9 %divide_subtract_fusion = f32[8192,400]{1,0:T(8,128)} fusion(f32[8192,400]{1,0:T(8,128)} %get-tuple-element.36, f32[8192,400]{1,0:T(8,128)} %scatter_custom_fusion.4, f32[8192]{0:T(1024)S(1)} %get-tuple-element.31), kind=kLoop, calls=%fused_computation.18 | loop fusion | flops 9830400 | bytes 39354368 | tf_op jit(solution)/shard_map/sub | solution.py:42
  1121.1 16.2 %copy.82 = f32[8192,400]{0,1:T(8,128)} copy(f32[8192,400]{1,0:T(8,128)} %divide_subtract_fusion) | data formatting | bytes 26214400
  (248 shorter events, 303.5 us)
Async XLA Ops:
  7.2 94.2 %all-reduce.10.cloned.1.call-start = ((), (), s32[]{:S(2)}) async-start(), calls=%async_computation | async-start | bytes 1638400 | tf_op jit(solution)/shard_map/psum | solution.py:70
  43.9 179.0 %all-reduce.20.cloned.1.call-start = ((), (), s32[]{:S(2)}) async-start(), calls=%async_computation.5 | async-start | bytes 8814592 | tf_op jit(solution)/shard_map/psum | solution.py:83
  48.5 9.0 copy-start.1
  121.4 15.1 %copy-start.15 = (f32[2048,200]{0,1:T(8,128)S(1)}, f32[2048,200]{0,1:T(8,128)}, u32[]{:S(2)}) copy-start(f32[2048,200]{0,1:T(8,128)} %copy-done.13) | copy-start | bytes 4915204
  121.4 15.2 %copy-start.18 = (f32[2048,200]{0,1:T(8,128)S(1)}, f32[2048,200]{0,1:T(8,128)}, u32[]{:S(2)}) copy-start(f32[2048,200]{0,1:T(8,128)} %copy-done.16) | copy-start | bytes 4915204
  136.5 240.4 %all-reduce.12.cloned.1.call-start = ((), (), s32[]{:S(2)}) async-start(), calls=%async_computation.1 | async-start | bytes 1638400 | tf_op jit(solution)/shard_map/psum | solution.py:70
  138.7 85.9 %copy-start.22 = (f32[2048,400]{0,1:T(8,128)S(1)}, f32[2048,400]{0,1:T(8,128)}, u32[]{:S(2)}) copy-start(f32[2048,400]{0,1:T(8,128)} %fusion.19) | copy-start | bytes 9830404
  278.6 7.1 copy-start.36
  301.0 11.0 copy-start.24
  301.0 11.3 copy-start.38
  311.8 84.5 %collective-permute-start.1 = (bf16[8192,400]{0,1:T(8,128)(2,1)}, bf16[8192,400]{0,1:T(8,128)(2,1)}, u32[]{:S(2)}, u32[]{:S(2)}) collective-permute-start(bf16[8192,400]{0,1:T(8,128)(2,1)} %copy.68), channel_id=1, source_target_pairs={{0,3},{1,0},{2,1},{3,2},{4,7},{5,4},{6,5},{7,6}} | collective-permute-start | bytes 19660808 | tf_op jit(solution)/shard_map/ppermute | solution.py:65
  343.9 216.0 %all-reduce.18.cloned.1.call-start = ((), (), s32[]{:S(2)}) async-start(), calls=%async_computation.4 | async-start | bytes 8814592 | tf_op jit(solution)/shard_map/psum | solution.py:83
  432.5 4.6 copy-start.19
  432.5 4.6 copy-start.20
  439.2 4.4 copy-start.6
  439.2 122.6 %collective-permute-start.2 = (f32[2048,400]{0,1:T(8,128)}, f32[2048,400]{0,1:T(8,128)}, u32[]{:S(2)}, u32[]{:S(2)}) collective-permute-start(f32[2048,400]{0,1:T(8,128)} %fusion.17), channel_id=1, source_target_pairs={{0,1},{1,2},{2,3},{3,0},{4,5},{5,6},{6,7},{7,4}} | collective-permute-start | bytes 9830408 | tf_op jit(solution)/shard_map/ppermute | solution.py:82
  475.0 263.5 %all-reduce.14.cloned.1.call-start = ((), (), s32[]{:S(2)}) async-start(), calls=%async_computation.2 | async-start | bytes 1638400 | tf_op jit(solution)/shard_map/psum | solution.py:70
  475.1 3.3 collective-permute-start
  650.5 11.2 copy-start.46
  650.5 11.2 copy-start.37
  650.5 11.2 copy-start.39
  650.5 11.2 copy-start.40
  661.2 155.7 %collective-permute-start.4 = (bf16[8192,400]{0,1:T(8,128)(2,1)}, bf16[8192,400]{0,1:T(8,128)(2,1)}, u32[]{:S(2)}, u32[]{:S(2)}) collective-permute-start(bf16[8192,400]{0,1:T(8,128)(2,1)} %copy.76), channel_id=1, source_target_pairs={{0,2},{1,3},{2,0},{3,1},{4,6},{5,7},{6,4},{7,5}} | collective-permute-start | bytes 19660808 | tf_op jit(solution)/shard_map/ppermute | solution.py:65
  698.8 332.2 %all-reduce.16.cloned.1.call-start = ((), (), s32[]{:S(2)}) async-start(), calls=%async_computation.3 | async-start | bytes 8814592 | tf_op jit(solution)/shard_map/psum | solution.py:83
  848.0 4.5 copy-start.41
  853.1 4.6 copy-start.11
  853.1 4.6 copy-start.12
  884.3 149.5 %copy-start = (f32[1345,400]{1,0:T(8,128)S(1)}, f32[1345,400]{1,0:T(8,128)}, u32[]{:S(2)}) copy-start(f32[1345,400]{1,0:T(8,128)} %divide_subtract_fusion.4) | copy-start | bytes 6456004
  888.6 152.5 %collective-permute-start.5 = (f32[2048,400]{0,1:T(8,128)}, f32[2048,400]{0,1:T(8,128)}, u32[]{:S(2)}, u32[]{:S(2)}) collective-permute-start(f32[2048,400]{0,1:T(8,128)} %fusion.15), channel_id=1, source_target_pairs={{0,2},{1,3},{2,0},{3,1},{4,6},{5,7},{6,4},{7,5}} | collective-permute-start | bytes 9830408 | tf_op jit(solution)/shard_map/ppermute | solution.py:82
  889.5 134.4 %collective-permute-start.3 = (s32[2048]{0:T(1024)S(1)}, s32[2048]{0:T(1024)S(1)}, u32[]{:S(2)}, u32[]{:S(2)}) collective-permute-start(s32[2048]{0:T(1024)S(1)} %bitcast.46), channel_id=1, source_target_pairs={{0,2},{1,3},{2,0},{3,1},{4,6},{5,7},{6,4},{7,5}} | collective-permute-start | bytes 24584 | tf_op jit(solution)/shard_map/ppermute | solution.py:82
  1035.8 5.3 copy-start.31
  1035.8 5.3 copy-start.32
  (30 other events, 74.5 us)
Sparse Core Ops, SparseCore 0:
  44.0 32.4 all-reduce.9
  136.6 86.2 all-reduce.19
  344.0 32.8 all-reduce.11
  475.2 84.7 all-reduce.17
  698.9 39.5 all-reduce.13
  884.4 146.4 all-reduce.15
where the time goes:
time: 1150 us; the launch traced here: 1140 us
  waiting for transfers between devices  411 us (36%)
  other arithmetic  354 us (31%)
  local copies, waits for them, and re-layouts  318 us (28%)
  matrix products  38.7 us (3%)
  between operations  17.4 us (2%)
    psum x3, waiting for transfers between devices, device_fn(): neg_sum = lax.psum(negrow_grad, 'ent')  170 us
    ppermute x4, waiting for transfers between devices, device_fn(): lax.ppermute((tail_grad, tail_ids), 'ent', [(sender, (sender + round_no)...  135 us
    scatter-add x3, other arithmetic, device_fn(): grad_ent = jax.ops.segment_sum(row_grads, row_ids, num_segments=part_rows)  114 us
    ppermute x2, waiting for transfers between devices, device_fn(): lax.ppermute(table_bf, 'ent', [(sender, (sender - round_no) % ent_size) f...  82.5 us
    gather x6, local copies, waits for them, and re-layouts, device_fn(): jnp.take(table_bf, head_ids, axis=0)  53 us
    convert_element_type x3, other arithmetic, device_fn(): table_bf = table.astype(jnp.bfloat16)  50.4 us
    gather x6, local copies, waits for them, and re-layouts, device_fn(): jnp.take(tail_tab, tail_ids, axis=0)  49.4 us
    unnamed x104, local copies, waits for them, and re-layouts  48.8 us
  transfers between devices with their start and end apart: 12, of which 9 were waited for; matrix products, arithmetic and copies ran while one was open for 20% of the time, Pallas kernels for 0%

commit v1 on v0

v1 whole, which is shorter than its diff:
```python
import functools

import jax
import jax.numpy as jnp
from jax import lax
from jax.experimental import pallas as pl
from jax.experimental.pallas import tpu as pltpu
from jax.sharding import PartitionSpec as P

LEARN_RATE = 0.05
ADA_EPS = 1e-10
LANES = 128
SLICES = 4
CHUNK = 256
BATCH = 4
F32 = jnp.float32
BF16 = jnp.bfloat16


def ceil_to(value, unit):
    return -(-value // unit) * unit


def vmem():
    return pl.BlockSpec(memory_space=pltpu.VMEM)


def smem():
    return pl.BlockSpec(memory_space=pltpu.SMEM)


def hbm():
    return pl.BlockSpec(memory_space=pltpu.MemorySpace.HBM)


def four(index):
    return pl.multiple_of(index, SLICES)


def gather_rows(src, ids, base, stage, count):
    for k in range(count):
        stage[pl.ds(SLICES * k, SLICES), :] = src[pl.ds(four(ids[base + k]), SLICES), :]


def stage_cols(stage, slice_no):
    return stage[pl.ds(slice_no, LANES, stride=SLICES), :].T


def add_rows(acc, ids, base, rows, row_base, count):
    for first in range(0, count, BATCH):
        index = [ids[base + first + k] for k in range(BATCH)]
        grads = [rows[pl.ds(four(row_base + SLICES * (first + k)), SLICES), :] for k in range(BATCH)]
        total = [acc[pl.ds(four(index[k]), SLICES), :] + grads[k] for k in range(BATCH)]
        for k in range(1, BATCH):
            for earlier in range(k):
                total[k] = total[k] + jnp.where(index[earlier] == index[k], grads[earlier], 0.0)
        for k in range(BATCH):
            acc[pl.ds(four(index[k]), SLICES), :] = total[k]


def zero_rows(ref, step=1024):
    rows = ref.shape[0]
    whole = rows // step

    def body(i, _):
        ref[pl.ds(pl.multiple_of(i * step, 8), step), :] = jnp.zeros((step, LANES), ref.dtype)
        return 0

    lax.fori_loop(0, whole, body, 0)
    if rows % step:
        ref[pl.ds(whole * step, rows % step), :] = jnp.zeros((rows % step, LANES), ref.dtype)


def gather_out(dim, table, ids, out, stage, count):
    def body(b, _):
        gather_rows(table, ids, b * LANES, stage, LANES)
        cols = pl.ds(pl.multiple_of(b * LANES, LANES), LANES)
        for j in range(SLICES):
            size = min(LANES, dim - j * LANES)
            out[pl.ds(j * LANES, size), cols] = stage_cols(stage, j)[:size].astype(BF16)
        return 0

    lax.fori_loop(0, count // LANES, body, 0)


def gather_all(dim, core, table, heads, tails, negs, hb, tb, nk, ns, nbuf, stage):
    half = nbuf.shape[1] // 2
    gather_out(dim, table, negs, nbuf, stage, nbuf.shape[1])
    nk[...] = nbuf[:, pl.ds(pl.multiple_of(core * half, LANES), half)]
    ns[...] = nbuf[:, pl.ds(pl.multiple_of((1 - core) * half, LANES), half)]
    gather_out(dim, table, tails, tb, stage, tb.shape[1])
    gather_out(dim, table, heads, hb, stage, hb.shape[1])


def entry_kernel(dim, rows, core_ref, heads, tails, negs, et, g, t4_out, v_out, hb, tb, nk, ns,
                 t4, v, inbuf, stage, nbuf, in_sem, out_sem):
    cols = inbuf.shape[2]
    steps = rows // cols
    per = cols // LANES

    def fetch(step, slot):
        return pltpu.make_async_copy(et.at[:, pl.ds(pl.multiple_of(step * cols, LANES), cols)],
                                     inbuf.at[slot, pl.ds(0, dim)], in_sem.at[slot])

    fetch(0, 0).start()
    for slot in range(2):
        inbuf[slot, pl.ds(dim, SLICES * LANES - dim), :] = jnp.zeros((SLICES * LANES - dim, cols), F32)
    t4[pl.ds(rows * SLICES, 32), :] = jnp.zeros((32, LANES), F32)

    def body(step, _):
        slot = lax.rem(step, 2)

        @pl.when(step + 1 < steps)
        def _():
            fetch(step + 1, 1 - slot).start()

        fetch(step, slot).wait()
        for b in range(per):
            row0 = (step * per + b) * LANES
            for j in range(SLICES):
                t4[pl.ds(SLICES * row0 + j, LANES, stride=SLICES), :] = inbuf[slot, pl.ds(j * LANES, LANES), pl.ds(b * LANES, LANES)].T
            v[pl.ds(pl.multiple_of(row0, 8), LANES), :] = jnp.broadcast_to(g[pl.ds(step * per + b, 1), :], (LANES, LANES)).T
        return 0

    lax.fori_loop(0, steps, body, 0)
    save_t = pltpu.make_async_copy(t4.at[pl.ds(0, rows * SLICES)], t4_out, out_sem.at[0])
    save_v = pltpu.make_async_copy(v, v_out, out_sem.at[1])
    save_v.start()
    gather_all(dim, core_ref[0], t4, heads, tails, negs, hb, tb, nk, ns, nbuf, stage)
    save_t.start()
    save_t.wait()
    save_v.wait()


def bucket_kernel(dim, neg_count, num_rel, edges, first, *refs):
    if first:
        (core_ref, rel, w, hb, tb, nfull, nother, rfm, vr,
         loss, dp_out, hg, nk, ns, rk, rs, r4,
         nb, nbt, ds, sc, rt, ng, racc, stage, qs, fm) = refs
    else:
        (core_ref, rel, w, hb, tb, nfull, nother, rfm_in, vr_in, rmine, rother,
         loss, dp_out, hg, nk, ns, rk, rs, r4, rfm, vr,
         nb, nbt, ds, sc, rt, ng, racc, stage, qs, fm) = refs
    core = core_ref[0]
    half = dim // 2
    relp = rfm.shape[1]
    negp = nb.shape[1]
    tops = SLICES * LANES
    my_half = pl.ds(pl.multiple_of(core * half, 8), half)
    other_half = pl.ds(pl.multiple_of((1 - core) * half, 8), half)

    if not first:
        fm[my_half, pl.ds(0, relp)] = rmine[...]
        fm[other_half, pl.ds(0, relp)] = rother[...]
        grad = fm[pl.ds(0, dim), pl.ds(0, relp)]
        vr[...] = vr_in[...] + jnp.sum(grad * grad, axis=0, keepdims=True) / dim
        rate = LEARN_RATE / jnp.sqrt(vr[...] + ADA_EPS)
        rfm[...] = rfm_in[...] - fm[pl.ds(0, dim), pl.ds(0, relp)] * rate

    fm[pl.ds(dim, tops - dim), :] = jnp.zeros((tops - dim, fm.shape[1]), F32)
    rt[pl.ds(dim, tops - dim), :] = jnp.zeros((tops - dim, CHUNK), F32)
    qs[pl.ds(dim, tops - dim), :] = jnp.zeros((tops - dim, CHUNK), F32)
    for b in range(relp // LANES):
        for j in range(SLICES):
            if (j + 1) * LANES <= dim:
                block = rfm[pl.ds(j * LANES, LANES), pl.ds(b * LANES, LANES)]
            else:
                fm[pl.ds(j * LANES, dim - j * LANES), pl.ds(0, LANES)] = rfm[pl.ds(j * LANES, dim - j * LANES), pl.ds(b * LANES, LANES)]
                block = fm[pl.ds(j * LANES, LANES), pl.ds(0, LANES)]
            r4[pl.ds(SLICES * b * LANES + j, LANES, stride=SLICES), :] = block.T

    nhalf = negp // 2
    nb[:, pl.ds(pl.multiple_of(core * nhalf, LANES), nhalf)] = nfull[...]
    nb[:, pl.ds(pl.multiple_of((1 - core) * nhalf, LANES), nhalf)] = nother[...]
    for b in range(negp // LANES):
        nbt[pl.ds(b * LANES, LANES), :] = nb[:, pl.ds(b * LANES, LANES)].astype(F32).T.astype(BF16)
    zero_rows(racc)
    ng[...] = jnp.zeros(ng.shape, F32)
    ds[pl.ds(neg_count, negp - neg_count), :] = jnp.zeros((negp - neg_count, CHUNK), BF16)

    def step(c, loss_row):
        cols = pl.ds(pl.multiple_of(c * CHUNK, LANES), CHUNK)
        for b in range(CHUNK // LANES):
            gather_rows(r4, rel, c * CHUNK + b * LANES, stage, LANES)
            for j in range(SLICES):
                rt[pl.ds(j * LANES, LANES), pl.ds(b * LANES, LANES)] = stage_cols(stage, j)
        h = hb[:, cols].astype(F32)
        q_re = h[:half] * rt[pl.ds(0, half), :] - h[half:] * rt[pl.ds(half, half), :]
        q_im = h[:half] * rt[pl.ds(half, half), :] + h[half:] * rt[pl.ds(0, half), :]
        q = jnp.concatenate([q_re, q_im], axis=0)
        qb = q.astype(BF16)
        t = tb[:, cols].astype(F32)
        pos = jnp.sum(q * t, axis=0, keepdims=True)
        sc[...] = lax.dot_general(nbt[...], qb, (((1,), (0,)), ((), ())), preferred_element_type=F32)
        top = jnp.maximum(pos, jnp.max(sc[pl.ds(0, neg_count), :], axis=0, keepdims=True))
        pos_exp = jnp.exp(pos - top)
        norm = pos_exp
        part = 200
        for i in range(0, neg_count, part):
            size = min(part, neg_count - i)
            e = jnp.exp(sc[pl.ds(i, size), :] - top)
            sc[pl.ds(i, size), :] = e
            norm = norm + jnp.sum(e, axis=0, keepdims=True)
        wt = w[:, cols]
        loss_row = loss_row + wt * (top + jnp.log(norm) - pos)
        dp = wt * (pos_exp / norm - 1.0)
        dp_out[:, cols] = dp
        scale = wt / norm
        ds[pl.ds(0, neg_count), :] = (sc[pl.ds(0, neg_count), :] * scale).astype(BF16)
        ng[...] += lax.dot_general(ds[...], qb, (((1,), (1,)), ((), ())), preferred_element_type=F32)
        gq = lax.dot_general(nb[...], ds[...], (((1,), (0,)), ((), ())), preferred_element_type=F32) + dp * tb[:, cols].astype(F32)
        g_re, g_im = gq[:half], gq[half:]
        h = hb[:, cols].astype(F32)
        r_re, r_im = rt[pl.ds(0, half), :], rt[pl.ds(half, half), :]
        qs[pl.ds(0, half), :] = g_re * r_re + g_im * r_im
        qs[pl.ds(half, half), :] = g_im * r_re - g_re * r_im
        for b in range(CHUNK // LANES):
            for j in range(SLICES):
                hg[pl.ds(SLICES * (c * CHUNK + b * LANES) + j, LANES, stride=SLICES), :] = qs[pl.ds(j * LANES, LANES), pl.ds(b * LANES, LANES)].T
        h_re, h_im = h[:half], h[half:]
        qs[pl.ds(0, half), :] = g_re * h_re + g_im * h_im
        qs[pl.ds(half, half), :] = g_im * h_re - g_re * h_im
        for b in range(CHUNK // LANES):
            for j in range(SLICES):
                stage[pl.ds(j, LANES, stride=SLICES), :] = qs[pl.ds(j * LANES, LANES), pl.ds(b * LANES, LANES)].T
            add_rows(racc, rel, c * CHUNK + b * LANES, stage, 0, LANES)
        return loss_row

    loss_row = lax.fori_loop(0, edges // CHUNK, step, jnp.zeros((1, CHUNK), F32))
    loss[...] = jnp.broadcast_to(jnp.sum(loss_row, axis=1, keepdims=True) / edges, loss.shape)

    for b in range(negp // LANES):
        for j in range(SLICES):
            size = min(LANES, dim - j * LANES)
            fm[pl.ds(j * LANES, size), pl.ds(b * LANES, LANES)] = ng[pl.ds(b * LANES, LANES), pl.ds(j * LANES, size)].T
    nk[...] = fm[my_half, pl.ds(0, negp)]
    ns[...] = fm[other_half, pl.ds(0, negp)]
    for b in range(relp // LANES):
        for j in range(SLICES):
            size = min(LANES, dim - j * LANES)
            fm[pl.ds(j * LANES, size), pl.ds(b * LANES, LANES)] = racc[pl.ds(SLICES * b * LANES + j, LANES, stride=SLICES), :].T[:size]
    rk[...] = fm[my_half, pl.ds(0, relp)]
    rs[...] = fm[other_half, pl.ds(0, relp)]


def update_kernel(dim, rows, edges, last, *refs):
    if last:
        (core_ref, heads, tails, rel, negs, t4_in, v_in, hg, hb_in, dp, r4, nmine, nother,
         et_out, g_out, t4, v, acc, stage, rt, outbuf, in_sem, out_sem) = refs
    else:
        (core_ref, heads, tails, rel, negs, heads_n, tails_n, negs_n, t4_in, v_in, hg, hb_in, dp, r4, nmine, nother,
         t4_out, v_out, hb, tb, nk, ns, t4, v, acc, stage, rt, nbuf, in_sem, out_sem) = refs
    core = core_ref[0]
    half = dim // 2
    tops = SLICES * LANES
    load_t = pltpu.make_async_copy(t4_in, t4.at[pl.ds(0, rows * SLICES)], in_sem.at[0])
    load_v = pltpu.make_async_copy(v_in, v, in_sem.at[1])
    load_t.start()
    load_v.start()
    zero_rows(acc)
    t4[pl.ds(rows * SLICES, 32), :] = jnp.zeros((32, LANES), F32)
    rt[pl.ds(dim, tops - dim), :] = jnp.zeros((tops - dim, LANES), F32)

    def head_step(b, _):
        add_rows(acc, heads, b * 32, hg, b * 32 * SLICES, 32)
        return 0

    lax.fori_loop(0, edges // 32, head_step, 0)

    def unstage():
        for j in range(SLICES):
            stage[pl.ds(j, LANES, stride=SLICES), :] = rt[pl.ds(j * LANES, LANES), :].T

    def tail_step(b, _):
        cols = pl.ds(pl.multiple_of(b * LANES, LANES), LANES)
        gather_rows(r4, rel, b * LANES, stage, LANES)
        for j in range(SLICES):
            rt[pl.ds(j * LANES, LANES), :] = stage_cols(stage, j)
        h = hb_in[:, cols].astype(F32)
        r_re, r_im = rt[pl.ds(0, half), :], rt[pl.ds(half, half), :]
        scale = dp[:, cols]
        q_re = scale * (h[:half] * r_re - h[half:] * r_im)
        q_im = scale * (h[:half] * r_im + h[half:] * r_re)
        rt[pl.ds(0, half), :] = q_re
        rt[pl.ds(half, half), :] = q_im
        unstage()
        add_rows(acc, tails, b * LANES, stage, 0, LANES)
        return 0

    lax.fori_loop(0, edges // LANES, tail_step, 0)

    def neg_step(b, _):
        cols = pl.ds(pl.multiple_of(b * LANES, LANES), LANES)
        rt[pl.ds(pl.multiple_of(core * half, 8), half), :] = nmine[:, cols]
        rt[pl.ds(pl.multiple_of((1 - core) * half, 8), half), :] = nother[:, cols]
        unstage()
        add_rows(acc, negs, b * LANES, stage, 0, LANES)
        return 0

    lax.fori_loop(0, nmine.shape[1] // LANES, neg_step, 0)
    load_t.wait()
    load_v.wait()

    block = LANES

    def ada_step(b, _):
        row0 = b * block
        parts = [acc[pl.ds(SLICES * row0 + j, block, stride=SLICES), :] for j in range(SLICES)]
        square = parts[0] * parts[0]
        for j in range(1, SLICES):
            square = square + parts[j] * parts[j]
        vrows = pl.ds(pl.multiple_of(row0, 8), block)
        new_v = v[vrows, :] + jnp.sum(square, axis=1, keepdims=True) / dim
        v[vrows, :] = new_v
        rate = LEARN_RATE / jnp.sqrt(new_v + ADA_EPS)
        for j in range(SLICES):
            where = pl.ds(SLICES * row0 + j, block, stride=SLICES)
            t4[where, :] = t4[where, :] - acc[where, :] * rate
        return 0

    lax.fori_loop(0, rows // block, ada_step, 0)

    if not last:
        save_v = pltpu.make_async_copy(v, v_out, out_sem.at[1])
        save_v.start()
        gather_all(dim, core, t4, heads_n, tails_n, negs_n, hb, tb, nk, ns, nbuf, stage)
        save_t = pltpu.make_async_copy(t4.at[pl.ds(0, rows * SLICES)], t4_out, out_sem.at[0])
        save_t.start()
        save_t.wait()
        save_v.wait()
        return

    width = outbuf.shape[2]
    per = width // LANES
    steps = rows // width

    def save(step, slot):
        return pltpu.make_async_copy(outbuf.at[slot], et_out.at[:, pl.ds(pl.multiple_of(step * width, LANES), width)], out_sem.at[slot])

    def exit_step(step, _):
        slot = lax.rem(step, 2)

        @pl.when(step >= 2)
        def _():
            save(step - 2, slot).wait()

        for b in range(per):
            row0 = (step * per + b) * LANES
            for j in range(SLICES):
                size = min(LANES, dim - j * LANES)
                outbuf[slot, pl.ds(j * LANES, size), pl.ds(b * LANES, LANES)] = t4[pl.ds(SLICES * row0 + j, LANES, stride=SLICES), :].T[:size]
            g_out[pl.ds(step * per + b, 1), :] = v[pl.ds(pl.multiple_of(row0, 8), LANES), :].T[:1]
        save(step, slot).start()
        return 0

    lax.fori_loop(0, steps, exit_step, 0)
    save(steps - 2, (steps - 2) % 2).wait()
    save(steps - 1, (steps - 1) % 2).wait()


def params():
    return pltpu.CompilerParams(vmem_limit_bytes=63 * 1024 * 1024)


def cost(micros):
    return pl.CostEstimate(flops=int(micros * 5e6), bytes_accessed=0, transcendentals=0)


def shape(dims, dtype=F32):
    return jax.ShapeDtypeStruct(dims, dtype)


def solution(mesh):
    ent_size = mesh.shape['ent']
    row_spec = P(('sweep', 'ent'), None)
    flat_spec = P(('sweep', 'ent'))
    rel_spec = P('sweep', None)
    state_spec = P('sweep')
    edge_spec = P(('sweep', 'ent'), None, None)
    swap = [(i, i ^ 1) for i in range(ent_size)]
    cross = [(i, i ^ 2) for i in range(ent_size)]

    def shift(amount):
        return [(i, (i + amount) % ent_size) for i in range(ent_size)]

    def group_sum(keep, send):
        part = keep + lax.ppermute(send, 'ent', swap)
        mine = part + lax.ppermute(part, 'ent', cross)
        return mine, lax.ppermute(mine, 'ent', swap)

    def device_fn(ent_emb, ent_ada, rel_emb, rel_ada, head_idx, tail_idx, rel_idx, edge_mask, neg_idx):
        rows, dim = ent_emb.shape
        num_rel = rel_emb.shape[0]
        _, rounds, edges = head_idx.shape
        neg_count = neg_idx.shape[1]
        negp = ceil_to(neg_count, 2 * LANES)
        relp = ceil_to(num_rel, LANES)
        half = dim // 2
        my_dev = lax.axis_index('ent')
        core = (my_dev % 2).reshape(1)

        heads = [head_idx[0, s] * SLICES for s in range(rounds)]
        own_tails = [tail_idx[0, s] * SLICES for s in range(rounds)]
        own_rels = [rel_idx[0, s] * SLICES for s in range(rounds)]
        tails, rels = [own_tails[0]], [own_rels[0]]
        for s in range(1, rounds):
            got = lax.ppermute(jnp.stack([own_tails[s], own_rels[s]]), 'ent', shift(s))
            tails.append(got[0])
            rels.append(got[1])
        owned = (neg_idx // rows) == my_dev
        neg_local = jnp.where(owned, neg_idx % rows, rows) * SLICES
        neg_local = jnp.pad(neg_local, ((0, 0), (0, negp - neg_count)), constant_values=rows * SLICES)
        negs = [neg_local[s] for s in range(rounds)]
        weights = edge_mask[0].astype(F32)

        wide_rows = (rows + 8) * SLICES
        bucket_out = [shape((dim, edges), BF16), shape((dim, edges), BF16), shape((dim, negp // 2), BF16), shape((dim, negp // 2), BF16)]
        stage_shape = pltpu.VMEM((SLICES * LANES, LANES), F32)
        t4, v, hb, tb, nk, ns = pl.pallas_call(
            functools.partial(entry_kernel, dim, rows),
            out_shape=[shape((rows * SLICES, LANES)), shape((rows, LANES))] + bucket_out,
            in_specs=[smem()] * 4 + [hbm(), vmem()],
            out_specs=[hbm(), hbm()] + [vmem()] * 4,
            scratch_shapes=[pltpu.VMEM((wide_rows, LANES), F32), pltpu.VMEM((rows, LANES), F32),
                            pltpu.VMEM((2, SLICES * LANES, 4 * LANES), F32), stage_shape, pltpu.VMEM((dim, negp), BF16),
                            pltpu.SemaphoreType.DMA((2,)), pltpu.SemaphoreType.DMA((2,))],
            compiler_params=params(), cost_estimate=cost(40), name='entry',
        )(core, heads[0], tails[0], negs[0], ent_emb.T, ent_ada.reshape(rows // LANES, LANES))

        rfm = jnp.pad(rel_emb.T, ((0, 0), (0, relp - num_rel)))
        vr = jnp.pad(rel_ada, (0, relp - num_rel), constant_values=1.0).reshape(1, relp)
        losses = []
        rel_grads = None
        for s in range(rounds):
            nmine, nother = group_sum(nk, ns)
            if s == 0:
                tail_cols, head_cols = tb, hb
            else:
                tail_cols = lax.ppermute(tb, 'ent', shift(-s))
                head_cols = lax.ppermute(hb, 'ent', shift(s))
            first = s == 0
            outs = [shape((1, LANES)), shape((1, edges)), shape((edges * SLICES, LANES)),
                    shape((half, negp)), shape((half, negp)), shape((half, relp)), shape((half, relp)), shape((relp * SLICES, LANES))]
            args = [core, own_rels[s], weights[s].reshape(1, edges), hb, tail_cols, nmine, nother, rfm, vr]
            if not first:
                outs += [shape((dim, relp)), shape((1, relp))]
                args += list(rel_grads)
            res = pl.pallas_call(
                functools.partial(bucket_kernel, dim, neg_count, num_rel, edges, first),
                out_shape=outs,
                in_specs=[smem()] * 2 + [vmem()] * (len(args) - 2),
                out_specs=[vmem()] * len(outs),
                scratch_shapes=[pltpu.VMEM((dim, negp), BF16), pltpu.VMEM((negp, dim), BF16), pltpu.VMEM((negp, CHUNK), BF16),
                                pltpu.VMEM((negp, CHUNK), F32), pltpu.VMEM((SLICES * LANES, CHUNK), F32), pltpu.VMEM((negp, dim), F32),
                                pltpu.VMEM((relp * SLICES, LANES), F32), stage_shape, pltpu.VMEM((SLICES * LANES, CHUNK), F32),
                                pltpu.VMEM((SLICES * LANES, max(relp, negp)), F32)],
                compiler_params=params(), cost_estimate=cost(40), name='bucket',
            )(*args)
            loss, dp, hg, gk, gs, rk, rs, r4 = res[:8]
            if not first:
                rfm, vr = res[8:]
            losses.append(loss[0, 0])
            gmine, gother = group_sum(gk, gs)
            rel_grads = group_sum(rk, rs)
            if s > 0:
                dp = lax.ppermute(dp, 'ent', shift(s))
            last = s == rounds - 1
            args = [core, heads[s], tails[s], rels[s], negs[s]]
            if not last:
                args += [heads[s + 1], tails[s + 1], negs[s + 1]]
            scalars = len(args)
            args += [t4, v, hg, head_cols, dp, r4, gmine, gother]
            scratch = [pltpu.VMEM((wide_rows, LANES), F32), pltpu.VMEM((rows, LANES), F32), pltpu.VMEM((wide_rows, LANES), F32),
                       stage_shape, pltpu.VMEM((SLICES * LANES, LANES), F32)]
            if last:
                outs = [shape((dim, rows)), shape((rows // LANES, LANES))]
                specs = [hbm(), vmem()]
                scratch += [pltpu.VMEM((2, dim, 4 * LANES), F32)]
            else:
                outs = [shape((rows * SLICES, LANES)), shape((rows, LANES))] + bucket_out
                specs = [hbm(), hbm()] + [vmem()] * 4
                scratch += [pltpu.VMEM((dim, negp), BF16)]
            res = pl.pallas_call(
                functools.partial(update_kernel, dim, rows, edges, last),
                out_shape=outs,
                in_specs=[smem()] * scalars + [hbm()] * 2 + [vmem()] * 6,
                out_specs=specs,
                scratch_shapes=scratch + [pltpu.SemaphoreType.DMA((2,)), pltpu.SemaphoreType.DMA((2,))],
                compiler_params=params(), cost_estimate=cost(60), name='update',
            )(*args)
            if last:
                et, g = res
            else:
                t4, v, hb, tb, nk, ns = res

        even = core[0] == 0
        rg = jnp.where(even, jnp.concatenate(rel_grads, axis=0), jnp.concatenate(rel_grads[::-1], axis=0))
        new_vr = vr + jnp.mean(rg * rg, axis=0, keepdims=True)
        new_r = rfm - LEARN_RATE * rg / jnp.sqrt(new_vr + ADA_EPS)
        return et.T, g.reshape(rows), new_r[:, :num_rel].T, new_vr[0, :num_rel], jnp.stack(losses)[None, :]

    return jax.shard_map(device_fn, mesh=mesh,
                         in_specs=(row_spec, flat_spec, rel_spec, state_spec, edge_spec, edge_spec, edge_spec, edge_spec, rel_spec),
                         out_specs=(row_spec, flat_spec, rel_spec, state_spec, row_spec), check_vma=False)
```

time: 1150 us -> 591 us (0.51)
  other arithmetic: 354 us -> 21.8 us
  local copies, waits for them, and re-layouts: 318 us -> 15.2 us
  Pallas kernels: 0 us -> 269 us
  waiting for transfers between devices: 411 us -> 251 us
  matrix products: 38.7 us -> 0 us
  starting transfers between devices: 5.83 us -> 32.7 us
  between operations: 17.4 us -> 1.13 us
    pallas_call x0 -> x7, Pallas kernels: none -> 269 us  [the longest x3 146 us: device_fn(): pl.pallas_call(functools.partial(update_kernel, dim, rows, edges, last),...]
    psum x6 -> x0, waiting for transfers between devices: 194 us -> none  [the longest x3 170 us: device_fn(): neg_sum = lax.psum(negrow_grad, 'ent')]
    gather x24 -> x0, local copies, waits for them, and re-layouts: 180 us -> none  [the longest x6 53 us: device_fn(): jnp.take(table_bf, head_ids, axis=0)]
    scatter-add x6 -> x0, other arithmetic: 159 us -> none  [the longest x3 114 us: device_fn(): grad_ent = jax.ops.segment_sum(row_grads, row_ids, num_segments=part_rows)]
    convert_element_type x10 -> x1, other arithmetic: 65.7 us -> 0.02 us  [device_fn(): weights = edge_mask[0].astype(F32)]
    concatenate x6 -> x0, local copies, waits for them, and re-layouts: 42.8 us -> none  [the longest x3 31.2 us: device_fn(): jnp.concatenate([head_grad, back_grad, jnp.where(owned[:, None], neg_sum,...]
    reduce_sum x15 -> x1, other arithmetic: 44.5 us -> 2.69 us  [device_fn(): new_vr = vr + jnp.mean(rg * rg, axis=0, keepdims=True)]
    unnamed x104 -> x68, local copies, waits for them, and re-layouts: 48.8 us -> 8.28 us
  transfers between devices with their start and end apart: 12 -> 35, of which waited for: 9 -> 18; matrix products, arithmetic and copies ran while one was open for 20% -> 3% of each run, Pallas kernels for 0% -> 25%
where the time goes in v1:
time: 591 us
  Pallas kernels  269 us (46%)
  waiting for transfers between devices  251 us (42%)
  starting transfers between devices  32.7 us (6%)
  other arithmetic  21.8 us (4%)
  local copies, waits for them, and re-layouts  15.2 us (3%)
    ppermute x9, waiting for transfers between devices, group_sum(): mine = part + lax.ppermute(part, 'ent', cross)  185 us
    pallas_call x3, Pallas kernels, device_fn(): pl.pallas_call(functools.partial(update_kernel, dim, rows, edges, last),...  146 us
    pallas_call x3, Pallas kernels, device_fn(): pl.pallas_call(functools.partial(bucket_kernel, dim, neg_count, num_rel,...  92.5 us
    ppermute x2, waiting for transfers between devices, device_fn(): got = lax.ppermute(jnp.stack([own_tails[s], own_rels[s]]), 'ent', shift(s))  50.2 us
    pallas_call x1, Pallas kernels, device_fn(): pl.pallas_call(functools.partial(entry_kernel, dim, rows), out_shape=[sha...  30.5 us
    ppermute x9, starting transfers between devices, group_sum(): return (mine, lax.ppermute(mine, 'ent', swap))  14.3 us
  transfers between devices with their start and end apart: 35, of which 18 were waited for; matrix products, arithmetic and copies ran while one was open for 3% of the time, Pallas kernels for 25%

profile of v1, /device:TPU:0, one launch (start us, length us, event | category | flops | bytes accessed | tf_op | source)
XLA Modules:
  0.0 590.7 jit_solution(18284710505489357625)
XLA Ops:
  4.8 30.5 %entry.1 = (f32[32768,128]{1,0:T(8,128)}, f32[8192,128]{1,0:T(8,128)}, bf16[400,2048]{1,0:T(8,128)(2,1)}, bf16[400,2048]{1,0:T(8,128)(2,1)}, bf16[400,512]{1,0:T(8,128)(2,1)}, /*index=5*/bf16[400,512]{1,0:T(8,128)(2,1)}) custom-call(s32[1]{0:T(128)} %bitcast.core_ref.refs_0_, s32[2048]{0:T(1024)} %bitcast.55, s32[2048]{0:T(1024)} %bitcast.47, ...), custom_call_target="tpu_custom_call" | custom-call | flops 200000000 | tf_op jit(solution)/shard_map/entry/pallas_call | solution.py:419
  38.7 2.9 collective-permute-start.3
  42.2 3.2 pad.13.refs_7_
  45.4 6.0 %collective-permute-done.3 = bf16[400,512]{1,0:T(8,128)(2,1)S(1)} collective-permute-done((bf16[400,512]{1,0:T(8,128)(2,1)S(1)}, bf16[400,512]{1,0:T(8,128)(2,1)S(1)}, u32[]{:S(2)}, u32[]{:S(2)}) %collective-permute-start.3) | collective-permute-done | bytes 409632 | tf_op jit(solution)/shard_map/ppermute | solution.py:388
  54.0 29.6 %bucket.3 = (f32[1,128]{1,0:T(1,128)}, f32[1,2048]{1,0:T(1,128)}, f32[8192,128]{1,0:T(8,128)}, f32[200,1024]{1,0:T(8,128)}, f32[200,1024]{1,0:T(8,128)}, /*index...) custom-call(s32[1]{0:T(128)} %bitcast.core_ref.refs_0_, s32[2048]{0:T(1024)} %bitcast.49, ...), custom_call_target="tpu_custom_call" | custom-call | flops 200000000 | tf_op jit(solution)/shard_map/bucket/pallas_call | solution.py:448
  84.1 1.8 collective-permute-done.5
  87.2 1.8 collective-permute-start.6
  89.0 18.5 %collective-permute-done.6 = f32[200,1024]{1,0:T(8,128)S(1)} collective-permute-done((f32[200,1024]{1,0:T(8,128)S(1)}, f32[200,1024]{1,0:T(8,128)S(1)}, u32[]{:S(2)}, u32[]{:S(2)}) %collective-permute-start.6) | collective-permute-done | bytes 819232 | tf_op jit(solution)/shard_map/ppermute | solution.py:388
  109.0 1.7 collective-permute-start.13
  110.8 24.9 %collective-permute-done.1 = s32[2,2048]{1,0:T(2,128)S(1)} collective-permute-done((s32[2,2048]{1,0:T(2,128)S(1)}, s32[2,2048]{1,0:T(2,128)S(1)}, u32[]{:S(2)}, u32[]{:S(2)}) %collective-permute-start.1) | collective-permute-done | bytes 16416 | tf_op jit(solution)/shard_map/ppermute | solution.py:407
  137.2 50.3 %update.3 = (f32[32768,128]{1,0:T(8,128)}, f32[8192,128]{1,0:T(8,128)}, bf16[400,2048]{1,0:T(8,128)(2,1)}, bf16[400,2048]{1,0:T(8,128)(2,1)}, bf16[400,512]{1,0:T(8,128)(2,1)}, /*index=5*/bf16[400,512]{1,0:T(8,128)(2,1)}) custom-call(s32[1]{0:T(128)} %bitcast.core_ref.refs_0_, s32[2048]{0:T(1024)} %bitcast.56, s32[2048]{0:T(1024)} %bitcast.48, ...), custom_call_target="tpu_custom_call" | custom-call | flops 300000000 | tf_op jit(solution)/shard_map/update/pallas_call | solution.py:483
  191.7 1.8 collective-permute-start.10
  193.5 23.7 %collective-permute-done.10 = bf16[400,512]{1,0:T(8,128)(2,1)S(1)} collective-permute-done((bf16[400,512]{1,0:T(8,128)(2,1)S(1)}, bf16[400,512]{1,0:T(8,128)(2,1)S(1)}, u32[]{:S(2)}, u32[]{:S(2)}) %collective-permute-start.10) | collective-permute-done | bytes 409632 | tf_op jit(solution)/shard_map/ppermute | solution.py:388
  217.3 1.7 collective-permute-done.11.refs_6_
  219.8 31.5 %bucket.4 = (f32[1,128]{1,0:T(1,128)}, f32[1,2048]{1,0:T(1,128)}, f32[8192,128]{1,0:T(8,128)}, f32[200,1024]{1,0:T(8,128)}, f32[200,1024]{1,0:T(8,128)}, /*index...) custom-call(s32[1]{0:T(128)} %bitcast.core_ref.refs_0_, ...), custom_call_target="tpu_custom_call" | custom-call | flops 200000000 | tf_op jit(solution)/shard_map/bucket/pallas_call | solution.py:448
  255.4 20.8 %collective-permute-done.18 = f32[200,1024]{1,0:T(8,128)S(1)} collective-permute-done((f32[200,1024]{1,0:T(8,128)S(1)}, f32[200,1024]{1,0:T(8,128)S(1)}, u32[]{:S(2)}, u32[]{:S(2)}) %collective-permute-start.18) | collective-permute-done | bytes 819232 | tf_op jit(solution)/shard_map/ppermute | solution.py:388
  276.4 13.6 %collective-permute-start.19 = (f32[200,1024]{1,0:T(8,128)S(1)}, f32[200,1024]{1,0:T(8,128)S(1)}, u32[]{:S(2)}, u32[]{:S(2)}) collective-permute-start(f32[200,1024]{1,0:T(8,128)S(1)} %add.91.refs_14_), channel_id=1, source_target_pairs={{0,1},{1,0},{2,3},{3,2},{4,5},{5,4},{6,7},{7,6}} | collective-permute-start | bytes 2457608 | tf_op jit(solution)/shard_map/ppermute | solution.py:389
  291.5 1.8 collective-permute-start
  293.2 25.3 %collective-permute-done = s32[2,2048]{1,0:T(2,128)S(1)} collective-permute-done((s32[2,2048]{1,0:T(2,128)S(1)}, s32[2,2048]{1,0:T(2,128)S(1)}, u32[]{:S(2)}, u32[]{:S(2)}) %collective-permute-start) | collective-permute-done | bytes 16416 | tf_op jit(solution)/shard_map/ppermute | solution.py:407
  321.2 50.2 %update.4 = (f32[32768,128]{1,0:T(8,128)}, f32[8192,128]{1,0:T(8,128)}, bf16[400,2048]{1,0:T(8,128)(2,1)}, bf16[400,2048]{1,0:T(8,128)(2,1)}, bf16[400,512]{1,0:T(8,128)(2,1)}, /*index=5*/bf16[400,512]{1,0:T(8,128)(2,1)}) custom-call(s32[1]{0:T(128)} %bitcast.core_ref.refs_0_, s32[2048]{0:T(1024)} %bitcast.52, s32[2048]{0:T(1024)} %bitcast.54, ...), custom_call_target="tpu_custom_call" | custom-call | flops 300000000 | tf_op jit(solution)/shard_map/update/pallas_call | solution.py:483
  375.0 1.8 collective-permute-start.22
  376.8 40.4 %collective-permute-done.22 = bf16[400,512]{1,0:T(8,128)(2,1)S(1)} collective-permute-done((bf16[400,512]{1,0:T(8,128)(2,1)S(1)}, bf16[400,512]{1,0:T(8,128)(2,1)S(1)}, u32[]{:S(2)}, u32[]{:S(2)}) %collective-permute-start.22) | collective-permute-done | bytes 409632 | tf_op jit(solution)/shard_map/ppermute | solution.py:388
  417.4 1.7 collective-permute-done.23.refs_6_
  420.0 31.4 %bucket.5 = (f32[1,128]{1,0:T(1,128)}, f32[1,2048]{1,0:T(1,128)}, f32[8192,128]{1,0:T(8,128)}, f32[200,1024]{1,0:T(8,128)}, f32[200,1024]{1,0:T(8,128)}, /*index...) custom-call(s32[1]{0:T(128)} %bitcast.core_ref.refs_0_, ...), custom_call_target="tpu_custom_call" | custom-call | flops 200000000 | tf_op jit(solution)/shard_map/bucket/pallas_call | solution.py:448
  451.9 2.3 collective-permute-done.32
  455.9 1.7 collective-permute-start.27
  458.1 25.2 %collective-permute-done.33 = f32[200,1408]{1,0:T(8,128)S(1)} collective-permute-done((f32[200,1408]{1,0:T(8,128)S(1)}, f32[200,1408]{1,0:T(8,128)S(1)}, u32[]{:S(2)}, u32[]{:S(2)}) %collective-permute-start.33) | collective-permute-done | bytes 1126432 | tf_op jit(solution)/shard_map/ppermute | solution.py:388
  484.5 50.6 %collective-permute-done.30 = f32[200,1024]{1,0:T(8,128)S(1)} collective-permute-done((f32[200,1024]{1,0:T(8,128)S(1)}, f32[200,1024]{1,0:T(8,128)S(1)}, u32[]{:S(2)}, u32[]{:S(2)}) %collective-permute-start.30) | collective-permute-done | bytes 819232 | tf_op jit(solution)/shard_map/ppermute | solution.py:388
  536.3 2.7 collective-permute-done.28.refs_9_
  540.0 45.5 %update.5 = (f32[400,8192]{1,0:T(8,128)}, f32[64,128]{1,0:T(8,128)}) custom-call(s32[1]{0:T(128)} %bitcast.core_ref.refs_0_, s32[2048]{0:T(1024)} %bitcast.58, s32[2048]{0:T(1024)} %bitcast.60, s32[2048]{0:T(1024)} %bitcast.72, s32[1024]{0:T(1024)} %bitcast.66, f32[32768,128]{1,0:T(8,128)} %get-tuple-element.77.refs_5_, ...), custom_call_target="tpu_custom_call" | custom-call | flops 300000000 | tf_op jit(solution)/shard_map/update/pallas_call | solution.py:483
  585.6 2.7 multiply_reduce_fusion
  588.9 1.7 fusion
  (150 shorter events, 40.1 us)
Async XLA Ops:
  35.3 2.3 collective-permute-start.2
  38.7 12.6 %collective-permute-start.3 = (bf16[400,512]{1,0:T(8,128)(2,1)S(1)}, bf16[400,512]{1,0:T(8,128)(2,1)S(1)}, u32[]{:S(2)}, u32[]{:S(2)}) collective-permute-start(bf16[400,512]{1,0:T(8,128)(2,1)S(1)} %add.82), channel_id=1, source_target_pairs={{0,2},{1,3},{2,0},{3,1},{4,6},{5,7},{6,4},{7,5}} | collective-permute-start | bytes 1228808 | tf_op jit(solution)/shard_map/ppermute | solution.py:388
  83.5 2.3 collective-permute-start.5
  83.7 24.0 %collective-permute-start.12 = (f32[200,1408]{1,0:T(8,128)}, f32[200,1408]{1,0:T(8,128)S(1)}, u32[]{:S(2)}, u32[]{:S(2)}) collective-permute-start(f32[200,1408]{1,0:T(8,128)} %get-tuple-element.71), channel_id=1, source_target_pairs={{0,1},{1,0},{2,3},{3,2},{4,5},{5,4},{6,7},{7,6}} | collective-permute-start | bytes 3379208 | tf_op jit(solution)/shard_map/ppermute | solution.py:387
  87.2 20.3 %collective-permute-start.6 = (f32[200,1024]{1,0:T(8,128)S(1)}, f32[200,1024]{1,0:T(8,128)S(1)}, u32[]{:S(2)}, u32[]{:S(2)}) collective-permute-start(f32[200,1024]{1,0:T(8,128)S(1)} %add.84), channel_id=1, source_target_pairs={{0,2},{1,3},{2,0},{3,1},{4,6},{5,7},{6,4},{7,5}} | collective-permute-start | bytes 2457608 | tf_op jit(solution)/shard_map/ppermute | solution.py:388
  107.6 28.7 %collective-permute-start.7 = (f32[200,1024]{1,0:T(8,128)S(1)}, f32[200,1024]{1,0:T(8,128)S(1)}, u32[]{:S(2)}, u32[]{:S(2)}) collective-permute-start(f32[200,1024]{1,0:T(8,128)S(1)} %add.85.refs_14_), channel_id=1, source_target_pairs={{0,1},{1,0},{2,3},{3,2},{4,5},{5,4},{6,7},{7,6}} | collective-permute-start | bytes 2457608 | tf_op jit(solution)/shard_map/ppermute | solution.py:389
  109.0 79.1 %collective-permute-start.13 = (f32[200,1408]{1,0:T(8,128)}, f32[200,1408]{1,0:T(8,128)}, u32[]{:S(2)}, u32[]{:S(2)}) collective-permute-start(f32[200,1408]{1,0:T(8,128)} %add.88), channel_id=1, source_target_pairs={{0,2},{1,3},{2,0},{3,1},{4,6},{5,7},{6,4},{7,5}} | collective-permute-start | bytes 3379208 | tf_op jit(solution)/shard_map/ppermute | solution.py:388
  110.7 25.0 %collective-permute-start.1 = (s32[2,2048]{1,0:T(2,128)S(1)}, s32[2,2048]{1,0:T(2,128)S(1)}, u32[]{:S(2)}, u32[]{:S(2)}) collective-permute-start(s32[2,2048]{1,0:T(2,128)S(1)} %pad_add_fusion.1), channel_id=1, source_target_pairs={{0,1},{1,2},{2,3},{3,0},{4,5},{5,6},{6,7},{7,4}} | collective-permute-start | bytes 49160 | tf_op jit(solution)/shard_map/ppermute | solution.py:407
  187.5 31.5 %collective-permute-start.8 = (bf16[400,2048]{1,0:T(8,128)(2,1)}, bf16[400,2048]{1,0:T(8,128)(2,1)}, u32[]{:S(2)}, u32[]{:S(2)}) collective-permute-start(bf16[400,2048]{1,0:T(8,128)(2,1)} %get-tuple-element.67), channel_id=1, source_target_pairs={{0,3},{1,0},{2,1},{3,2},{4,7},{5,4},{6,5},{7,6}} | collective-permute-start | bytes 4915208 | tf_op jit(solution)/shard_map/ppermute | solution.py:439
  187.6 4.1 collective-permute-start.9
  190.7 26.6 %collective-permute-start.14 = (f32[200,1408]{1,0:T(8,128)S(1)}, f32[200,1408]{1,0:T(8,128)S(1)}, u32[]{:S(2)}, u32[]{:S(2)}) collective-permute-start(f32[200,1408]{1,0:T(8,128)S(1)} %add.89.refs_9_), channel_id=1, source_target_pairs={{0,1},{1,0},{2,3},{3,2},{4,5},{5,4},{6,7},{7,6}} | collective-permute-start | bytes 3379208 | tf_op jit(solution)/shard_map/ppermute | solution.py:389
  191.7 25.4 %collective-permute-start.10 = (bf16[400,512]{1,0:T(8,128)(2,1)S(1)}, bf16[400,512]{1,0:T(8,128)(2,1)S(1)}, u32[]{:S(2)}, u32[]{:S(2)}) collective-permute-start(bf16[400,512]{1,0:T(8,128)(2,1)S(1)} %add.86), channel_id=1, source_target_pairs={{0,2},{1,3},{2,0},{3,1},{4,6},{5,7},{6,4},{7,5}} | collective-permute-start | bytes 1228808 | tf_op jit(solution)/shard_map/ppermute | solution.py:388
  251.4 2.3 collective-permute-start.17
  251.6 38.5 %collective-permute-start.24 = (f32[200,1408]{1,0:T(8,128)}, f32[200,1408]{1,0:T(8,128)S(1)}, u32[]{:S(2)}, u32[]{:S(2)}) collective-permute-start(f32[200,1408]{1,0:T(8,128)} %get-tuple-element.86), channel_id=1, source_target_pairs={{0,1},{1,0},{2,3},{3,2},{4,5},{5,4},{6,7},{7,6}} | collective-permute-start | bytes 3379208 | tf_op jit(solution)/shard_map/ppermute | solution.py:387
  251.9 67.2 %collective-permute-start.15 = (bf16[400,2048]{1,0:T(8,128)(2,1)}, bf16[400,2048]{1,0:T(8,128)(2,1)S(1)}, u32[]{:S(2)}, u32[]{:S(2)}) collective-permute-start(bf16[400,2048]{1,0:T(8,128)(2,1)} %get-tuple-element.66.refs_3_), channel_id=1, source_target_pairs={{0,1},{1,2},{2,3},{3,0},{4,5},{5,6},{6,7},{7,4}} | collective-permute-start | bytes 4915208 | tf_op jit(solution)/shard_map/ppermute | solution.py:440
  255.1 21.1 %collective-permute-start.18 = (f32[200,1024]{1,0:T(8,128)S(1)}, f32[200,1024]{1,0:T(8,128)S(1)}, u32[]{:S(2)}, u32[]{:S(2)}) collective-permute-start(f32[200,1024]{1,0:T(8,128)S(1)} %add.90), channel_id=1, source_target_pairs={{0,2},{1,3},{2,0},{3,1},{4,6},{5,7},{6,4},{7,5}} | collective-permute-start | bytes 2457608 | tf_op jit(solution)/shard_map/ppermute | solution.py:388
  276.4 42.8 %collective-permute-start.19 = (f32[200,1024]{1,0:T(8,128)S(1)}, f32[200,1024]{1,0:T(8,128)S(1)}, u32[]{:S(2)}, u32[]{:S(2)}) collective-permute-start(f32[200,1024]{1,0:T(8,128)S(1)} %add.91.refs_14_), channel_id=1, source_target_pairs={{0,1},{1,0},{2,3},{3,2},{4,5},{5,4},{6,7},{7,6}} | collective-permute-start | bytes 2457608 | tf_op jit(solution)/shard_map/ppermute | solution.py:389
  291.1 80.6 %collective-permute-start.25 = (f32[200,1408]{1,0:T(8,128)}, f32[200,1408]{1,0:T(8,128)}, u32[]{:S(2)}, u32[]{:S(2)}) collective-permute-start(f32[200,1408]{1,0:T(8,128)} %add.94), channel_id=1, source_target_pairs={{0,2},{1,3},{2,0},{3,1},{4,6},{5,7},{6,4},{7,5}} | collective-permute-start | bytes 3379208 | tf_op jit(solution)/shard_map/ppermute | solution.py:388
  291.5 27.0 %collective-permute-start = (s32[2,2048]{1,0:T(2,128)S(1)}, s32[2,2048]{1,0:T(2,128)S(1)}, u32[]{:S(2)}, u32[]{:S(2)}) collective-permute-start(s32[2,2048]{1,0:T(2,128)S(1)} %pad_add_fusion), channel_id=1, source_target_pairs={{0,2},{1,3},{2,0},{3,1},{4,6},{5,7},{6,4},{7,5}} | collective-permute-start | bytes 49160 | tf_op jit(solution)/shard_map/ppermute | solution.py:407
  293.2 25.9 %collective-permute-start.16 = (f32[1,2048]{1,0:T(1,128)S(1)}, f32[1,2048]{1,0:T(1,128)S(1)}, u32[]{:S(2)}, u32[]{:S(2)}) collective-permute-start(f32[1,2048]{1,0:T(1,128)S(1)} %copy-done.33), channel_id=1, source_target_pairs={{0,1},{1,2},{2,3},{3,0},{4,5},{5,6},{6,7},{7,4}} | collective-permute-start | bytes 24584 | tf_op jit(solution)/shard_map/ppermute | solution.py:466
  371.4 47.7 %collective-permute-start.20 = (bf16[400,2048]{1,0:T(8,128)(2,1)}, bf16[400,2048]{1,0:T(8,128)(2,1)}, u32[]{:S(2)}, u32[]{:S(2)}) collective-permute-start(bf16[400,2048]{1,0:T(8,128)(2,1)} %get-tuple-element.80), channel_id=1, source_target_pairs={{0,2},{1,3},{2,0},{3,1},{4,6},{5,7},{6,4},{7,5}} | collective-permute-start | bytes 4915208 | tf_op jit(solution)/shard_map/ppermute | solution.py:439
  371.7 3.2 collective-permute-start.21
  374.4 43.0 %collective-permute-start.26 = (f32[200,1408]{1,0:T(8,128)S(1)}, f32[200,1408]{1,0:T(8,128)S(1)}, u32[]{:S(2)}, u32[]{:S(2)}) collective-permute-start(f32[200,1408]{1,0:T(8,128)S(1)} %add.95.refs_9_), channel_id=1, source_target_pairs={{0,1},{1,0},{2,3},{3,2},{4,5},{5,4},{6,7},{7,6}} | collective-permute-start | bytes 3379208 | tf_op jit(solution)/shard_map/ppermute | solution.py:389
  375.0 42.2 %collective-permute-start.22 = (bf16[400,512]{1,0:T(8,128)(2,1)S(1)}, bf16[400,512]{1,0:T(8,128)(2,1)S(1)}, u32[]{:S(2)}, u32[]{:S(2)}) collective-permute-start(bf16[400,512]{1,0:T(8,128)(2,1)S(1)} %add.92), channel_id=1, source_target_pairs={{0,2},{1,3},{2,0},{3,1},{4,6},{5,7},{6,4},{7,5}} | collective-permute-start | bytes 1228808 | tf_op jit(solution)/shard_map/ppermute | solution.py:388
  451.4 2.8 collective-permute-start.32
  451.6 6.1 %collective-permute-start.29 = (f32[200,1024]{1,0:T(8,128)}, f32[200,1024]{1,0:T(8,128)S(1)}, u32[]{:S(2)}, u32[]{:S(2)}) collective-permute-start(f32[200,1024]{1,0:T(8,128)} %get-tuple-element.91), channel_id=1, source_target_pairs={{0,1},{1,0},{2,3},{3,2},{4,5},{5,4},{6,7},{7,6}} | collective-permute-start | bytes 2457608 | tf_op jit(solution)/shard_map/ppermute | solution.py:387
  455.6 27.7 %collective-permute-start.33 = (f32[200,1408]{1,0:T(8,128)S(1)}, f32[200,1408]{1,0:T(8,128)S(1)}, u32[]{:S(2)}, u32[]{:S(2)}) collective-permute-start(f32[200,1408]{1,0:T(8,128)S(1)} %add.98), channel_id=1, source_target_pairs={{0,2},{1,3},{2,0},{3,1},{4,6},{5,7},{6,4},{7,5}} | collective-permute-start | bytes 3379208 | tf_op jit(solution)/shard_map/ppermute | solution.py:388
  455.9 80.4 %collective-permute-start.27 = (bf16[400,2048]{1,0:T(8,128)(2,1)S(1)}, bf16[400,2048]{1,0:T(8,128)(2,1)}, u32[]{:S(2)}, u32[]{:S(2)}) collective-permute-start(bf16[400,2048]{1,0:T(8,128)(2,1)S(1)} %copy-done.7), channel_id=1, source_target_pairs={{0,2},{1,3},{2,0},{3,1},{4,6},{5,7},{6,4},{7,5}} | collective-permute-start | bytes 4915208 | tf_op jit(solution)/shard_map/ppermute | solution.py:440
  457.8 77.3 %collective-permute-start.30 = (f32[200,1024]{1,0:T(8,128)S(1)}, f32[200,1024]{1,0:T(8,128)S(1)}, u32[]{:S(2)}, u32[]{:S(2)}) collective-permute-start(f32[200,1024]{1,0:T(8,128)S(1)} %add.96), channel_id=1, source_target_pairs={{0,2},{1,3},{2,0},{3,1},{4,6},{5,7},{6,4},{7,5}} | collective-permute-start | bytes 2457608 | tf_op jit(solution)/shard_map/ppermute | solution.py:388
  484.5 101.1 %collective-permute-start.34 = (f32[200,1408]{1,0:T(8,128)}, f32[200,1408]{1,0:T(8,128)}, u32[]{:S(2)}, u32[]{:S(2)}) collective-permute-start(f32[200,1408]{1,0:T(8,128)} %add.99), channel_id=1, source_target_pairs={{0,1},{1,0},{2,3},{3,2},{4,5},{5,4},{6,7},{7,6}} | collective-permute-start | bytes 3379208 | tf_op jit(solution)/shard_map/ppermute | solution.py:389
  535.3 3.7 collective-permute-start.31
  535.3 3.7 collective-permute-start.28
  (37 other events, 588.7 us)

commit v2 on v1

v2 whole, which is shorter than its diff:
```python
import functools

import jax
import jax.numpy as jnp
from jax import lax
from jax.experimental import pallas as pl
from jax.experimental.pallas import tpu as pltpu
from jax.sharding import PartitionSpec as P


LEARN_RATE = 0.05
ADA_EPS = 1e-10
LANES = 128
SLICES = 4
CHUNK = 256
BATCH = 4
F32 = jnp.float32
BF16 = jnp.bfloat16


def ceil_to(value, unit):
    return -(-value // unit) * unit


def vmem():
    return pl.BlockSpec(memory_space=pltpu.VMEM)


def smem():
    return pl.BlockSpec(memory_space=pltpu.SMEM)


def hbm():
    return pl.BlockSpec(memory_space=pltpu.MemorySpace.HBM)


def four(index):
    return pl.multiple_of(index, SLICES)


def gather_rows(src, ids, base, stage, count):
    for k in range(count):
        stage[pl.ds(SLICES * k, SLICES), :] = src[pl.ds(four(ids[base + k]), SLICES), :]


def stage_cols(stage, slice_no):
    return stage[pl.ds(slice_no, LANES, stride=SLICES), :].T


def add_rows(acc, ids, base, rows, row_base, count):
    for first in range(0, count, BATCH):
        index = [ids[base + first + k] for k in range(BATCH)]
        grads = [rows[pl.ds(four(row_base + SLICES * (first + k)), SLICES), :] for k in range(BATCH)]
        total = [acc[pl.ds(four(index[k]), SLICES), :] + grads[k] for k in range(BATCH)]
        for k in range(1, BATCH):
            for earlier in range(k):
                total[k] = total[k] + jnp.where(index[earlier] == index[k], grads[earlier], 0.0)
        for k in range(BATCH):
            acc[pl.ds(four(index[k]), SLICES), :] = total[k]


def zero_rows(ref, step=1024):
    rows = ref.shape[0]
    whole = rows // step

    def body(i, _):
        ref[pl.ds(pl.multiple_of(i * step, 8), step), :] = jnp.zeros((step, LANES), ref.dtype)
        return 0

    lax.fori_loop(0, whole, body, 0)
    if rows % step:
        ref[pl.ds(whole * step, rows % step), :] = jnp.zeros((rows % step, LANES), ref.dtype)


def gather_out(dim, table, ids, out, stage, count):
    def body(b, _):
        gather_rows(table, ids, b * LANES, stage, LANES)
        cols = pl.ds(pl.multiple_of(b * LANES, LANES), LANES)
        for j in range(SLICES):
            size = min(LANES, dim - j * LANES)
            out[pl.ds(j * LANES, size), cols] = stage_cols(stage, j)[:size].astype(BF16)
        return 0

    lax.fori_loop(0, count // LANES, body, 0)


def gather_negs(dim, core, table, negs, nk, ns, nbuf, stage):
    half = nbuf.shape[1] // 2
    gather_out(dim, table, negs, nbuf, stage, nbuf.shape[1])
    nk[...] = nbuf[:, pl.ds(pl.multiple_of(core * half, LANES), half)]
    ns[...] = nbuf[:, pl.ds(pl.multiple_of((1 - core) * half, LANES), half)]


def entry_kernel(dim, rows, core_ref, negs, et, g, t4_out, v_out, nk, ns,
                 t4, v, inbuf, stage, nbuf, in_sem, out_sem):
    cols = inbuf.shape[2]
    steps = rows // cols
    per = cols // LANES

    def fetch(step, slot):
        return pltpu.make_async_copy(et.at[:, pl.ds(pl.multiple_of(step * cols, LANES), cols)],
                                     inbuf.at[slot, pl.ds(0, dim)], in_sem.at[slot])

    fetch(0, 0).start()
    for slot in range(2):
        inbuf[slot, pl.ds(dim, SLICES * LANES - dim), :] = jnp.zeros((SLICES * LANES - dim, cols), F32)
    t4[pl.ds(rows * SLICES, 32), :] = jnp.zeros((32, LANES), F32)

    def body(step, _):
        slot = lax.rem(step, 2)

        @pl.when(step + 1 < steps)
        def _():
            fetch(step + 1, 1 - slot).start()

        fetch(step, slot).wait()
        for b in range(per):
            row0 = (step * per + b) * LANES
            for j in range(SLICES):
                t4[pl.ds(SLICES * row0 + j, LANES, stride=SLICES), :] = inbuf[slot, pl.ds(j * LANES, LANES), pl.ds(b * LANES, LANES)].T
            v[pl.ds(pl.multiple_of(row0, 8), LANES), :] = jnp.broadcast_to(g[pl.ds(step * per + b, 1), :], (LANES, LANES)).T
        return 0

    lax.fori_loop(0, steps, body, 0)
    save_t = pltpu.make_async_copy(t4.at[pl.ds(0, rows * SLICES)], t4_out, out_sem.at[0])
    save_v = pltpu.make_async_copy(v, v_out, out_sem.at[1])
    save_t.start()
    save_v.start()
    gather_negs(dim, core_ref[0], t4, negs, nk, ns, nbuf, stage)
    save_t.wait()
    save_v.wait()


def gather_kernel(dim, lists, *refs):
    ids, t4_in, outs = refs[:lists], refs[lists], refs[lists + 1:2 * lists + 1]
    t4, stage, sem = refs[2 * lists + 1:]
    load = pltpu.make_async_copy(t4_in, t4, sem)
    load.start()
    load.wait()
    for i in range(lists):
        gather_out(dim, t4, ids[i], outs[i], stage, outs[i].shape[1])


def query_kernel(dim, edges, first, *refs):
    if first:
        core_ref, rel, hb, rfm, q_out, r_out, r4, stage, fm = refs
    else:
        core_ref, rel, hb, rfm_in, vr_in, rmine, rother, q_out, r_out, r4, rfm, vr, stage, fm = refs
        core = core_ref[0]
    half = dim // 2
    relp = rfm.shape[1]
    tops = SLICES * LANES
    if not first:
        fm[pl.ds(pl.multiple_of(core * half, 8), half), :] = rmine[...]
        fm[pl.ds(pl.multiple_of((1 - core) * half, 8), half), :] = rother[...]
        grad = fm[pl.ds(0, dim), :]
        vr[...] = vr_in[...] + jnp.sum(grad * grad, axis=0, keepdims=True) / dim
        rate = LEARN_RATE / jnp.sqrt(vr[...] + ADA_EPS)
        rfm[...] = rfm_in[...] - fm[pl.ds(0, dim), :] * rate
    fm[pl.ds(dim, tops - dim), pl.ds(0, LANES)] = jnp.zeros((tops - dim, LANES), F32)
    for b in range(relp // LANES):
        for j in range(SLICES):
            if (j + 1) * LANES <= dim:
                block = rfm[pl.ds(j * LANES, LANES), pl.ds(b * LANES, LANES)]
            else:
                fm[pl.ds(j * LANES, dim - j * LANES), pl.ds(0, LANES)] = rfm[pl.ds(j * LANES, dim - j * LANES), pl.ds(b * LANES, LANES)]
                block = fm[pl.ds(j * LANES, LANES), pl.ds(0, LANES)]
            r4[pl.ds(SLICES * b * LANES + j, LANES, stride=SLICES), :] = block.T

    def step(b, _):
        cols = pl.ds(pl.multiple_of(b * LANES, LANES), LANES)
        gather_rows(r4, rel, b * LANES, stage, LANES)
        for j in range(SLICES):
            size = min(LANES, dim - j * LANES)
            r_out[pl.ds(j * LANES, size), cols] = stage_cols(stage, j)[:size]
        h = hb[:, cols].astype(F32)
        r_re, r_im = r_out[pl.ds(0, half), cols], r_out[pl.ds(half, half), cols]
        q_out[pl.ds(0, half), cols] = h[:half] * r_re - h[half:] * r_im
        q_out[pl.ds(half, half), cols] = h[:half] * r_im + h[half:] * r_re
        return 0

    lax.fori_loop(0, edges // LANES, step, 0)


def place_negs(core, nb, nfull, nother):
    nhalf = nfull.shape[1]
    nb[:, pl.ds(pl.multiple_of(core * nhalf, LANES), nhalf)] = nfull[...]
    nb[:, pl.ds(pl.multiple_of((1 - core) * nhalf, LANES), nhalf)] = nother[...]


def score_kernel(dim, neg_count, edges, core_ref, w, q, tb, nfull, nother,
                 loss, dp_out, ds, nk, ns, nb, nbt, sc, ng, fm):
    core = core_ref[0]
    half = dim // 2
    negp = nb.shape[1]
    place_negs(core, nb, nfull, nother)
    for b in range(negp // LANES):
        nbt[pl.ds(b * LANES, LANES), :] = nb[:, pl.ds(b * LANES, LANES)].astype(F32).T.astype(BF16)
    ng[...] = jnp.zeros(ng.shape, F32)
    ds[pl.ds(neg_count, negp - neg_count), :] = jnp.zeros((negp - neg_count, edges), BF16)

    def step(c, loss_row):
        cols = pl.ds(pl.multiple_of(c * CHUNK, LANES), CHUNK)
        qb = q[:, cols].astype(BF16)
        pos = jnp.sum(q[:, cols] * tb[:, cols].astype(F32), axis=0, keepdims=True)
        sc[...] = lax.dot_general(nbt[...], qb, (((1,), (0,)), ((), ())), preferred_element_type=F32)
        top = jnp.maximum(pos, jnp.max(sc[pl.ds(0, neg_count), :], axis=0, keepdims=True))
        pos_exp = jnp.exp(pos - top)
        norm = pos_exp
        part = 200
        for i in range(0, neg_count, part):
            size = min(part, neg_count - i)
            e = jnp.exp(sc[pl.ds(i, size), :] - top)
            sc[pl.ds(i, size), :] = e
            norm = norm + jnp.sum(e, axis=0, keepdims=True)
        wt = w[:, cols]
        loss_row = loss_row + wt * (top + jnp.log(norm) - pos)
        dp_out[:, cols] = wt * (pos_exp / norm - 1.0)
        scale = wt / norm
        ds[pl.ds(0, neg_count), cols] = (sc[pl.ds(0, neg_count), :] * scale).astype(BF16)
        ng[...] += lax.dot_general(ds[:, cols], qb, (((1,), (1,)), ((), ())), preferred_element_type=F32)
        return loss_row

    loss_row = lax.fori_loop(0, edges // CHUNK, step, jnp.zeros((1, CHUNK), F32))
    loss[...] = jnp.broadcast_to(jnp.sum(loss_row, axis=1, keepdims=True) / edges, loss.shape)
    for b in range(negp // LANES):
        for j in range(SLICES):
            size = min(LANES, dim - j * LANES)
            fm[pl.ds(j * LANES, size), pl.ds(b * LANES, LANES)] = ng[pl.ds(b * LANES, LANES), pl.ds(j * LANES, size)].T
    nk[...] = fm[pl.ds(pl.multiple_of(core * half, 8), half), :]
    ns[...] = fm[pl.ds(pl.multiple_of((1 - core) * half, 8), half), :]


def grad_kernel(dim, edges, core_ref, rel, ds, dp, tb, hb, r, nfull, nother,
                hg, rk, rs, nb, racc, stage, qs, fm):
    core = core_ref[0]
    half = dim // 2
    relp = rk.shape[1]
    tops = SLICES * LANES
    place_negs(core, nb, nfull, nother)
    zero_rows(racc)
    qs[pl.ds(dim, tops - dim), :] = jnp.zeros((tops - dim, CHUNK), F32)

    def step(c, _):
        cols = pl.ds(pl.multiple_of(c * CHUNK, LANES), CHUNK)
        gq = lax.dot_general(nb[...], ds[:, cols], (((1,), (0,)), ((), ())), preferred_element_type=F32) + dp[:, cols] * tb[:, cols].astype(F32)
        g_re, g_im = gq[:half], gq[half:]
        h = hb[:, cols].astype(F32)
        h_re, h_im = h[:half], h[half:]
        qs[pl.ds(0, half), :] = g_re * h_re + g_im * h_im
        qs[pl.ds(half, half), :] = g_im * h_re - g_re * h_im
        for b in range(CHUNK // LANES):
            for j in range(SLICES):
                stage[pl.ds(SLICES * b * LANES + j, LANES, stride=SLICES), :] = qs[pl.ds(j * LANES, LANES), pl.ds(b * LANES, LANES)].T
        r_re, r_im = r[pl.ds(0, half), cols], r[pl.ds(half, half), cols]
        qs[pl.ds(0, half), :] = g_re * r_re + g_im * r_im
        qs[pl.ds(half, half), :] = g_im * r_re - g_re * r_im
        for b in range(CHUNK // LANES):
            for j in range(SLICES):
                hg[pl.ds(SLICES * (c * CHUNK + b * LANES) + j, LANES, stride=SLICES), :] = qs[pl.ds(j * LANES, LANES), pl.ds(b * LANES, LANES)].T
        add_rows(racc, rel, c * CHUNK, stage, 0, CHUNK)
        return 0

    lax.fori_loop(0, edges // CHUNK, step, 0)
    for b in range(relp // LANES):
        for j in range(SLICES):
            size = min(LANES, dim - j * LANES)
            fm[pl.ds(j * LANES, size), pl.ds(b * LANES, LANES)] = racc[pl.ds(SLICES * b * LANES + j, LANES, stride=SLICES), :].T[:size]
    rk[...] = fm[pl.ds(pl.multiple_of(core * half, 8), half), :]
    rs[...] = fm[pl.ds(pl.multiple_of((1 - core) * half, 8), half), :]


def unstage(rt, stage):
    for j in range(SLICES):
        stage[pl.ds(j, LANES, stride=SLICES), :] = rt[pl.ds(j * LANES, LANES), :].T


def scatter_kernel(dim, rows, edges, own, *refs):
    if own:
        heads, tails, hg, dp, q, acc_out, acc, stage, rt, sem = refs
    else:
        heads, tails, rel, hg, dp, hb_in, r4, acc_out, acc, stage, rt, sem = refs
    half = dim // 2
    tops = SLICES * LANES
    zero_rows(acc)
    rt[pl.ds(dim, tops - dim), :] = jnp.zeros((tops - dim, LANES), F32)

    def head_step(b, _):
        add_rows(acc, heads, b * 32, hg, b * 32 * SLICES, 32)
        return 0

    lax.fori_loop(0, edges // 32, head_step, 0)

    def tail_step(b, _):
        cols = pl.ds(pl.multiple_of(b * LANES, LANES), LANES)
        scale = dp[:, cols]
        if own:
            rt[pl.ds(0, dim), :] = q[:, cols] * scale
        else:
            gather_rows(r4, rel, b * LANES, stage, LANES)
            for j in range(SLICES):
                rt[pl.ds(j * LANES, LANES), :] = stage_cols(stage, j)
            h = hb_in[:, cols].astype(F32)
            r_re, r_im = rt[pl.ds(0, half), :], rt[pl.ds(half, half), :]
            q_re = scale * (h[:half] * r_re - h[half:] * r_im)
            q_im = scale * (h[:half] * r_im + h[half:] * r_re)
            rt[pl.ds(0, half), :] = q_re
            rt[pl.ds(half, half), :] = q_im
        unstage(rt, stage)
        add_rows(acc, tails, b * LANES, stage, 0, LANES)
        return 0

    lax.fori_loop(0, edges // LANES, tail_step, 0)
    save = pltpu.make_async_copy(acc.at[pl.ds(0, rows * SLICES)], acc_out, sem)
    save.start()
    save.wait()


def update_kernel(dim, rows, last, *refs):
    if last:
        (core_ref, negs, t4_in, v_in, acc_in, nmine, nother,
         et_out, g_out, t4, v, acc, stage, rt, outbuf, in_sem, out_sem) = refs
    else:
        (core_ref, negs, tails_n, negs_n, t4_in, v_in, acc_in, nmine, nother,
         t4_out, v_out, tb, nk, ns, t4, v, acc, stage, rt, nbuf, in_sem, out_sem) = refs
    core = core_ref[0]
    half = dim // 2
    tops = SLICES * LANES
    load_a = pltpu.make_async_copy(acc_in, acc.at[pl.ds(0, rows * SLICES)], in_sem.at[2])
    load_t = pltpu.make_async_copy(t4_in, t4.at[pl.ds(0, rows * SLICES)], in_sem.at[0])
    load_v = pltpu.make_async_copy(v_in, v, in_sem.at[1])
    load_a.start()
    load_t.start()
    load_v.start()
    acc[pl.ds(rows * SLICES, 32), :] = jnp.zeros((32, LANES), F32)
    t4[pl.ds(rows * SLICES, 32), :] = jnp.zeros((32, LANES), F32)
    rt[pl.ds(dim, tops - dim), :] = jnp.zeros((tops - dim, LANES), F32)
    load_a.wait()

    def neg_step(b, _):
        cols = pl.ds(pl.multiple_of(b * LANES, LANES), LANES)
        rt[pl.ds(pl.multiple_of(core * half, 8), half), :] = nmine[:, cols]
        rt[pl.ds(pl.multiple_of((1 - core) * half, 8), half), :] = nother[:, cols]
        unstage(rt, stage)
        add_rows(acc, negs, b * LANES, stage, 0, LANES)
        return 0

    lax.fori_loop(0, nmine.shape[1] // LANES, neg_step, 0)
    load_t.wait()
    load_v.wait()

    def ada_rows(row0, block):
        parts = [acc[pl.ds(SLICES * row0 + j, block, stride=SLICES), :] for j in range(SLICES)]
        square = parts[0] * parts[0]
        for j in range(1, SLICES):
            square = square + parts[j] * parts[j]
        vrows = pl.ds(pl.multiple_of(row0, 8), block)
        new_v = v[vrows, :] + jnp.sum(square, axis=1, keepdims=True) / dim
        v[vrows, :] = new_v
        rate = LEARN_RATE / jnp.sqrt(new_v + ADA_EPS)
        for j in range(SLICES):
            where = pl.ds(SLICES * row0 + j, block, stride=SLICES)
            t4[where, :] = t4[where, :] - acc[where, :] * rate

    if not last:
        def ada_step(b, _):
            ada_rows(b * LANES, LANES)
            return 0

        lax.fori_loop(0, rows // LANES, ada_step, 0)
        save_v = pltpu.make_async_copy(v, v_out, out_sem.at[1])
        save_t = pltpu.make_async_copy(t4.at[pl.ds(0, rows * SLICES)], t4_out, out_sem.at[0])
        save_v.start()
        gather_negs(dim, core, t4, negs_n, nk, ns, nbuf, stage)
        save_t.start()
        gather_out(dim, t4, tails_n, tb, stage, tb.shape[1])
        save_t.wait()
        save_v.wait()
        return

    width = outbuf.shape[2]
    per = width // LANES
    steps = rows // width

    def save(step, slot):
        return pltpu.make_async_copy(outbuf.at[slot], et_out.at[:, pl.ds(pl.multiple_of(step * width, LANES), width)], out_sem.at[slot])

    def exit_step(step, _):
        slot = lax.rem(step, 2)

        @pl.when(step >= 2)
        def _():
            save(step - 2, slot).wait()

        for b in range(per):
            row0 = (step * per + b) * LANES
            ada_rows(row0, LANES)
            for j in range(SLICES):
                size = min(LANES, dim - j * LANES)
                outbuf[slot, pl.ds(j * LANES, size), pl.ds(b * LANES, LANES)] = t4[pl.ds(SLICES * row0 + j, LANES, stride=SLICES), :].T[:size]
            g_out[pl.ds(step * per + b, 1), :] = v[pl.ds(pl.multiple_of(row0, 8), LANES), :].T[:1]
        save(step, slot).start()
        return 0

    lax.fori_loop(0, steps, exit_step, 0)
    save(steps - 2, (steps - 2) % 2).wait()
    save(steps - 1, (steps - 1) % 2).wait()


def params():
    return pltpu.CompilerParams(vmem_limit_bytes=63 * 1024 * 1024)


def cost(micros):
    return pl.CostEstimate(flops=int(micros * 5e6), bytes_accessed=0, transcendentals=0)


def shape(dims, dtype=F32):
    return jax.ShapeDtypeStruct(dims, dtype)


def solution(mesh):
    ent_size = mesh.shape['ent']
    row_spec = P(('sweep', 'ent'), None)
    flat_spec = P(('sweep', 'ent'))
    rel_spec = P('sweep', None)
    state_spec = P('sweep')
    edge_spec = P(('sweep', 'ent'), None, None)
    swap = [(i, i ^ 1) for i in range(ent_size)]
    cross = [(i, i ^ 2) for i in range(ent_size)]

    def shift(amount):
        return [(i, (i + amount) % ent_size) for i in range(ent_size)]

    tie = lax.optimization_barrier

    def chip_sum(keep, send):
        return keep + lax.ppermute(send, 'ent', swap)

    def send(value, pairs):
        return lax.ppermute(value, 'ent', pairs)

    def link(part):
        return send(part, cross)

    def finish(part, got):
        mine = part + got
        return mine, lax.ppermute(mine, 'ent', swap)

    def device_fn(ent_emb, ent_ada, rel_emb, rel_ada, head_idx, tail_idx, rel_idx, edge_mask, neg_idx):
        rows, dim = ent_emb.shape
        num_rel = rel_emb.shape[0]
        _, rounds, edges = head_idx.shape
        neg_count = neg_idx.shape[1]
        negp = ceil_to(neg_count, 2 * LANES)
        relp = ceil_to(num_rel, LANES)
        half = dim // 2
        my_dev = lax.axis_index('ent')
        core = (my_dev % 2).reshape(1)

        heads = [head_idx[0, s] * SLICES for s in range(rounds)]
        own_tails = [tail_idx[0, s] * SLICES for s in range(rounds)]
        own_rels = [rel_idx[0, s] * SLICES for s in range(rounds)]
        tails, rels = [own_tails[0]], [own_rels[0]]
        for s in range(1, rounds):
            got = lax.ppermute(jnp.stack([own_tails[s], own_rels[s]]), 'ent', shift(s))
            tails.append(got[0])
            rels.append(got[1])
        owned = (neg_idx // rows) == my_dev
        neg_local = jnp.where(owned, neg_idx % rows, rows) * SLICES
        neg_local = jnp.pad(neg_local, ((0, 0), (0, negp - neg_count)), constant_values=rows * SLICES)
        negs = [neg_local[s] for s in range(rounds)]
        weights = edge_mask[0].astype(F32)

        wide_rows = (rows + 8) * SLICES
        stage_shape = pltpu.VMEM((SLICES * LANES, LANES), F32)
        square_shape = pltpu.VMEM((SLICES * LANES, LANES), F32)
        table_shape = pltpu.VMEM((wide_rows, LANES), F32)
        cols_bf = shape((dim, edges), BF16)
        neg_half = shape((dim, negp // 2), BF16)

        def call(kernel, args, kinds, outs, out_kinds, scratch, micros):
            places = {'s': smem, 'h': hbm, 'v': vmem}
            return pl.pallas_call(
                kernel, out_shape=outs, in_specs=[places[k]() for k in kinds], out_specs=[places[k]() for k in out_kinds],
                scratch_shapes=scratch, compiler_params=params(), cost_estimate=cost(micros))(*args)

        def gather(lists, t4):
            return call(functools.partial(gather_kernel, dim, len(lists)), lists + [t4], 's' * len(lists) + 'h',
                        [cols_bf] * len(lists), 'v' * len(lists),
                        [pltpu.VMEM((rows * SLICES, LANES), F32), stage_shape, pltpu.SemaphoreType.DMA], 6 + 5 * len(lists))

        t4, v, nk, ns = call(
            functools.partial(entry_kernel, dim, rows), [core, negs[0], ent_emb.T, ent_ada.reshape(rows // LANES, LANES)], 'sshv',
            [shape((rows * SLICES, LANES)), shape((rows, LANES)), neg_half, neg_half], 'hhvv',
            [table_shape, pltpu.VMEM((rows, LANES), F32), pltpu.VMEM((2, SLICES * LANES, 4 * LANES), F32), stage_shape,
             pltpu.VMEM((dim, negp), BF16), pltpu.SemaphoreType.DMA((2,)), pltpu.SemaphoreType.DMA((2,))], 20)

        rfm = jnp.pad(rel_emb.T, ((0, 0), (0, relp - num_rel)))
        vr = jnp.pad(rel_ada, (0, relp - num_rel), constant_values=1.0).reshape(1, relp)
        losses = []
        rel_grads = None
        for s in range(rounds):
            first, last = s == 0, s == rounds - 1
            neg_part = chip_sum(nk, ns)
            if first:
                neg_part, t4, tails, rels = tie((neg_part, t4, tails, rels))
                neg_got = link(neg_part)
                tail_cols, hb = gather([tails[0], heads[0]], t4)
                head_cols = hb
                neg_got, hb = tie((neg_got, hb))
            else:
                neg_part, t4, tb = tie((neg_part, t4, tb))
                neg_got = link(neg_part)
                tail_cols = send(tb, shift(-s))
                hb, = gather([heads[s]], t4)
                head_cols = send(hb, shift(s))
                rel_got, hb = tie((rel_got, hb))
                rel_grads = finish(rel_part, rel_got)
            wide = shape((dim, edges))
            outs = [wide, wide, shape((relp * SLICES, LANES))]
            args = [core, own_rels[s], hb, rfm]
            if not first:
                outs += [shape((dim, relp)), shape((1, relp))]
                args += [vr] + list(rel_grads)
            res = call(functools.partial(query_kernel, dim, edges, first), args, 'ss' + 'v' * (len(args) - 2), outs, 'v' * len(outs),
                       [stage_shape, pltpu.VMEM((SLICES * LANES, relp), F32)], 10)
            q, r, r4 = res[:3]
            neg_got, q = tie((neg_got, q))
            nmine, nother = finish(neg_part, neg_got)
            if not first:
                rfm, vr = res[3:]
            loss, dp, ds, gk, gs = call(
                functools.partial(score_kernel, dim, neg_count, edges), [core, weights[s].reshape(1, edges), q, tail_cols, nmine, nother], 'svvvvv',
                [shape((1, LANES)), shape((1, edges)), shape((negp, edges), BF16), shape((half, negp)), shape((half, negp))], 'vvvvv',
                [pltpu.VMEM((dim, negp), BF16), pltpu.VMEM((negp, dim), BF16), pltpu.VMEM((negp, CHUNK), F32),
                 pltpu.VMEM((negp, dim), F32), pltpu.VMEM((SLICES * LANES, negp), F32)], 15)
            losses.append(loss[0, 0])
            neg_part = chip_sum(gk, gs)
            neg_part, ds = tie((neg_part, ds))
            neg_got = link(neg_part)
            hg, rk, rs = call(
                functools.partial(grad_kernel, dim, edges), [core, own_rels[s], ds, dp, tail_cols, hb, r, nmine, nother], 'ssvvvvvvv',
                [shape((edges * SLICES, LANES)), shape((half, relp)), shape((half, relp))], 'vvv',
                [pltpu.VMEM((dim, negp), BF16), pltpu.VMEM((relp * SLICES, LANES), F32), pltpu.VMEM((SLICES * CHUNK, LANES), F32),
                 pltpu.VMEM((SLICES * LANES, CHUNK), F32), pltpu.VMEM((SLICES * LANES, relp), F32)], 15)
            rel_part = chip_sum(rk, rs)
            rel_part, hg = tie((rel_part, hg))
            rel_got = link(rel_part)
            if first:
                args, kinds = [heads[s], tails[s], hg, dp, q], 'ssvvv'
            else:
                dp = lax.ppermute(dp, 'ent', shift(s))
                args, kinds = [heads[s], tails[s], rels[s], hg, dp, head_cols, r4], 'sssvvvv'
            acc, = call(functools.partial(scatter_kernel, dim, rows, edges, first), args, kinds, [shape((rows * SLICES, LANES))], 'h',
                        [table_shape, stage_shape, square_shape, pltpu.SemaphoreType.DMA], 25)
            neg_got, acc = tie((neg_got, acc))
            gmine, gother = finish(neg_part, neg_got)
            scratch = [table_shape, pltpu.VMEM((rows, LANES), F32), table_shape, stage_shape, square_shape]
            if last:
                args, kinds = [core, negs[s]], 'sshhhvv'
                outs, out_kinds = [shape((dim, rows)), shape((rows // LANES, LANES))], 'hv'
                scratch += [pltpu.VMEM((2, dim, 4 * LANES), F32)]
            else:
                args, kinds = [core, negs[s], tails[s + 1], negs[s + 1]], 'sssshhhvv'
                outs, out_kinds = [shape((rows * SLICES, LANES)), shape((rows, LANES)), cols_bf, neg_half, neg_half], 'hhvvv'
                scratch += [pltpu.VMEM((dim, negp), BF16)]
            res = call(functools.partial(update_kernel, dim, rows, last), args + [t4, v, acc, gmine, gother], kinds, outs, out_kinds,
                       scratch + [pltpu.SemaphoreType.DMA((3,)), pltpu.SemaphoreType.DMA((2,))], 30)
            if last:
                et, g = res
            else:
                t4, v, tb, nk, ns = res

        even = core[0] == 0
        rel_grads = finish(rel_part, rel_got)
        rg = jnp.where(even, jnp.concatenate(rel_grads, axis=0), jnp.concatenate(rel_grads[::-1], axis=0))
        new_vr = vr + jnp.mean(rg * rg, axis=0, keepdims=True)
        new_r = rfm - LEARN_RATE * rg / jnp.sqrt(new_vr + ADA_EPS)
        return et.T, g.reshape(rows), new_r[:, :num_rel].T, new_vr[0, :num_rel], jnp.stack(losses)[None, :]

    return jax.shard_map(device_fn, mesh=mesh,
                         in_specs=(row_spec, flat_spec, rel_spec, state_spec, edge_spec, edge_spec, edge_spec, edge_spec, rel_spec),
                         out_specs=(row_spec, flat_spec, rel_spec, state_spec, row_spec), check_vma=False)
```

time: 591 us -> 568 us (0.961)
  waiting for transfers between devices: 251 us -> 129 us
  Pallas kernels: 269 us -> 365 us
  starting transfers between devices: 32.7 us -> 20.1 us
  other arithmetic: 21.8 us -> 31.7 us
    ppermute x31, waiting for transfers between devices: 198 us -> 99.1 us  [the longest x13 72.9 us: send(): return lax.ppermute(value, 'ent', pairs)]
    pallas_call x7 -> x19, Pallas kernels: 269 us -> 365 us  [call(): pl.pallas_call(kernel, out_shape=outs, in_specs=[places[k]() for k in kin...]
    ppermute x2, waiting for transfers between devices: 50.2 us -> 0.01 us  [device_fn(): got = lax.ppermute(jnp.stack([own_tails[s], own_rels[s]]), 'ent', shift(s))]
    ppermute x2, waiting for transfers between devices: 2.73 us -> 29.8 us  [device_fn(): dp = lax.ppermute(dp, 'ent', shift(s))]
    ppermute x31, starting transfers between devices: 30.6 us -> 16 us  [the longest x13 11.6 us: send(): return lax.ppermute(value, 'ent', pairs)]
    add x18, other arithmetic: 13.2 us -> 24.5 us  [the longest x9 12.3 us: chip_sum(): return keep + lax.ppermute(send, 'ent', swap)]
    unnamed x68 -> x72, local copies, waits for them, and re-layouts: 8.28 us -> 12.7 us
  transfers between devices with their start and end apart: 35 -> 35, of which waited for: 18 -> 20; matrix products, arithmetic and copies ran while one was open for 3% -> 4% of each run, Pallas kernels for 25% -> 43%
where the time goes in v2:
time: 568 us; the launch traced here: 566 us
  Pallas kernels  365 us (64%)
  waiting for transfers between devices  129 us (23%)
  other arithmetic  31.7 us (6%)
  starting transfers between devices  20.1 us (4%)
  local copies, waits for them, and re-layouts  19.6 us (3%)
    pallas_call x19, Pallas kernels, call(): pl.pallas_call(kernel, out_shape=outs, in_specs=[places[k]() for k in kin...  365 us
    ppermute x13, waiting for transfers between devices, send(): return lax.ppermute(value, 'ent', pairs)  72.9 us
    ppermute x2, waiting for transfers between devices, device_fn(): dp = lax.ppermute(dp, 'ent', shift(s))  29.8 us
    ppermute x9, waiting for transfers between devices, chip_sum(): return keep + lax.ppermute(send, 'ent', swap)  15.2 us
    unnamed x72, local copies, waits for them, and re-layouts  12.7 us
    add x9, other arithmetic, chip_sum(): return keep + lax.ppermute(send, 'ent', swap)  12.3 us
    add x9, other arithmetic, finish(): mine = part + got  12.2 us
    ppermute x13, starting transfers between devices, send(): return lax.ppermute(value, 'ent', pairs)  11.6 us
  transfers between devices with their start and end apart: 35, of which 20 were waited for; matrix products, arithmetic and copies ran while one was open for 4% of the time, Pallas kernels for 43%

profile of v2, /device:TPU:0, one launch (start us, length us, event | category | flops | bytes accessed | tf_op | source)
XLA Modules:
  0.0 566.4 jit_solution(12618586597556437136)
XLA Ops:
  2.0 22.6 %shard_map.128 = (f32[32768,128]{1,0:T(8,128)}, f32[8192,128]{1,0:T(8,128)}, bf16[400,512]{1,0:T(8,128)(2,1)}, bf16[400,512]{1,0:T(8,128)(2,1)}) custom-call(s32[1]{0:T(128)} %bitcast.core_ref.refs_0_, s32[1024]{0:T(1024)} %bitcast.69, f32[400,8192]{1,0:T(8,128)} %bitcast.45, f32[64,128]{1,0:T(8,128)} %bitcast.71), custom_call_target="tpu_custom_call" | custom-call | flops 100000000 | tf_op jit(solution)/shard_map/pallas_call | solution.py:484
  26.2 3.0 collective-permute-start.2
  29.2 3.2 pad.13.refs_3_
  34.5 15.1 %shard_map.129 = (bf16[400,2048]{1,0:T(8,128)(2,1)}, bf16[400,2048]{1,0:T(8,128)(2,1)}) custom-call(s32[2048]{0:T(1024)} %bitcast.47, s32[2048]{0:T(1024)} %bitcast.49, f32[32768,128]{1,0:T(8,128)} %get-tuple-element.107.refs_2_.refs_4_), custom_call_target="tpu_custom_call" | custom-call | flops 80000000 | tf_op jit(solution)/shard_map/pallas_call | solution.py:484
  49.6 10.6 %shard_map.130 = (f32[400,2048]{1,0:T(8,128)}, f32[400,2048]{1,0:T(8,128)}, f32[5632,128]{1,0:T(8,128)}) custom-call(s32[1]{0:T(128)} %bitcast.core_ref.refs_0_, s32[2048]{0:T(1024)} %bitcast.63, bf16[400,2048]{1,0:T(8,128)(2,1)} %get-tuple-element.113.refs_2_.hb, f32[400,1408]{1,0:T(8,128)} %pad.13.refs_3_), custom_call_target="tpu_custom_call" | custom-call | flops 50000000 | tf_op jit(solution)/shard_map/pallas_call | solution.py:484
  64.5 18.4 %shard_map.131 = (f32[1,128]{1,0:T(1,128)}, f32[1,2048]{1,0:T(1,128)}, bf16[1024,2048]{1,0:T(8,128)(2,1)}, f32[200,1024]{1,0:T(8,128)}, f32[200,1024]{1,0:T(8,128)}) custom-call(s32[1]{0:T(128)} %bitcast.core_ref.refs_0_, f32[1,2048]{1,0:T(1,128)} %get-tuple-element.213.w, f32[400,2048]{1,0:T(8,128)} %get-tuple-element.115.q.refs_4_, ...), custom_call_target="tpu_custom_call" | custom-call | flops 75000000 | tf_op jit(solution)/shard_map/pallas_call | solution.py:484
  83.2 2.2 collective-permute-done.5
  86.7 17.2 %shard_map.132 = (f32[8192,128]{1,0:T(8,128)}, f32[200,1408]{1,0:T(8,128)}, f32[200,1408]{1,0:T(8,128)}) custom-call(s32[1]{0:T(128)} %bitcast.core_ref.refs_0_, s32[2048]{0:T(1024)} %bitcast.64, bf16[1024,2048]{1,0:T(8,128)(2,1)} %get-tuple-element.122.ds, f32[1,2048]{1,0:T(1,128)} %get-tuple-element.123.dp.refs_3_, ...), custom_call_target="tpu_custom_call" | custom-call | flops 75000000 | tf_op jit(solution)/shard_map/pallas_call | solution.py:484
  106.8 2.4 add.85
  109.3 22.0 %shard_map.133.refs_6_ = f32[32768,128]{1,0:T(8,128)} custom-call(s32[2048]{0:T(1024)} %bitcast.50, s32[2048]{0:T(1024)} %bitcast.48, f32[8192,128]{1,0:T(8,128)} %get-tuple-element.128.refs_2_, f32[1,2048]{1,0:T(1,128)} %get-tuple-element.123.dp.refs_3_, f32[400,2048]{1,0:T(8,128)} %get-tuple-element.115.q.refs_4_), custom_call_target="tpu_custom_call" | custom-call | flops 125000000 | tf_op jit(solution)/shard_map/pallas_call | solution.py:484
  136.0 31.0 %shard_map.134 = (f32[32768,128]{1,0:T(8,128)}, f32[8192,128]{1,0:T(8,128)}, bf16[400,2048]{1,0:T(8,128)(2,1)}, bf16[400,512]{1,0:T(8,128)(2,1)}, bf16[400,512]{1,0:T(8,128)(2,1)}) custom-call(s32[1]{0:T(128)} %bitcast.core_ref.refs_0_, s32[1024]{0:T(1024)} %bitcast.70, s32[2048]{0:T(1024)} %bitcast.55, s32[1024]{0:T(1024)} %bitcast.67, ...), custom_call_target="tpu_custom_call" | custom-call | flops 150000000 | tf_op jit(solution)/shard_map/pallas_call | solution.py:484
  171.1 11.1 %shard_map.135.refs_2_.hb = bf16[400,2048]{1,0:T(8,128)(2,1)} custom-call(s32[2048]{0:T(1024)} %bitcast.57, f32[32768,128]{1,0:T(8,128)} %get-tuple-element.135.refs_1_.refs_4_), custom_call_target="tpu_custom_call" | custom-call | flops 55000000 | tf_op jit(solution)/shard_map/pallas_call | solution.py:484
  188.8 12.1 %shard_map.136 = (f32[400,2048]{1,0:T(8,128)}, f32[400,2048]{1,0:T(8,128)}, f32[5632,128]{1,0:T(8,128)}, f32[400,1408]{1,0:T(8,128)}, f32[1,1408]{1,0:T(1,128)}) custom-call(s32[1]{0:T(128)} %bitcast.core_ref.refs_0_, s32[2048]{0:T(1024)} %bitcast.61, bf16[400,2048]{1,0:T(8,128)(2,1)} %shard_map.135.refs_2_.hb, f32[400,1408]{1,0:T(8,128)} %pad.13.refs_3_, ...), custom_call_target="tpu_custom_call" | custom-call | flops 50000000 | tf_op jit(solution)/shard_map/pallas_call | solution.py:484
  205.3 18.5 %shard_map.137 = (f32[1,128]{1,0:T(1,128)}, f32[1,2048]{1,0:T(1,128)}, bf16[1024,2048]{1,0:T(8,128)(2,1)}, f32[200,1024]{1,0:T(8,128)}, f32[200,1024]{1,0:T(8,128)}) custom-call(s32[1]{0:T(128)} %bitcast.core_ref.refs_0_, f32[1,2048]{1,0:T(1,128)} %get-tuple-element.212.w, f32[400,2048]{1,0:T(8,128)} %get-tuple-element.142.q, ...), custom_call_target="tpu_custom_call" | custom-call | flops 75000000 | tf_op jit(solution)/shard_map/pallas_call | solution.py:484
  224.3 2.0 collective-permute-done.15
  227.6 17.1 %shard_map.138 = (f32[8192,128]{1,0:T(8,128)}, f32[200,1408]{1,0:T(8,128)}, f32[200,1408]{1,0:T(8,128)}) custom-call(s32[1]{0:T(128)} %bitcast.core_ref.refs_0_, s32[2048]{0:T(1024)} %bitcast.62, bf16[1024,2048]{1,0:T(8,128)(2,1)} %get-tuple-element.150.ds, f32[1,2048]{1,0:T(1,128)} %get-tuple-element.151.dp, bf16[400,2048]{1,0:T(8,128)(2,1)} %collective-permute-done.13.tb, ...), custom_call_target="tpu_custom_call" | custom-call | flops 75000000 | tf_op jit(solution)/shard_map/pallas_call | solution.py:484
  247.7 2.4 add.91
  250.1 14.8 %collective-permute-done.18.refs_4_ = f32[1,2048]{1,0:T(1,128)S(1)} collective-permute-done((f32[1,2048]{1,0:T(1,128)S(1)}, f32[1,2048]{1,0:T(1,128)S(1)}, u32[]{:S(2)}, u32[]{:S(2)}) %collective-permute-start.18) | collective-permute-done | bytes 8224 | tf_op jit(solution)/shard_map/ppermute | solution.py:553
  265.5 26.8 %shard_map.139.refs_6_ = f32[32768,128]{1,0:T(8,128)} custom-call(s32[2048]{0:T(1024)} %bitcast.58, s32[2048]{0:T(1024)} %bitcast.56, s32[2048]{0:T(1024)} %bitcast.74, f32[8192,128]{1,0:T(8,128)} %get-tuple-element.156.refs_3_, f32[1,2048]{1,0:T(1,128)} %copy-done.27, bf16[400,2048]{1,0:T(8,128)(2,1)} %collective-permute-done.19.refs_5_, ...), custom_call_target="tpu_custom_call" | custom-call | flops 125000000 | tf_op jit(solution)/shard_map/pallas_call | solution.py:484
  297.2 31.0 %shard_map.140 = (f32[32768,128]{1,0:T(8,128)}, f32[8192,128]{1,0:T(8,128)}, bf16[400,2048]{1,0:T(8,128)(2,1)}, bf16[400,512]{1,0:T(8,128)(2,1)}, bf16[400,512]{1,0:T(8,128)(2,1)}) custom-call(s32[1]{0:T(128)} %bitcast.core_ref.refs_0_, s32[1024]{0:T(1024)} %bitcast.68, s32[2048]{0:T(1024)} %bitcast.51, s32[1024]{0:T(1024)} %bitcast.65, ...), custom_call_target="tpu_custom_call" | custom-call | flops 150000000 | tf_op jit(solution)/shard_map/pallas_call | solution.py:484
  332.3 11.1 %shard_map.141.refs_2_.hb = bf16[400,2048]{1,0:T(8,128)(2,1)} custom-call(s32[2048]{0:T(1024)} %bitcast.53, f32[32768,128]{1,0:T(8,128)} %get-tuple-element.164.refs_1_.refs_2_), custom_call_target="tpu_custom_call" | custom-call | flops 55000000 | tf_op jit(solution)/shard_map/pallas_call | solution.py:484
  349.9 12.1 %shard_map.142 = (f32[400,2048]{1,0:T(8,128)}, f32[400,2048]{1,0:T(8,128)}, f32[5632,128]{1,0:T(8,128)}, f32[400,1408]{1,0:T(8,128)}, f32[1,1408]{1,0:T(1,128)}) custom-call(s32[1]{0:T(128)} %bitcast.core_ref.refs_0_, s32[2048]{0:T(1024)} %bitcast.59, bf16[400,2048]{1,0:T(8,128)(2,1)} %shard_map.141.refs_2_.hb, f32[400,1408]{1,0:T(8,128)} %get-tuple-element.169.refs_3_, ...), custom_call_target="tpu_custom_call" | custom-call | flops 50000000 | tf_op jit(solution)/shard_map/pallas_call | solution.py:484
  362.0 16.2 %collective-permute-done.22 = bf16[400,512]{1,0:T(8,128)(2,1)S(1)} collective-permute-done((bf16[400,512]{1,0:T(8,128)(2,1)S(1)}, bf16[400,512]{1,0:T(8,128)(2,1)S(1)}, u32[]{:S(2)}, u32[]{:S(2)}) %collective-permute-start.22) | collective-permute-done | bytes 409632 | tf_op jit(solution)/shard_map/ppermute | solution.py:441
  382.5 18.4 %shard_map.143 = (f32[1,128]{1,0:T(1,128)}, f32[1,2048]{1,0:T(1,128)}, bf16[1024,2048]{1,0:T(8,128)(2,1)}, f32[200,1024]{1,0:T(8,128)}, f32[200,1024]{1,0:T(8,128)}) custom-call(s32[1]{0:T(128)} %bitcast.core_ref.refs_0_, f32[1,2048]{1,0:T(1,128)} %get-tuple-element.211.w, f32[400,2048]{1,0:T(8,128)} %get-tuple-element.173.q, ...), custom_call_target="tpu_custom_call" | custom-call | flops 75000000 | tf_op jit(solution)/shard_map/pallas_call | solution.py:484
  401.0 2.4 collective-permute-done.27
  404.7 17.0 %shard_map.144 = (f32[8192,128]{1,0:T(8,128)}, f32[200,1408]{1,0:T(8,128)}, f32[200,1408]{1,0:T(8,128)}) custom-call(s32[1]{0:T(128)} %bitcast.core_ref.refs_0_, s32[2048]{0:T(1024)} %bitcast.60, bf16[1024,2048]{1,0:T(8,128)(2,1)} %get-tuple-element.181.ds, f32[1,2048]{1,0:T(1,128)} %get-tuple-element.182.dp, bf16[400,2048]{1,0:T(8,128)(2,1)} %collective-permute-done.25.tb, ...), custom_call_target="tpu_custom_call" | custom-call | flops 75000000 | tf_op jit(solution)/shard_map/pallas_call | solution.py:484
  422.8 1.9 collective-permute-done.29
  428.1 56.7 %collective-permute-done.33 = f32[200,1408]{1,0:T(8,128)S(1)} collective-permute-done((f32[200,1408]{1,0:T(8,128)S(1)}, f32[200,1408]{1,0:T(8,128)S(1)}, u32[]{:S(2)}, u32[]{:S(2)}) %collective-permute-start.33) | collective-permute-done | bytes 1126432 | tf_op jit(solution)/shard_map/ppermute | solution.py:441
  487.0 15.0 %collective-permute-done.30.refs_4_ = f32[1,2048]{1,0:T(1,128)S(1)} collective-permute-done((f32[1,2048]{1,0:T(1,128)S(1)}, f32[1,2048]{1,0:T(1,128)S(1)}, u32[]{:S(2)}, u32[]{:S(2)}) %collective-permute-start.30) | collective-permute-done | bytes 8224 | tf_op jit(solution)/shard_map/ppermute | solution.py:553
  502.6 26.7 %shard_map.145.refs_4_ = f32[32768,128]{1,0:T(8,128)} custom-call(s32[2048]{0:T(1024)} %bitcast.54, s32[2048]{0:T(1024)} %bitcast.52, s32[2048]{0:T(1024)} %bitcast.73, f32[8192,128]{1,0:T(8,128)} %get-tuple-element.187.refs_3_, f32[1,2048]{1,0:T(1,128)} %copy-done.28, bf16[400,2048]{1,0:T(8,128)(2,1)} %collective-permute-done.31.refs_5_, ...), custom_call_target="tpu_custom_call" | custom-call | flops 125000000 | tf_op jit(solution)/shard_map/pallas_call | solution.py:484
  534.7 26.4 %shard_map.146 = (f32[400,8192]{1,0:T(8,128)}, f32[64,128]{1,0:T(8,128)}) custom-call(s32[1]{0:T(128)} %bitcast.core_ref.refs_0_, s32[1024]{0:T(1024)} %bitcast.66, f32[32768,128]{1,0:T(8,128)} %get-tuple-element.164.refs_1_.refs_2_, f32[8192,128]{1,0:T(8,128)} %get-tuple-element.165.refs_3_, f32[32768,128]{1,0:T(8,128)} %shard_map.145.refs_4_, ...), custom_call_target="tpu_custom_call" | custom-call | flops 150000000 | tf_op jit(solution)/shard_map/pallas_call | solution.py:484
  561.2 2.7 multiply_reduce_fusion
  (166 shorter events, 75.3 us)
Async XLA Ops:
  24.6 9.1 %collective-permute-start = (bf16[400,512]{1,0:T(8,128)(2,1)}, bf16[400,512]{1,0:T(8,128)(2,1)S(1)}, u32[]{:S(2)}, u32[]{:S(2)}) collective-permute-start(bf16[400,512]{1,0:T(8,128)(2,1)} %get-tuple-element.103), channel_id=1, source_target_pairs={{0,1},{1,0},{2,3},{3,2},{4,5},{5,4},{6,7},{7,6}} | collective-permute-start | bytes 1228808 | tf_op jit(solution)/shard_map/ppermute | solution.py:438
  26.1 6.3 %collective-permute-start.1 = (s32[2,2048]{1,0:T(2,128)S(1)}, s32[2,2048]{1,0:T(2,128)S(1)}, u32[]{:S(2)}, u32[]{:S(2)}) collective-permute-start(s32[2,2048]{1,0:T(2,128)S(1)} %pad_add_fusion), channel_id=1, source_target_pairs={{0,1},{1,2},{2,3},{3,0},{4,5},{5,6},{6,7},{7,4}} | collective-permute-start | bytes 49160 | tf_op jit(solution)/shard_map/ppermute | solution.py:466
  26.2 6.8 %collective-permute-start.2 = (s32[2,2048]{1,0:T(2,128)S(1)}, s32[2,2048]{1,0:T(2,128)S(1)}, u32[]{:S(2)}, u32[]{:S(2)}) collective-permute-start(s32[2,2048]{1,0:T(2,128)S(1)} %pad_add_fusion.1), channel_id=1, source_target_pairs={{0,2},{1,3},{2,0},{3,1},{4,6},{5,7},{6,4},{7,5}} | collective-permute-start | bytes 49160 | tf_op jit(solution)/shard_map/ppermute | solution.py:466
  33.8 15.8 %collective-permute-start.3 = (bf16[400,512]{1,0:T(8,128)(2,1)S(1)}, bf16[400,512]{1,0:T(8,128)(2,1)S(1)}, u32[]{:S(2)}, u32[]{:S(2)}) collective-permute-start(bf16[400,512]{1,0:T(8,128)(2,1)S(1)} %add.82), channel_id=1, source_target_pairs={{0,2},{1,3},{2,0},{3,1},{4,6},{5,7},{6,4},{7,5}} | collective-permute-start | bytes 1228808 | tf_op jit(solution)/shard_map/ppermute | solution.py:441
  61.3 2.5 collective-permute-start.4
  82.8 2.5 collective-permute-start.5
  103.9 3.0 collective-permute-start.7
  104.2 27.0 %collective-permute-start.6 = (f32[200,1024]{1,0:T(8,128)S(1)}, f32[200,1024]{1,0:T(8,128)}, u32[]{:S(2)}, u32[]{:S(2)}) collective-permute-start(f32[200,1024]{1,0:T(8,128)S(1)} %add.84), channel_id=1, source_target_pairs={{0,2},{1,3},{2,0},{3,1},{4,6},{5,7},{6,4},{7,5}} | collective-permute-start | bytes 2457608 | tf_op jit(solution)/shard_map/ppermute | solution.py:441
  132.8 2.4 collective-permute-start.8
  133.2 49.1 %collective-permute-start.11 = (f32[200,1408]{1,0:T(8,128)}, f32[200,1408]{1,0:T(8,128)}, u32[]{:S(2)}, u32[]{:S(2)}) collective-permute-start(f32[200,1408]{1,0:T(8,128)} %add.85), channel_id=1, source_target_pairs={{0,2},{1,3},{2,0},{3,1},{4,6},{5,7},{6,4},{7,5}} | collective-permute-start | bytes 3379208 | tf_op jit(solution)/shard_map/ppermute | solution.py:441
  167.0 2.0 collective-permute-start.9
  170.1 34.4 %collective-permute-start.13 = (bf16[400,2048]{1,0:T(8,128)(2,1)}, bf16[400,2048]{1,0:T(8,128)(2,1)}, u32[]{:S(2)}, u32[]{:S(2)}) collective-permute-start(bf16[400,2048]{1,0:T(8,128)(2,1)} %get-tuple-element.143), channel_id=1, source_target_pairs={{0,3},{1,0},{2,1},{3,2},{4,7},{5,4},{6,5},{7,6}} | collective-permute-start | bytes 4915208 | tf_op jit(solution)/shard_map/ppermute | solution.py:441
  185.0 2.8 collective-permute-start.12
  185.0 15.9 %collective-permute-start.10 = (bf16[400,512]{1,0:T(8,128)(2,1)S(1)}, bf16[400,512]{1,0:T(8,128)(2,1)S(1)}, u32[]{:S(2)}, u32[]{:S(2)}) collective-permute-start(bf16[400,512]{1,0:T(8,128)(2,1)S(1)} %add.87), channel_id=1, source_target_pairs={{0,2},{1,3},{2,0},{3,1},{4,6},{5,7},{6,4},{7,5}} | collective-permute-start | bytes 1228808 | tf_op jit(solution)/shard_map/ppermute | solution.py:441
  223.8 2.5 collective-permute-start.15
  223.9 26.2 %collective-permute-start.19 = (bf16[400,2048]{1,0:T(8,128)(2,1)}, bf16[400,2048]{1,0:T(8,128)(2,1)}, u32[]{:S(2)}, u32[]{:S(2)}) collective-permute-start(bf16[400,2048]{1,0:T(8,128)(2,1)} %shard_map.135.refs_2_.hb), channel_id=1, source_target_pairs={{0,1},{1,2},{2,3},{3,0},{4,5},{5,6},{6,7},{7,4}} | collective-permute-start | bytes 4915208 | tf_op jit(solution)/shard_map/ppermute | solution.py:441
  244.7 3.0 collective-permute-start.17
  244.9 47.5 %collective-permute-start.16 = (f32[200,1024]{1,0:T(8,128)S(1)}, f32[200,1024]{1,0:T(8,128)}, u32[]{:S(2)}, u32[]{:S(2)}) collective-permute-start(f32[200,1024]{1,0:T(8,128)S(1)} %add.90), channel_id=1, source_target_pairs={{0,2},{1,3},{2,0},{3,1},{4,6},{5,7},{6,4},{7,5}} | collective-permute-start | bytes 2457608 | tf_op jit(solution)/shard_map/ppermute | solution.py:441
  245.8 19.1 %collective-permute-start.18 = (f32[1,2048]{1,0:T(1,128)S(1)}, f32[1,2048]{1,0:T(1,128)S(1)}, u32[]{:S(2)}, u32[]{:S(2)}) collective-permute-start(f32[1,2048]{1,0:T(1,128)S(1)} %copy-done.31), channel_id=1, source_target_pairs={{0,1},{1,2},{2,3},{3,0},{4,5},{5,6},{6,7},{7,4}} | collective-permute-start | bytes 24584 | tf_op jit(solution)/shard_map/ppermute | solution.py:553
  293.9 2.4 collective-permute-start.20
  293.9 49.5 %collective-permute-start.23 = (f32[200,1408]{1,0:T(8,128)}, f32[200,1408]{1,0:T(8,128)}, u32[]{:S(2)}, u32[]{:S(2)}) collective-permute-start(f32[200,1408]{1,0:T(8,128)} %add.91), channel_id=1, source_target_pairs={{0,2},{1,3},{2,0},{3,1},{4,6},{5,7},{6,4},{7,5}} | collective-permute-start | bytes 3379208 | tf_op jit(solution)/shard_map/ppermute | solution.py:441
  331.3 50.5 %collective-permute-start.25 = (bf16[400,2048]{1,0:T(8,128)(2,1)}, bf16[400,2048]{1,0:T(8,128)(2,1)}, u32[]{:S(2)}, u32[]{:S(2)}) collective-permute-start(bf16[400,2048]{1,0:T(8,128)(2,1)} %get-tuple-element.174), channel_id=1, source_target_pairs={{0,2},{1,3},{2,0},{3,1},{4,6},{5,7},{6,4},{7,5}} | collective-permute-start | bytes 4915208 | tf_op jit(solution)/shard_map/ppermute | solution.py:441
  346.1 2.8 collective-permute-start.24
  346.1 32.0 %collective-permute-start.22 = (bf16[400,512]{1,0:T(8,128)(2,1)S(1)}, bf16[400,512]{1,0:T(8,128)(2,1)S(1)}, u32[]{:S(2)}, u32[]{:S(2)}) collective-permute-start(bf16[400,512]{1,0:T(8,128)(2,1)S(1)} %add.93), channel_id=1, source_target_pairs={{0,2},{1,3},{2,0},{3,1},{4,6},{5,7},{6,4},{7,5}} | collective-permute-start | bytes 1228808 | tf_op jit(solution)/shard_map/ppermute | solution.py:441
  400.9 2.5 collective-permute-start.27
  421.7 3.0 collective-permute-start.29
  421.8 65.2 %collective-permute-start.31 = (bf16[400,2048]{1,0:T(8,128)(2,1)}, bf16[400,2048]{1,0:T(8,128)(2,1)}, u32[]{:S(2)}, u32[]{:S(2)}) collective-permute-start(bf16[400,2048]{1,0:T(8,128)(2,1)} %shard_map.141.refs_2_.hb), channel_id=1, source_target_pairs={{0,2},{1,3},{2,0},{3,1},{4,6},{5,7},{6,4},{7,5}} | collective-permute-start | bytes 4915208 | tf_op jit(solution)/shard_map/ppermute | solution.py:441
  426.1 58.8 %collective-permute-start.33 = (f32[200,1408]{1,0:T(8,128)S(1)}, f32[200,1408]{1,0:T(8,128)S(1)}, u32[]{:S(2)}, u32[]{:S(2)}) collective-permute-start(f32[200,1408]{1,0:T(8,128)S(1)} %add.97), channel_id=1, source_target_pairs={{0,2},{1,3},{2,0},{3,1},{4,6},{5,7},{6,4},{7,5}} | collective-permute-start | bytes 3379208 | tf_op jit(solution)/shard_map/ppermute | solution.py:441
  427.1 102.2 %collective-permute-start.28 = (f32[200,1024]{1,0:T(8,128)S(1)}, f32[200,1024]{1,0:T(8,128)}, u32[]{:S(2)}, u32[]{:S(2)}) collective-permute-start(f32[200,1024]{1,0:T(8,128)S(1)} %add.96), channel_id=1, source_target_pairs={{0,2},{1,3},{2,0},{3,1},{4,6},{5,7},{6,4},{7,5}} | collective-permute-start | bytes 2457608 | tf_op jit(solution)/shard_map/ppermute | solution.py:441
  486.0 75.2 %collective-permute-start.34 = (f32[200,1408]{1,0:T(8,128)}, f32[200,1408]{1,0:T(8,128)}, u32[]{:S(2)}, u32[]{:S(2)}) collective-permute-start(f32[200,1408]{1,0:T(8,128)} %add.99), channel_id=1, source_target_pairs={{0,1},{1,0},{2,3},{3,2},{4,5},{5,4},{6,7},{7,6}} | collective-permute-start | bytes 3379208 | tf_op jit(solution)/shard_map/ppermute | solution.py:448
  486.0 16.0 %collective-permute-start.30 = (f32[1,2048]{1,0:T(1,128)S(1)}, f32[1,2048]{1,0:T(1,128)S(1)}, u32[]{:S(2)}, u32[]{:S(2)}) collective-permute-start(f32[1,2048]{1,0:T(1,128)S(1)} %copy-done.30), channel_id=1, source_target_pairs={{0,2},{1,3},{2,0},{3,1},{4,6},{5,7},{6,4},{7,5}} | collective-permute-start | bytes 24584 | tf_op jit(solution)/shard_map/ppermute | solution.py:553
  531.5 2.3 collective-permute-start.32
  (39 other events, 254.2 us)

commit v3 on v2

--- a/solution.py
+++ b/solution.py
@@ -91,8 +91,7 @@
     ns[...] = nbuf[:, pl.ds(pl.multiple_of((1 - core) * half, LANES), half)]
 
 
-def entry_kernel(dim, rows, core_ref, negs, et, g, t4_out, v_out, nk, ns,
-                 t4, v, inbuf, stage, nbuf, in_sem, out_sem):
+def entry_kernel(dim, rows, core_ref, negs, et, g, t4, v, nk, ns, inbuf, stage, nbuf, in_sem):
     cols = inbuf.shape[2]
     steps = rows // cols
     per = cols // LANES
@@ -122,21 +121,11 @@
         return 0
 
     lax.fori_loop(0, steps, body, 0)
-    save_t = pltpu.make_async_copy(t4.at[pl.ds(0, rows * SLICES)], t4_out, out_sem.at[0])
-    save_v = pltpu.make_async_copy(v, v_out, out_sem.at[1])
-    save_t.start()
-    save_v.start()
     gather_negs(dim, core_ref[0], t4, negs, nk, ns, nbuf, stage)
-    save_t.wait()
-    save_v.wait()
 
 
 def gather_kernel(dim, lists, *refs):
-    ids, t4_in, outs = refs[:lists], refs[lists], refs[lists + 1:2 * lists + 1]
-    t4, stage, sem = refs[2 * lists + 1:]
-    load = pltpu.make_async_copy(t4_in, t4, sem)
-    load.start()
-    load.wait()
+    ids, t4, outs, stage = refs[:lists], refs[lists], refs[lists + 1:2 * lists + 1], refs[2 * lists + 1]
     for i in range(lists):
         gather_out(dim, t4, ids[i], outs[i], stage, outs[i].shape[1])
 
@@ -275,11 +264,11 @@
         stage[pl.ds(j, LANES, stride=SLICES), :] = rt[pl.ds(j * LANES, LANES), :].T
 
 
-def scatter_kernel(dim, rows, edges, own, *refs):
+def scatter_kernel(dim, edges, own, *refs):
     if own:
-        heads, tails, hg, dp, q, acc_out, acc, stage, rt, sem = refs
+        heads, tails, hg, dp, q, acc, stage, rt = refs
     else:
-        heads, tails, rel, hg, dp, hb_in, r4, acc_out, acc, stage, rt, sem = refs
+        heads, tails, rel, hg, dp, hb_in, r4, acc, stage, rt = refs
     half = dim // 2
     tops = SLICES * LANES
     zero_rows(acc)
@@ -311,31 +300,17 @@
         return 0
 
     lax.fori_loop(0, edges // LANES, tail_step, 0)
-    save = pltpu.make_async_copy(acc.at[pl.ds(0, rows * SLICES)], acc_out, sem)
-    save.start()
-    save.wait()
 
 
 def update_kernel(dim, rows, last, *refs):
     if last:
-        (core_ref, negs, t4_in, v_in, acc_in, nmine, nother,
-         et_out, g_out, t4, v, acc, stage, rt, outbuf, in_sem, out_sem) = refs
+        core_ref, negs, t4, v, _, nmine, nother, acc, et_out, g_out, stage, rt, outbuf, out_sem = refs
     else:
-        (core_ref, negs, tails_n, negs_n, t4_in, v_in, acc_in, nmine, nother,
-         t4_out, v_out, tb, nk, ns, t4, v, acc, stage, rt, nbuf, in_sem, out_sem) = refs
+        core_ref, negs, tails_n, negs_n, t4, v, _, nmine, nother, acc, new_t4, new_v, tb, nk, ns, stage, rt, nbuf = refs
     core = core_ref[0]
     half = dim // 2
     tops = SLICES * LANES
-    load_a = pltpu.make_async_copy(acc_in, acc.at[pl.ds(0, rows * SLICES)], in_sem.at[2])
-    load_t = pltpu.make_async_copy(t4_in, t4.at[pl.ds(0, rows * SLICES)], in_sem.at[0])
-    load_v = pltpu.make_async_copy(v_in, v, in_sem.at[1])
-    load_a.start()
-    load_t.start()
-    load_v.start()
-    acc[pl.ds(rows * SLICES, 32), :] = jnp.zeros((32, LANES), F32)
-    t4[pl.ds(rows * SLICES, 32), :] = jnp.zeros((32, LANES), F32)
     rt[pl.ds(dim, tops - dim), :] = jnp.zeros((tops - dim, LANES), F32)
-    load_a.wait()
 
     def neg_step(b, _):
         cols = pl.ds(pl.multiple_of(b * LANES, LANES), LANES)
@@ -346,36 +321,28 @@
         return 0
 
     lax.fori_loop(0, nmine.shape[1] // LANES, neg_step, 0)
-    load_t.wait()
-    load_v.wait()
-
-    def ada_rows(row0, block):
-        parts = [acc[pl.ds(SLICES * row0 + j, block, stride=SLICES), :] for j in range(SLICES)]
-        square = parts[0] * parts[0]
+
+    def ada_rows(row0):
+        where = [pl.ds(SLICES * row0 + j, LANES, stride=SLICES) for j in range(SLICES)]
+        square = acc[where[0], :] * acc[where[0], :]
         for j in range(1, SLICES):
-            square = square + parts[j] * parts[j]
-        vrows = pl.ds(pl.multiple_of(row0, 8), block)
-        new_v = v[vrows, :] + jnp.sum(square, axis=1, keepdims=True) / dim
-        v[vrows, :] = new_v
-        rate = LEARN_RATE / jnp.sqrt(new_v + ADA_EPS)
-        for j in range(SLICES):
-            where = pl.ds(SLICES * row0 + j, block, stride=SLICES)
-            t4[where, :] = t4[where, :] - acc[where, :] * rate
+            square = square + acc[where[j], :] * acc[where[j], :]
+        state = v[pl.ds(pl.multiple_of(row0, 8), LANES), :] + jnp.sum(square, axis=1, keepdims=True) / dim
+        rate = LEARN_RATE / jnp.sqrt(state + ADA_EPS)
+        return state, where, [t4[w, :] - acc[w, :] * rate for w in where]
 
     if not last:
         def ada_step(b, _):
-            ada_rows(b * LANES, LANES)
+            state, where, values = ada_rows(b * LANES)
+            new_v[pl.ds(pl.multiple_of(b * LANES, 8), LANES), :] = state
+            for w, value in zip(where, values):
+                new_t4[w, :] = value
             return 0
 
         lax.fori_loop(0, rows // LANES, ada_step, 0)
-        save_v = pltpu.make_async_copy(v, v_out, out_sem.at[1])
-        save_t = pltpu.make_async_copy(t4.at[pl.ds(0, rows * SLICES)], t4_out, out_sem.at[0])
-        save_v.start()
-        gather_negs(dim, core, t4, negs_n, nk, ns, nbuf, stage)
-        save_t.start()
-        gather_out(dim, t4, tails_n, tb, stage, tb.shape[1])
-        save_t.wait()
-        save_v.wait()
+        new_t4[pl.ds(rows * SLICES, 32), :] = jnp.zeros((32, LANES), F32)
+        gather_negs(dim, core, new_t4, negs_n, nk, ns, nbuf, stage)
+        gather_out(dim, new_t4, tails_n, tb, stage, tb.shape[1])
         return
 
     width = outbuf.shape[2]
@@ -393,12 +360,11 @@
             save(step - 2, slot).wait()
 
         for b in range(per):
-            row0 = (step * per + b) * LANES
-            ada_rows(row0, LANES)
+            state, _, values = ada_rows((step * per + b) * LANES)
             for j in range(SLICES):
                 size = min(LANES, dim - j * LANES)
-                outbuf[slot, pl.ds(j * LANES, size), pl.ds(b * LANES, LANES)] = t4[pl.ds(SLICES * row0 + j, LANES, stride=SLICES), :].T[:size]
-            g_out[pl.ds(step * per + b, 1), :] = v[pl.ds(pl.multiple_of(row0, 8), LANES), :].T[:1]
+                outbuf[slot, pl.ds(j * LANES, size), pl.ds(b * LANES, LANES)] = values[j].T[:size]
+            g_out[pl.ds(step * per + b, 1), :] = state.T[:1]
         save(step, slot).start()
         return 0
 
@@ -407,8 +373,13 @@
     save(steps - 1, (steps - 1) % 2).wait()
 
 
-def params():
-    return pltpu.CompilerParams(vmem_limit_bytes=63 * 1024 * 1024)
+def padded_bytes(dims, dtype):
+    size = jnp.dtype(dtype).itemsize
+    dims = (1,) * (2 - len(dims)) + tuple(dims)
+    total = ceil_to(dims[-2], 32 // size) * ceil_to(dims[-1], LANES) * size
+    for d in dims[:-2]:
+        total *= d
+    return total
 
 
 def cost(micros):
@@ -475,26 +446,30 @@
         wide_rows = (rows + 8) * SLICES
         stage_shape = pltpu.VMEM((SLICES * LANES, LANES), F32)
         square_shape = pltpu.VMEM((SLICES * LANES, LANES), F32)
-        table_shape = pltpu.VMEM((wide_rows, LANES), F32)
+        table_out, state_out = shape((wide_rows, LANES)), shape((rows, LANES))
         cols_bf = shape((dim, edges), BF16)
         neg_half = shape((dim, negp // 2), BF16)
 
-        def call(kernel, args, kinds, outs, out_kinds, scratch, micros):
-            places = {'s': smem, 'h': hbm, 'v': vmem}
+        def call(kernel, args, kinds, outs, out_kinds, scratch, micros, aliases=None):
+            places = {'s': smem, 'h': hbm, 'v': vmem, 'V': vmem}
+            windows = [a for a, k in zip(list(args) + outs, kinds + out_kinds) if k == 'v']
+            limit = 3 * 2 ** 20 + sum(padded_bytes(a.shape, a.dtype) for a in windows)
+            limit += sum(padded_bytes(a.shape, a.dtype) for a in scratch if a.memory_space == pltpu.VMEM)
+            args = [pltpu.with_memory_space_constraint(a, pltpu.VMEM) if k == 'V' else a for a, k in zip(args, kinds)]
+            outs = [pltpu.VMEM(o.shape, o.dtype) if k == 'V' else o for o, k in zip(outs, out_kinds)]
             return pl.pallas_call(
                 kernel, out_shape=outs, in_specs=[places[k]() for k in kinds], out_specs=[places[k]() for k in out_kinds],
-                scratch_shapes=scratch, compiler_params=params(), cost_estimate=cost(micros))(*args)
+                scratch_shapes=scratch, compiler_params=pltpu.CompilerParams(vmem_limit_bytes=limit),
+                input_output_aliases=aliases or {}, cost_estimate=cost(micros))(*args)
 
         def gather(lists, t4):
-            return call(functools.partial(gather_kernel, dim, len(lists)), lists + [t4], 's' * len(lists) + 'h',
-                        [cols_bf] * len(lists), 'v' * len(lists),
-                        [pltpu.VMEM((rows * SLICES, LANES), F32), stage_shape, pltpu.SemaphoreType.DMA], 6 + 5 * len(lists))
+            return call(functools.partial(gather_kernel, dim, len(lists)), lists + [t4], 's' * len(lists) + 'V',
+                        [cols_bf] * len(lists), 'V' * len(lists), [stage_shape], 1 + 5 * len(lists))
 
         t4, v, nk, ns = call(
             functools.partial(entry_kernel, dim, rows), [core, negs[0], ent_emb.T, ent_ada.reshape(rows // LANES, LANES)], 'sshv',
-            [shape((rows * SLICES, LANES)), shape((rows, LANES)), neg_half, neg_half], 'hhvv',
-            [table_shape, pltpu.VMEM((rows, LANES), F32), pltpu.VMEM((2, SLICES * LANES, 4 * LANES), F32), stage_shape,
-             pltpu.VMEM((dim, negp), BF16), pltpu.SemaphoreType.DMA((2,)), pltpu.SemaphoreType.DMA((2,))], 20)
+            [table_out, state_out, neg_half, neg_half], 'VVVV',
+            [pltpu.VMEM((2, SLICES * LANES, 4 * LANES), F32), stage_shape, pltpu.VMEM((dim, negp), BF16), pltpu.SemaphoreType.DMA((2,))], 20)
 
         rfm = jnp.pad(rel_emb.T, ((0, 0), (0, relp - num_rel)))
         vr = jnp.pad(rel_ada, (0, relp - num_rel), constant_values=1.0).reshape(1, relp)
@@ -518,12 +493,14 @@
                 rel_got, hb = tie((rel_got, hb))
                 rel_grads = finish(rel_part, rel_got)
             wide = shape((dim, edges))
-            outs = [wide, wide, shape((relp * SLICES, LANES))]
-            args = [core, own_rels[s], hb, rfm]
+            outs, out_kinds = [wide, wide, shape((relp * SLICES, LANES))], 'VVV'
+            args, kinds = [core, own_rels[s], hb, rfm], 'ssV' + ('v' if first else 'V')
             if not first:
                 outs += [shape((dim, relp)), shape((1, relp))]
+                out_kinds += 'Vv'
                 args += [vr] + list(rel_grads)
-            res = call(functools.partial(query_kernel, dim, edges, first), args, 'ss' + 'v' * (len(args) - 2), outs, 'v' * len(outs),
+                kinds += 'vVV'
+            res = call(functools.partial(query_kernel, dim, edges, first), args, kinds, outs, out_kinds,
                        [stage_shape, pltpu.VMEM((SLICES * LANES, relp), F32)], 10)
             q, r, r4 = res[:3]
             neg_got, q = tie((neg_got, q))
@@ -531,8 +508,8 @@
             if not first:
                 rfm, vr = res[3:]
             loss, dp, ds, gk, gs = call(
-                functools.partial(score_kernel, dim, neg_count, edges), [core, weights[s].reshape(1, edges), q, tail_cols, nmine, nother], 'svvvvv',
-                [shape((1, LANES)), shape((1, edges)), shape((negp, edges), BF16), shape((half, negp)), shape((half, negp))], 'vvvvv',
+                functools.partial(score_kernel, dim, neg_count, edges), [core, weights[s].reshape(1, edges), q, tail_cols, nmine, nother], 'svVVVV',
+                [shape((1, LANES)), shape((1, edges)), shape((negp, edges), BF16), shape((half, negp)), shape((half, negp))], 'vvVVV',
                 [pltpu.VMEM((dim, negp), BF16), pltpu.VMEM((negp, dim), BF16), pltpu.VMEM((negp, CHUNK), F32),
                  pltpu.VMEM((negp, dim), F32), pltpu.VMEM((SLICES * LANES, negp), F32)], 15)
             losses.append(loss[0, 0])
@@ -540,37 +517,38 @@
             neg_part, ds = tie((neg_part, ds))
             neg_got = link(neg_part)
             hg, rk, rs = call(
-                functools.partial(grad_kernel, dim, edges), [core, own_rels[s], ds, dp, tail_cols, hb, r, nmine, nother], 'ssvvvvvvv',
-                [shape((edges * SLICES, LANES)), shape((half, relp)), shape((half, relp))], 'vvv',
+                functools.partial(grad_kernel, dim, edges), [core, own_rels[s], ds, dp, tail_cols, hb, r, nmine, nother], 'ssVvVVVVV',
+                [shape((edges * SLICES, LANES)), shape((half, relp)), shape((half, relp))], 'VVV',
                 [pltpu.VMEM((dim, negp), BF16), pltpu.VMEM((relp * SLICES, LANES), F32), pltpu.VMEM((SLICES * CHUNK, LANES), F32),
                  pltpu.VMEM((SLICES * LANES, CHUNK), F32), pltpu.VMEM((SLICES * LANES, relp), F32)], 15)
             rel_part = chip_sum(rk, rs)
             rel_part, hg = tie((rel_part, hg))
             rel_got = link(rel_part)
             if first:
-                args, kinds = [heads[s], tails[s], hg, dp, q], 'ssvvv'
+                args, kinds = [heads[s], tails[s], hg, dp, q], 'ssVvV'
             else:
                 dp = lax.ppermute(dp, 'ent', shift(s))
-                args, kinds = [heads[s], tails[s], rels[s], hg, dp, head_cols, r4], 'sssvvvv'
-            acc, = call(functools.partial(scatter_kernel, dim, rows, edges, first), args, kinds, [shape((rows * SLICES, LANES))], 'h',
-                        [table_shape, stage_shape, square_shape, pltpu.SemaphoreType.DMA], 25)
+                args, kinds = [heads[s], tails[s], rels[s], hg, dp, head_cols, r4], 'sssVvVV'
+            acc, = call(functools.partial(scatter_kernel, dim, edges, first), args, kinds, [table_out], 'V',
+                        [stage_shape, square_shape], 25)
             neg_got, acc = tie((neg_got, acc))
             gmine, gother = finish(neg_part, neg_got)
-            scratch = [table_shape, pltpu.VMEM((rows, LANES), F32), table_shape, stage_shape, square_shape]
+            scratch = [stage_shape, square_shape]
             if last:
-                args, kinds = [core, negs[s]], 'sshhhvv'
-                outs, out_kinds = [shape((dim, rows)), shape((rows // LANES, LANES))], 'hv'
-                scratch += [pltpu.VMEM((2, dim, 4 * LANES), F32)]
+                args, outs, out_kinds = [core, negs[s]], [table_out, shape((dim, rows)), shape((rows // LANES, LANES))], 'Vhv'
+                scratch += [pltpu.VMEM((2, dim, 4 * LANES), F32), pltpu.SemaphoreType.DMA((2,))]
+                aliases = {4: 0}
             else:
-                args, kinds = [core, negs[s], tails[s + 1], negs[s + 1]], 'sssshhhvv'
-                outs, out_kinds = [shape((rows * SLICES, LANES)), shape((rows, LANES)), cols_bf, neg_half, neg_half], 'hhvvv'
+                args = [core, negs[s], tails[s + 1], negs[s + 1]]
+                outs, out_kinds = [table_out, table_out, state_out, cols_bf, neg_half, neg_half], 'VVVVVV'
                 scratch += [pltpu.VMEM((dim, negp), BF16)]
-            res = call(functools.partial(update_kernel, dim, rows, last), args + [t4, v, acc, gmine, gother], kinds, outs, out_kinds,
-                       scratch + [pltpu.SemaphoreType.DMA((3,)), pltpu.SemaphoreType.DMA((2,))], 30)
+                aliases = {6: 0, 4: 1, 5: 2}
+            res = call(functools.partial(update_kernel, dim, rows, last), args + [t4, v, acc, gmine, gother], 's' * len(args) + 'VVVVV',
+                       outs, out_kinds, scratch, 30, aliases)
             if last:
-                et, g = res
+                _, et, g = res
             else:
-                t4, v, tb, nk, ns = res
+                _, t4, v, tb, nk, ns = res
 
         even = core[0] == 0
         rel_grads = finish(rel_part, rel_got)

time: 568 us -> 467 us (0.82)
  Pallas kernels: 365 us -> 228 us
  waiting for transfers between devices: 129 us -> 182 us
  other arithmetic: 31.7 us -> 10.2 us
  local copies, waits for them, and re-layouts: 19.6 us -> 27.9 us
    pallas_call x19, Pallas kernels: 365 us -> 228 us  [call(): pl.pallas_call(kernel, out_shape=outs, in_specs=[places[k]() for k in kin...]
    ppermute x13, waiting for transfers between devices: 72.9 us -> 121 us  [send(): return lax.ppermute(value, 'ent', pairs)]
    unnamed x72 -> x48, local copies, waits for them, and re-layouts: 12.7 us -> 27.1 us
    add x9, other arithmetic: 12.3 us -> 1.06 us  [chip_sum(): return keep + lax.ppermute(send, 'ent', swap)]
    add x9, other arithmetic: 12.2 us -> 3.23 us  [finish(): mine = part + got]
  transfers between devices with their start and end apart: 35 -> 35, of which waited for: 20 -> 26; matrix products, arithmetic and copies ran while one was open for 4% -> 1% of each run, Pallas kernels for 43% -> 31%
where the time goes in v3:
time: 467 us; the launch traced here: 466 us
  Pallas kernels  228 us (49%)
  waiting for transfers between devices  182 us (39%)
  local copies, waits for them, and re-layouts  27.9 us (6%)
  starting transfers between devices  17.1 us (4%)
  other arithmetic  10.2 us (2%)
    pallas_call x19, Pallas kernels, call(): pl.pallas_call(kernel, out_shape=outs, in_specs=[places[k]() for k in kin...  228 us
    ppermute x13, waiting for transfers between devices, send(): return lax.ppermute(value, 'ent', pairs)  121 us
    ppermute x2, waiting for transfers between devices, device_fn(): dp = lax.ppermute(dp, 'ent', shift(s))  30.2 us
    unnamed x48, local copies, waits for them, and re-layouts  27.1 us
    ppermute x9, waiting for transfers between devices, chip_sum(): return keep + lax.ppermute(send, 'ent', swap)  15.6 us
    ppermute x9, waiting for transfers between devices, finish(): return (mine, lax.ppermute(mine, 'ent', swap))  13 us
    ppermute x13, starting transfers between devices, send(): return lax.ppermute(value, 'ent', pairs)  10.9 us
  transfers between devices with their start and end apart: 35, of which 26 were waited for; matrix products, arithmetic and copies ran while one was open for 1% of the time, Pallas kernels for 31%

profile of v3, /device:TPU:0, one launch (start us, length us, event | category | flops | bytes accessed | tf_op | source)
XLA Modules:
  0.0 466.3 jit_solution(7994547090471277603)
XLA Ops:
  1.4 4.7 %copy-done.10 = f32[8192,400]{0,1:T(8,128)S(1)} copy-done((f32[8192,400]{0,1:T(8,128)S(1)}, f32[8192,400]{0,1:T(8,128)}, u32[]{:S(2)}) %copy-start.10) | copy-done | bytes 13107224
  6.9 9.8 %shard_map.128 = (f32[32800,128]{1,0:T(8,128)S(1)}, f32[8192,128]{1,0:T(8,128)S(1)}, bf16[400,512]{1,0:T(8,128)(2,1)S(1)}, bf16[400,512]{1,0:T(8,128)(2,1)S(1)}) custom-call(s32[1]{0:T(128)} %bitcast.core_ref.refs_0_, s32[1024]{0:T(1024)S(1)} %bitcast.68, f32[400,8192]{1,0:T(8,128)S(1)} %bitcast.45, f32[64,128]{1,0:T(8,128)S(1)} %bitcast.70), custom_call_target="tpu_custom_call" | custom-call | flops 100000000 | tf_op jit(solution)/shard_map/pallas_call | solution.py:460
  17.7 3.0 collective-permute-start.2
  24.6 7.5 %shard_map.129 = (bf16[400,2048]{1,0:T(8,128)(2,1)S(1)}, bf16[400,2048]{1,0:T(8,128)(2,1)S(1)}) custom-call(s32[2048]{0:T(1024)S(1)} %bitcast.50, s32[2048]{0:T(1024)S(1)} %bitcast.52, f32[32800,128]{1,0:T(8,128)S(1)} %get-tuple-element.107.refs_2_.refs_4_), custom_call_target="tpu_custom_call" | custom-call | flops 55000000 | tf_op jit(solution)/shard_map/pallas_call | solution.py:460
  34.5 6.8 %shard_map.130 = (f32[400,2048]{1,0:T(8,128)S(1)}, f32[400,2048]{1,0:T(8,128)S(1)}, f32[5632,128]{1,0:T(8,128)}) custom-call(s32[1]{0:T(128)} %bitcast.core_ref.refs_0_, s32[2048]{0:T(1024)S(1)} %bitcast.58, bf16[400,2048]{1,0:T(8,128)(2,1)S(1)} %get-tuple-element.113.refs_2_.hb, f32[400,1408]{1,0:T(8,128)S(1)} %pad.13.refs_3_), custom_call_target="tpu_custom_call" | custom-call | flops 50000000 | tf_op jit(solution)/shard_map/pallas_call | solution.py:460
  43.1 14.5 %shard_map.131 = (f32[1,128]{1,0:T(1,128)S(1)}, f32[1,2048]{1,0:T(1,128)S(1)}, bf16[1024,2048]{1,0:T(8,128)(2,1)S(1)}, f32[200,1024]{1,0:T(8,128)S(1)}, f32[200,1024]{1,0:T(8,128)S(1)}) custom-call(s32[1]{0:T(128)} %bitcast.core_ref.refs_0_, f32[1,2048]{1,0:T(1,128)S(1)} %get-tuple-element.213.w, f32[400,2048]{1,0:T(8,128)S(1)} %get-tuple-element.115.q.refs_4_, ...), custom_call_target="tpu_custom_call" | custom-call | flops 75000000 | tf_op jit(solution)/shard_map/pallas_call | solution.py:460
  60.1 11.6 %shard_map.132 = (f32[8192,128]{1,0:T(8,128)S(1)}, f32[200,1408]{1,0:T(8,128)S(1)}, f32[200,1408]{1,0:T(8,128)S(1)}) custom-call(s32[1]{0:T(128)} %bitcast.core_ref.refs_0_, s32[2048]{0:T(1024)S(1)} %bitcast.59, bf16[1024,2048]{1,0:T(8,128)(2,1)S(1)} %get-tuple-element.122.ds, f32[1,2048]{1,0:T(1,128)S(1)} %get-tuple-element.123.dp.refs_3_, ...), custom_call_target="tpu_custom_call" | custom-call | flops 75000000 | tf_op jit(solution)/shard_map/pallas_call | solution.py:460
  74.6 13.8 %shard_map.133.refs_6_ = f32[32800,128]{1,0:T(8,128)S(1)} custom-call(s32[2048]{0:T(1024)S(1)} %bitcast.53, s32[2048]{0:T(1024)S(1)} %bitcast.51, f32[8192,128]{1,0:T(8,128)S(1)} %get-tuple-element.128.refs_2_, f32[1,2048]{1,0:T(1,128)S(1)} %get-tuple-element.123.dp.refs_3_, f32[400,2048]{1,0:T(8,128)S(1)} %get-tuple-element.115.q.refs_4_), custom_call_target="tpu_custom_call" | custom-call | flops 125000000 | tf_op jit(solution)/shard_map/pallas_call | solution.py:460
  88.4 3.9 collective-permute-done.6
  94.8 19.3 %shard_map.134 = (f32[32800,128]{1,0:T(8,128)S(1)}, f32[32800,128]{1,0:T(8,128)S(1)}, f32[8192,128]{1,0:T(8,128)S(1)}, bf16[400,2048]{1,0:T(8,128)(2,1)S(1)}, bf...) custom-call(s32[1]{0:T(128)} %bitcast.core_ref.refs_0_, ...), custom_call_target="tpu_custom_call", output_to_operand_aliasing={{0}: (6, {}), {1}: (4, {}), {2}: (5, {})} | custom-call | flops 150000000 | tf_op jit(solution)/shard_map/pallas_call | solution.py:460
  116.3 4.0 shard_map.135.refs_2_.hb
  123.3 5.6 %shard_map.136 = (f32[400,2048]{1,0:T(8,128)S(1)}, f32[400,2048]{1,0:T(8,128)S(1)}, f32[5632,128]{1,0:T(8,128)S(1)}, f32[400,1408]{1,0:T(8,128)S(1)}, f32[1,1408]{1,0:T(1,128)S(1)}) custom-call(s32[1]{0:T(128)} %bitcast.core_ref.refs_0_, s32[2048]{0:T(1024)S(1)} %bitcast.56, bf16[400,2048]{1,0:T(8,128)(2,1)S(1)} %shard_map.135.refs_2_.hb, ...), custom_call_target="tpu_custom_call" | custom-call | flops 50000000 | tf_op jit(solution)/shard_map/pallas_call | solution.py:460
  128.9 17.1 %collective-permute-done.10 = bf16[400,512]{1,0:T(8,128)(2,1)S(1)} collective-permute-done((bf16[400,512]{1,0:T(8,128)(2,1)S(1)}, bf16[400,512]{1,0:T(8,128)(2,1)S(1)}, u32[]{:S(2)}, u32[]{:S(2)}) %collective-permute-start.10) | collective-permute-done | bytes 409632 | tf_op jit(solution)/shard_map/ppermute | solution.py:412
  147.9 14.7 %shard_map.137 = (f32[1,128]{1,0:T(1,128)S(1)}, f32[1,2048]{1,0:T(1,128)S(1)}, bf16[1024,2048]{1,0:T(8,128)(2,1)S(1)}, f32[200,1024]{1,0:T(8,128)S(1)}, f32[200,1024]{1,0:T(8,128)S(1)}) custom-call(s32[1]{0:T(128)} %bitcast.core_ref.refs_0_, f32[1,2048]{1,0:T(1,128)S(1)} %get-tuple-element.212.w, f32[400,2048]{1,0:T(8,128)S(1)} %get-tuple-element.142.q, ...), custom_call_target="tpu_custom_call" | custom-call | flops 75000000 | tf_op jit(solution)/shard_map/pallas_call | solution.py:460
  165.1 11.6 %shard_map.138 = (f32[8192,128]{1,0:T(8,128)S(1)}, f32[200,1408]{1,0:T(8,128)S(1)}, f32[200,1408]{1,0:T(8,128)S(1)}) custom-call(s32[1]{0:T(128)} %bitcast.core_ref.refs_0_, s32[2048]{0:T(1024)S(1)} %bitcast.57, bf16[1024,2048]{1,0:T(8,128)(2,1)S(1)} %get-tuple-element.150.ds, f32[1,2048]{1,0:T(1,128)S(1)} %get-tuple-element.151.dp, ...), custom_call_target="tpu_custom_call" | custom-call | flops 75000000 | tf_op jit(solution)/shard_map/pallas_call | solution.py:460
  179.6 6.6 %collective-permute-done.19.refs_5_ = bf16[400,2048]{1,0:T(8,128)(2,1)S(1)} collective-permute-done((bf16[400,2048]{1,0:T(8,128)(2,1)S(1)}, bf16[400,2048]{1,0:T(8,128)(2,1)S(1)}, u32[]{:S(2)}, u32[]{:S(2)}) %collective-permute-start.19) | collective-permute-done | bytes 1638432 | tf_op jit(solution)/shard_map/ppermute | solution.py:412
  186.2 14.7 %collective-permute-done.18.refs_4_ = f32[1,2048]{1,0:T(1,128)S(1)} collective-permute-done((f32[1,2048]{1,0:T(1,128)S(1)}, f32[1,2048]{1,0:T(1,128)S(1)}, u32[]{:S(2)}, u32[]{:S(2)}) %collective-permute-start.18) | collective-permute-done | bytes 8224 | tf_op jit(solution)/shard_map/ppermute | solution.py:530
  201.0 18.4 %shard_map.139.refs_6_ = f32[32800,128]{1,0:T(8,128)S(1)} custom-call(s32[2048]{0:T(1024)S(1)} %bitcast.49, s32[2048]{0:T(1024)S(1)} %bitcast.63, s32[2048]{0:T(1024)S(1)} %bitcast.72, f32[8192,128]{1,0:T(8,128)S(1)} %get-tuple-element.156.refs_3_, f32[1,2048]{1,0:T(1,128)S(1)} %collective-permute-done.18.refs_4_, ...), custom_call_target="tpu_custom_call" | custom-call | flops 125000000 | tf_op jit(solution)/shard_map/pallas_call | solution.py:460
  223.1 19.3 %shard_map.140 = (f32[32800,128]{1,0:T(8,128)S(1)}, f32[32800,128]{1,0:T(8,128)S(1)}, f32[8192,128]{1,0:T(8,128)S(1)}, bf16[400,2048]{1,0:T(8,128)(2,1)S(1)}, bf...) custom-call(s32[1]{0:T(128)} %bitcast.core_ref.refs_0_, ...), custom_call_target="tpu_custom_call", output_to_operand_aliasing={{0}: (6, {}), {1}: (4, {}), {2}: (5, {})} | custom-call | flops 150000000 | tf_op jit(solution)/shard_map/pallas_call | solution.py:460
  246.8 4.0 shard_map.141.refs_2_.hb
  253.8 5.6 %shard_map.142 = (f32[400,2048]{1,0:T(8,128)S(1)}, f32[400,2048]{1,0:T(8,128)S(1)}, f32[5632,128]{1,0:T(8,128)S(1)}, f32[400,1408]{1,0:T(8,128)S(1)}, f32[1,1408]{1,0:T(1,128)S(1)}) custom-call(s32[1]{0:T(128)} %bitcast.core_ref.refs_0_, s32[2048]{0:T(1024)S(1)} %bitcast.54, bf16[400,2048]{1,0:T(8,128)(2,1)S(1)} %shard_map.141.refs_2_.hb, ...), custom_call_target="tpu_custom_call" | custom-call | flops 50000000 | tf_op jit(solution)/shard_map/pallas_call | solution.py:460
  259.5 33.4 %collective-permute-done.22 = bf16[400,512]{1,0:T(8,128)(2,1)S(1)} collective-permute-done((bf16[400,512]{1,0:T(8,128)(2,1)S(1)}, bf16[400,512]{1,0:T(8,128)(2,1)S(1)}, u32[]{:S(2)}, u32[]{:S(2)}) %collective-permute-start.22) | collective-permute-done | bytes 409632 | tf_op jit(solution)/shard_map/ppermute | solution.py:412
  294.8 14.5 %shard_map.143 = (f32[1,128]{1,0:T(1,128)S(1)}, f32[1,2048]{1,0:T(1,128)S(1)}, bf16[1024,2048]{1,0:T(8,128)(2,1)S(1)}, f32[200,1024]{1,0:T(8,128)S(1)}, f32[200,1024]{1,0:T(8,128)S(1)}) custom-call(s32[1]{0:T(128)} %bitcast.core_ref.refs_0_, f32[1,2048]{1,0:T(1,128)S(1)} %get-tuple-element.211.w, f32[400,2048]{1,0:T(8,128)S(1)} %get-tuple-element.173.q, ...), custom_call_target="tpu_custom_call" | custom-call | flops 75000000 | tf_op jit(solution)/shard_map/pallas_call | solution.py:460
  311.7 11.8 %shard_map.144 = (f32[8192,128]{1,0:T(8,128)S(1)}, f32[200,1408]{1,0:T(8,128)S(1)}, f32[200,1408]{1,0:T(8,128)S(1)}) custom-call(s32[1]{0:T(128)} %bitcast.core_ref.refs_0_, s32[2048]{0:T(1024)S(1)} %bitcast.55, bf16[1024,2048]{1,0:T(8,128)(2,1)S(1)} %get-tuple-element.181.ds, f32[1,2048]{1,0:T(1,128)S(1)} %get-tuple-element.182.dp, ...), custom_call_target="tpu_custom_call" | custom-call | flops 75000000 | tf_op jit(solution)/shard_map/pallas_call | solution.py:460
  328.5 58.0 %collective-permute-done.33 = f32[200,1408]{1,0:T(8,128)S(1)} collective-permute-done((f32[200,1408]{1,0:T(8,128)S(1)}, f32[200,1408]{1,0:T(8,128)S(1)}, u32[]{:S(2)}, u32[]{:S(2)}) %collective-permute-start.33) | collective-permute-done | bytes 1126432 | tf_op jit(solution)/shard_map/ppermute | solution.py:412
  388.2 15.5 %collective-permute-done.30.refs_4_ = f32[1,2048]{1,0:T(1,128)S(1)} collective-permute-done((f32[1,2048]{1,0:T(1,128)S(1)}, f32[1,2048]{1,0:T(1,128)S(1)}, u32[]{:S(2)}, u32[]{:S(2)}) %collective-permute-start.30) | collective-permute-done | bytes 8224 | tf_op jit(solution)/shard_map/ppermute | solution.py:530
  403.6 18.4 %shard_map.145.refs_4_ = f32[32800,128]{1,0:T(8,128)S(1)} custom-call(s32[2048]{0:T(1024)S(1)} %bitcast.47, s32[2048]{0:T(1024)S(1)} %bitcast.61, s32[2048]{0:T(1024)S(1)} %bitcast.71, f32[8192,128]{1,0:T(8,128)S(1)} %get-tuple-element.187.refs_3_, f32[1,2048]{1,0:T(1,128)S(1)} %collective-permute-done.30.refs_4_, ...), custom_call_target="tpu_custom_call" | custom-call | flops 125000000 | tf_op jit(solution)/shard_map/pallas_call | solution.py:460
  422.1 5.8 %copy-done.2 = f32[32800,128]{1,0:T(8,128)} copy-done((f32[32800,128]{1,0:T(8,128)}, f32[32800,128]{1,0:T(8,128)S(1)}, u32[]{:S(2)}) %copy-start.2) | copy-done | bytes 16793624
  430.5 5.8 %copy-done.1 = f32[32800,128]{1,0:T(8,128)S(1)} copy-done((f32[32800,128]{1,0:T(8,128)S(1)}, f32[32800,128]{1,0:T(8,128)}, u32[]{:S(2)}) %copy-start.1) | copy-done | bytes 16793624
  436.2 5.8 %copy-done.3 = f32[32800,128]{1,0:T(8,128)S(1)} copy-done((f32[32800,128]{1,0:T(8,128)S(1)}, f32[32800,128]{1,0:T(8,128)}, u32[]{:S(2)}) %copy-start.3) | copy-done | bytes 16793624
  444.2 17.1 %shard_map.146 = (f32[32800,128]{1,0:T(8,128)S(1)}, f32[400,8192]{1,0:T(8,128)}, f32[64,128]{1,0:T(8,128)}) custom-call(s32[1]{0:T(128)} %bitcast.core_ref.refs_0_, s32[1024]{0:T(1024)S(1)} %bitcast.65, f32[32800,128]{1,0:T(8,128)S(1)} %copy-done.1, f32[8192,128]{1,0:T(8,128)S(1)} %copy-done.9, ...), custom_call_target="tpu_custom_call", output_to_operand_aliasing={{0}: (4, {})} | custom-call | flops 150000000 | tf_op jit(solution)/shard_map/pallas_call | solution.py:460
  461.3 2.7 multiply_reduce_fusion
  (142 shorter events, 59.9 us)
Async XLA Ops:
  16.7 5.7 %collective-permute-start = (bf16[400,512]{1,0:T(8,128)(2,1)S(1)}, bf16[400,512]{1,0:T(8,128)(2,1)S(1)}, u32[]{:S(2)}, u32[]{:S(2)}) collective-permute-start(bf16[400,512]{1,0:T(8,128)(2,1)S(1)} %get-tuple-element.103), channel_id=1, source_target_pairs={{0,1},{1,0},{2,3},{3,2},{4,5},{5,4},{6,7},{7,6}} | collective-permute-start | bytes 1228808 | tf_op jit(solution)/shard_map/ppermute | solution.py:409
  17.6 4.0 collective-permute-start.1
  17.7 4.7 %collective-permute-start.2 = (s32[2,2048]{1,0:T(2,128)S(1)}, s32[2,2048]{1,0:T(2,128)S(1)}, u32[]{:S(2)}, u32[]{:S(2)}) collective-permute-start(s32[2,2048]{1,0:T(2,128)S(1)} %pad_add_fusion.1), channel_id=1, source_target_pairs={{0,2},{1,3},{2,0},{3,1},{4,6},{5,7},{6,4},{7,5}} | collective-permute-start | bytes 49160 | tf_op jit(solution)/shard_map/ppermute | solution.py:437
  22.6 11.9 %collective-permute-start.3 = (bf16[400,512]{1,0:T(8,128)(2,1)S(1)}, bf16[400,512]{1,0:T(8,128)(2,1)S(1)}, u32[]{:S(2)}, u32[]{:S(2)}) collective-permute-start(bf16[400,512]{1,0:T(8,128)(2,1)S(1)} %add.82), channel_id=1, source_target_pairs={{0,2},{1,3},{2,0},{3,1},{4,6},{5,7},{6,4},{7,5}} | collective-permute-start | bytes 1228808 | tf_op jit(solution)/shard_map/ppermute | solution.py:412
  57.6 2.4 collective-permute-start.5
  71.6 2.8 collective-permute-start.7
  71.8 20.5 %collective-permute-start.6 = (f32[200,1024]{1,0:T(8,128)S(1)}, f32[200,1024]{1,0:T(8,128)S(1)}, u32[]{:S(2)}, u32[]{:S(2)}) collective-permute-start(f32[200,1024]{1,0:T(8,128)S(1)} %add.84), channel_id=1, source_target_pairs={{0,2},{1,3},{2,0},{3,1},{4,6},{5,7},{6,4},{7,5}} | collective-permute-start | bytes 2457608 | tf_op jit(solution)/shard_map/ppermute | solution.py:412
  92.5 2.4 collective-permute-start.8
  92.5 27.9 %collective-permute-start.11 = (f32[200,1408]{1,0:T(8,128)S(1)}, f32[200,1408]{1,0:T(8,128)S(1)}, u32[]{:S(2)}, u32[]{:S(2)}) collective-permute-start(f32[200,1408]{1,0:T(8,128)S(1)} %add.85), channel_id=1, source_target_pairs={{0,2},{1,3},{2,0},{3,1},{4,6},{5,7},{6,4},{7,5}} | collective-permute-start | bytes 3379208 | tf_op jit(solution)/shard_map/ppermute | solution.py:412
  116.0 31.9 %collective-permute-start.13 = (bf16[400,2048]{1,0:T(8,128)(2,1)S(1)}, bf16[400,2048]{1,0:T(8,128)(2,1)S(1)}, u32[]{:S(2)}, u32[]{:S(2)}) collective-permute-start(bf16[400,2048]{1,0:T(8,128)(2,1)S(1)} %get-tuple-element.143), channel_id=1, source_target_pairs={{0,3},{1,0},{2,1},{3,2},{4,7},{5,4},{6,5},{7,6}} | collective-permute-start | bytes 4915208 | tf_op jit(solution)/shard_map/ppermute | solution.py:412
  120.5 2.8 collective-permute-start.12
  120.8 25.3 %collective-permute-start.10 = (bf16[400,512]{1,0:T(8,128)(2,1)S(1)}, bf16[400,512]{1,0:T(8,128)(2,1)S(1)}, u32[]{:S(2)}, u32[]{:S(2)}) collective-permute-start(bf16[400,512]{1,0:T(8,128)(2,1)S(1)} %add.87), channel_id=1, source_target_pairs={{0,2},{1,3},{2,0},{3,1},{4,6},{5,7},{6,4},{7,5}} | collective-permute-start | bytes 1228808 | tf_op jit(solution)/shard_map/ppermute | solution.py:412
  146.2 1.8 collective-permute-start.14
  162.6 2.4 collective-permute-start.15
  162.8 23.4 %collective-permute-start.19 = (bf16[400,2048]{1,0:T(8,128)(2,1)S(1)}, bf16[400,2048]{1,0:T(8,128)(2,1)S(1)}, u32[]{:S(2)}, u32[]{:S(2)}) collective-permute-start(bf16[400,2048]{1,0:T(8,128)(2,1)S(1)} %shard_map.135.refs_2_.hb), channel_id=1, source_target_pairs={{0,1},{1,2},{2,3},{3,0},{4,5},{5,6},{6,7},{7,4}} | collective-permute-start | bytes 4915208 | tf_op jit(solution)/shard_map/ppermute | solution.py:412
  176.7 2.8 collective-permute-start.17
  176.9 42.6 %collective-permute-start.16 = (f32[200,1024]{1,0:T(8,128)S(1)}, f32[200,1024]{1,0:T(8,128)}, u32[]{:S(2)}, u32[]{:S(2)}) collective-permute-start(f32[200,1024]{1,0:T(8,128)S(1)} %add.90), channel_id=1, source_target_pairs={{0,2},{1,3},{2,0},{3,1},{4,6},{5,7},{6,4},{7,5}} | collective-permute-start | bytes 2457608 | tf_op jit(solution)/shard_map/ppermute | solution.py:412
  177.4 23.6 %collective-permute-start.18 = (f32[1,2048]{1,0:T(1,128)S(1)}, f32[1,2048]{1,0:T(1,128)S(1)}, u32[]{:S(2)}, u32[]{:S(2)}) collective-permute-start(f32[1,2048]{1,0:T(1,128)S(1)} %get-tuple-element.151.dp), channel_id=1, source_target_pairs={{0,1},{1,2},{2,3},{3,0},{4,5},{5,6},{6,7},{7,4}} | collective-permute-start | bytes 24584 | tf_op jit(solution)/shard_map/ppermute | solution.py:530
  220.7 2.4 collective-permute-start.20
  220.7 30.1 %collective-permute-start.23 = (f32[200,1408]{1,0:T(8,128)S(1)}, f32[200,1408]{1,0:T(8,128)S(1)}, u32[]{:S(2)}, u32[]{:S(2)}) collective-permute-start(f32[200,1408]{1,0:T(8,128)S(1)} %add.91), channel_id=1, source_target_pairs={{0,2},{1,3},{2,0},{3,1},{4,6},{5,7},{6,4},{7,5}} | collective-permute-start | bytes 3379208 | tf_op jit(solution)/shard_map/ppermute | solution.py:412
  246.2 48.6 %collective-permute-start.25 = (bf16[400,2048]{1,0:T(8,128)(2,1)S(1)}, bf16[400,2048]{1,0:T(8,128)(2,1)S(1)}, u32[]{:S(2)}, u32[]{:S(2)}) collective-permute-start(bf16[400,2048]{1,0:T(8,128)(2,1)S(1)} %get-tuple-element.174), channel_id=1, source_target_pairs={{0,2},{1,3},{2,0},{3,1},{4,6},{5,7},{6,4},{7,5}} | collective-permute-start | bytes 4915208 | tf_op jit(solution)/shard_map/ppermute | solution.py:412
  251.0 2.8 collective-permute-start.24
  251.1 41.8 %collective-permute-start.22 = (bf16[400,512]{1,0:T(8,128)(2,1)S(1)}, bf16[400,512]{1,0:T(8,128)(2,1)S(1)}, u32[]{:S(2)}, u32[]{:S(2)}) collective-permute-start(bf16[400,512]{1,0:T(8,128)(2,1)S(1)} %add.93), channel_id=1, source_target_pairs={{0,2},{1,3},{2,0},{3,1},{4,6},{5,7},{6,4},{7,5}} | collective-permute-start | bytes 1228808 | tf_op jit(solution)/shard_map/ppermute | solution.py:412
  293.0 1.8 collective-permute-start.26
  309.3 2.4 collective-permute-start.27
  323.5 2.8 collective-permute-start.29
  323.7 64.5 %collective-permute-start.31 = (bf16[400,2048]{1,0:T(8,128)(2,1)S(1)}, bf16[400,2048]{1,0:T(8,128)(2,1)S(1)}, u32[]{:S(2)}, u32[]{:S(2)}) collective-permute-start(bf16[400,2048]{1,0:T(8,128)(2,1)S(1)} %shard_map.141.refs_2_.hb), channel_id=1, source_target_pairs={{0,2},{1,3},{2,0},{3,1},{4,6},{5,7},{6,4},{7,5}} | collective-permute-start | bytes 4915208 | tf_op jit(solution)/shard_map/ppermute | solution.py:412
  326.5 60.0 %collective-permute-start.33 = (f32[200,1408]{1,0:T(8,128)S(1)}, f32[200,1408]{1,0:T(8,128)S(1)}, u32[]{:S(2)}, u32[]{:S(2)}) collective-permute-start(f32[200,1408]{1,0:T(8,128)S(1)} %add.97), channel_id=1, source_target_pairs={{0,2},{1,3},{2,0},{3,1},{4,6},{5,7},{6,4},{7,5}} | collective-permute-start | bytes 3379208 | tf_op jit(solution)/shard_map/ppermute | solution.py:412
  327.0 100.8 %collective-permute-start.28 = (f32[200,1024]{1,0:T(8,128)S(1)}, f32[200,1024]{1,0:T(8,128)S(1)}, u32[]{:S(2)}, u32[]{:S(2)}) collective-permute-start(f32[200,1024]{1,0:T(8,128)S(1)} %add.96), channel_id=1, source_target_pairs={{0,2},{1,3},{2,0},{3,1},{4,6},{5,7},{6,4},{7,5}} | collective-permute-start | bytes 2457608 | tf_op jit(solution)/shard_map/ppermute | solution.py:412
  387.6 73.7 %collective-permute-start.34 = (f32[200,1408]{1,0:T(8,128)}, f32[200,1408]{1,0:T(8,128)}, u32[]{:S(2)}, u32[]{:S(2)}) collective-permute-start(f32[200,1408]{1,0:T(8,128)} %add.99), channel_id=1, source_target_pairs={{0,1},{1,0},{2,3},{3,2},{4,5},{5,4},{6,7},{7,6}} | collective-permute-start | bytes 3379208 | tf_op jit(solution)/shard_map/ppermute | solution.py:419
  387.6 16.0 %collective-permute-start.30 = (f32[1,2048]{1,0:T(1,128)S(1)}, f32[1,2048]{1,0:T(1,128)S(1)}, u32[]{:S(2)}, u32[]{:S(2)}) collective-permute-start(f32[1,2048]{1,0:T(1,128)S(1)} %get-tuple-element.182.dp), channel_id=1, source_target_pairs={{0,2},{1,3},{2,0},{3,1},{4,6},{5,7},{6,4},{7,5}} | collective-permute-start | bytes 24584 | tf_op jit(solution)/shard_map/ppermute | solution.py:530
  428.0 2.5 collective-permute-start.32
  (27 other events, 249.8 us)

commit v4 on v3

--- a/solution.py
+++ b/solution.py
@@ -177,37 +177,50 @@
     nb[:, pl.ds(pl.multiple_of((1 - core) * nhalf, LANES), nhalf)] = nother[...]
 
 
-def score_kernel(dim, neg_count, edges, core_ref, w, q, tb, nfull, nother,
-                 loss, dp_out, ds, nk, ns, nb, nbt, sc, ng, fm):
-    core = core_ref[0]
-    half = dim // 2
+def exp_kernel(neg_count, edges, core_ref, q, nfull, nother, e_out, top_out, sum_out, nb, nbt, sc):
     negp = nb.shape[1]
-    place_negs(core, nb, nfull, nother)
+    place_negs(core_ref[0], nb, nfull, nother)
     for b in range(negp // LANES):
         nbt[pl.ds(b * LANES, LANES), :] = nb[:, pl.ds(b * LANES, LANES)].astype(F32).T.astype(BF16)
-    ng[...] = jnp.zeros(ng.shape, F32)
-    ds[pl.ds(neg_count, negp - neg_count), :] = jnp.zeros((negp - neg_count, edges), BF16)
-
-    def step(c, loss_row):
+
+    def step(c, _):
         cols = pl.ds(pl.multiple_of(c * CHUNK, LANES), CHUNK)
-        qb = q[:, cols].astype(BF16)
-        pos = jnp.sum(q[:, cols] * tb[:, cols].astype(F32), axis=0, keepdims=True)
-        sc[...] = lax.dot_general(nbt[...], qb, (((1,), (0,)), ((), ())), preferred_element_type=F32)
-        top = jnp.maximum(pos, jnp.max(sc[pl.ds(0, neg_count), :], axis=0, keepdims=True))
-        pos_exp = jnp.exp(pos - top)
-        norm = pos_exp
+        sc[...] = lax.dot_general(nbt[pl.ds(0, neg_count), :], q[:, cols].astype(BF16), (((1,), (0,)), ((), ())), preferred_element_type=F32)
+        top = jnp.max(sc[...], axis=0, keepdims=True)
+        top_out[:, cols] = top
+        total = jnp.zeros((1, CHUNK), F32)
         part = 200
         for i in range(0, neg_count, part):
             size = min(part, neg_count - i)
             e = jnp.exp(sc[pl.ds(i, size), :] - top)
-            sc[pl.ds(i, size), :] = e
-            norm = norm + jnp.sum(e, axis=0, keepdims=True)
+            e_out[pl.ds(i, size), cols] = e
+            total = total + jnp.sum(e, axis=0, keepdims=True)
+        sum_out[:, cols] = total
+        return 0
+
+    lax.fori_loop(0, edges // CHUNK, step, 0)
+
+
+def score_kernel(dim, neg_count, edges, core_ref, w, q, tb, e, neg_top, neg_sum,
+                 loss, dp_out, ds, nk, ns, ng, fm):
+    core = core_ref[0]
+    half = dim // 2
+    negp = ds.shape[0]
+    ng[...] = jnp.zeros(ng.shape, F32)
+    ds[pl.ds(neg_count, negp - neg_count), :] = jnp.zeros((negp - neg_count, edges), BF16)
+
+    def step(c, loss_row):
+        cols = pl.ds(pl.multiple_of(c * CHUNK, LANES), CHUNK)
+        pos = jnp.sum(q[:, cols] * tb[:, cols].astype(F32), axis=0, keepdims=True)
+        top = jnp.maximum(pos, neg_top[:, cols])
+        pos_exp = jnp.exp(pos - top)
+        shrink = jnp.exp(neg_top[:, cols] - top)
+        norm = pos_exp + shrink * neg_sum[:, cols]
         wt = w[:, cols]
         loss_row = loss_row + wt * (top + jnp.log(norm) - pos)
         dp_out[:, cols] = wt * (pos_exp / norm - 1.0)
-        scale = wt / norm
-        ds[pl.ds(0, neg_count), cols] = (sc[pl.ds(0, neg_count), :] * scale).astype(BF16)
-        ng[...] += lax.dot_general(ds[:, cols], qb, (((1,), (1,)), ((), ())), preferred_element_type=F32)
+        ds[pl.ds(0, neg_count), cols] = (e[:, cols] * (wt * shrink / norm)).astype(BF16)
+        ng[...] += lax.dot_general(ds[:, cols], q[:, cols].astype(BF16), (((1,), (1,)), ((), ())), preferred_element_type=F32)
         return loss_row
 
     loss_row = lax.fori_loop(0, edges // CHUNK, step, jnp.zeros((1, CHUNK), F32))
@@ -434,7 +447,7 @@
         own_rels = [rel_idx[0, s] * SLICES for s in range(rounds)]
         tails, rels = [own_tails[0]], [own_rels[0]]
         for s in range(1, rounds):
-            got = lax.ppermute(jnp.stack([own_tails[s], own_rels[s]]), 'ent', shift(s))
+            got = send(jnp.stack([own_tails[s], own_rels[s]]), shift(s))
             tails.append(got[0])
             rels.append(got[1])
         owned = (neg_idx // rows) == my_dev
@@ -467,7 +480,7 @@
                         [cols_bf] * len(lists), 'V' * len(lists), [stage_shape], 1 + 5 * len(lists))
 
         t4, v, nk, ns = call(
-            functools.partial(entry_kernel, dim, rows), [core, negs[0], ent_emb.T, ent_ada.reshape(rows // LANES, LANES)], 'sshv',
+            functools.partial(entry_kernel, dim, rows), [core, negs[0], pltpu.with_memory_space_constraint(ent_emb.T, pltpu.HBM), ent_ada.reshape(rows // LANES, LANES)], 'sshv',
             [table_out, state_out, neg_half, neg_half], 'VVVV',
             [pltpu.VMEM((2, SLICES * LANES, 4 * LANES), F32), stage_shape, pltpu.VMEM((dim, negp), BF16), pltpu.SemaphoreType.DMA((2,))], 20)
 
@@ -489,7 +502,6 @@
                 neg_got = link(neg_part)
                 tail_cols = send(tb, shift(-s))
                 hb, = gather([heads[s]], t4)
-                head_cols = send(hb, shift(s))
                 rel_got, hb = tie((rel_got, hb))
                 rel_grads = finish(rel_part, rel_got)
             wide = shape((dim, edges))
@@ -507,12 +519,21 @@
             nmine, nother = finish(neg_part, neg_got)
             if not first:
                 rfm, vr = res[3:]
+            e, neg_top, neg_total = call(
+                functools.partial(exp_kernel, neg_count, edges), [core, q, nmine, nother], 'sVVV',
+                [shape((neg_count, edges)), shape((1, edges)), shape((1, edges))], 'Vvv',
+                [pltpu.VMEM((dim, negp), BF16), pltpu.VMEM((negp, dim), BF16), pltpu.VMEM((neg_count, CHUNK), F32)], 8)
+            if not first:
+                e, tail_cols = tie((e, tail_cols))
+                tail_cols, hb = tie((tail_cols, hb))
+                head_cols = send(hb, shift(s))
             loss, dp, ds, gk, gs = call(
-                functools.partial(score_kernel, dim, neg_count, edges), [core, weights[s].reshape(1, edges), q, tail_cols, nmine, nother], 'svVVVV',
+                functools.partial(score_kernel, dim, neg_count, edges), [core, weights[s].reshape(1, edges), q, tail_cols, e, neg_top, neg_total], 'svVVVvv',
                 [shape((1, LANES)), shape((1, edges)), shape((negp, edges), BF16), shape((half, negp)), shape((half, negp))], 'vvVVV',
-                [pltpu.VMEM((dim, negp), BF16), pltpu.VMEM((negp, dim), BF16), pltpu.VMEM((negp, CHUNK), F32),
-                 pltpu.VMEM((negp, dim), F32), pltpu.VMEM((SLICES * LANES, negp), F32)], 15)
+                [pltpu.VMEM((negp, dim), F32), pltpu.VMEM((SLICES * LANES, negp), F32)], 8)
             losses.append(loss[0, 0])
+            if not first:
+                dp_away = send(dp, shift(s))
             neg_part = chip_sum(gk, gs)
             neg_part, ds = tie((neg_part, ds))
             neg_got = link(neg_part)
@@ -527,8 +548,7 @@
             if first:
                 args, kinds = [heads[s], tails[s], hg, dp, q], 'ssVvV'
             else:
-                dp = lax.ppermute(dp, 'ent', shift(s))
-                args, kinds = [heads[s], tails[s], rels[s], hg, dp, head_cols, r4], 'sssVvVV'
+                args, kinds = [heads[s], tails[s], rels[s], hg, dp_away, head_cols, r4], 'sssVvVV'
             acc, = call(functools.partial(scatter_kernel, dim, edges, first), args, kinds, [table_out], 'V',
                         [stage_shape, square_shape], 25)
             neg_got, acc = tie((neg_got, acc))

time: 467 us -> 459 us (0.983)
  Pallas kernels: 228 us -> 223 us
  local copies, waits for them, and re-layouts: 27.9 us -> 23.2 us
    ppermute x4 -> x0, waiting for transfers between devices: 31.7 us -> none  [the longest x2 30.2 us: device_fn(): dp = lax.ppermute(dp, 'ent', shift(s))]
    ppermute x13 -> x17, waiting for transfers between devices: 121 us -> 151 us  [send(): return lax.ppermute(value, 'ent', pairs)]
    pallas_call x19 -> x22, Pallas kernels: 228 us -> 223 us  [call(): pl.pallas_call(kernel, out_shape=outs, in_specs=[places[k]() for k in kin...]
    unnamed x48 -> x42, local copies, waits for them, and re-layouts: 27.1 us -> 22.3 us
    ppermute x13 -> x17, starting transfers between devices: 10.9 us -> 14.5 us  [send(): return lax.ppermute(value, 'ent', pairs)]
  transfers between devices with their start and end apart: 35 -> 35, of which waited for: 26 -> 25; matrix products, arithmetic and copies ran while one was open for 1% -> 1% of each run, Pallas kernels for 31% -> 34%
where the time goes in v4:
time: 459 us; the launch traced here: 458 us
  Pallas kernels  223 us (49%)
  waiting for transfers between devices  179 us (39%)
  local copies, waits for them, and re-layouts  23.2 us (5%)
  starting transfers between devices  17.1 us (4%)
  other arithmetic  13.6 us (3%)
    pallas_call x22, Pallas kernels, call(): pl.pallas_call(kernel, out_shape=outs, in_specs=[places[k]() for k in kin...  223 us
    ppermute x17, waiting for transfers between devices, send(): return lax.ppermute(value, 'ent', pairs)  151 us
    unnamed x42, local copies, waits for them, and re-layouts  22.3 us
    ppermute x9, waiting for transfers between devices, chip_sum(): return keep + lax.ppermute(send, 'ent', swap)  15.6 us
    ppermute x17, starting transfers between devices, send(): return lax.ppermute(value, 'ent', pairs)  14.5 us
    ppermute x9, waiting for transfers between devices, finish(): return (mine, lax.ppermute(mine, 'ent', swap))  13 us
  transfers between devices with their start and end apart: 35, of which 25 were waited for; matrix products, arithmetic and copies ran while one was open for 1% of the time, Pallas kernels for 34%

profile of v4, /device:TPU:0, one launch (start us, length us, event | category | flops | bytes accessed | tf_op | source)
XLA Modules:
  0.0 457.8 jit_solution(18280426175062639365)
XLA Ops:
  2.2 15.7 %shard_map.128 = (f32[32800,128]{1,0:T(8,128)S(1)}, f32[8192,128]{1,0:T(8,128)S(1)}, bf16[400,512]{1,0:T(8,128)(2,1)S(1)}, bf16[400,512]{1,0:T(8,128)(2,1)S(1)}) custom-call(s32[1]{0:T(128)} %bitcast.core_ref.refs_0_, s32[1024]{0:T(1024)S(1)} %bitcast.67, f32[400,8192]{1,0:T(8,128)} %bitcast.75, f32[64,128]{1,0:T(8,128)S(1)} %bitcast.69), custom_call_target="tpu_custom_call" | custom-call | flops 100000000 | tf_op jit(solution)/shard_map/pallas_call | solution.py:473
  18.9 3.0 collective-permute-start.2
  25.8 7.5 %shard_map.129 = (bf16[400,2048]{1,0:T(8,128)(2,1)S(1)}, bf16[400,2048]{1,0:T(8,128)(2,1)S(1)}) custom-call(s32[2048]{0:T(1024)S(1)} %bitcast.49, s32[2048]{0:T(1024)S(1)} %bitcast.51, f32[32800,128]{1,0:T(8,128)S(1)} %get-tuple-element.124.refs_2_.refs_4_), custom_call_target="tpu_custom_call" | custom-call | flops 55000000 | tf_op jit(solution)/shard_map/pallas_call | solution.py:473
  35.6 6.8 %shard_map.130 = (f32[400,2048]{1,0:T(8,128)S(1)}, f32[400,2048]{1,0:T(8,128)S(1)}, f32[5632,128]{1,0:T(8,128)}) custom-call(s32[1]{0:T(128)} %bitcast.core_ref.refs_0_, s32[2048]{0:T(1024)S(1)} %bitcast.57, bf16[400,2048]{1,0:T(8,128)(2,1)S(1)} %get-tuple-element.130.refs_2_.hb, f32[400,1408]{1,0:T(8,128)S(1)} %pad.13.refs_3_), custom_call_target="tpu_custom_call" | custom-call | flops 50000000 | tf_op jit(solution)/shard_map/pallas_call | solution.py:473
  44.3 5.4 %shard_map.131 = (f32[1000,2048]{1,0:T(8,128)S(1)}, f32[1,2048]{1,0:T(1,128)S(1)}, f32[1,2048]{1,0:T(1,128)S(1)}) custom-call(s32[1]{0:T(128)} %bitcast.core_ref.refs_0_, f32[400,2048]{1,0:T(8,128)S(1)} %get-tuple-element.132.q.refs_4_, bf16[400,512]{1,0:T(8,128)(2,1)S(1)} %add.83.nfull, bf16[400,512]{1,0:T(8,128)(2,1)S(1)} %collective-permute-done.4.nother), custom_call_target="tpu_custom_call" | custom-call | flops 40000000 | tf_op jit(solution)/shard_map/pallas_call | solution.py:473
  49.6 5.4 %shard_map.132 = (f32[1,128]{1,0:T(1,128)S(1)}, f32[1,2048]{1,0:T(1,128)S(1)}, bf16[1024,2048]{1,0:T(8,128)(2,1)S(1)}, f32[200,1024]{1,0:T(8,128)S(1)}, f32[200,1024]{1,0:T(8,128)S(1)}) custom-call(s32[1]{0:T(128)} %bitcast.core_ref.refs_0_, f32[1,2048]{1,0:T(1,128)S(1)} %get-tuple-element.247.w, f32[400,2048]{1,0:T(8,128)S(1)} %get-tuple-element.132.q.refs_4_, ...), custom_call_target="tpu_custom_call" | custom-call | flops 40000000 | tf_op jit(solution)/shard_map/pallas_call | solution.py:473
  57.6 11.6 %shard_map.133 = (f32[8192,128]{1,0:T(8,128)S(1)}, f32[200,1408]{1,0:T(8,128)S(1)}, f32[200,1408]{1,0:T(8,128)S(1)}) custom-call(s32[1]{0:T(128)} %bitcast.core_ref.refs_0_, s32[2048]{0:T(1024)S(1)} %bitcast.58, bf16[1024,2048]{1,0:T(8,128)(2,1)S(1)} %get-tuple-element.142.ds, f32[1,2048]{1,0:T(1,128)S(1)} %get-tuple-element.143.dp.refs_3_, ...), custom_call_target="tpu_custom_call" | custom-call | flops 75000000 | tf_op jit(solution)/shard_map/pallas_call | solution.py:473
  72.1 13.8 %shard_map.134.refs_6_ = f32[32800,128]{1,0:T(8,128)S(1)} custom-call(s32[2048]{0:T(1024)S(1)} %bitcast.52, s32[2048]{0:T(1024)S(1)} %bitcast.50, f32[8192,128]{1,0:T(8,128)S(1)} %get-tuple-element.148.refs_2_, f32[1,2048]{1,0:T(1,128)S(1)} %get-tuple-element.143.dp.refs_3_, f32[400,2048]{1,0:T(8,128)S(1)} %get-tuple-element.132.q.refs_4_), custom_call_target="tpu_custom_call" | custom-call | flops 125000000 | tf_op jit(solution)/shard_map/pallas_call | solution.py:473
  85.9 4.0 collective-permute-done.6
  93.6 19.3 %shard_map.135 = (f32[32800,128]{1,0:T(8,128)S(1)}, f32[32800,128]{1,0:T(8,128)S(1)}, f32[8192,128]{1,0:T(8,128)S(1)}, bf16[400,2048]{1,0:T(8,128)(2,1)S(1)}, bf...) custom-call(s32[1]{0:T(128)} %bitcast.core_ref.refs_0_, ...), custom_call_target="tpu_custom_call", output_to_operand_aliasing={{0}: (6, {}), {1}: (4, {}), {2}: (5, {})} | custom-call | flops 150000000 | tf_op jit(solution)/shard_map/pallas_call | solution.py:473
  115.1 4.0 shard_map.136.refs_2_.hb
  122.1 5.7 %shard_map.137 = (f32[400,2048]{1,0:T(8,128)S(1)}, f32[400,2048]{1,0:T(8,128)S(1)}, f32[5632,128]{1,0:T(8,128)S(1)}, f32[400,1408]{1,0:T(8,128)S(1)}, f32[1,1408]{1,0:T(1,128)S(1)}) custom-call(s32[1]{0:T(128)} %bitcast.core_ref.refs_0_, s32[2048]{0:T(1024)S(1)} %bitcast.55, bf16[400,2048]{1,0:T(8,128)(2,1)S(1)} %shard_map.136.refs_2_.hb, ...), custom_call_target="tpu_custom_call" | custom-call | flops 50000000 | tf_op jit(solution)/shard_map/pallas_call | solution.py:473
  127.8 17.0 %collective-permute-done.10 = bf16[400,512]{1,0:T(8,128)(2,1)S(1)} collective-permute-done((bf16[400,512]{1,0:T(8,128)(2,1)S(1)}, bf16[400,512]{1,0:T(8,128)(2,1)S(1)}, u32[]{:S(2)}, u32[]{:S(2)}) %collective-permute-start.10) | collective-permute-done | bytes 409632 | tf_op jit(solution)/shard_map/ppermute | solution.py:425
  146.7 5.4 %shard_map.138 = (f32[1000,2048]{1,0:T(8,128)S(1)}, f32[1,2048]{1,0:T(1,128)S(1)}, f32[1,2048]{1,0:T(1,128)S(1)}) custom-call(s32[1]{0:T(128)} %bitcast.core_ref.refs_0_, f32[400,2048]{1,0:T(8,128)S(1)} %get-tuple-element.162.q, bf16[400,512]{1,0:T(8,128)(2,1)S(1)} %add.89.nfull, bf16[400,512]{1,0:T(8,128)(2,1)S(1)} %collective-permute-done.13.nother), custom_call_target="tpu_custom_call" | custom-call | flops 40000000 | tf_op jit(solution)/shard_map/pallas_call | solution.py:473
  152.1 5.6 %shard_map.139 = (f32[1,128]{1,0:T(1,128)S(1)}, f32[1,2048]{1,0:T(1,128)S(1)}, bf16[1024,2048]{1,0:T(8,128)(2,1)S(1)}, f32[200,1024]{1,0:T(8,128)S(1)}, f32[200,1024]{1,0:T(8,128)S(1)}) custom-call(s32[1]{0:T(128)} %bitcast.core_ref.refs_0_, f32[1,2048]{1,0:T(1,128)S(1)} %get-tuple-element.246.w, f32[400,2048]{1,0:T(8,128)S(1)} %get-tuple-element.162.q, ...), custom_call_target="tpu_custom_call" | custom-call | flops 40000000 | tf_op jit(solution)/shard_map/pallas_call | solution.py:473
  160.2 11.6 %shard_map.140 = (f32[8192,128]{1,0:T(8,128)S(1)}, f32[200,1408]{1,0:T(8,128)S(1)}, f32[200,1408]{1,0:T(8,128)S(1)}) custom-call(s32[1]{0:T(128)} %bitcast.core_ref.refs_0_, s32[2048]{0:T(1024)S(1)} %bitcast.56, bf16[1024,2048]{1,0:T(8,128)(2,1)S(1)} %get-tuple-element.176.ds, f32[1,2048]{1,0:T(1,128)S(1)} %get-tuple-element.177.dp, ...), custom_call_target="tpu_custom_call" | custom-call | flops 75000000 | tf_op jit(solution)/shard_map/pallas_call | solution.py:473
  175.7 20.4 %collective-permute-done.18.refs_4_ = f32[1,2048]{1,0:T(1,128)S(1)} collective-permute-done((f32[1,2048]{1,0:T(1,128)S(1)}, f32[1,2048]{1,0:T(1,128)S(1)}, u32[]{:S(2)}, u32[]{:S(2)}) %collective-permute-start.18) | collective-permute-done | bytes 8224 | tf_op jit(solution)/shard_map/ppermute | solution.py:425
  196.1 18.4 %shard_map.141.refs_6_ = f32[32800,128]{1,0:T(8,128)S(1)} custom-call(s32[2048]{0:T(1024)S(1)} %bitcast.48, s32[2048]{0:T(1024)S(1)} %bitcast.62, s32[2048]{0:T(1024)S(1)} %bitcast.71, f32[8192,128]{1,0:T(8,128)S(1)} %get-tuple-element.183.refs_3_, f32[1,2048]{1,0:T(1,128)S(1)} %collective-permute-done.18.refs_4_, ...), custom_call_target="tpu_custom_call" | custom-call | flops 125000000 | tf_op jit(solution)/shard_map/pallas_call | solution.py:473
  218.2 19.3 %shard_map.142 = (f32[32800,128]{1,0:T(8,128)S(1)}, f32[32800,128]{1,0:T(8,128)S(1)}, f32[8192,128]{1,0:T(8,128)S(1)}, bf16[400,2048]{1,0:T(8,128)(2,1)S(1)}, bf...) custom-call(s32[1]{0:T(128)} %bitcast.core_ref.refs_0_, ...), custom_call_target="tpu_custom_call", output_to_operand_aliasing={{0}: (6, {}), {1}: (4, {}), {2}: (5, {})} | custom-call | flops 150000000 | tf_op jit(solution)/shard_map/pallas_call | solution.py:473
  241.9 4.0 shard_map.143.refs_2_.hb
  250.3 5.7 %shard_map.144 = (f32[400,2048]{1,0:T(8,128)S(1)}, f32[400,2048]{1,0:T(8,128)S(1)}, f32[5632,128]{1,0:T(8,128)S(1)}, f32[400,1408]{1,0:T(8,128)S(1)}, f32[1,1408]{1,0:T(1,128)S(1)}) custom-call(s32[1]{0:T(128)} %bitcast.core_ref.refs_0_, s32[2048]{0:T(1024)S(1)} %bitcast.53, bf16[400,2048]{1,0:T(8,128)(2,1)S(1)} %shard_map.143.refs_2_.hb, ...), custom_call_target="tpu_custom_call" | custom-call | flops 50000000 | tf_op jit(solution)/shard_map/pallas_call | solution.py:473
  256.0 32.0 %collective-permute-done.22 = bf16[400,512]{1,0:T(8,128)(2,1)S(1)} collective-permute-done((bf16[400,512]{1,0:T(8,128)(2,1)S(1)}, bf16[400,512]{1,0:T(8,128)(2,1)S(1)}, u32[]{:S(2)}, u32[]{:S(2)}) %collective-permute-start.22) | collective-permute-done | bytes 409632 | tf_op jit(solution)/shard_map/ppermute | solution.py:425
  289.9 5.4 %shard_map.145 = (f32[1000,2048]{1,0:T(8,128)S(1)}, f32[1,2048]{1,0:T(1,128)S(1)}, f32[1,2048]{1,0:T(1,128)S(1)}) custom-call(s32[1]{0:T(128)} %bitcast.core_ref.refs_0_, f32[400,2048]{1,0:T(8,128)S(1)} %get-tuple-element.200.q, bf16[400,512]{1,0:T(8,128)(2,1)S(1)} %add.95.nfull, bf16[400,512]{1,0:T(8,128)(2,1)S(1)} %collective-permute-done.25.nother), custom_call_target="tpu_custom_call" | custom-call | flops 40000000 | tf_op jit(solution)/shard_map/pallas_call | solution.py:473
  295.3 5.5 %shard_map.146 = (f32[1,128]{1,0:T(1,128)S(1)}, f32[1,2048]{1,0:T(1,128)S(1)}, bf16[1024,2048]{1,0:T(8,128)(2,1)S(1)}, f32[200,1024]{1,0:T(8,128)S(1)}, f32[200,1024]{1,0:T(8,128)S(1)}) custom-call(s32[1]{0:T(128)} %bitcast.core_ref.refs_0_, f32[1,2048]{1,0:T(1,128)S(1)} %get-tuple-element.245.w, f32[400,2048]{1,0:T(8,128)S(1)} %get-tuple-element.200.q, ...), custom_call_target="tpu_custom_call" | custom-call | flops 40000000 | tf_op jit(solution)/shard_map/pallas_call | solution.py:473
  303.2 11.6 %shard_map.147 = (f32[8192,128]{1,0:T(8,128)S(1)}, f32[200,1408]{1,0:T(8,128)S(1)}, f32[200,1408]{1,0:T(8,128)S(1)}) custom-call(s32[1]{0:T(128)} %bitcast.core_ref.refs_0_, s32[2048]{0:T(1024)S(1)} %bitcast.54, bf16[1024,2048]{1,0:T(8,128)(2,1)S(1)} %get-tuple-element.214.ds, f32[1,2048]{1,0:T(1,128)S(1)} %get-tuple-element.215.dp, ...), custom_call_target="tpu_custom_call" | custom-call | flops 75000000 | tf_op jit(solution)/shard_map/pallas_call | solution.py:473
  319.8 58.0 %collective-permute-done.33 = f32[200,1408]{1,0:T(8,128)S(1)} collective-permute-done((f32[200,1408]{1,0:T(8,128)S(1)}, f32[200,1408]{1,0:T(8,128)S(1)}, u32[]{:S(2)}, u32[]{:S(2)}) %collective-permute-start.33) | collective-permute-done | bytes 1126432 | tf_op jit(solution)/shard_map/ppermute | solution.py:425
  379.4 15.5 %collective-permute-done.30.refs_4_ = f32[1,2048]{1,0:T(1,128)S(1)} collective-permute-done((f32[1,2048]{1,0:T(1,128)S(1)}, f32[1,2048]{1,0:T(1,128)S(1)}, u32[]{:S(2)}, u32[]{:S(2)}) %collective-permute-start.30) | collective-permute-done | bytes 8224 | tf_op jit(solution)/shard_map/ppermute | solution.py:425
  394.9 18.7 %shard_map.148.refs_4_ = f32[32800,128]{1,0:T(8,128)S(1)} custom-call(s32[2048]{0:T(1024)S(1)} %bitcast.46, s32[2048]{0:T(1024)S(1)} %bitcast.60, s32[2048]{0:T(1024)S(1)} %bitcast.70, f32[8192,128]{1,0:T(8,128)S(1)} %get-tuple-element.221.refs_3_, f32[1,2048]{1,0:T(1,128)S(1)} %collective-permute-done.30.refs_4_, ...), custom_call_target="tpu_custom_call" | custom-call | flops 125000000 | tf_op jit(solution)/shard_map/pallas_call | solution.py:473
  413.6 5.8 %copy-done.2 = f32[32800,128]{1,0:T(8,128)} copy-done((f32[32800,128]{1,0:T(8,128)}, f32[32800,128]{1,0:T(8,128)S(1)}, u32[]{:S(2)}) %copy-start.2) | copy-done | bytes 16793624
  422.0 5.8 %copy-done.1 = f32[32800,128]{1,0:T(8,128)S(1)} copy-done((f32[32800,128]{1,0:T(8,128)S(1)}, f32[32800,128]{1,0:T(8,128)}, u32[]{:S(2)}) %copy-start.1) | copy-done | bytes 16793624
  427.7 5.8 %copy-done.3 = f32[32800,128]{1,0:T(8,128)S(1)} copy-done((f32[32800,128]{1,0:T(8,128)S(1)}, f32[32800,128]{1,0:T(8,128)}, u32[]{:S(2)}) %copy-start.3) | copy-done | bytes 16793624
  435.7 17.1 %shard_map.149 = (f32[32800,128]{1,0:T(8,128)S(1)}, f32[400,8192]{1,0:T(8,128)}, f32[64,128]{1,0:T(8,128)}) custom-call(s32[1]{0:T(128)} %bitcast.core_ref.refs_0_, s32[1024]{0:T(1024)S(1)} %bitcast.64, f32[32800,128]{1,0:T(8,128)S(1)} %copy-done.1, f32[8192,128]{1,0:T(8,128)S(1)} %copy-done.9, ...), custom_call_target="tpu_custom_call", output_to_operand_aliasing={{0}: (4, {})} | custom-call | flops 150000000 | tf_op jit(solution)/shard_map/pallas_call | solution.py:473
  (139 shorter events, 66.1 us)
Async XLA Ops:
  17.9 5.7 %collective-permute-start = (bf16[400,512]{1,0:T(8,128)(2,1)S(1)}, bf16[400,512]{1,0:T(8,128)(2,1)S(1)}, u32[]{:S(2)}, u32[]{:S(2)}) collective-permute-start(bf16[400,512]{1,0:T(8,128)(2,1)S(1)} %get-tuple-element.120), channel_id=1, source_target_pairs={{0,1},{1,0},{2,3},{3,2},{4,5},{5,4},{6,7},{7,6}} | collective-permute-start | bytes 1228808 | tf_op jit(solution)/shard_map/ppermute | solution.py:422
  18.8 4.0 collective-permute-start.1
  18.9 4.7 %collective-permute-start.2 = (s32[2,2048]{1,0:T(2,128)S(1)}, s32[2,2048]{1,0:T(2,128)S(1)}, u32[]{:S(2)}, u32[]{:S(2)}) collective-permute-start(s32[2,2048]{1,0:T(2,128)S(1)} %pad_add_fusion.1), channel_id=1, source_target_pairs={{0,2},{1,3},{2,0},{3,1},{4,6},{5,7},{6,4},{7,5}} | collective-permute-start | bytes 49160 | tf_op jit(solution)/shard_map/ppermute | solution.py:425
  23.7 11.9 %collective-permute-start.3 = (bf16[400,512]{1,0:T(8,128)(2,1)S(1)}, bf16[400,512]{1,0:T(8,128)(2,1)S(1)}, u32[]{:S(2)}, u32[]{:S(2)}) collective-permute-start(bf16[400,512]{1,0:T(8,128)(2,1)S(1)} %add.82), channel_id=1, source_target_pairs={{0,2},{1,3},{2,0},{3,1},{4,6},{5,7},{6,4},{7,5}} | collective-permute-start | bytes 1228808 | tf_op jit(solution)/shard_map/ppermute | solution.py:425
  42.5 1.8 collective-permute-start.4
  55.1 2.4 collective-permute-start.5
  69.2 2.8 collective-permute-start.7
  69.3 20.6 %collective-permute-start.6 = (f32[200,1024]{1,0:T(8,128)S(1)}, f32[200,1024]{1,0:T(8,128)}, u32[]{:S(2)}, u32[]{:S(2)}) collective-permute-start(f32[200,1024]{1,0:T(8,128)S(1)} %add.84), channel_id=1, source_target_pairs={{0,2},{1,3},{2,0},{3,1},{4,6},{5,7},{6,4},{7,5}} | collective-permute-start | bytes 2457608 | tf_op jit(solution)/shard_map/ppermute | solution.py:425
  91.2 2.4 collective-permute-start.8
  91.3 27.9 %collective-permute-start.11 = (f32[200,1408]{1,0:T(8,128)S(1)}, f32[200,1408]{1,0:T(8,128)S(1)}, u32[]{:S(2)}, u32[]{:S(2)}) collective-permute-start(f32[200,1408]{1,0:T(8,128)S(1)} %add.85), channel_id=1, source_target_pairs={{0,2},{1,3},{2,0},{3,1},{4,6},{5,7},{6,4},{7,5}} | collective-permute-start | bytes 3379208 | tf_op jit(solution)/shard_map/ppermute | solution.py:425
  112.9 1.8 collective-permute-start.9
  114.8 37.3 %collective-permute-start.14 = (bf16[400,2048]{1,0:T(8,128)(2,1)S(1)}, bf16[400,2048]{1,0:T(8,128)(2,1)S(1)}, u32[]{:S(2)}, u32[]{:S(2)}) collective-permute-start(bf16[400,2048]{1,0:T(8,128)(2,1)S(1)} %get-tuple-element.165), channel_id=1, source_target_pairs={{0,3},{1,0},{2,1},{3,2},{4,7},{5,4},{6,5},{7,6}} | collective-permute-start | bytes 4915208 | tf_op jit(solution)/shard_map/ppermute | solution.py:425
  119.3 2.8 collective-permute-start.12
  119.5 25.3 %collective-permute-start.10 = (bf16[400,512]{1,0:T(8,128)(2,1)S(1)}, bf16[400,512]{1,0:T(8,128)(2,1)S(1)}, u32[]{:S(2)}, u32[]{:S(2)}) collective-permute-start(bf16[400,512]{1,0:T(8,128)(2,1)S(1)} %add.87), channel_id=1, source_target_pairs={{0,2},{1,3},{2,0},{3,1},{4,6},{5,7},{6,4},{7,5}} | collective-permute-start | bytes 1228808 | tf_op jit(solution)/shard_map/ppermute | solution.py:425
  157.7 2.4 collective-permute-start.15
  157.9 38.2 %collective-permute-start.19 = (bf16[400,2048]{1,0:T(8,128)(2,1)S(1)}, bf16[400,2048]{1,0:T(8,128)(2,1)S(1)}, u32[]{:S(2)}, u32[]{:S(2)}) collective-permute-start(bf16[400,2048]{1,0:T(8,128)(2,1)S(1)} %shard_map.136.refs_2_.hb), channel_id=1, source_target_pairs={{0,1},{1,2},{2,3},{3,0},{4,5},{5,6},{6,7},{7,4}} | collective-permute-start | bytes 4915208 | tf_op jit(solution)/shard_map/ppermute | solution.py:425
  171.8 2.8 collective-permute-start.17
  171.9 42.6 %collective-permute-start.16 = (f32[200,1024]{1,0:T(8,128)S(1)}, f32[200,1024]{1,0:T(8,128)}, u32[]{:S(2)}, u32[]{:S(2)}) collective-permute-start(f32[200,1024]{1,0:T(8,128)S(1)} %add.90), channel_id=1, source_target_pairs={{0,2},{1,3},{2,0},{3,1},{4,6},{5,7},{6,4},{7,5}} | collective-permute-start | bytes 2457608 | tf_op jit(solution)/shard_map/ppermute | solution.py:425
  172.5 23.6 %collective-permute-start.18 = (f32[1,2048]{1,0:T(1,128)S(1)}, f32[1,2048]{1,0:T(1,128)S(1)}, u32[]{:S(2)}, u32[]{:S(2)}) collective-permute-start(f32[1,2048]{1,0:T(1,128)S(1)} %get-tuple-element.177.dp), channel_id=1, source_target_pairs={{0,1},{1,2},{2,3},{3,0},{4,5},{5,6},{6,7},{7,4}} | collective-permute-start | bytes 24584 | tf_op jit(solution)/shard_map/ppermute | solution.py:425
  215.8 2.4 collective-permute-start.20
  215.8 30.1 %collective-permute-start.23 = (f32[200,1408]{1,0:T(8,128)}, f32[200,1408]{1,0:T(8,128)S(1)}, u32[]{:S(2)}, u32[]{:S(2)}) collective-permute-start(f32[200,1408]{1,0:T(8,128)} %add.91), channel_id=1, source_target_pairs={{0,2},{1,3},{2,0},{3,1},{4,6},{5,7},{6,4},{7,5}} | collective-permute-start | bytes 3379208 | tf_op jit(solution)/shard_map/ppermute | solution.py:425
  241.3 53.9 %collective-permute-start.26 = (bf16[400,2048]{1,0:T(8,128)(2,1)S(1)}, bf16[400,2048]{1,0:T(8,128)(2,1)S(1)}, u32[]{:S(2)}, u32[]{:S(2)}) collective-permute-start(bf16[400,2048]{1,0:T(8,128)(2,1)S(1)} %get-tuple-element.203), channel_id=1, source_target_pairs={{0,2},{1,3},{2,0},{3,1},{4,6},{5,7},{6,4},{7,5}} | collective-permute-start | bytes 4915208 | tf_op jit(solution)/shard_map/ppermute | solution.py:425
  247.5 2.8 collective-permute-start.24
  247.5 40.5 %collective-permute-start.22 = (bf16[400,512]{1,0:T(8,128)(2,1)S(1)}, bf16[400,512]{1,0:T(8,128)(2,1)S(1)}, u32[]{:S(2)}, u32[]{:S(2)}) collective-permute-start(bf16[400,512]{1,0:T(8,128)(2,1)S(1)} %add.93), channel_id=1, source_target_pairs={{0,2},{1,3},{2,0},{3,1},{4,6},{5,7},{6,4},{7,5}} | collective-permute-start | bytes 1228808 | tf_op jit(solution)/shard_map/ppermute | solution.py:425
  300.7 2.4 collective-permute-start.27
  314.8 2.8 collective-permute-start.29
  315.0 80.0 %collective-permute-start.31 = (bf16[400,2048]{1,0:T(8,128)(2,1)S(1)}, bf16[400,2048]{1,0:T(8,128)(2,1)S(1)}, u32[]{:S(2)}, u32[]{:S(2)}) collective-permute-start(bf16[400,2048]{1,0:T(8,128)(2,1)S(1)} %shard_map.143.refs_2_.hb), channel_id=1, source_target_pairs={{0,2},{1,3},{2,0},{3,1},{4,6},{5,7},{6,4},{7,5}} | collective-permute-start | bytes 4915208 | tf_op jit(solution)/shard_map/ppermute | solution.py:425
  317.7 60.1 %collective-permute-start.33 = (f32[200,1408]{1,0:T(8,128)S(1)}, f32[200,1408]{1,0:T(8,128)S(1)}, u32[]{:S(2)}, u32[]{:S(2)}) collective-permute-start(f32[200,1408]{1,0:T(8,128)S(1)} %add.97), channel_id=1, source_target_pairs={{0,2},{1,3},{2,0},{3,1},{4,6},{5,7},{6,4},{7,5}} | collective-permute-start | bytes 3379208 | tf_op jit(solution)/shard_map/ppermute | solution.py:425
  318.3 101.1 %collective-permute-start.28 = (f32[200,1024]{1,0:T(8,128)S(1)}, f32[200,1024]{1,0:T(8,128)S(1)}, u32[]{:S(2)}, u32[]{:S(2)}) collective-permute-start(f32[200,1024]{1,0:T(8,128)S(1)} %add.96), channel_id=1, source_target_pairs={{0,2},{1,3},{2,0},{3,1},{4,6},{5,7},{6,4},{7,5}} | collective-permute-start | bytes 2457608 | tf_op jit(solution)/shard_map/ppermute | solution.py:425
  378.9 73.9 %collective-permute-start.34 = (f32[200,1408]{1,0:T(8,128)}, f32[200,1408]{1,0:T(8,128)}, u32[]{:S(2)}, u32[]{:S(2)}) collective-permute-start(f32[200,1408]{1,0:T(8,128)} %add.99), channel_id=1, source_target_pairs={{0,1},{1,0},{2,3},{3,2},{4,5},{5,4},{6,7},{7,6}} | collective-permute-start | bytes 3379208 | tf_op jit(solution)/shard_map/ppermute | solution.py:432
  378.9 16.0 %collective-permute-start.30 = (f32[1,2048]{1,0:T(1,128)S(1)}, f32[1,2048]{1,0:T(1,128)S(1)}, u32[]{:S(2)}, u32[]{:S(2)}) collective-permute-start(f32[1,2048]{1,0:T(1,128)S(1)} %get-tuple-element.215.dp), channel_id=1, source_target_pairs={{0,2},{1,3},{2,0},{3,1},{4,6},{5,7},{6,4},{7,5}} | collective-permute-start | bytes 24584 | tf_op jit(solution)/shard_map/ppermute | solution.py:425
  419.5 2.5 collective-permute-start.32
  (24 other events, 218.0 us)

commit v5 on v4

--- a/solution.py
+++ b/solution.py
@@ -47,16 +47,35 @@
     return stage[pl.ds(slice_no, LANES, stride=SLICES), :].T
 
 
-def add_rows(acc, ids, base, rows, row_base, count):
+def batch_sums(acc, ids, base, rows, row_base):
+    index = [ids[base + k] for k in range(BATCH)]
+    grads = [rows[pl.ds(four(row_base + SLICES * k), SLICES), :] for k in range(BATCH)]
+    total = [acc[pl.ds(four(index[k]), SLICES), :] + grads[k] for k in range(BATCH)]
+    for k in range(1, BATCH):
+        for earlier in range(k):
+            total[k] = total[k] + jnp.where(index[earlier] == index[k], grads[earlier], 0.0)
+    return index, total
+
+
+def add_rows(chains, count):
     for first in range(0, count, BATCH):
-        index = [ids[base + first + k] for k in range(BATCH)]
-        grads = [rows[pl.ds(four(row_base + SLICES * (first + k)), SLICES), :] for k in range(BATCH)]
-        total = [acc[pl.ds(four(index[k]), SLICES), :] + grads[k] for k in range(BATCH)]
-        for k in range(1, BATCH):
-            for earlier in range(k):
-                total[k] = total[k] + jnp.where(index[earlier] == index[k], grads[earlier], 0.0)
-        for k in range(BATCH):
-            acc[pl.ds(four(index[k]), SLICES), :] = total[k]
+        done = [batch_sums(acc, ids, base + first, rows, row_base + SLICES * first) for acc, ids, base, rows, row_base in chains]
+        for (acc, *_), (index, total) in zip(chains, done):
+            for k in range(BATCH):
+                acc[pl.ds(four(index[k]), SLICES), :] = total[k]
+
+
+def put_halves(core, keep, sent, cols, block_of, dim):
+    half = dim // 2
+    for side in range(2):
+        @pl.when(core == side)
+        def _():
+            for j in range(SLICES):
+                block = block_of(j)
+                for h in range(2):
+                    lo, hi = max(j * LANES, h * half), min((j + 1) * LANES, (h + 1) * half)
+                    if lo < hi:
+                        (keep if h == side else sent)[pl.ds(lo - h * half, hi - lo), cols] = block[lo - j * LANES:hi - j * LANES]
 
 
 def zero_rows(ref, step=1024):
@@ -100,17 +119,19 @@
         return pltpu.make_async_copy(et.at[:, pl.ds(pl.multiple_of(step * cols, LANES), cols)],
                                      inbuf.at[slot, pl.ds(0, dim)], in_sem.at[slot])
 
-    fetch(0, 0).start()
-    for slot in range(2):
+    slots = inbuf.shape[0]
+    for slot in range(slots - 1):
+        fetch(slot, slot).start()
+    for slot in range(slots):
         inbuf[slot, pl.ds(dim, SLICES * LANES - dim), :] = jnp.zeros((SLICES * LANES - dim, cols), F32)
     t4[pl.ds(rows * SLICES, 32), :] = jnp.zeros((32, LANES), F32)
 
     def body(step, _):
-        slot = lax.rem(step, 2)
-
-        @pl.when(step + 1 < steps)
+        slot = lax.rem(step, slots)
+
+        @pl.when(step + slots - 1 < steps)
         def _():
-            fetch(step + 1, 1 - slot).start()
+            fetch(step + slots - 1, lax.rem(step + slots - 1, slots)).start()
 
         fetch(step, slot).wait()
         for b in range(per):
@@ -202,9 +223,8 @@
 
 
 def score_kernel(dim, neg_count, edges, core_ref, w, q, tb, e, neg_top, neg_sum,
-                 loss, dp_out, ds, nk, ns, ng, fm):
+                 loss, dp_out, ds, nk, ns, ng):
     core = core_ref[0]
-    half = dim // 2
     negp = ds.shape[0]
     ng[...] = jnp.zeros(ng.shape, F32)
     ds[pl.ds(neg_count, negp - neg_count), :] = jnp.zeros((negp - neg_count, edges), BF16)
@@ -225,22 +245,24 @@
 
     loss_row = lax.fori_loop(0, edges // CHUNK, step, jnp.zeros((1, CHUNK), F32))
     loss[...] = jnp.broadcast_to(jnp.sum(loss_row, axis=1, keepdims=True) / edges, loss.shape)
-    for b in range(negp // LANES):
-        for j in range(SLICES):
-            size = min(LANES, dim - j * LANES)
-            fm[pl.ds(j * LANES, size), pl.ds(b * LANES, LANES)] = ng[pl.ds(b * LANES, LANES), pl.ds(j * LANES, size)].T
-    nk[...] = fm[pl.ds(pl.multiple_of(core * half, 8), half), :]
-    ns[...] = fm[pl.ds(pl.multiple_of((1 - core) * half, 8), half), :]
-
-
-def grad_kernel(dim, edges, core_ref, rel, ds, dp, tb, hb, r, nfull, nother,
-                hg, rk, rs, nb, racc, stage, qs, fm):
+
+    def save(b, _):
+        rows = pl.ds(pl.multiple_of(b * LANES, LANES), LANES)
+        put_halves(core, nk, ns, rows, lambda j: ng[rows, pl.ds(j * LANES, min(LANES, dim - j * LANES))].T, dim)
+        return 0
+
+    lax.fori_loop(0, negp // LANES, save, 0)
+
+
+def grad_kernel(dim, edges, core_ref, rel, heads, ds, dp, tb, hb, r, nfull, nother,
+                acc, rk, rs, nb, racc, stage_r, stage_h, qs):
     core = core_ref[0]
     half = dim // 2
     relp = rk.shape[1]
     tops = SLICES * LANES
     place_negs(core, nb, nfull, nother)
     zero_rows(racc)
+    zero_rows(acc)
     qs[pl.ds(dim, tops - dim), :] = jnp.zeros((tops - dim, CHUNK), F32)
 
     def step(c, _):
@@ -249,27 +271,24 @@
         g_re, g_im = gq[:half], gq[half:]
         h = hb[:, cols].astype(F32)
         h_re, h_im = h[:half], h[half:]
-        qs[pl.ds(0, half), :] = g_re * h_re + g_im * h_im
-        qs[pl.ds(half, half), :] = g_im * h_re - g_re * h_im
-        for b in range(CHUNK // LANES):
-            for j in range(SLICES):
-                stage[pl.ds(SLICES * b * LANES + j, LANES, stride=SLICES), :] = qs[pl.ds(j * LANES, LANES), pl.ds(b * LANES, LANES)].T
         r_re, r_im = r[pl.ds(0, half), cols], r[pl.ds(half, half), cols]
-        qs[pl.ds(0, half), :] = g_re * r_re + g_im * r_im
-        qs[pl.ds(half, half), :] = g_im * r_re - g_re * r_im
-        for b in range(CHUNK // LANES):
-            for j in range(SLICES):
-                hg[pl.ds(SLICES * (c * CHUNK + b * LANES) + j, LANES, stride=SLICES), :] = qs[pl.ds(j * LANES, LANES), pl.ds(b * LANES, LANES)].T
-        add_rows(racc, rel, c * CHUNK, stage, 0, CHUNK)
+        for stage, f_re, f_im in ((stage_r, h_re, h_im), (stage_h, r_re, r_im)):
+            qs[pl.ds(0, half), :] = g_re * f_re + g_im * f_im
+            qs[pl.ds(half, half), :] = g_im * f_re - g_re * f_im
+            for b in range(CHUNK // LANES):
+                for j in range(SLICES):
+                    stage[pl.ds(SLICES * b * LANES + j, LANES, stride=SLICES), :] = qs[pl.ds(j * LANES, LANES), pl.ds(b * LANES, LANES)].T
+        add_rows([(racc, rel, c * CHUNK, stage_r, 0), (acc, heads, c * CHUNK, stage_h, 0)], CHUNK)
         return 0
 
     lax.fori_loop(0, edges // CHUNK, step, 0)
-    for b in range(relp // LANES):
-        for j in range(SLICES):
-            size = min(LANES, dim - j * LANES)
-            fm[pl.ds(j * LANES, size), pl.ds(b * LANES, LANES)] = racc[pl.ds(SLICES * b * LANES + j, LANES, stride=SLICES), :].T[:size]
-    rk[...] = fm[pl.ds(pl.multiple_of(core * half, 8), half), :]
-    rs[...] = fm[pl.ds(pl.multiple_of((1 - core) * half, 8), half), :]
+
+    def save(b, _):
+        cols = pl.ds(pl.multiple_of(b * LANES, LANES), LANES)
+        put_halves(core, rk, rs, cols, lambda j: racc[pl.ds(SLICES * LANES * b + j, LANES, stride=SLICES), :].T, dim)
+        return 0
+
+    lax.fori_loop(0, relp // LANES, save, 0)
 
 
 def unstage(rt, stage):
@@ -279,19 +298,12 @@
 
 def scatter_kernel(dim, edges, own, *refs):
     if own:
-        heads, tails, hg, dp, q, acc, stage, rt = refs
+        tails, dp, q, _, acc, stage, rt = refs
     else:
-        heads, tails, rel, hg, dp, hb_in, r4, acc, stage, rt = refs
+        tails, rel, dp, hb_in, r4, _, acc, stage, rt = refs
     half = dim // 2
     tops = SLICES * LANES
-    zero_rows(acc)
     rt[pl.ds(dim, tops - dim), :] = jnp.zeros((tops - dim, LANES), F32)
-
-    def head_step(b, _):
-        add_rows(acc, heads, b * 32, hg, b * 32 * SLICES, 32)
-        return 0
-
-    lax.fori_loop(0, edges // 32, head_step, 0)
 
     def tail_step(b, _):
         cols = pl.ds(pl.multiple_of(b * LANES, LANES), LANES)
@@ -309,7 +321,7 @@
             rt[pl.ds(0, half), :] = q_re
             rt[pl.ds(half, half), :] = q_im
         unstage(rt, stage)
-        add_rows(acc, tails, b * LANES, stage, 0, LANES)
+        add_rows([(acc, tails, b * LANES, stage, 0)], LANES)
         return 0
 
     lax.fori_loop(0, edges // LANES, tail_step, 0)
@@ -317,9 +329,9 @@
 
 def update_kernel(dim, rows, last, *refs):
     if last:
-        core_ref, negs, t4, v, _, nmine, nother, acc, et_out, g_out, stage, rt, outbuf, out_sem = refs
+        core_ref, negs, t4, v, _, nmine, nother, acc, et_out, g_out, stage, rt, rate, outbuf, out_sem = refs
     else:
-        core_ref, negs, tails_n, negs_n, t4, v, _, nmine, nother, acc, new_t4, new_v, tb, nk, ns, stage, rt, nbuf = refs
+        core_ref, negs, negs_n, t4, v, _, nmine, nother, acc, new_t4, new_v, nk, ns, stage, rt, rate, nbuf = refs
     core = core_ref[0]
     half = dim // 2
     tops = SLICES * LANES
@@ -330,32 +342,45 @@
         rt[pl.ds(pl.multiple_of(core * half, 8), half), :] = nmine[:, cols]
         rt[pl.ds(pl.multiple_of((1 - core) * half, 8), half), :] = nother[:, cols]
         unstage(rt, stage)
-        add_rows(acc, negs, b * LANES, stage, 0, LANES)
+        add_rows([(acc, negs, b * LANES, stage, 0)], LANES)
         return 0
 
     lax.fori_loop(0, nmine.shape[1] // LANES, neg_step, 0)
 
-    def ada_rows(row0):
-        where = [pl.ds(SLICES * row0 + j, LANES, stride=SLICES) for j in range(SLICES)]
+    blocks = rows // LANES
+
+    def slices(b):
+        return [pl.ds(SLICES * LANES * b + j, LANES, stride=SLICES) for j in range(SLICES)]
+
+    def advance(b):
+        where = slices(b)
         square = acc[where[0], :] * acc[where[0], :]
         for j in range(1, SLICES):
             square = square + acc[where[j], :] * acc[where[j], :]
-        state = v[pl.ds(pl.multiple_of(row0, 8), LANES), :] + jnp.sum(square, axis=1, keepdims=True) / dim
-        rate = LEARN_RATE / jnp.sqrt(state + ADA_EPS)
-        return state, where, [t4[w, :] - acc[w, :] * rate for w in where]
+        state = v[pl.ds(pl.multiple_of(b * LANES, 8), LANES), :] + jnp.sum(square, axis=1, keepdims=True) / dim
+        return state, LEARN_RATE / jnp.sqrt(state + ADA_EPS)
 
     if not last:
+        def open_block(b):
+            state, step_size = advance(b)
+            new_v[pl.ds(pl.multiple_of(b * LANES, 8), LANES), :] = state
+            rate[...] = step_size
+
+        def close_block(b, step_size):
+            for w in slices(b):
+                new_t4[w, :] = t4[w, :] - acc[w, :] * step_size
+
         def ada_step(b, _):
-            state, where, values = ada_rows(b * LANES)
-            new_v[pl.ds(pl.multiple_of(b * LANES, 8), LANES), :] = state
-            for w, value in zip(where, values):
-                new_t4[w, :] = value
+            step_size = rate[...]
+            close_block(b - 1, step_size)
+            open_block(b)
             return 0
 
-        lax.fori_loop(0, rows // LANES, ada_step, 0)
+        open_block(0)
+        lax.fori_loop(1, blocks, ada_step, 0)
+        close_block(blocks - 1, rate[...])
         new_t4[pl.ds(rows * SLICES, 32), :] = jnp.zeros((32, LANES), F32)
         gather_negs(dim, core, new_t4, negs_n, nk, ns, nbuf, stage)
-        gather_out(dim, new_t4, tails_n, tb, stage, tb.shape[1])
         return
 
     width = outbuf.shape[2]
@@ -365,6 +390,13 @@
     def save(step, slot):
         return pltpu.make_async_copy(outbuf.at[slot], et_out.at[:, pl.ds(pl.multiple_of(step * width, LANES), width)], out_sem.at[slot])
 
+    def open_last(b):
+        state, step_size = advance(b)
+        g_out[pl.ds(b, 1), :] = state.T[:1]
+        rate[...] = step_size
+
+    open_last(0)
+
     def exit_step(step, _):
         slot = lax.rem(step, 2)
 
@@ -372,12 +404,13 @@
         def _():
             save(step - 2, slot).wait()
 
-        for b in range(per):
-            state, _, values = ada_rows((step * per + b) * LANES)
-            for j in range(SLICES):
+        for i in range(per):
+            b = step * per + i
+            step_size = rate[...]
+            for j, w in enumerate(slices(b)):
                 size = min(LANES, dim - j * LANES)
-                outbuf[slot, pl.ds(j * LANES, size), pl.ds(b * LANES, LANES)] = values[j].T[:size]
-            g_out[pl.ds(step * per + b, 1), :] = state.T[:1]
+                outbuf[slot, pl.ds(j * LANES, size), pl.ds(i * LANES, LANES)] = (t4[w, :] - acc[w, :] * step_size).T[:size]
+            open_last(jnp.minimum(b + 1, blocks - 1))
         save(step, slot).start()
         return 0
 
@@ -482,7 +515,7 @@
         t4, v, nk, ns = call(
             functools.partial(entry_kernel, dim, rows), [core, negs[0], pltpu.with_memory_space_constraint(ent_emb.T, pltpu.HBM), ent_ada.reshape(rows // LANES, LANES)], 'sshv',
             [table_out, state_out, neg_half, neg_half], 'VVVV',
-            [pltpu.VMEM((2, SLICES * LANES, 4 * LANES), F32), stage_shape, pltpu.VMEM((dim, negp), BF16), pltpu.SemaphoreType.DMA((2,))], 20)
+            [pltpu.VMEM((4, SLICES * LANES, 4 * LANES), F32), stage_shape, pltpu.VMEM((dim, negp), BF16), pltpu.SemaphoreType.DMA((4,))], 20)
 
         rfm = jnp.pad(rel_emb.T, ((0, 0), (0, relp - num_rel)))
         vr = jnp.pad(rel_ada, (0, relp - num_rel), constant_values=1.0).reshape(1, relp)
@@ -498,9 +531,11 @@
                 head_cols = hb
                 neg_got, hb = tie((neg_got, hb))
             else:
-                neg_part, t4, tb = tie((neg_part, t4, tb))
+                neg_part, t4 = tie((neg_part, t4))
                 neg_got = link(neg_part)
+                tb, = gather([tails[s]], t4)
                 tail_cols = send(tb, shift(-s))
+                t4, tb = tie((t4, tb))
                 hb, = gather([heads[s]], t4)
                 rel_got, hb = tie((rel_got, hb))
                 rel_grads = finish(rel_part, rel_got)
@@ -530,45 +565,45 @@
             loss, dp, ds, gk, gs = call(
                 functools.partial(score_kernel, dim, neg_count, edges), [core, weights[s].reshape(1, edges), q, tail_cols, e, neg_top, neg_total], 'svVVVvv',
                 [shape((1, LANES)), shape((1, edges)), shape((negp, edges), BF16), shape((half, negp)), shape((half, negp))], 'vvVVV',
-                [pltpu.VMEM((negp, dim), F32), pltpu.VMEM((SLICES * LANES, negp), F32)], 8)
+                [pltpu.VMEM((negp, dim), F32)], 8)
             losses.append(loss[0, 0])
             if not first:
                 dp_away = send(dp, shift(s))
             neg_part = chip_sum(gk, gs)
             neg_part, ds = tie((neg_part, ds))
             neg_got = link(neg_part)
-            hg, rk, rs = call(
-                functools.partial(grad_kernel, dim, edges), [core, own_rels[s], ds, dp, tail_cols, hb, r, nmine, nother], 'ssVvVVVVV',
-                [shape((edges * SLICES, LANES)), shape((half, relp)), shape((half, relp))], 'VVV',
+            acc, rk, rs = call(
+                functools.partial(grad_kernel, dim, edges), [core, own_rels[s], heads[s], ds, dp, tail_cols, hb, r, nmine, nother], 'sssVvVVVVV',
+                [table_out, shape((half, relp)), shape((half, relp))], 'VVV',
                 [pltpu.VMEM((dim, negp), BF16), pltpu.VMEM((relp * SLICES, LANES), F32), pltpu.VMEM((SLICES * CHUNK, LANES), F32),
-                 pltpu.VMEM((SLICES * LANES, CHUNK), F32), pltpu.VMEM((SLICES * LANES, relp), F32)], 15)
+                 pltpu.VMEM((SLICES * CHUNK, LANES), F32), pltpu.VMEM((SLICES * LANES, CHUNK), F32)], 15)
             rel_part = chip_sum(rk, rs)
-            rel_part, hg = tie((rel_part, hg))
+            rel_part, acc = tie((rel_part, acc))
             rel_got = link(rel_part)
             if first:
-                args, kinds = [heads[s], tails[s], hg, dp, q], 'ssVvV'
+                args, kinds = [tails[s], dp, q, acc], 'svVV'
             else:
-                args, kinds = [heads[s], tails[s], rels[s], hg, dp_away, head_cols, r4], 'sssVvVV'
+                args, kinds = [tails[s], rels[s], dp_away, head_cols, r4, acc], 'ssvVVV'
             acc, = call(functools.partial(scatter_kernel, dim, edges, first), args, kinds, [table_out], 'V',
-                        [stage_shape, square_shape], 25)
+                        [stage_shape, square_shape], 12, {len(args) - 1: 0})
             neg_got, acc = tie((neg_got, acc))
             gmine, gother = finish(neg_part, neg_got)
-            scratch = [stage_shape, square_shape]
+            scratch = [stage_shape, square_shape, pltpu.VMEM((LANES, LANES), F32)]
             if last:
                 args, outs, out_kinds = [core, negs[s]], [table_out, shape((dim, rows)), shape((rows // LANES, LANES))], 'Vhv'
                 scratch += [pltpu.VMEM((2, dim, 4 * LANES), F32), pltpu.SemaphoreType.DMA((2,))]
                 aliases = {4: 0}
             else:
-                args = [core, negs[s], tails[s + 1], negs[s + 1]]
-                outs, out_kinds = [table_out, table_out, state_out, cols_bf, neg_half, neg_half], 'VVVVVV'
+                args = [core, negs[s], negs[s + 1]]
+                outs, out_kinds = [table_out, table_out, state_out, neg_half, neg_half], 'VVVVV'
                 scratch += [pltpu.VMEM((dim, negp), BF16)]
-                aliases = {6: 0, 4: 1, 5: 2}
+                aliases = {5: 0, 3: 1, 4: 2}
             res = call(functools.partial(update_kernel, dim, rows, last), args + [t4, v, acc, gmine, gother], 's' * len(args) + 'VVVVV',
                        outs, out_kinds, scratch, 30, aliases)
             if last:
                 _, et, g = res
             else:
-                _, t4, v, tb, nk, ns = res
+                _, t4, v, nk, ns = res
 
         even = core[0] == 0
         rel_grads = finish(rel_part, rel_got)

time: 459 us -> 503 us (1.096)
  local copies, waits for them, and re-layouts: 23.2 us -> 77.6 us
    unnamed x42 -> x82, local copies, waits for them, and re-layouts: 22.3 us -> 76.8 us
    ppermute x17, waiting for transfers between devices: 151 us -> 146 us  [send(): return lax.ppermute(value, 'ent', pairs)]
    pallas_call x22 -> x24, Pallas kernels: 223 us -> 219 us  [call(): pl.pallas_call(kernel, out_shape=outs, in_specs=[places[k]() for k in kin...]
  transfers between devices with their start and end apart: 35 -> 35, of which waited for: 25 -> 25; matrix products, arithmetic and copies ran while one was open for 1% -> 1% of each run, Pallas kernels for 34% -> 28%
where the time goes in v5:
time: 503 us; the launch traced here: 502 us
  Pallas kernels  219 us (44%)
  waiting for transfers between devices  174 us (35%)
  local copies, waits for them, and re-layouts  77.6 us (15%)
  starting transfers between devices  17 us (3%)
  other arithmetic  13.1 us (3%)
    pallas_call x24, Pallas kernels, call(): pl.pallas_call(kernel, out_shape=outs, in_specs=[places[k]() for k in kin...  219 us
    ppermute x17, waiting for transfers between devices, send(): return lax.ppermute(value, 'ent', pairs)  146 us
    unnamed x82, local copies, waits for them, and re-layouts  76.8 us
    ppermute x9, waiting for transfers between devices, chip_sum(): return keep + lax.ppermute(send, 'ent', swap)  15.6 us
    ppermute x17, starting transfers between devices, send(): return lax.ppermute(value, 'ent', pairs)  14.5 us
    ppermute x9, waiting for transfers between devices, finish(): return (mine, lax.ppermute(mine, 'ent', swap))  12.9 us
  transfers between devices with their start and end apart: 35, of which 25 were waited for; matrix products, arithmetic and copies ran while one was open for 1% of the time, Pallas kernels for 28%

profile of v5, /device:TPU:0, one launch (start us, length us, event | category | flops | bytes accessed | tf_op | source)
XLA Modules:
  0.0 502.4 jit_solution(13174965420329172360)
XLA Ops:
  2.2 10.3 %shard_map.128 = (f32[32800,128]{1,0:T(8,128)S(1)}, f32[8192,128]{1,0:T(8,128)S(1)}, bf16[400,512]{1,0:T(8,128)(2,1)S(1)}, bf16[400,512]{1,0:T(8,128)(2,1)S(1)}) custom-call(s32[1]{0:T(128)} %bitcast.core_ref.refs_0_, s32[1024]{0:T(1024)S(1)} %bitcast.67, f32[400,8192]{1,0:T(8,128)} %bitcast.75, f32[64,128]{1,0:T(8,128)S(1)} %bitcast.69), custom_call_target="tpu_custom_call" | custom-call | flops 100000000 | tf_op jit(solution)/shard_map/pallas_call | solution.py:506
  20.4 7.5 %shard_map.129 = (bf16[400,2048]{1,0:T(8,128)(2,1)S(1)}, bf16[400,2048]{1,0:T(8,128)(2,1)S(1)}) custom-call(s32[2048]{0:T(1024)S(1)} %bitcast.53, s32[2048]{0:T(1024)S(1)} %bitcast.57, f32[32800,128]{1,0:T(8,128)S(1)} %get-tuple-element.120.refs_2_.refs_3_), custom_call_target="tpu_custom_call" | custom-call | flops 55000000 | tf_op jit(solution)/shard_map/pallas_call | solution.py:506
  30.2 6.9 %shard_map.130 = (f32[400,2048]{1,0:T(8,128)S(1)}, f32[400,2048]{1,0:T(8,128)S(1)}, f32[5632,128]{1,0:T(8,128)}) custom-call(s32[1]{0:T(128)} %bitcast.core_ref.refs_0_, s32[2048]{0:T(1024)S(1)} %bitcast.55, bf16[400,2048]{1,0:T(8,128)(2,1)S(1)} %get-tuple-element.126.refs_2_.hb, f32[400,1408]{1,0:T(8,128)S(1)} %pad.13.refs_3_), custom_call_target="tpu_custom_call" | custom-call | flops 50000000 | tf_op jit(solution)/shard_map/pallas_call | solution.py:506
  40.6 5.4 %shard_map.131 = (f32[1000,2048]{1,0:T(8,128)S(1)}, f32[1,2048]{1,0:T(1,128)S(1)}, f32[1,2048]{1,0:T(1,128)S(1)}) custom-call(s32[1]{0:T(128)} %bitcast.core_ref.refs_0_, f32[400,2048]{1,0:T(8,128)S(1)} %get-tuple-element.128.q.refs_2_, bf16[400,512]{1,0:T(8,128)(2,1)S(1)} %add.83.nfull, bf16[400,512]{1,0:T(8,128)(2,1)S(1)} %collective-permute-done.4.nother), custom_call_target="tpu_custom_call" | custom-call | flops 40000000 | tf_op jit(solution)/shard_map/pallas_call | solution.py:506
  46.0 5.9 %shard_map.132 = (f32[1,128]{1,0:T(1,128)S(1)}, f32[1,2048]{1,0:T(1,128)S(1)}, bf16[1024,2048]{1,0:T(8,128)(2,1)S(1)}, f32[200,1024]{1,0:T(8,128)S(1)}, f32[200,1024]{1,0:T(8,128)S(1)}) custom-call(s32[1]{0:T(128)} %bitcast.core_ref.refs_0_, f32[1,2048]{1,0:T(1,128)S(1)} %get-tuple-element.243.w, f32[400,2048]{1,0:T(8,128)S(1)} %get-tuple-element.128.q.refs_2_, ...), custom_call_target="tpu_custom_call" | custom-call | flops 40000000 | tf_op jit(solution)/shard_map/pallas_call | solution.py:506
  62.9 18.7 %shard_map.133 = (f32[32800,128]{1,0:T(8,128)S(1)}, f32[200,1408]{1,0:T(8,128)S(1)}, f32[200,1408]{1,0:T(8,128)S(1)}) custom-call(s32[1]{0:T(128)} %bitcast.core_ref.refs_0_, s32[2048]{0:T(1024)S(1)} %bitcast.56, s32[2048]{0:T(1024)S(1)} %bitcast.58, bf16[1024,2048]{1,0:T(8,128)(2,1)S(1)} %copy-done.23, f32[1,2048]{1,0:T(1,128)S(1)} %get-tuple-element.138.dp.refs_1_, ...), custom_call_target="tpu_custom_call" | custom-call | flops 75000000 | tf_op jit(solution)/shard_map/pallas_call | solution.py:506
  84.5 7.4 %shard_map.134.refs_5_ = f32[32800,128]{1,0:T(8,128)S(1)} custom-call(s32[2048]{0:T(1024)S(1)} %bitcast.54, f32[1,2048]{1,0:T(1,128)S(1)} %get-tuple-element.138.dp.refs_1_, f32[400,2048]{1,0:T(8,128)S(1)} %get-tuple-element.128.q.refs_2_, f32[32800,128]{1,0:T(8,128)S(1)} %get-tuple-element.144.refs_3_), custom_call_target="tpu_custom_call", output_to_operand_aliasing={{}: (3, {})} | custom-call | flops 60000000 | tf_op jit(solution)/shard_map/pallas_call | solution.py:506
  91.9 5.8 %copy-done.6 = f32[32800,128]{1,0:T(8,128)} copy-done((f32[32800,128]{1,0:T(8,128)}, f32[32800,128]{1,0:T(8,128)S(1)}, u32[]{:S(2)}) %copy-start.6) | copy-done | bytes 16793624
  106.1 5.8 %copy-done.7 = f32[32800,128]{1,0:T(8,128)S(1)} copy-done((f32[32800,128]{1,0:T(8,128)S(1)}, f32[32800,128]{1,0:T(8,128)}, u32[]{:S(2)}) %copy-start.7) | copy-done | bytes 16793624
  111.9 14.0 %shard_map.135 = (f32[32800,128]{1,0:T(8,128)S(1)}, f32[32800,128]{1,0:T(8,128)S(1)}, f32[8192,128]{1,0:T(8,128)S(1)}, bf16[400,512]{1,0:T(8,128)(2,1)S(1)}, bf16[400,512]{1,0:T(8,128)(2,1)S(1)}) custom-call(s32[1]{0:T(128)} %bitcast.core_ref.refs_0_, s32[1024]{0:T(1024)S(1)} %bitcast.68, ...), custom_call_target="tpu_custom_call", output_to_operand_aliasing={{0}: (5, {}), {1}: (3, {}), {2}: (4, {})} | custom-call | flops 150000000 | tf_op jit(solution)/shard_map/pallas_call | solution.py:506
  139.1 5.6 %shard_map.138 = (f32[400,2048]{1,0:T(8,128)S(1)}, f32[400,2048]{1,0:T(8,128)S(1)}, f32[5632,128]{1,0:T(8,128)S(1)}, f32[400,1408]{1,0:T(8,128)S(1)}, f32[1,1408]{1,0:T(1,128)S(1)}) custom-call(s32[1]{0:T(128)} %bitcast.core_ref.refs_0_, s32[2048]{0:T(1024)S(1)} %bitcast.51, bf16[400,2048]{1,0:T(8,128)(2,1)S(1)} %shard_map.137.refs_2_.hb, ...), custom_call_target="tpu_custom_call" | custom-call | flops 50000000 | tf_op jit(solution)/shard_map/pallas_call | solution.py:506
  147.7 13.8 %collective-permute-done.10 = bf16[400,512]{1,0:T(8,128)(2,1)S(1)} collective-permute-done((bf16[400,512]{1,0:T(8,128)(2,1)S(1)}, bf16[400,512]{1,0:T(8,128)(2,1)S(1)}, u32[]{:S(2)}, u32[]{:S(2)}) %collective-permute-start.10) | collective-permute-done | bytes 409632 | tf_op jit(solution)/shard_map/ppermute | solution.py:458
  168.8 6.1 %shard_map.140 = (f32[1,128]{1,0:T(1,128)S(1)}, f32[1,2048]{1,0:T(1,128)S(1)}, bf16[1024,2048]{1,0:T(8,128)(2,1)S(1)}, f32[200,1024]{1,0:T(8,128)S(1)}, f32[200,1024]{1,0:T(8,128)S(1)}) custom-call(s32[1]{0:T(128)} %bitcast.core_ref.refs_0_, f32[1,2048]{1,0:T(1,128)S(1)} %get-tuple-element.242.w, f32[400,2048]{1,0:T(8,128)S(1)} %get-tuple-element.159.q, ...), custom_call_target="tpu_custom_call" | custom-call | flops 40000000 | tf_op jit(solution)/shard_map/pallas_call | solution.py:506
  184.4 18.7 %shard_map.141 = (f32[32800,128]{1,0:T(8,128)S(1)}, f32[200,1408]{1,0:T(8,128)S(1)}, f32[200,1408]{1,0:T(8,128)S(1)}) custom-call(s32[1]{0:T(128)} %bitcast.core_ref.refs_0_, s32[2048]{0:T(1024)S(1)} %bitcast.52, s32[2048]{0:T(1024)S(1)} %bitcast.48, bf16[1024,2048]{1,0:T(8,128)(2,1)S(1)} %copy-done.21, f32[1,2048]{1,0:T(1,128)S(1)} %get-tuple-element.172.dp, ...), custom_call_target="tpu_custom_call" | custom-call | flops 75000000 | tf_op jit(solution)/shard_map/pallas_call | solution.py:506
  203.1 5.8 %copy-done.2 = f32[32800,128]{1,0:T(8,128)} copy-done((f32[32800,128]{1,0:T(8,128)}, f32[32800,128]{1,0:T(8,128)S(1)}, u32[]{:S(2)}) %copy-start.2) | copy-done | bytes 16793624
  211.8 17.5 %collective-permute-done.17.refs_2_ = f32[1,2048]{1,0:T(1,128)S(1)} collective-permute-done((f32[1,2048]{1,0:T(1,128)S(1)}, f32[1,2048]{1,0:T(1,128)S(1)}, u32[]{:S(2)}, u32[]{:S(2)}) %collective-permute-start.17) | collective-permute-done | bytes 8224 | tf_op jit(solution)/shard_map/ppermute | solution.py:458
  229.4 5.8 %copy-done.3 = f32[32800,128]{1,0:T(8,128)S(1)} copy-done((f32[32800,128]{1,0:T(8,128)S(1)}, f32[32800,128]{1,0:T(8,128)}, u32[]{:S(2)}) %copy-start.3) | copy-done | bytes 16793624
  235.2 12.6 %shard_map.142.refs_5_ = f32[32800,128]{1,0:T(8,128)S(1)} custom-call(s32[2048]{0:T(1024)S(1)} %bitcast.62, s32[2048]{0:T(1024)S(1)} %bitcast.71, f32[1,2048]{1,0:T(1,128)S(1)} %collective-permute-done.17.refs_2_, bf16[400,2048]{1,0:T(8,128)(2,1)} %collective-permute-done.18.refs_3_, f32[5632,128]{1,0:T(8,128)S(1)} %copy-done.29, ...), custom_call_target="tpu_custom_call", output_to_operand_aliasing={{}: (5, {})} | custom-call | flops 60000000 | tf_op jit(solution)/shard_map/pallas_call | solution.py:506
  247.8 5.8 %copy-done.4 = f32[32800,128]{1,0:T(8,128)} copy-done((f32[32800,128]{1,0:T(8,128)}, f32[32800,128]{1,0:T(8,128)S(1)}, u32[]{:S(2)}) %copy-start.4) | copy-done | bytes 16793624
  257.2 5.8 %copy-done.5 = f32[32800,128]{1,0:T(8,128)S(1)} copy-done((f32[32800,128]{1,0:T(8,128)S(1)}, f32[32800,128]{1,0:T(8,128)}, u32[]{:S(2)}) %copy-start.5) | copy-done | bytes 16793624
  263.0 14.0 %shard_map.143 = (f32[32800,128]{1,0:T(8,128)S(1)}, f32[32800,128]{1,0:T(8,128)S(1)}, f32[8192,128]{1,0:T(8,128)S(1)}, bf16[400,512]{1,0:T(8,128)(2,1)S(1)}, bf16[400,512]{1,0:T(8,128)(2,1)S(1)}) custom-call(s32[1]{0:T(128)} %bitcast.core_ref.refs_0_, s32[1024]{0:T(1024)S(1)} %bitcast.66, ...), custom_call_target="tpu_custom_call", output_to_operand_aliasing={{0}: (5, {}), {1}: (3, {}), {2}: (4, {})} | custom-call | flops 150000000 | tf_op jit(solution)/shard_map/pallas_call | solution.py:506
  292.5 5.6 %shard_map.146 = (f32[400,2048]{1,0:T(8,128)S(1)}, f32[400,2048]{1,0:T(8,128)S(1)}, f32[5632,128]{1,0:T(8,128)S(1)}, f32[400,1408]{1,0:T(8,128)S(1)}, f32[1,1408]{1,0:T(1,128)S(1)}) custom-call(s32[1]{0:T(128)} %bitcast.core_ref.refs_0_, s32[2048]{0:T(1024)S(1)} %bitcast.49, bf16[400,2048]{1,0:T(8,128)(2,1)S(1)} %shard_map.145.refs_2_.hb, ...), custom_call_target="tpu_custom_call" | custom-call | flops 50000000 | tf_op jit(solution)/shard_map/pallas_call | solution.py:506
  299.5 32.1 %collective-permute-done.22 = bf16[400,512]{1,0:T(8,128)(2,1)S(1)} collective-permute-done((bf16[400,512]{1,0:T(8,128)(2,1)S(1)}, bf16[400,512]{1,0:T(8,128)(2,1)S(1)}, u32[]{:S(2)}, u32[]{:S(2)}) %collective-permute-start.22) | collective-permute-done | bytes 409632 | tf_op jit(solution)/shard_map/ppermute | solution.py:458
  338.9 5.9 %shard_map.148 = (f32[1,128]{1,0:T(1,128)S(1)}, f32[1,2048]{1,0:T(1,128)S(1)}, bf16[1024,2048]{1,0:T(8,128)(2,1)S(1)}, f32[200,1024]{1,0:T(8,128)S(1)}, f32[200,1024]{1,0:T(8,128)S(1)}) custom-call(s32[1]{0:T(128)} %bitcast.core_ref.refs_0_, f32[1,2048]{1,0:T(1,128)S(1)} %get-tuple-element.241.w, f32[400,2048]{1,0:T(8,128)S(1)} %get-tuple-element.197.q, ...), custom_call_target="tpu_custom_call" | custom-call | flops 40000000 | tf_op jit(solution)/shard_map/pallas_call | solution.py:506
  347.3 18.7 %shard_map.149 = (f32[32800,128]{1,0:T(8,128)S(1)}, f32[200,1408]{1,0:T(8,128)S(1)}, f32[200,1408]{1,0:T(8,128)S(1)}) custom-call(s32[1]{0:T(128)} %bitcast.core_ref.refs_0_, s32[2048]{0:T(1024)S(1)} %bitcast.50, s32[2048]{0:T(1024)S(1)} %bitcast.46, bf16[1024,2048]{1,0:T(8,128)(2,1)S(1)} %get-tuple-element.213.ds, f32[1,2048]{1,0:T(1,128)S(1)} %get-tuple-element.210.dp, ...), custom_call_target="tpu_custom_call" | custom-call | flops 75000000 | tf_op jit(solution)/shard_map/pallas_call | solution.py:506
  371.0 58.0 %collective-permute-done.33 = f32[200,1408]{1,0:T(8,128)S(1)} collective-permute-done((f32[200,1408]{1,0:T(8,128)S(1)}, f32[200,1408]{1,0:T(8,128)S(1)}, u32[]{:S(2)}, u32[]{:S(2)}) %collective-permute-start.33) | collective-permute-done | bytes 1126432 | tf_op jit(solution)/shard_map/ppermute | solution.py:458
  430.6 15.5 %collective-permute-done.29.refs_2_ = f32[1,2048]{1,0:T(1,128)S(1)} collective-permute-done((f32[1,2048]{1,0:T(1,128)S(1)}, f32[1,2048]{1,0:T(1,128)S(1)}, u32[]{:S(2)}, u32[]{:S(2)}) %collective-permute-start.29) | collective-permute-done | bytes 8224 | tf_op jit(solution)/shard_map/ppermute | solution.py:458
  446.1 12.2 %shard_map.150.refs_4_ = f32[32800,128]{1,0:T(8,128)S(1)} custom-call(s32[2048]{0:T(1024)S(1)} %bitcast.60, s32[2048]{0:T(1024)S(1)} %bitcast.70, f32[1,2048]{1,0:T(1,128)S(1)} %collective-permute-done.29.refs_2_, bf16[400,2048]{1,0:T(8,128)(2,1)S(1)} %collective-permute-done.30.refs_3_, ...), custom_call_target="tpu_custom_call", output_to_operand_aliasing={{}: (5, {})} | custom-call | flops 60000000 | tf_op jit(solution)/shard_map/pallas_call | solution.py:506
  458.3 5.8 %copy-done.8 = f32[32800,128]{1,0:T(8,128)} copy-done((f32[32800,128]{1,0:T(8,128)}, f32[32800,128]{1,0:T(8,128)S(1)}, u32[]{:S(2)}) %copy-start.8) | copy-done | bytes 16793624
  466.6 5.8 %copy-done.1 = f32[32800,128]{1,0:T(8,128)S(1)} copy-done((f32[32800,128]{1,0:T(8,128)S(1)}, f32[32800,128]{1,0:T(8,128)}, u32[]{:S(2)}) %copy-start.1) | copy-done | bytes 16793624
  472.4 5.8 %copy-done.9 = f32[32800,128]{1,0:T(8,128)S(1)} copy-done((f32[32800,128]{1,0:T(8,128)S(1)}, f32[32800,128]{1,0:T(8,128)}, u32[]{:S(2)}) %copy-start.9) | copy-done | bytes 16793624
  480.3 17.0 %shard_map.151 = (f32[32800,128]{1,0:T(8,128)S(1)}, f32[400,8192]{1,0:T(8,128)}, f32[64,128]{1,0:T(8,128)}) custom-call(s32[1]{0:T(128)} %bitcast.core_ref.refs_0_, s32[1024]{0:T(1024)S(1)} %bitcast.64, f32[32800,128]{1,0:T(8,128)S(1)} %copy-done.1, f32[8192,128]{1,0:T(8,128)S(1)} %copy-done.11, ...), custom_call_target="tpu_custom_call", output_to_operand_aliasing={{0}: (4, {})} | custom-call | flops 150000000 | tf_op jit(solution)/shard_map/pallas_call | solution.py:506
  (181 shorter events, 119.5 us)
Async XLA Ops:
  12.5 5.7 %collective-permute-start = (bf16[400,512]{1,0:T(8,128)(2,1)S(1)}, bf16[400,512]{1,0:T(8,128)(2,1)S(1)}, u32[]{:S(2)}, u32[]{:S(2)}) collective-permute-start(bf16[400,512]{1,0:T(8,128)(2,1)S(1)} %get-tuple-element.118), channel_id=1, source_target_pairs={{0,1},{1,0},{2,3},{3,2},{4,5},{5,4},{6,7},{7,6}} | collective-permute-start | bytes 1228808 | tf_op jit(solution)/shard_map/ppermute | solution.py:455
  13.4 4.0 collective-permute-start.1
  13.5 4.7 collective-permute-start.2
  18.3 11.9 %collective-permute-start.3 = (bf16[400,512]{1,0:T(8,128)(2,1)S(1)}, bf16[400,512]{1,0:T(8,128)(2,1)S(1)}, u32[]{:S(2)}, u32[]{:S(2)}) collective-permute-start(bf16[400,512]{1,0:T(8,128)(2,1)S(1)} %add.82), channel_id=1, source_target_pairs={{0,2},{1,3},{2,0},{3,1},{4,6},{5,7},{6,4},{7,5}} | collective-permute-start | bytes 1228808 | tf_op jit(solution)/shard_map/ppermute | solution.py:458
  38.9 1.8 collective-permute-start.4
  54.0 2.3 collective-permute-start.5
  81.6 2.8 collective-permute-start.7
  81.8 20.7 %collective-permute-start.6 = (f32[200,1024]{1,0:T(8,128)}, f32[200,1024]{1,0:T(8,128)S(1)}, u32[]{:S(2)}, u32[]{:S(2)}) collective-permute-start(f32[200,1024]{1,0:T(8,128)} %add.84), channel_id=1, source_target_pairs={{0,2},{1,3},{2,0},{3,1},{4,6},{5,7},{6,4},{7,5}} | collective-permute-start | bytes 2457608 | tf_op jit(solution)/shard_map/ppermute | solution.py:458
  103.7 2.4 collective-permute-start.8
  103.8 32.4 %collective-permute-start.11 = (f32[200,1408]{1,0:T(8,128)S(1)}, f32[200,1408]{1,0:T(8,128)S(1)}, u32[]{:S(2)}, u32[]{:S(2)}) collective-permute-start(f32[200,1408]{1,0:T(8,128)S(1)} %add.85), channel_id=1, source_target_pairs={{0,2},{1,3},{2,0},{3,1},{4,6},{5,7},{6,4},{7,5}} | collective-permute-start | bytes 3379208 | tf_op jit(solution)/shard_map/ppermute | solution.py:458
  125.9 1.8 collective-permute-start.9
  131.8 36.9 %collective-permute-start.14 = (bf16[400,2048]{1,0:T(8,128)(2,1)S(1)}, bf16[400,2048]{1,0:T(8,128)(2,1)S(1)}, u32[]{:S(2)}, u32[]{:S(2)}) collective-permute-start(bf16[400,2048]{1,0:T(8,128)(2,1)S(1)} %shard_map.136), channel_id=1, source_target_pairs={{0,3},{1,0},{2,1},{3,2},{4,7},{5,4},{6,5},{7,6}} | collective-permute-start | bytes 4915208 | tf_op jit(solution)/shard_map/ppermute | solution.py:458
  136.3 2.8 collective-permute-start.12
  136.6 24.9 %collective-permute-start.10 = (bf16[400,512]{1,0:T(8,128)(2,1)S(1)}, bf16[400,512]{1,0:T(8,128)(2,1)S(1)}, u32[]{:S(2)}, u32[]{:S(2)}) collective-permute-start(bf16[400,512]{1,0:T(8,128)(2,1)S(1)} %add.87), channel_id=1, source_target_pairs={{0,2},{1,3},{2,0},{3,1},{4,6},{5,7},{6,4},{7,5}} | collective-permute-start | bytes 1228808 | tf_op jit(solution)/shard_map/ppermute | solution.py:458
  176.9 2.3 collective-permute-start.15
  177.0 52.4 %collective-permute-start.18 = (bf16[400,2048]{1,0:T(8,128)(2,1)S(1)}, bf16[400,2048]{1,0:T(8,128)(2,1)}, u32[]{:S(2)}, u32[]{:S(2)}) collective-permute-start(bf16[400,2048]{1,0:T(8,128)(2,1)S(1)} %shard_map.137.refs_2_.hb), channel_id=1, source_target_pairs={{0,1},{1,2},{2,3},{3,0},{4,5},{5,6},{6,7},{7,4}} | collective-permute-start | bytes 4915208 | tf_op jit(solution)/shard_map/ppermute | solution.py:458
  208.9 2.8 collective-permute-start.19
  209.1 44.5 %collective-permute-start.16 = (f32[200,1024]{1,0:T(8,128)}, f32[200,1024]{1,0:T(8,128)S(1)}, u32[]{:S(2)}, u32[]{:S(2)}) collective-permute-start(f32[200,1024]{1,0:T(8,128)} %add.90), channel_id=1, source_target_pairs={{0,2},{1,3},{2,0},{3,1},{4,6},{5,7},{6,4},{7,5}} | collective-permute-start | bytes 2457608 | tf_op jit(solution)/shard_map/ppermute | solution.py:458
  209.6 19.8 %collective-permute-start.17 = (f32[1,2048]{1,0:T(1,128)S(1)}, f32[1,2048]{1,0:T(1,128)S(1)}, u32[]{:S(2)}, u32[]{:S(2)}) collective-permute-start(f32[1,2048]{1,0:T(1,128)S(1)} %get-tuple-element.172.dp), channel_id=1, source_target_pairs={{0,1},{1,2},{2,3},{3,0},{4,5},{5,6},{6,7},{7,4}} | collective-permute-start | bytes 24584 | tf_op jit(solution)/shard_map/ppermute | solution.py:458
  254.9 2.4 collective-permute-start.20
  254.9 34.6 %collective-permute-start.23 = (f32[200,1408]{1,0:T(8,128)S(1)}, f32[200,1408]{1,0:T(8,128)S(1)}, u32[]{:S(2)}, u32[]{:S(2)}) collective-permute-start(f32[200,1408]{1,0:T(8,128)S(1)} %add.91), channel_id=1, source_target_pairs={{0,2},{1,3},{2,0},{3,1},{4,6},{5,7},{6,4},{7,5}} | collective-permute-start | bytes 3379208 | tf_op jit(solution)/shard_map/ppermute | solution.py:458
  284.9 53.9 %collective-permute-start.26 = (bf16[400,2048]{1,0:T(8,128)(2,1)S(1)}, bf16[400,2048]{1,0:T(8,128)(2,1)S(1)}, u32[]{:S(2)}, u32[]{:S(2)}) collective-permute-start(bf16[400,2048]{1,0:T(8,128)(2,1)S(1)} %shard_map.144), channel_id=1, source_target_pairs={{0,2},{1,3},{2,0},{3,1},{4,6},{5,7},{6,4},{7,5}} | collective-permute-start | bytes 4915208 | tf_op jit(solution)/shard_map/ppermute | solution.py:458
  289.7 2.8 collective-permute-start.24
  289.7 41.9 %collective-permute-start.22 = (bf16[400,512]{1,0:T(8,128)(2,1)S(1)}, bf16[400,512]{1,0:T(8,128)(2,1)S(1)}, u32[]{:S(2)}, u32[]{:S(2)}) collective-permute-start(bf16[400,512]{1,0:T(8,128)(2,1)S(1)} %add.93), channel_id=1, source_target_pairs={{0,2},{1,3},{2,0},{3,1},{4,6},{5,7},{6,4},{7,5}} | collective-permute-start | bytes 1228808 | tf_op jit(solution)/shard_map/ppermute | solution.py:458
  344.8 2.4 collective-permute-start.27
  366.0 2.8 collective-permute-start.31
  366.2 79.9 %collective-permute-start.30 = (bf16[400,2048]{1,0:T(8,128)(2,1)S(1)}, bf16[400,2048]{1,0:T(8,128)(2,1)S(1)}, u32[]{:S(2)}, u32[]{:S(2)}) collective-permute-start(bf16[400,2048]{1,0:T(8,128)(2,1)S(1)} %shard_map.145.refs_2_.hb), channel_id=1, source_target_pairs={{0,2},{1,3},{2,0},{3,1},{4,6},{5,7},{6,4},{7,5}} | collective-permute-start | bytes 4915208 | tf_op jit(solution)/shard_map/ppermute | solution.py:458
  368.9 60.1 %collective-permute-start.33 = (f32[200,1408]{1,0:T(8,128)S(1)}, f32[200,1408]{1,0:T(8,128)S(1)}, u32[]{:S(2)}, u32[]{:S(2)}) collective-permute-start(f32[200,1408]{1,0:T(8,128)S(1)} %add.97), channel_id=1, source_target_pairs={{0,2},{1,3},{2,0},{3,1},{4,6},{5,7},{6,4},{7,5}} | collective-permute-start | bytes 3379208 | tf_op jit(solution)/shard_map/ppermute | solution.py:458
  369.5 94.6 %collective-permute-start.28 = (f32[200,1024]{1,0:T(8,128)S(1)}, f32[200,1024]{1,0:T(8,128)S(1)}, u32[]{:S(2)}, u32[]{:S(2)}) collective-permute-start(f32[200,1024]{1,0:T(8,128)S(1)} %add.96), channel_id=1, source_target_pairs={{0,2},{1,3},{2,0},{3,1},{4,6},{5,7},{6,4},{7,5}} | collective-permute-start | bytes 2457608 | tf_op jit(solution)/shard_map/ppermute | solution.py:458
  430.1 67.3 %collective-permute-start.34 = (f32[200,1408]{1,0:T(8,128)}, f32[200,1408]{1,0:T(8,128)}, u32[]{:S(2)}, u32[]{:S(2)}) collective-permute-start(f32[200,1408]{1,0:T(8,128)} %add.99), channel_id=1, source_target_pairs={{0,1},{1,0},{2,3},{3,2},{4,5},{5,4},{6,7},{7,6}} | collective-permute-start | bytes 3379208 | tf_op jit(solution)/shard_map/ppermute | solution.py:465
  430.1 16.0 %collective-permute-start.29 = (f32[1,2048]{1,0:T(1,128)S(1)}, f32[1,2048]{1,0:T(1,128)S(1)}, u32[]{:S(2)}, u32[]{:S(2)}) collective-permute-start(f32[1,2048]{1,0:T(1,128)S(1)} %get-tuple-element.210.dp), channel_id=1, source_target_pairs={{0,2},{1,3},{2,0},{3,1},{4,6},{5,7},{6,4},{7,5}} | collective-permute-start | bytes 24584 | tf_op jit(solution)/shard_map/ppermute | solution.py:458
  464.2 2.4 collective-permute-start.32
  (44 other events, 249.5 us)

commit v6 on v5

--- a/solution.py
+++ b/solution.py
@@ -110,7 +110,7 @@
     ns[...] = nbuf[:, pl.ds(pl.multiple_of((1 - core) * half, LANES), half)]
 
 
-def entry_kernel(dim, rows, core_ref, negs, et, g, t4, v, nk, ns, inbuf, stage, nbuf, in_sem):
+def entry_kernel(dim, rows, core_ref, negs, et, t4, nk, ns, inbuf, stage, nbuf, in_sem):
     cols = inbuf.shape[2]
     steps = rows // cols
     per = cols // LANES
@@ -138,7 +138,6 @@
             row0 = (step * per + b) * LANES
             for j in range(SLICES):
                 t4[pl.ds(SLICES * row0 + j, LANES, stride=SLICES), :] = inbuf[slot, pl.ds(j * LANES, LANES), pl.ds(b * LANES, LANES)].T
-            v[pl.ds(pl.multiple_of(row0, 8), LANES), :] = jnp.broadcast_to(g[pl.ds(step * per + b, 1), :], (LANES, LANES)).T
         return 0
 
     lax.fori_loop(0, steps, body, 0)
@@ -254,41 +253,49 @@
     lax.fori_loop(0, negp // LANES, save, 0)
 
 
-def grad_kernel(dim, edges, core_ref, rel, heads, ds, dp, tb, hb, r, nfull, nother,
-                acc, rk, rs, nb, racc, stage_r, stage_h, qs):
-    core = core_ref[0]
+def grad_kernel(dim, edges, core_ref, rel, ds, dp, tb, hb, r, nfull, nother, hg, rk, rs, nb, racc, stage, qs):
     half = dim // 2
-    relp = rk.shape[1]
     tops = SLICES * LANES
-    place_negs(core, nb, nfull, nother)
+    place_negs(core_ref[0], nb, nfull, nother)
     zero_rows(racc)
-    zero_rows(acc)
-    qs[pl.ds(dim, tops - dim), :] = jnp.zeros((tops - dim, CHUNK), F32)
-
-    def step(c, _):
+    qs[:, pl.ds(dim, tops - dim), :] = jnp.zeros((2, tops - dim, CHUNK), F32)
+
+    def compute(c, slot):
         cols = pl.ds(pl.multiple_of(c * CHUNK, LANES), CHUNK)
         gq = lax.dot_general(nb[...], ds[:, cols], (((1,), (0,)), ((), ())), preferred_element_type=F32) + dp[:, cols] * tb[:, cols].astype(F32)
         g_re, g_im = gq[:half], gq[half:]
         h = hb[:, cols].astype(F32)
         h_re, h_im = h[:half], h[half:]
         r_re, r_im = r[pl.ds(0, half), cols], r[pl.ds(half, half), cols]
-        for stage, f_re, f_im in ((stage_r, h_re, h_im), (stage_h, r_re, r_im)):
-            qs[pl.ds(0, half), :] = g_re * f_re + g_im * f_im
-            qs[pl.ds(half, half), :] = g_im * f_re - g_re * f_im
-            for b in range(CHUNK // LANES):
-                for j in range(SLICES):
-                    stage[pl.ds(SLICES * b * LANES + j, LANES, stride=SLICES), :] = qs[pl.ds(j * LANES, LANES), pl.ds(b * LANES, LANES)].T
-        add_rows([(racc, rel, c * CHUNK, stage_r, 0), (acc, heads, c * CHUNK, stage_h, 0)], CHUNK)
-        return 0
-
-    lax.fori_loop(0, edges // CHUNK, step, 0)
+        for part, (f_re, f_im) in enumerate(((h_re, h_im), (r_re, r_im))):
+            qs[part, pl.ds(0, half), :] = g_re * f_re + g_im * f_im
+            qs[part, pl.ds(half, half), :] = g_im * f_re - g_re * f_im
+        for b in range(CHUNK // LANES):
+            for j in range(SLICES):
+                place = pl.ds(j * LANES, LANES), pl.ds(b * LANES, LANES)
+                stage[slot, pl.ds(SLICES * b * LANES + j, LANES, stride=SLICES), :] = qs[(0,) + place].T
+                hg[pl.ds(SLICES * (c * CHUNK + b * LANES) + j, LANES, stride=SLICES), :] = qs[(1,) + place].T
+
+    def scatter(c, slot):
+        add_rows([(racc, rel, c * CHUNK, stage.at[slot], 0)], CHUNK)
+
+    compute(0, 0)
+
+    def step(i, _):
+        for slot in range(2):
+            c = 2 * i + slot
+            scatter(c, slot)
+            compute(jnp.minimum(c + 1, edges // CHUNK - 1), 1 - slot)
+        return 0
+
+    lax.fori_loop(0, edges // CHUNK // 2, step, 0)
 
     def save(b, _):
         cols = pl.ds(pl.multiple_of(b * LANES, LANES), LANES)
-        put_halves(core, rk, rs, cols, lambda j: racc[pl.ds(SLICES * LANES * b + j, LANES, stride=SLICES), :].T, dim)
-        return 0
-
-    lax.fori_loop(0, relp // LANES, save, 0)
+        put_halves(core_ref[0], rk, rs, cols, lambda j: racc[pl.ds(SLICES * LANES * b + j, LANES, stride=SLICES), :].T, dim)
+        return 0
+
+    lax.fori_loop(0, rk.shape[1] // LANES, save, 0)
 
 
 def unstage(rt, stage):
@@ -298,44 +305,50 @@
 
 def scatter_kernel(dim, edges, own, *refs):
     if own:
-        tails, dp, q, _, acc, stage, rt = refs
+        heads, tails, hg, dp, q, acc, stage, rows, rt = refs
     else:
-        tails, rel, dp, hb_in, r4, _, acc, stage, rt = refs
+        heads, tails, rel, hg, dp, hb_in, r4, acc, stage, rows, rt = refs
     half = dim // 2
-    tops = SLICES * LANES
-    rt[pl.ds(dim, tops - dim), :] = jnp.zeros((tops - dim, LANES), F32)
-
-    def tail_step(b, _):
+    blocks = edges // LANES
+    zero_rows(acc)
+    rt[:, pl.ds(dim, SLICES * LANES - dim), :] = jnp.zeros((2, SLICES * LANES - dim, LANES), F32)
+
+    def compute(b, slot):
         cols = pl.ds(pl.multiple_of(b * LANES, LANES), LANES)
         scale = dp[:, cols]
         if own:
-            rt[pl.ds(0, dim), :] = q[:, cols] * scale
+            rt[1, pl.ds(0, dim), :] = q[:, cols] * scale
         else:
             gather_rows(r4, rel, b * LANES, stage, LANES)
             for j in range(SLICES):
-                rt[pl.ds(j * LANES, LANES), :] = stage_cols(stage, j)
+                rt[0, pl.ds(j * LANES, LANES), :] = stage_cols(stage, j)
             h = hb_in[:, cols].astype(F32)
-            r_re, r_im = rt[pl.ds(0, half), :], rt[pl.ds(half, half), :]
-            q_re = scale * (h[:half] * r_re - h[half:] * r_im)
-            q_im = scale * (h[:half] * r_im + h[half:] * r_re)
-            rt[pl.ds(0, half), :] = q_re
-            rt[pl.ds(half, half), :] = q_im
-        unstage(rt, stage)
-        add_rows([(acc, tails, b * LANES, stage, 0)], LANES)
-        return 0
-
-    lax.fori_loop(0, edges // LANES, tail_step, 0)
+            r_re, r_im = rt[0, pl.ds(0, half), :], rt[0, pl.ds(half, half), :]
+            rt[1, pl.ds(0, half), :] = scale * (h[:half] * r_re - h[half:] * r_im)
+            rt[1, pl.ds(half, half), :] = scale * (h[:half] * r_im + h[half:] * r_re)
+        unstage(rt.at[1], rows.at[slot])
+
+    compute(0, 0)
+
+    def step(i, _):
+        for slot in range(2):
+            b = 2 * i + slot
+            add_rows([(acc, tails, b * LANES, rows.at[slot], 0)], LANES)
+            add_rows([(acc, heads, b * LANES, hg, b * LANES * SLICES)], LANES)
+            compute(jnp.minimum(b + 1, blocks - 1), 1 - slot)
+        return 0
+
+    lax.fori_loop(0, blocks // 2, step, 0)
 
 
 def update_kernel(dim, rows, last, *refs):
     if last:
         core_ref, negs, t4, v, _, nmine, nother, acc, et_out, g_out, stage, rt, rate, outbuf, out_sem = refs
     else:
-        core_ref, negs, negs_n, t4, v, _, nmine, nother, acc, new_t4, new_v, nk, ns, stage, rt, rate, nbuf = refs
+        core_ref, negs, negs_n, old_t4, v, _, nmine, nother, acc, t4, new_v, nk, ns, stage, rt, rate, nbuf = refs
     core = core_ref[0]
     half = dim // 2
-    tops = SLICES * LANES
-    rt[pl.ds(dim, tops - dim), :] = jnp.zeros((tops - dim, LANES), F32)
+    rt[pl.ds(dim, SLICES * LANES - dim), :] = jnp.zeros((SLICES * LANES - dim, LANES), F32)
 
     def neg_step(b, _):
         cols = pl.ds(pl.multiple_of(b * LANES, LANES), LANES)
@@ -352,35 +365,37 @@
     def slices(b):
         return [pl.ds(SLICES * LANES * b + j, LANES, stride=SLICES) for j in range(SLICES)]
 
-    def advance(b):
+    def advance(b, out):
         where = slices(b)
         square = acc[where[0], :] * acc[where[0], :]
         for j in range(1, SLICES):
             square = square + acc[where[j], :] * acc[where[j], :]
-        state = v[pl.ds(pl.multiple_of(b * LANES, 8), LANES), :] + jnp.sum(square, axis=1, keepdims=True) / dim
-        return state, LEARN_RATE / jnp.sqrt(state + ADA_EPS)
+        state = v[pl.ds(b, 1), :] + jnp.sum(square.T, axis=0, keepdims=True) / dim
+        out[pl.ds(b, 1), :] = state
+        return jnp.broadcast_to(LEARN_RATE / jnp.sqrt(state + ADA_EPS), (LANES, LANES)).T
 
     if not last:
-        def open_block(b):
-            state, step_size = advance(b)
-            new_v[pl.ds(pl.multiple_of(b * LANES, 8), LANES), :] = state
-            rate[...] = step_size
-
-        def close_block(b, step_size):
-            for w in slices(b):
-                new_t4[w, :] = t4[w, :] - acc[w, :] * step_size
-
-        def ada_step(b, _):
-            step_size = rate[...]
-            close_block(b - 1, step_size)
-            open_block(b)
+        def open_pair(p):
+            steps = [advance(2 * p + i, new_v) for i in range(2)]
+            for i in range(2):
+                rate[i] = steps[i]
+
+        def close_pair(p, steps):
+            for i in range(2):
+                for w in slices(2 * p + i):
+                    t4[w, :] = old_t4[w, :] - acc[w, :] * steps[i]
+
+        def ada_step(p, _):
+            steps = [rate[0], rate[1]]
+            close_pair(p - 1, steps)
+            open_pair(p)
             return 0
 
-        open_block(0)
-        lax.fori_loop(1, blocks, ada_step, 0)
-        close_block(blocks - 1, rate[...])
-        new_t4[pl.ds(rows * SLICES, 32), :] = jnp.zeros((32, LANES), F32)
-        gather_negs(dim, core, new_t4, negs_n, nk, ns, nbuf, stage)
+        open_pair(0)
+        lax.fori_loop(1, blocks // 2, ada_step, 0)
+        close_pair(blocks // 2 - 1, [rate[0], rate[1]])
+        t4[pl.ds(rows * SLICES, 32), :] = jnp.zeros((32, LANES), F32)
+        gather_negs(dim, core, t4, negs_n, nk, ns, nbuf, stage)
         return
 
     width = outbuf.shape[2]
@@ -390,12 +405,11 @@
     def save(step, slot):
         return pltpu.make_async_copy(outbuf.at[slot], et_out.at[:, pl.ds(pl.multiple_of(step * width, LANES), width)], out_sem.at[slot])
 
-    def open_last(b):
-        state, step_size = advance(b)
-        g_out[pl.ds(b, 1), :] = state.T[:1]
-        rate[...] = step_size
-
-    open_last(0)
+    def open_group(step, slot):
+        for i in range(per):
+            rate[slot, i] = advance(step * per + i, g_out)
+
+    open_group(0, 0)
 
     def exit_step(step, _):
         slot = lax.rem(step, 2)
@@ -405,12 +419,11 @@
             save(step - 2, slot).wait()
 
         for i in range(per):
-            b = step * per + i
-            step_size = rate[...]
-            for j, w in enumerate(slices(b)):
+            step_size = rate[slot, i]
+            for j, w in enumerate(slices(step * per + i)):
                 size = min(LANES, dim - j * LANES)
                 outbuf[slot, pl.ds(j * LANES, size), pl.ds(i * LANES, LANES)] = (t4[w, :] - acc[w, :] * step_size).T[:size]
-            open_last(jnp.minimum(b + 1, blocks - 1))
+        open_group(jnp.minimum(step + 1, steps - 1), 1 - slot)
         save(step, slot).start()
         return 0
 
@@ -492,14 +505,14 @@
         wide_rows = (rows + 8) * SLICES
         stage_shape = pltpu.VMEM((SLICES * LANES, LANES), F32)
         square_shape = pltpu.VMEM((SLICES * LANES, LANES), F32)
-        table_out, state_out = shape((wide_rows, LANES)), shape((rows, LANES))
+        table_out, state_out = shape((wide_rows, LANES)), shape((rows // LANES, LANES))
         cols_bf = shape((dim, edges), BF16)
         neg_half = shape((dim, negp // 2), BF16)
 
-        def call(kernel, args, kinds, outs, out_kinds, scratch, micros, aliases=None):
+        def call(kernel, args, kinds, outs, out_kinds, scratch, micros, name, aliases=None):
             places = {'s': smem, 'h': hbm, 'v': vmem, 'V': vmem}
             windows = [a for a, k in zip(list(args) + outs, kinds + out_kinds) if k == 'v']
-            limit = 3 * 2 ** 20 + sum(padded_bytes(a.shape, a.dtype) for a in windows)
+            limit = (4 if name == 'grad' else 3) * 2 ** 20 + sum(padded_bytes(a.shape, a.dtype) for a in windows)
             limit += sum(padded_bytes(a.shape, a.dtype) for a in scratch if a.memory_space == pltpu.VMEM)
             args = [pltpu.with_memory_space_constraint(a, pltpu.VMEM) if k == 'V' else a for a, k in zip(args, kinds)]
             outs = [pltpu.VMEM(o.shape, o.dtype) if k == 'V' else o for o, k in zip(outs, out_kinds)]
@@ -510,12 +523,13 @@
 
         def gather(lists, t4):
             return call(functools.partial(gather_kernel, dim, len(lists)), lists + [t4], 's' * len(lists) + 'V',
-                        [cols_bf] * len(lists), 'V' * len(lists), [stage_shape], 1 + 5 * len(lists))
-
-        t4, v, nk, ns = call(
-            functools.partial(entry_kernel, dim, rows), [core, negs[0], pltpu.with_memory_space_constraint(ent_emb.T, pltpu.HBM), ent_ada.reshape(rows // LANES, LANES)], 'sshv',
-            [table_out, state_out, neg_half, neg_half], 'VVVV',
-            [pltpu.VMEM((4, SLICES * LANES, 4 * LANES), F32), stage_shape, pltpu.VMEM((dim, negp), BF16), pltpu.SemaphoreType.DMA((4,))], 20)
+                        [cols_bf] * len(lists), 'V' * len(lists), [stage_shape], 1 + 5 * len(lists), 'gather')
+
+        t4, nk, ns = call(
+            functools.partial(entry_kernel, dim, rows), [core, negs[0], pltpu.with_memory_space_constraint(ent_emb.T, pltpu.HBM)], 'ssh',
+            [table_out, neg_half, neg_half], 'VVV',
+            [pltpu.VMEM((4, SLICES * LANES, 4 * LANES), F32), stage_shape, pltpu.VMEM((dim, negp), BF16), pltpu.SemaphoreType.DMA((4,))], 20, 'entry')
+        v = ent_ada.reshape(rows // LANES, LANES)
 
         rfm = jnp.pad(rel_emb.T, ((0, 0), (0, relp - num_rel)))
         vr = jnp.pad(rel_ada, (0, relp - num_rel), constant_values=1.0).reshape(1, relp)
@@ -548,7 +562,7 @@
                 args += [vr] + list(rel_grads)
                 kinds += 'vVV'
             res = call(functools.partial(query_kernel, dim, edges, first), args, kinds, outs, out_kinds,
-                       [stage_shape, pltpu.VMEM((SLICES * LANES, relp), F32)], 10)
+                       [stage_shape, pltpu.VMEM((SLICES * LANES, relp), F32)], 10, 'query')
             q, r, r4 = res[:3]
             neg_got, q = tie((neg_got, q))
             nmine, nother = finish(neg_part, neg_got)
@@ -557,7 +571,7 @@
             e, neg_top, neg_total = call(
                 functools.partial(exp_kernel, neg_count, edges), [core, q, nmine, nother], 'sVVV',
                 [shape((neg_count, edges)), shape((1, edges)), shape((1, edges))], 'Vvv',
-                [pltpu.VMEM((dim, negp), BF16), pltpu.VMEM((negp, dim), BF16), pltpu.VMEM((neg_count, CHUNK), F32)], 8)
+                [pltpu.VMEM((dim, negp), BF16), pltpu.VMEM((negp, dim), BF16), pltpu.VMEM((neg_count, CHUNK), F32)], 8, 'exp')
             if not first:
                 e, tail_cols = tie((e, tail_cols))
                 tail_cols, hb = tie((tail_cols, hb))
@@ -565,41 +579,42 @@
             loss, dp, ds, gk, gs = call(
                 functools.partial(score_kernel, dim, neg_count, edges), [core, weights[s].reshape(1, edges), q, tail_cols, e, neg_top, neg_total], 'svVVVvv',
                 [shape((1, LANES)), shape((1, edges)), shape((negp, edges), BF16), shape((half, negp)), shape((half, negp))], 'vvVVV',
-                [pltpu.VMEM((negp, dim), F32)], 8)
+                [pltpu.VMEM((negp, dim), F32)], 8, 'score')
             losses.append(loss[0, 0])
             if not first:
                 dp_away = send(dp, shift(s))
             neg_part = chip_sum(gk, gs)
             neg_part, ds = tie((neg_part, ds))
             neg_got = link(neg_part)
-            acc, rk, rs = call(
-                functools.partial(grad_kernel, dim, edges), [core, own_rels[s], heads[s], ds, dp, tail_cols, hb, r, nmine, nother], 'sssVvVVVVV',
-                [table_out, shape((half, relp)), shape((half, relp))], 'VVV',
-                [pltpu.VMEM((dim, negp), BF16), pltpu.VMEM((relp * SLICES, LANES), F32), pltpu.VMEM((SLICES * CHUNK, LANES), F32),
-                 pltpu.VMEM((SLICES * CHUNK, LANES), F32), pltpu.VMEM((SLICES * LANES, CHUNK), F32)], 15)
+            hg, rk, rs = call(
+                functools.partial(grad_kernel, dim, edges), [core, own_rels[s], ds, dp, tail_cols, hb, r, nmine, nother], 'ssVvVVVVV',
+                [shape((edges * SLICES, LANES)), shape((half, relp)), shape((half, relp))], 'VVV',
+                [pltpu.VMEM((dim, negp), BF16), pltpu.VMEM((relp * SLICES, LANES), F32), pltpu.VMEM((2, SLICES * CHUNK, LANES), F32),
+                 pltpu.VMEM((2, SLICES * LANES, CHUNK), F32)], 12, 'grad')
             rel_part = chip_sum(rk, rs)
-            rel_part, acc = tie((rel_part, acc))
+            rel_part, hg = tie((rel_part, hg))
             rel_got = link(rel_part)
             if first:
-                args, kinds = [tails[s], dp, q, acc], 'svVV'
+                args, kinds = [heads[s], tails[s], hg, dp, q], 'ssVvV'
             else:
-                args, kinds = [tails[s], rels[s], dp_away, head_cols, r4, acc], 'ssvVVV'
+                args, kinds = [heads[s], tails[s], rels[s], hg, dp_away, head_cols, r4], 'sssVvVV'
             acc, = call(functools.partial(scatter_kernel, dim, edges, first), args, kinds, [table_out], 'V',
-                        [stage_shape, square_shape], 12, {len(args) - 1: 0})
+                        [stage_shape] + [pltpu.VMEM((2, SLICES * LANES, LANES), F32)] * 2, 15, 'scatter')
             neg_got, acc = tie((neg_got, acc))
             gmine, gother = finish(neg_part, neg_got)
-            scratch = [stage_shape, square_shape, pltpu.VMEM((LANES, LANES), F32)]
+            scratch = [stage_shape, square_shape, pltpu.VMEM((2, 4, LANES, LANES) if last else (2, LANES, LANES), F32)]
             if last:
-                args, outs, out_kinds = [core, negs[s]], [table_out, shape((dim, rows)), shape((rows // LANES, LANES))], 'Vhv'
+                args, kinds = [core, negs[s], t4, v, acc], 'ssVVV'
+                outs, out_kinds = [table_out, shape((dim, rows)), shape((rows // LANES, LANES))], 'Vhv'
                 scratch += [pltpu.VMEM((2, dim, 4 * LANES), F32), pltpu.SemaphoreType.DMA((2,))]
                 aliases = {4: 0}
             else:
-                args = [core, negs[s], negs[s + 1]]
+                args, kinds = [core, negs[s], negs[s + 1], t4, v, acc], 'sssVVV'
                 outs, out_kinds = [table_out, table_out, state_out, neg_half, neg_half], 'VVVVV'
                 scratch += [pltpu.VMEM((dim, negp), BF16)]
                 aliases = {5: 0, 3: 1, 4: 2}
-            res = call(functools.partial(update_kernel, dim, rows, last), args + [t4, v, acc, gmine, gother], 's' * len(args) + 'VVVVV',
-                       outs, out_kinds, scratch, 30, aliases)
+            res = call(functools.partial(update_kernel, dim, rows, last), args + [gmine, gother], kinds + 'VV',
+                       outs, out_kinds, scratch, 30, 'update', aliases)
             if last:
                 _, et, g = res
             else:

time: 503 us -> 452 us (0.90)
  local copies, waits for them, and re-layouts: 77.6 us -> 27.3 us
    unnamed x82 -> x41, local copies, waits for them, and re-layouts: 76.8 us -> 26.5 us
    pallas_call x24, Pallas kernels: 219 us -> 214 us  [call(): pl.pallas_call(kernel, out_shape=outs, in_specs=[places[k]() for k in kin...]
  transfers between devices with their start and end apart: 35 -> 35, of which waited for: 25 -> 25; matrix products, arithmetic and copies ran while one was open for 1% -> 1% of each run, Pallas kernels for 28% -> 33%
where the time goes in v6:
time: 452 us; the launch traced here: 451 us
  Pallas kernels  214 us (47%)
  waiting for transfers between devices  179 us (40%)
  local copies, waits for them, and re-layouts  27.3 us (6%)
  starting transfers between devices  17.2 us (4%)
  other arithmetic  13.1 us (3%)
    pallas_call x24, Pallas kernels, call(): pl.pallas_call(kernel, out_shape=outs, in_specs=[places[k]() for k in kin...  214 us
    ppermute x17, waiting for transfers between devices, send(): return lax.ppermute(value, 'ent', pairs)  150 us
    unnamed x41, local copies, waits for them, and re-layouts  26.5 us
    ppermute x9, waiting for transfers between devices, chip_sum(): return keep + lax.ppermute(send, 'ent', swap)  15.5 us
    ppermute x17, starting transfers between devices, send(): return lax.ppermute(value, 'ent', pairs)  14.7 us
    ppermute x9, waiting for transfers between devices, finish(): return (mine, lax.ppermute(mine, 'ent', swap))  13 us
  transfers between devices with their start and end apart: 35, of which 25 were waited for; matrix products, arithmetic and copies ran while one was open for 1% of the time, Pallas kernels for 33%

profile of v6, /device:TPU:0, one launch (start us, length us, event | category | flops | bytes accessed | tf_op | source)
XLA Modules:
  0.0 451.4 jit_solution(3923672936677387456)
XLA Ops:
  2.2 9.9 %shard_map.128 = (f32[32800,128]{1,0:T(8,128)S(1)}, bf16[400,512]{1,0:T(8,128)(2,1)S(1)}, bf16[400,512]{1,0:T(8,128)(2,1)S(1)}) custom-call(s32[1]{0:T(128)} %bitcast.core_ref.refs_0_, s32[1024]{0:T(1024)S(1)} %bitcast.66, f32[400,8192]{1,0:T(8,128)} %bitcast.75), custom_call_target="tpu_custom_call" | custom-call | flops 100000000 | tf_op jit(solution)/shard_map/pallas_call | solution.py:519
  20.0 7.5 %shard_map.129 = (bf16[400,2048]{1,0:T(8,128)(2,1)S(1)}, bf16[400,2048]{1,0:T(8,128)(2,1)S(1)}) custom-call(s32[2048]{0:T(1024)S(1)} %bitcast.54, s32[2048]{0:T(1024)S(1)} %bitcast.56, f32[32800,128]{1,0:T(8,128)S(1)} %get-tuple-element.119.refs_2_.refs_3_), custom_call_target="tpu_custom_call" | custom-call | flops 55000000 | tf_op jit(solution)/shard_map/pallas_call | solution.py:519
  29.9 6.8 %shard_map.130 = (f32[400,2048]{1,0:T(8,128)S(1)}, f32[400,2048]{1,0:T(8,128)S(1)}, f32[5632,128]{1,0:T(8,128)}) custom-call(s32[1]{0:T(128)} %bitcast.core_ref.refs_0_, s32[2048]{0:T(1024)S(1)} %bitcast.62, bf16[400,2048]{1,0:T(8,128)(2,1)S(1)} %get-tuple-element.124.refs_2_.hb, f32[400,1408]{1,0:T(8,128)S(1)} %pad.13.refs_3_), custom_call_target="tpu_custom_call" | custom-call | flops 50000000 | tf_op jit(solution)/shard_map/pallas_call | solution.py:519
  38.5 5.4 %shard_map.131 = (f32[1000,2048]{1,0:T(8,128)S(1)}, f32[1,2048]{1,0:T(1,128)S(1)}, f32[1,2048]{1,0:T(1,128)S(1)}) custom-call(s32[1]{0:T(128)} %bitcast.core_ref.refs_0_, f32[400,2048]{1,0:T(8,128)S(1)} %get-tuple-element.126.q.refs_4_, bf16[400,512]{1,0:T(8,128)(2,1)S(1)} %add.83.nfull, bf16[400,512]{1,0:T(8,128)(2,1)S(1)} %collective-permute-done.4.nother), custom_call_target="tpu_custom_call" | custom-call | flops 40000000 | tf_op jit(solution)/shard_map/pallas_call | solution.py:519
  43.9 5.9 %shard_map.132 = (f32[1,128]{1,0:T(1,128)S(1)}, f32[1,2048]{1,0:T(1,128)S(1)}, bf16[1024,2048]{1,0:T(8,128)(2,1)S(1)}, f32[200,1024]{1,0:T(8,128)S(1)}, f32[200,1024]{1,0:T(8,128)S(1)}) custom-call(s32[1]{0:T(128)} %bitcast.core_ref.refs_0_, f32[1,2048]{1,0:T(1,128)S(1)} %get-tuple-element.241.w, f32[400,2048]{1,0:T(8,128)S(1)} %get-tuple-element.126.q.refs_4_, ...), custom_call_target="tpu_custom_call" | custom-call | flops 40000000 | tf_op jit(solution)/shard_map/pallas_call | solution.py:519
  53.1 11.5 %shard_map.133 = (f32[8192,128]{1,0:T(8,128)S(1)}, f32[200,1408]{1,0:T(8,128)S(1)}, f32[200,1408]{1,0:T(8,128)S(1)}) custom-call(s32[1]{0:T(128)} %bitcast.core_ref.refs_0_, s32[2048]{0:T(1024)S(1)} %bitcast.63, bf16[1024,2048]{1,0:T(8,128)(2,1)S(1)} %get-tuple-element.136.ds, f32[1,2048]{1,0:T(1,128)S(1)} %get-tuple-element.137.dp.refs_3_, ...), custom_call_target="tpu_custom_call" | custom-call | flops 60000000 | tf_op jit(solution)/shard_map/pallas_call | solution.py:519
  67.7 13.3 %shard_map.134.refs_5_ = f32[32800,128]{1,0:T(8,128)S(1)} custom-call(s32[2048]{0:T(1024)S(1)} %bitcast.57, s32[2048]{0:T(1024)S(1)} %bitcast.55, f32[8192,128]{1,0:T(8,128)S(1)} %get-tuple-element.142.refs_2_, f32[1,2048]{1,0:T(1,128)S(1)} %get-tuple-element.137.dp.refs_3_, f32[400,2048]{1,0:T(8,128)S(1)} %get-tuple-element.126.q.refs_4_), custom_call_target="tpu_custom_call" | custom-call | flops 75000000 | tf_op jit(solution)/shard_map/pallas_call | solution.py:519
  81.0 4.6 %collective-permute-done.6 = f32[200,1024]{1,0:T(8,128)S(1)} collective-permute-done((f32[200,1024]{1,0:T(8,128)}, f32[200,1024]{1,0:T(8,128)S(1)}, u32[]{:S(2)}, u32[]{:S(2)}) %collective-permute-start.6) | collective-permute-done | bytes 819232 | tf_op jit(solution)/shard_map/ppermute | solution.py:471
  89.2 15.1 %shard_map.135 = (f32[32800,128]{1,0:T(8,128)S(1)}, f32[32800,128]{1,0:T(8,128)S(1)}, f32[64,128]{1,0:T(8,128)S(1)}, bf16[400,512]{1,0:T(8,128)(2,1)S(1)}, bf16[400,512]{1,0:T(8,128)(2,1)S(1)}) custom-call(s32[1]{0:T(128)} %bitcast.core_ref.refs_0_, s32[1024]{0:T(1024)S(1)} %bitcast.67, ...), custom_call_target="tpu_custom_call", output_to_operand_aliasing={{0}: (5, {}), {1}: (3, {}), {2}: (4, {})} | custom-call | flops 150000000 | tf_op jit(solution)/shard_map/pallas_call | solution.py:519
  106.2 4.0 shard_map.136
  110.5 4.2 shard_map.137.refs_2_.hb
  117.7 5.7 %shard_map.138 = (f32[400,2048]{1,0:T(8,128)S(1)}, f32[400,2048]{1,0:T(8,128)S(1)}, f32[5632,128]{1,0:T(8,128)S(1)}, f32[400,1408]{1,0:T(8,128)S(1)}, f32[1,1408]{1,0:T(1,128)S(1)}) custom-call(s32[1]{0:T(128)} %bitcast.core_ref.refs_0_, s32[2048]{0:T(1024)S(1)} %bitcast.60, bf16[400,2048]{1,0:T(8,128)(2,1)S(1)} %shard_map.137.refs_2_.hb, ...), custom_call_target="tpu_custom_call" | custom-call | flops 50000000 | tf_op jit(solution)/shard_map/pallas_call | solution.py:519
  125.0 15.5 %collective-permute-done.10 = bf16[400,512]{1,0:T(8,128)(2,1)S(1)} collective-permute-done((bf16[400,512]{1,0:T(8,128)(2,1)S(1)}, bf16[400,512]{1,0:T(8,128)(2,1)S(1)}, u32[]{:S(2)}, u32[]{:S(2)}) %collective-permute-start.10) | collective-permute-done | bytes 409632 | tf_op jit(solution)/shard_map/ppermute | solution.py:471
  142.3 5.4 %shard_map.139 = (f32[1000,2048]{1,0:T(8,128)S(1)}, f32[1,2048]{1,0:T(1,128)S(1)}, f32[1,2048]{1,0:T(1,128)S(1)}) custom-call(s32[1]{0:T(128)} %bitcast.core_ref.refs_0_, f32[400,2048]{1,0:T(8,128)S(1)} %get-tuple-element.157.q, bf16[400,512]{1,0:T(8,128)(2,1)S(1)} %add.89.nfull, bf16[400,512]{1,0:T(8,128)(2,1)S(1)} %collective-permute-done.13.nother), custom_call_target="tpu_custom_call" | custom-call | flops 40000000 | tf_op jit(solution)/shard_map/pallas_call | solution.py:519
  147.7 5.9 %shard_map.140 = (f32[1,128]{1,0:T(1,128)S(1)}, f32[1,2048]{1,0:T(1,128)S(1)}, bf16[1024,2048]{1,0:T(8,128)(2,1)S(1)}, f32[200,1024]{1,0:T(8,128)S(1)}, f32[200,1024]{1,0:T(8,128)S(1)}) custom-call(s32[1]{0:T(128)} %bitcast.core_ref.refs_0_, f32[1,2048]{1,0:T(1,128)S(1)} %get-tuple-element.240.w, f32[400,2048]{1,0:T(8,128)S(1)} %get-tuple-element.157.q, ...), custom_call_target="tpu_custom_call" | custom-call | flops 40000000 | tf_op jit(solution)/shard_map/pallas_call | solution.py:519
  157.0 11.5 %shard_map.141 = (f32[8192,128]{1,0:T(8,128)S(1)}, f32[200,1408]{1,0:T(8,128)S(1)}, f32[200,1408]{1,0:T(8,128)S(1)}) custom-call(s32[1]{0:T(128)} %bitcast.core_ref.refs_0_, s32[2048]{0:T(1024)S(1)} %bitcast.61, bf16[1024,2048]{1,0:T(8,128)(2,1)S(1)} %get-tuple-element.170.ds, f32[1,2048]{1,0:T(1,128)S(1)} %get-tuple-element.171.dp, ...), custom_call_target="tpu_custom_call" | custom-call | flops 60000000 | tf_op jit(solution)/shard_map/pallas_call | solution.py:519
  173.5 18.5 %collective-permute-done.18.refs_4_ = f32[1,2048]{1,0:T(1,128)S(1)} collective-permute-done((f32[1,2048]{1,0:T(1,128)S(1)}, f32[1,2048]{1,0:T(1,128)S(1)}, u32[]{:S(2)}, u32[]{:S(2)}) %collective-permute-start.18) | collective-permute-done | bytes 8224 | tf_op jit(solution)/shard_map/ppermute | solution.py:471
  196.8 16.4 %shard_map.142.refs_5_ = f32[32800,128]{1,0:T(8,128)S(1)} custom-call(s32[2048]{0:T(1024)S(1)} %bitcast.53, s32[2048]{0:T(1024)S(1)} %bitcast.51, s32[2048]{0:T(1024)S(1)} %bitcast.71, f32[8192,128]{1,0:T(8,128)S(1)} %copy-done.5, f32[1,2048]{1,0:T(1,128)S(1)} %collective-permute-done.18.refs_4_, bf16[400,2048]{1,0:T(8,128)(2,1)S(1)} %copy-done.13, ...), custom_call_target="tpu_custom_call" | custom-call | flops 75000000 | tf_op jit(solution)/shard_map/pallas_call | solution.py:519
  216.8 15.1 %shard_map.143 = (f32[32800,128]{1,0:T(8,128)S(1)}, f32[32800,128]{1,0:T(8,128)S(1)}, f32[64,128]{1,0:T(8,128)S(1)}, bf16[400,512]{1,0:T(8,128)(2,1)S(1)}, bf16[400,512]{1,0:T(8,128)(2,1)S(1)}) custom-call(s32[1]{0:T(128)} %bitcast.core_ref.refs_0_, s32[1024]{0:T(1024)S(1)} %bitcast.69, ...), custom_call_target="tpu_custom_call", output_to_operand_aliasing={{0}: (5, {}), {1}: (3, {}), {2}: (4, {})} | custom-call | flops 150000000 | tf_op jit(solution)/shard_map/pallas_call | solution.py:519
  233.7 4.0 shard_map.144
  245.3 5.9 %shard_map.146 = (f32[400,2048]{1,0:T(8,128)S(1)}, f32[400,2048]{1,0:T(8,128)S(1)}, f32[5632,128]{1,0:T(8,128)S(1)}, f32[400,1408]{1,0:T(8,128)S(1)}, f32[1,1408]{1,0:T(1,128)S(1)}) custom-call(s32[1]{0:T(128)} %bitcast.core_ref.refs_0_, s32[2048]{0:T(1024)S(1)} %bitcast.58, bf16[400,2048]{1,0:T(8,128)(2,1)S(1)} %shard_map.145.refs_2_.hb, ...), custom_call_target="tpu_custom_call" | custom-call | flops 50000000 | tf_op jit(solution)/shard_map/pallas_call | solution.py:519
  251.3 34.3 %collective-permute-done.22 = bf16[400,512]{1,0:T(8,128)(2,1)S(1)} collective-permute-done((bf16[400,512]{1,0:T(8,128)(2,1)S(1)}, bf16[400,512]{1,0:T(8,128)(2,1)S(1)}, u32[]{:S(2)}, u32[]{:S(2)}) %collective-permute-start.22) | collective-permute-done | bytes 409632 | tf_op jit(solution)/shard_map/ppermute | solution.py:471
  287.4 5.4 %shard_map.147 = (f32[1000,2048]{1,0:T(8,128)S(1)}, f32[1,2048]{1,0:T(1,128)S(1)}, f32[1,2048]{1,0:T(1,128)S(1)}) custom-call(s32[1]{0:T(128)} %bitcast.core_ref.refs_0_, f32[400,2048]{1,0:T(8,128)S(1)} %get-tuple-element.195.q, bf16[400,512]{1,0:T(8,128)(2,1)S(1)} %add.95.nfull, bf16[400,512]{1,0:T(8,128)(2,1)S(1)} %collective-permute-done.25.nother), custom_call_target="tpu_custom_call" | custom-call | flops 40000000 | tf_op jit(solution)/shard_map/pallas_call | solution.py:519
  292.8 5.9 %shard_map.148 = (f32[1,128]{1,0:T(1,128)S(1)}, f32[1,2048]{1,0:T(1,128)S(1)}, bf16[1024,2048]{1,0:T(8,128)(2,1)S(1)}, f32[200,1024]{1,0:T(8,128)S(1)}, f32[200,1024]{1,0:T(8,128)S(1)}) custom-call(s32[1]{0:T(128)} %bitcast.core_ref.refs_0_, f32[1,2048]{1,0:T(1,128)S(1)} %get-tuple-element.239.w, f32[400,2048]{1,0:T(8,128)S(1)} %get-tuple-element.195.q, ...), custom_call_target="tpu_custom_call" | custom-call | flops 40000000 | tf_op jit(solution)/shard_map/pallas_call | solution.py:519
  301.2 11.5 %shard_map.149 = (f32[8192,128]{1,0:T(8,128)S(1)}, f32[200,1408]{1,0:T(8,128)S(1)}, f32[200,1408]{1,0:T(8,128)S(1)}) custom-call(s32[1]{0:T(128)} %bitcast.core_ref.refs_0_, s32[2048]{0:T(1024)S(1)} %bitcast.59, bf16[1024,2048]{1,0:T(8,128)(2,1)S(1)} %get-tuple-element.208.ds, f32[1,2048]{1,0:T(1,128)S(1)} %get-tuple-element.209.dp, ...), custom_call_target="tpu_custom_call" | custom-call | flops 60000000 | tf_op jit(solution)/shard_map/pallas_call | solution.py:519
  317.8 58.0 %collective-permute-done.33 = f32[200,1408]{1,0:T(8,128)S(1)} collective-permute-done((f32[200,1408]{1,0:T(8,128)S(1)}, f32[200,1408]{1,0:T(8,128)S(1)}, u32[]{:S(2)}, u32[]{:S(2)}) %collective-permute-start.33) | collective-permute-done | bytes 1126432 | tf_op jit(solution)/shard_map/ppermute | solution.py:471
  377.4 15.5 %collective-permute-done.30.refs_4_ = f32[1,2048]{1,0:T(1,128)S(1)} collective-permute-done((f32[1,2048]{1,0:T(1,128)S(1)}, f32[1,2048]{1,0:T(1,128)S(1)}, u32[]{:S(2)}, u32[]{:S(2)}) %collective-permute-start.30) | collective-permute-done | bytes 8224 | tf_op jit(solution)/shard_map/ppermute | solution.py:471
  392.9 16.4 %shard_map.150.refs_4_ = f32[32800,128]{1,0:T(8,128)S(1)} custom-call(s32[2048]{0:T(1024)S(1)} %bitcast.49, s32[2048]{0:T(1024)S(1)} %bitcast.47, s32[2048]{0:T(1024)S(1)} %bitcast.70, f32[8192,128]{1,0:T(8,128)S(1)} %get-tuple-element.215.refs_3_, f32[1,2048]{1,0:T(1,128)S(1)} %collective-permute-done.30.refs_4_, ...), custom_call_target="tpu_custom_call" | custom-call | flops 75000000 | tf_op jit(solution)/shard_map/pallas_call | solution.py:519
  409.3 5.8 %copy-done.2 = f32[32800,128]{1,0:T(8,128)} copy-done((f32[32800,128]{1,0:T(8,128)}, f32[32800,128]{1,0:T(8,128)S(1)}, u32[]{:S(2)}) %copy-start.2) | copy-done | bytes 16793624
  417.6 5.8 %copy-done.1 = f32[32800,128]{1,0:T(8,128)S(1)} copy-done((f32[32800,128]{1,0:T(8,128)S(1)}, f32[32800,128]{1,0:T(8,128)}, u32[]{:S(2)}) %copy-start.1) | copy-done | bytes 16793624
  423.4 5.8 %copy-done.3 = f32[32800,128]{1,0:T(8,128)S(1)} copy-done((f32[32800,128]{1,0:T(8,128)S(1)}, f32[32800,128]{1,0:T(8,128)}, u32[]{:S(2)}) %copy-start.3) | copy-done | bytes 16793624
  429.2 17.1 %shard_map.151 = (f32[32800,128]{1,0:T(8,128)S(1)}, f32[400,8192]{1,0:T(8,128)}, f32[64,128]{1,0:T(8,128)}) custom-call(s32[1]{0:T(128)} %bitcast.core_ref.refs_0_, s32[1024]{0:T(1024)S(1)} %bitcast.65, f32[32800,128]{1,0:T(8,128)S(1)} %copy-done.1, f32[64,128]{1,0:T(8,128)S(1)} %get-tuple-element.187.refs_3_, ...), custom_call_target="tpu_custom_call", output_to_operand_aliasing={{0}: (4, {})} | custom-call | flops 150000000 | tf_op jit(solution)/shard_map/pallas_call | solution.py:519
  (140 shorter events, 76.8 us)
Async XLA Ops:
  12.1 5.7 %collective-permute-start = (bf16[400,512]{1,0:T(8,128)(2,1)S(1)}, bf16[400,512]{1,0:T(8,128)(2,1)S(1)}, u32[]{:S(2)}, u32[]{:S(2)}) collective-permute-start(bf16[400,512]{1,0:T(8,128)(2,1)S(1)} %get-tuple-element.117), channel_id=1, source_target_pairs={{0,1},{1,0},{2,3},{3,2},{4,5},{5,4},{6,7},{7,6}} | collective-permute-start | bytes 1228808 | tf_op jit(solution)/shard_map/ppermute | solution.py:468
  13.1 4.0 collective-permute-start.1
  13.1 4.7 %collective-permute-start.2 = (s32[2,2048]{1,0:T(2,128)S(1)}, s32[2,2048]{1,0:T(2,128)S(1)}, u32[]{:S(2)}, u32[]{:S(2)}) collective-permute-start(s32[2,2048]{1,0:T(2,128)S(1)} %pad_add_fusion.1), channel_id=1, source_target_pairs={{0,2},{1,3},{2,0},{3,1},{4,6},{5,7},{6,4},{7,5}} | collective-permute-start | bytes 49160 | tf_op jit(solution)/shard_map/ppermute | solution.py:471
  18.0 11.9 %collective-permute-start.3 = (bf16[400,512]{1,0:T(8,128)(2,1)S(1)}, bf16[400,512]{1,0:T(8,128)(2,1)S(1)}, u32[]{:S(2)}, u32[]{:S(2)}) collective-permute-start(bf16[400,512]{1,0:T(8,128)(2,1)S(1)} %add.82), channel_id=1, source_target_pairs={{0,2},{1,3},{2,0},{3,1},{4,6},{5,7},{6,4},{7,5}} | collective-permute-start | bytes 1228808 | tf_op jit(solution)/shard_map/ppermute | solution.py:471
  36.8 1.8 collective-permute-start.4
  49.8 2.4 collective-permute-start.5
  64.7 2.8 collective-permute-start.7
  64.9 20.7 %collective-permute-start.6 = (f32[200,1024]{1,0:T(8,128)}, f32[200,1024]{1,0:T(8,128)S(1)}, u32[]{:S(2)}, u32[]{:S(2)}) collective-permute-start(f32[200,1024]{1,0:T(8,128)} %add.84), channel_id=1, source_target_pairs={{0,2},{1,3},{2,0},{3,1},{4,6},{5,7},{6,4},{7,5}} | collective-permute-start | bytes 2457608 | tf_op jit(solution)/shard_map/ppermute | solution.py:471
  86.9 2.4 collective-permute-start.8
  86.9 27.9 %collective-permute-start.11 = (f32[200,1408]{1,0:T(8,128)S(1)}, f32[200,1408]{1,0:T(8,128)S(1)}, u32[]{:S(2)}, u32[]{:S(2)}) collective-permute-start(f32[200,1408]{1,0:T(8,128)S(1)} %add.85), channel_id=1, source_target_pairs={{0,2},{1,3},{2,0},{3,1},{4,6},{5,7},{6,4},{7,5}} | collective-permute-start | bytes 3379208 | tf_op jit(solution)/shard_map/ppermute | solution.py:471
  104.3 1.8 collective-permute-start.9
  110.2 37.5 %collective-permute-start.14 = (bf16[400,2048]{1,0:T(8,128)(2,1)S(1)}, bf16[400,2048]{1,0:T(8,128)(2,1)S(1)}, u32[]{:S(2)}, u32[]{:S(2)}) collective-permute-start(bf16[400,2048]{1,0:T(8,128)(2,1)S(1)} %shard_map.136), channel_id=1, source_target_pairs={{0,3},{1,0},{2,1},{3,2},{4,7},{5,4},{6,5},{7,6}} | collective-permute-start | bytes 4915208 | tf_op jit(solution)/shard_map/ppermute | solution.py:471
  114.9 2.8 collective-permute-start.12
  115.1 25.3 %collective-permute-start.10 = (bf16[400,512]{1,0:T(8,128)(2,1)S(1)}, bf16[400,512]{1,0:T(8,128)(2,1)S(1)}, u32[]{:S(2)}, u32[]{:S(2)}) collective-permute-start(bf16[400,512]{1,0:T(8,128)(2,1)S(1)} %add.87), channel_id=1, source_target_pairs={{0,2},{1,3},{2,0},{3,1},{4,6},{5,7},{6,4},{7,5}} | collective-permute-start | bytes 1228808 | tf_op jit(solution)/shard_map/ppermute | solution.py:471
  153.6 2.4 collective-permute-start.15
  153.8 38.2 %collective-permute-start.19 = (bf16[400,2048]{1,0:T(8,128)(2,1)S(1)}, bf16[400,2048]{1,0:T(8,128)(2,1)S(1)}, u32[]{:S(2)}, u32[]{:S(2)}) collective-permute-start(bf16[400,2048]{1,0:T(8,128)(2,1)S(1)} %shard_map.137.refs_2_.hb), channel_id=1, source_target_pairs={{0,1},{1,2},{2,3},{3,0},{4,5},{5,6},{6,7},{7,4}} | collective-permute-start | bytes 4915208 | tf_op jit(solution)/shard_map/ppermute | solution.py:471
  170.5 2.8 collective-permute-start.17
  170.7 42.5 %collective-permute-start.16 = (f32[200,1024]{1,0:T(8,128)}, f32[200,1024]{1,0:T(8,128)S(1)}, u32[]{:S(2)}, u32[]{:S(2)}) collective-permute-start(f32[200,1024]{1,0:T(8,128)} %add.90), channel_id=1, source_target_pairs={{0,2},{1,3},{2,0},{3,1},{4,6},{5,7},{6,4},{7,5}} | collective-permute-start | bytes 2457608 | tf_op jit(solution)/shard_map/ppermute | solution.py:471
  171.3 20.7 %collective-permute-start.18 = (f32[1,2048]{1,0:T(1,128)S(1)}, f32[1,2048]{1,0:T(1,128)S(1)}, u32[]{:S(2)}, u32[]{:S(2)}) collective-permute-start(f32[1,2048]{1,0:T(1,128)S(1)} %get-tuple-element.171.dp), channel_id=1, source_target_pairs={{0,1},{1,2},{2,3},{3,0},{4,5},{5,6},{6,7},{7,4}} | collective-permute-start | bytes 24584 | tf_op jit(solution)/shard_map/ppermute | solution.py:471
  214.4 2.4 collective-permute-start.20
  214.5 27.9 %collective-permute-start.23 = (f32[200,1408]{1,0:T(8,128)S(1)}, f32[200,1408]{1,0:T(8,128)S(1)}, u32[]{:S(2)}, u32[]{:S(2)}) collective-permute-start(f32[200,1408]{1,0:T(8,128)S(1)} %add.91), channel_id=1, source_target_pairs={{0,2},{1,3},{2,0},{3,1},{4,6},{5,7},{6,4},{7,5}} | collective-permute-start | bytes 3379208 | tf_op jit(solution)/shard_map/ppermute | solution.py:471
  237.8 55.1 %collective-permute-start.26 = (bf16[400,2048]{1,0:T(8,128)(2,1)S(1)}, bf16[400,2048]{1,0:T(8,128)(2,1)S(1)}, u32[]{:S(2)}, u32[]{:S(2)}) collective-permute-start(bf16[400,2048]{1,0:T(8,128)(2,1)S(1)} %shard_map.144), channel_id=1, source_target_pairs={{0,2},{1,3},{2,0},{3,1},{4,6},{5,7},{6,4},{7,5}} | collective-permute-start | bytes 4915208 | tf_op jit(solution)/shard_map/ppermute | solution.py:471
  242.5 2.8 collective-permute-start.24
  242.6 43.0 %collective-permute-start.22 = (bf16[400,512]{1,0:T(8,128)(2,1)S(1)}, bf16[400,512]{1,0:T(8,128)(2,1)S(1)}, u32[]{:S(2)}, u32[]{:S(2)}) collective-permute-start(bf16[400,512]{1,0:T(8,128)(2,1)S(1)} %add.93), channel_id=1, source_target_pairs={{0,2},{1,3},{2,0},{3,1},{4,6},{5,7},{6,4},{7,5}} | collective-permute-start | bytes 1228808 | tf_op jit(solution)/shard_map/ppermute | solution.py:471
  298.8 2.4 collective-permute-start.27
  312.8 2.8 collective-permute-start.29
  312.9 80.0 %collective-permute-start.31 = (bf16[400,2048]{1,0:T(8,128)(2,1)S(1)}, bf16[400,2048]{1,0:T(8,128)(2,1)S(1)}, u32[]{:S(2)}, u32[]{:S(2)}) collective-permute-start(bf16[400,2048]{1,0:T(8,128)(2,1)S(1)} %shard_map.145.refs_2_.hb), channel_id=1, source_target_pairs={{0,2},{1,3},{2,0},{3,1},{4,6},{5,7},{6,4},{7,5}} | collective-permute-start | bytes 4915208 | tf_op jit(solution)/shard_map/ppermute | solution.py:471
  315.7 60.0 %collective-permute-start.33 = (f32[200,1408]{1,0:T(8,128)S(1)}, f32[200,1408]{1,0:T(8,128)S(1)}, u32[]{:S(2)}, u32[]{:S(2)}) collective-permute-start(f32[200,1408]{1,0:T(8,128)S(1)} %add.97), channel_id=1, source_target_pairs={{0,2},{1,3},{2,0},{3,1},{4,6},{5,7},{6,4},{7,5}} | collective-permute-start | bytes 3379208 | tf_op jit(solution)/shard_map/ppermute | solution.py:471
  316.3 98.7 %collective-permute-start.28 = (f32[200,1024]{1,0:T(8,128)S(1)}, f32[200,1024]{1,0:T(8,128)S(1)}, u32[]{:S(2)}, u32[]{:S(2)}) collective-permute-start(f32[200,1024]{1,0:T(8,128)S(1)} %add.96), channel_id=1, source_target_pairs={{0,2},{1,3},{2,0},{3,1},{4,6},{5,7},{6,4},{7,5}} | collective-permute-start | bytes 2457608 | tf_op jit(solution)/shard_map/ppermute | solution.py:471
  376.9 69.5 %collective-permute-start.34 = (f32[200,1408]{1,0:T(8,128)}, f32[200,1408]{1,0:T(8,128)}, u32[]{:S(2)}, u32[]{:S(2)}) collective-permute-start(f32[200,1408]{1,0:T(8,128)} %add.99), channel_id=1, source_target_pairs={{0,1},{1,0},{2,3},{3,2},{4,5},{5,4},{6,7},{7,6}} | collective-permute-start | bytes 3379208 | tf_op jit(solution)/shard_map/ppermute | solution.py:478
  376.9 16.0 %collective-permute-start.30 = (f32[1,2048]{1,0:T(1,128)S(1)}, f32[1,2048]{1,0:T(1,128)S(1)}, u32[]{:S(2)}, u32[]{:S(2)}) collective-permute-start(f32[1,2048]{1,0:T(1,128)S(1)} %get-tuple-element.209.dp), channel_id=1, source_target_pairs={{0,2},{1,3},{2,0},{3,1},{4,6},{5,7},{6,4},{7,5}} | collective-permute-start | bytes 24584 | tf_op jit(solution)/shard_map/ppermute | solution.py:471
  415.1 2.5 collective-permute-start.32
  (23 other events, 157.3 us)

commit v7 on v6

--- a/solution.py
+++ b/solution.py
@@ -50,10 +50,11 @@
 def batch_sums(acc, ids, base, rows, row_base):
     index = [ids[base + k] for k in range(BATCH)]
     grads = [rows[pl.ds(four(row_base + SLICES * k), SLICES), :] for k in range(BATCH)]
-    total = [acc[pl.ds(four(index[k]), SLICES), :] + grads[k] for k in range(BATCH)]
-    for k in range(1, BATCH):
-        for earlier in range(k):
-            total[k] = total[k] + jnp.where(index[earlier] == index[k], grads[earlier], 0.0)
+    total = []
+    for k in range(BATCH):
+        repeats = [jnp.where(index[earlier] == index[k], grads[earlier], 0.0) for earlier in range(k)]
+        total.append(functools.reduce(jnp.add, repeats, grads[k]))
+    total = [acc[pl.ds(four(index[k]), SLICES), :] + total[k] for k in range(BATCH)]
     return index, total
 
 
@@ -152,9 +153,9 @@
 
 def query_kernel(dim, edges, first, *refs):
     if first:
-        core_ref, rel, hb, rfm, q_out, r_out, r4, stage, fm = refs
+        core_ref, rel, hb, rfm, q_out, r_out, stage, fm, r4 = refs
     else:
-        core_ref, rel, hb, rfm_in, vr_in, rmine, rother, q_out, r_out, r4, rfm, vr, stage, fm = refs
+        core_ref, rel, hb, rfm_in, vr_in, rmine, rother, q_out, r_out, r4_out, rfm, vr, stage, fm, r4, out_sem = refs
         core = core_ref[0]
     half = dim // 2
     relp = rfm.shape[1]
@@ -188,7 +189,13 @@
         q_out[pl.ds(half, half), cols] = h[:half] * r_im + h[half:] * r_re
         return 0
 
-    lax.fori_loop(0, edges // LANES, step, 0)
+    step(0, 0)
+    if not first:
+        save = pltpu.make_async_copy(r4, r4_out, out_sem)
+        save.start()
+    lax.fori_loop(1, edges // LANES, step, 0)
+    if not first:
+        save.wait()
 
 
 def place_negs(core, nb, nfull, nother):
@@ -307,7 +314,10 @@
     if own:
         heads, tails, hg, dp, q, acc, stage, rows, rt = refs
     else:
-        heads, tails, rel, hg, dp, hb_in, r4, acc, stage, rows, rt = refs
+        heads, tails, rel, hg, dp, hb_hbm, r4_hbm, acc, stage, rows, rt, hb_in, r4, in_sem = refs
+        loads = [pltpu.make_async_copy(hb_hbm, hb_in, in_sem.at[0]), pltpu.make_async_copy(r4_hbm, r4, in_sem.at[1])]
+        for load in loads:
+            load.start()
     half = dim // 2
     blocks = edges // LANES
     zero_rows(acc)
@@ -328,6 +338,9 @@
             rt[1, pl.ds(half, half), :] = scale * (h[:half] * r_im + h[half:] * r_re)
         unstage(rt.at[1], rows.at[slot])
 
+    if not own:
+        for load in loads:
+            load.wait()
     compute(0, 0)
 
     def step(i, _):
@@ -492,10 +505,6 @@
         own_tails = [tail_idx[0, s] * SLICES for s in range(rounds)]
         own_rels = [rel_idx[0, s] * SLICES for s in range(rounds)]
         tails, rels = [own_tails[0]], [own_rels[0]]
-        for s in range(1, rounds):
-            got = send(jnp.stack([own_tails[s], own_rels[s]]), shift(s))
-            tails.append(got[0])
-            rels.append(got[1])
         owned = (neg_idx // rows) == my_dev
         neg_local = jnp.where(owned, neg_idx % rows, rows) * SLICES
         neg_local = jnp.pad(neg_local, ((0, 0), (0, negp - neg_count)), constant_values=rows * SLICES)
@@ -513,9 +522,9 @@
             places = {'s': smem, 'h': hbm, 'v': vmem, 'V': vmem}
             windows = [a for a, k in zip(list(args) + outs, kinds + out_kinds) if k == 'v']
             limit = (4 if name == 'grad' else 3) * 2 ** 20 + sum(padded_bytes(a.shape, a.dtype) for a in windows)
-            limit += sum(padded_bytes(a.shape, a.dtype) for a in scratch if a.memory_space == pltpu.VMEM)
-            args = [pltpu.with_memory_space_constraint(a, pltpu.VMEM) if k == 'V' else a for a, k in zip(args, kinds)]
-            outs = [pltpu.VMEM(o.shape, o.dtype) if k == 'V' else o for o, k in zip(outs, out_kinds)]
+            limit += sum(padded_bytes(a.shape, a.dtype) for a in scratch if getattr(a, 'memory_space', None) == pltpu.VMEM)
+            args = [pltpu.with_memory_space_constraint(a, pltpu.VMEM if k == 'V' else pltpu.HBM) if k in 'Vh' else a for a, k in zip(args, kinds)]
+            outs = [{'V': pltpu.VMEM, 'h': pltpu.HBM}[k](o.shape, o.dtype) if k in 'Vh' else o for o, k in zip(outs, out_kinds)]
             return pl.pallas_call(
                 kernel, out_shape=outs, in_specs=[places[k]() for k in kinds], out_specs=[places[k]() for k in out_kinds],
                 scratch_shapes=scratch, compiler_params=pltpu.CompilerParams(vmem_limit_bytes=limit),
@@ -526,7 +535,7 @@
                         [cols_bf] * len(lists), 'V' * len(lists), [stage_shape], 1 + 5 * len(lists), 'gather')
 
         t4, nk, ns = call(
-            functools.partial(entry_kernel, dim, rows), [core, negs[0], pltpu.with_memory_space_constraint(ent_emb.T, pltpu.HBM)], 'ssh',
+            functools.partial(entry_kernel, dim, rows), [core, negs[0], ent_emb.T], 'ssh',
             [table_out, neg_half, neg_half], 'VVV',
             [pltpu.VMEM((4, SLICES * LANES, 4 * LANES), F32), stage_shape, pltpu.VMEM((dim, negp), BF16), pltpu.SemaphoreType.DMA((4,))], 20, 'entry')
         v = ent_ada.reshape(rows // LANES, LANES)
@@ -539,10 +548,14 @@
             first, last = s == 0, s == rounds - 1
             neg_part = chip_sum(nk, ns)
             if first:
-                neg_part, t4, tails, rels = tie((neg_part, t4, tails, rels))
+                neg_part, t4 = tie((neg_part, t4))
                 neg_got = link(neg_part)
                 tail_cols, hb = gather([tails[0], heads[0]], t4)
-                head_cols = hb
+                hb, own_tails, own_rels = tie((hb, own_tails, own_rels))
+                for later in range(1, rounds):
+                    got = send(jnp.stack([own_tails[later], own_rels[later]]), shift(later))
+                    tails.append(got[0])
+                    rels.append(got[1])
                 neg_got, hb = tie((neg_got, hb))
             else:
                 neg_part, t4 = tie((neg_part, t4))
@@ -554,20 +567,23 @@
                 rel_got, hb = tie((rel_got, hb))
                 rel_grads = finish(rel_part, rel_got)
             wide = shape((dim, edges))
-            outs, out_kinds = [wide, wide, shape((relp * SLICES, LANES))], 'VVV'
+            outs, out_kinds = [wide, wide], 'VV'
+            rel_rows = pltpu.VMEM((relp * SLICES, LANES), F32)
+            scratch = [stage_shape, pltpu.VMEM((SLICES * LANES, relp), F32), rel_rows]
             args, kinds = [core, own_rels[s], hb, rfm], 'ssV' + ('v' if first else 'V')
             if not first:
-                outs += [shape((dim, relp)), shape((1, relp))]
-                out_kinds += 'Vv'
+                outs += [shape((relp * SLICES, LANES)), shape((dim, relp)), shape((1, relp))]
+                out_kinds += 'hVv'
+                scratch += [pltpu.SemaphoreType.DMA]
                 args += [vr] + list(rel_grads)
                 kinds += 'vVV'
             res = call(functools.partial(query_kernel, dim, edges, first), args, kinds, outs, out_kinds,
-                       [stage_shape, pltpu.VMEM((SLICES * LANES, relp), F32)], 10, 'query')
-            q, r, r4 = res[:3]
+                       scratch, 10, 'query')
+            q, r = res[:2]
             neg_got, q = tie((neg_got, q))
             nmine, nother = finish(neg_part, neg_got)
             if not first:
-                rfm, vr = res[3:]
+                r4, rfm, vr = res[2:]
             e, neg_top, neg_total = call(
                 functools.partial(exp_kernel, neg_count, edges), [core, q, nmine, nother], 'sVVV',
                 [shape((neg_count, edges)), shape((1, edges)), shape((1, edges))], 'Vvv',
@@ -594,12 +610,13 @@
             rel_part = chip_sum(rk, rs)
             rel_part, hg = tie((rel_part, hg))
             rel_got = link(rel_part)
+            scratch = [stage_shape] + [pltpu.VMEM((2, SLICES * LANES, LANES), F32)] * 2
             if first:
                 args, kinds = [heads[s], tails[s], hg, dp, q], 'ssVvV'
             else:
-                args, kinds = [heads[s], tails[s], rels[s], hg, dp_away, head_cols, r4], 'sssVvVV'
-            acc, = call(functools.partial(scatter_kernel, dim, edges, first), args, kinds, [table_out], 'V',
-                        [stage_shape] + [pltpu.VMEM((2, SLICES * LANES, LANES), F32)] * 2, 15, 'scatter')
+                args, kinds = [heads[s], tails[s], rels[s], hg, dp_away, head_cols, r4], 'sssVvhh'
+                scratch += [pltpu.VMEM((dim, edges), BF16), rel_rows, pltpu.SemaphoreType.DMA((2,))]
+            acc, = call(functools.partial(scatter_kernel, dim, edges, first), args, kinds, [table_out], 'V', scratch, 15, 'scatter')
             neg_got, acc = tie((neg_got, acc))
             gmine, gother = finish(neg_part, neg_got)
             scratch = [stage_shape, square_shape, pltpu.VMEM((2, 4, LANES, LANES) if last else (2, LANES, LANES), F32)]

time: 452 us -> 461 us (1.020)
  waiting for transfers between devices: 179 us -> 189 us
    ppermute x17, waiting for transfers between devices: 150 us -> 167 us  [send(): return lax.ppermute(value, 'ent', pairs)]
    unnamed x41 -> x33, local copies, waits for them, and re-layouts: 26.5 us -> 26.6 us
  transfers between devices with their start and end apart: 35 -> 35, of which waited for: 25 -> 24; matrix products, arithmetic and copies ran while one was open for 1% -> 1% of each run, Pallas kernels for 33% -> 32%
where the time goes in v7:
time: 461 us
  Pallas kernels  211 us (46%)
  waiting for transfers between devices  189 us (41%)
  local copies, waits for them, and re-layouts  27.4 us (6%)
  starting transfers between devices  18.9 us (4%)
  other arithmetic  13.1 us (3%)
    pallas_call x24, Pallas kernels, call(): pl.pallas_call(kernel, out_shape=outs, in_specs=[places[k]() for k in kin...  211 us
    ppermute x17, waiting for transfers between devices, send(): return lax.ppermute(value, 'ent', pairs)  167 us
    unnamed x33, local copies, waits for them, and re-layouts  26.6 us
    ppermute x17, starting transfers between devices, send(): return lax.ppermute(value, 'ent', pairs)  16 us
    ppermute x9, waiting for transfers between devices, chip_sum(): return keep + lax.ppermute(send, 'ent', swap)  12.1 us
    ppermute x9, waiting for transfers between devices, finish(): return (mine, lax.ppermute(mine, 'ent', swap))  9.25 us
  transfers between devices with their start and end apart: 35, of which 24 were waited for; matrix products, arithmetic and copies ran while one was open for 1% of the time, Pallas kernels for 32%

profile of v7, /device:TPU:0, one launch (start us, length us, event | category | flops | bytes accessed | tf_op | source)
XLA Modules:
  0.0 460.6 jit_solution(9314734663287121096)
XLA Ops:
  2.2 9.9 %shard_map.128 = (f32[32800,128]{1,0:T(8,128)S(1)}, bf16[400,512]{1,0:T(8,128)(2,1)S(1)}, bf16[400,512]{1,0:T(8,128)(2,1)S(1)}) custom-call(s32[1]{0:T(128)} %bitcast.core_ref.refs_0_, s32[1024]{0:T(1024)S(1)} %bitcast.66, f32[400,8192]{1,0:T(8,128)} %bitcast.75), custom_call_target="tpu_custom_call" | custom-call | flops 100000000 | tf_op jit(solution)/shard_map/pallas_call | solution.py:528
  17.3 7.5 %shard_map.129 = (bf16[400,2048]{1,0:T(8,128)(2,1)S(1)}, bf16[400,2048]{1,0:T(8,128)(2,1)S(1)}) custom-call(s32[2048]{0:T(1024)S(1)} %bitcast.58, s32[2048]{0:T(1024)S(1)} %bitcast.60, f32[32800,128]{1,0:T(8,128)S(1)} %get-tuple-element.120.refs_2_.refs_3_), custom_call_target="tpu_custom_call" | custom-call | flops 55000000 | tf_op jit(solution)/shard_map/pallas_call | solution.py:528
  27.1 5.3 %shard_map.130 = (f32[400,2048]{1,0:T(8,128)S(1)}, f32[400,2048]{1,0:T(8,128)S(1)}) custom-call(s32[1]{0:T(128)} %bitcast.core_ref.refs_0_, s32[2048]{0:T(1024)S(1)} %bitcast.62, bf16[400,2048]{1,0:T(8,128)(2,1)S(1)} %get-tuple-element.126.refs_2_.hb, f32[400,1408]{1,0:T(8,128)S(1)} %pad.13.refs_3_), custom_call_target="tpu_custom_call" | custom-call | flops 50000000 | tf_op jit(solution)/shard_map/pallas_call | solution.py:528
  34.2 5.4 %shard_map.131 = (f32[1000,2048]{1,0:T(8,128)S(1)}, f32[1,2048]{1,0:T(1,128)S(1)}, f32[1,2048]{1,0:T(1,128)S(1)}) custom-call(s32[1]{0:T(128)} %bitcast.core_ref.refs_0_, f32[400,2048]{1,0:T(8,128)S(1)} %get-tuple-element.128.q.refs_4_, bf16[400,512]{1,0:T(8,128)(2,1)S(1)} %add.83.nfull, bf16[400,512]{1,0:T(8,128)(2,1)S(1)} %collective-permute-done.2.nother), custom_call_target="tpu_custom_call" | custom-call | flops 40000000 | tf_op jit(solution)/shard_map/pallas_call | solution.py:528
  39.6 5.9 %shard_map.132 = (f32[1,128]{1,0:T(1,128)S(1)}, f32[1,2048]{1,0:T(1,128)S(1)}, bf16[1024,2048]{1,0:T(8,128)(2,1)S(1)}, f32[200,1024]{1,0:T(8,128)S(1)}, f32[200,1024]{1,0:T(8,128)S(1)}) custom-call(s32[1]{0:T(128)} %bitcast.core_ref.refs_0_, f32[1,2048]{1,0:T(1,128)S(1)} %get-tuple-element.238.w, f32[400,2048]{1,0:T(8,128)S(1)} %get-tuple-element.128.q.refs_4_, ...), custom_call_target="tpu_custom_call" | custom-call | flops 40000000 | tf_op jit(solution)/shard_map/pallas_call | solution.py:528
  48.8 11.7 %shard_map.133 = (f32[8192,128]{1,0:T(8,128)S(1)}, f32[200,1408]{1,0:T(8,128)S(1)}, f32[200,1408]{1,0:T(8,128)S(1)}) custom-call(s32[1]{0:T(128)} %bitcast.core_ref.refs_0_, s32[2048]{0:T(1024)S(1)} %bitcast.63, bf16[1024,2048]{1,0:T(8,128)(2,1)S(1)} %get-tuple-element.138.ds, f32[1,2048]{1,0:T(1,128)S(1)} %get-tuple-element.139.dp.refs_3_, ...), custom_call_target="tpu_custom_call" | custom-call | flops 60000000 | tf_op jit(solution)/shard_map/pallas_call | solution.py:528
  63.5 12.6 %shard_map.134.refs_5_ = f32[32800,128]{1,0:T(8,128)S(1)} custom-call(s32[2048]{0:T(1024)S(1)} %bitcast.61, s32[2048]{0:T(1024)S(1)} %bitcast.59, f32[8192,128]{1,0:T(8,128)S(1)} %get-tuple-element.144.refs_2_, f32[1,2048]{1,0:T(1,128)S(1)} %get-tuple-element.139.dp.refs_3_, f32[400,2048]{1,0:T(8,128)S(1)} %get-tuple-element.128.q.refs_4_), custom_call_target="tpu_custom_call" | custom-call | flops 75000000 | tf_op jit(solution)/shard_map/pallas_call | solution.py:528
  76.0 5.4 %collective-permute-done.4 = f32[200,1024]{1,0:T(8,128)S(1)} collective-permute-done((f32[200,1024]{1,0:T(8,128)}, f32[200,1024]{1,0:T(8,128)S(1)}, u32[]{:S(2)}, u32[]{:S(2)}) %collective-permute-start.4) | collective-permute-done | bytes 819232 | tf_op jit(solution)/shard_map/ppermute | solution.py:484
  85.1 14.8 %shard_map.135 = (f32[32800,128]{1,0:T(8,128)S(1)}, f32[32800,128]{1,0:T(8,128)S(1)}, f32[64,128]{1,0:T(8,128)S(1)}, bf16[400,512]{1,0:T(8,128)(2,1)S(1)}, bf16[400,512]{1,0:T(8,128)(2,1)S(1)}) custom-call(s32[1]{0:T(128)} %bitcast.core_ref.refs_0_, s32[1024]{0:T(1024)S(1)} %bitcast.67, ...), custom_call_target="tpu_custom_call", output_to_operand_aliasing={{0}: (5, {}), {1}: (3, {}), {2}: (4, {})} | custom-call | flops 150000000 | tf_op jit(solution)/shard_map/pallas_call | solution.py:528
  100.1 9.8 %collective-permute-done.8 = s32[2,2048]{1,0:T(2,128)S(1)} collective-permute-done((s32[2,2048]{1,0:T(2,128)S(1)}, s32[2,2048]{1,0:T(2,128)S(1)}, u32[]{:S(2)}, u32[]{:S(2)}) %collective-permute-start.8) | collective-permute-done | bytes 16416 | tf_op jit(solution)/shard_map/ppermute | solution.py:484
  121.3 5.7 %shard_map.138 = (f32[400,2048]{1,0:T(8,128)S(1)}, f32[400,2048]{1,0:T(8,128)S(1)}, f32[5632,128]{1,0:T(8,128)}, f32[400,1408]{1,0:T(8,128)S(1)}, f32[1,1408]{1,0:T(1,128)S(1)}) custom-call(s32[1]{0:T(128)} %bitcast.core_ref.refs_0_, s32[2048]{0:T(1024)S(1)} %bitcast.48, bf16[400,2048]{1,0:T(8,128)(2,1)S(1)} %shard_map.137.refs_2_.hb, ...), custom_call_target="tpu_custom_call" | custom-call | flops 50000000 | tf_op jit(solution)/shard_map/pallas_call | solution.py:528
  128.3 15.3 %collective-permute-done.9 = bf16[400,512]{1,0:T(8,128)(2,1)S(1)} collective-permute-done((bf16[400,512]{1,0:T(8,128)(2,1)S(1)}, bf16[400,512]{1,0:T(8,128)(2,1)S(1)}, u32[]{:S(2)}, u32[]{:S(2)}) %collective-permute-start.9) | collective-permute-done | bytes 409632 | tf_op jit(solution)/shard_map/ppermute | solution.py:484
  145.5 5.4 %shard_map.139 = (f32[1000,2048]{1,0:T(8,128)S(1)}, f32[1,2048]{1,0:T(1,128)S(1)}, f32[1,2048]{1,0:T(1,128)S(1)}) custom-call(s32[1]{0:T(128)} %bitcast.core_ref.refs_0_, f32[400,2048]{1,0:T(8,128)S(1)} %get-tuple-element.160.q, bf16[400,512]{1,0:T(8,128)(2,1)S(1)} %add.89.nfull, bf16[400,512]{1,0:T(8,128)(2,1)S(1)} %collective-permute-done.12.nother), custom_call_target="tpu_custom_call" | custom-call | flops 40000000 | tf_op jit(solution)/shard_map/pallas_call | solution.py:528
  150.9 5.9 %shard_map.140 = (f32[1,128]{1,0:T(1,128)S(1)}, f32[1,2048]{1,0:T(1,128)S(1)}, bf16[1024,2048]{1,0:T(8,128)(2,1)S(1)}, f32[200,1024]{1,0:T(8,128)S(1)}, f32[200,1024]{1,0:T(8,128)S(1)}) custom-call(s32[1]{0:T(128)} %bitcast.core_ref.refs_0_, f32[1,2048]{1,0:T(1,128)S(1)} %get-tuple-element.237.w, f32[400,2048]{1,0:T(8,128)S(1)} %get-tuple-element.160.q, ...), custom_call_target="tpu_custom_call" | custom-call | flops 40000000 | tf_op jit(solution)/shard_map/pallas_call | solution.py:528
  160.2 11.7 %shard_map.141 = (f32[8192,128]{1,0:T(8,128)S(1)}, f32[200,1408]{1,0:T(8,128)S(1)}, f32[200,1408]{1,0:T(8,128)S(1)}) custom-call(s32[1]{0:T(128)} %bitcast.core_ref.refs_0_, s32[2048]{0:T(1024)S(1)} %bitcast.49, bf16[1024,2048]{1,0:T(8,128)(2,1)S(1)} %get-tuple-element.172.ds, f32[1,2048]{1,0:T(1,128)S(1)} %get-tuple-element.173.dp, ...), custom_call_target="tpu_custom_call" | custom-call | flops 60000000 | tf_op jit(solution)/shard_map/pallas_call | solution.py:528
  176.8 18.0 %collective-permute-done.17.refs_4_ = f32[1,2048]{1,0:T(1,128)S(1)} collective-permute-done((f32[1,2048]{1,0:T(1,128)S(1)}, f32[1,2048]{1,0:T(1,128)S(1)}, u32[]{:S(2)}, u32[]{:S(2)}) %collective-permute-start.17) | collective-permute-done | bytes 8224 | tf_op jit(solution)/shard_map/ppermute | solution.py:484
  198.3 16.4 %shard_map.142.refs_5_ = f32[32800,128]{1,0:T(8,128)S(1)} custom-call(s32[2048]{0:T(1024)S(1)} %bitcast.53, s32[2048]{0:T(1024)S(1)} %bitcast.57, s32[2048]{0:T(1024)S(1)} %bitcast.71, f32[8192,128]{1,0:T(8,128)S(1)} %copy-done.5, f32[1,2048]{1,0:T(1,128)S(1)} %collective-permute-done.17.refs_4_, bf16[400,2048]{1,0:T(8,128)(2,1)} %copy-done.9, ...), custom_call_target="tpu_custom_call" | custom-call | flops 75000000 | tf_op jit(solution)/shard_map/pallas_call | solution.py:528
  218.3 14.8 %shard_map.143 = (f32[32800,128]{1,0:T(8,128)S(1)}, f32[32800,128]{1,0:T(8,128)S(1)}, f32[64,128]{1,0:T(8,128)S(1)}, bf16[400,512]{1,0:T(8,128)(2,1)S(1)}, bf16[400,512]{1,0:T(8,128)(2,1)S(1)}) custom-call(s32[1]{0:T(128)} %bitcast.core_ref.refs_0_, s32[1024]{0:T(1024)S(1)} %bitcast.69, ...), custom_call_target="tpu_custom_call", output_to_operand_aliasing={{0}: (5, {}), {1}: (3, {}), {2}: (4, {})} | custom-call | flops 150000000 | tf_op jit(solution)/shard_map/pallas_call | solution.py:528
  233.3 10.2 %collective-permute-done.21 = s32[2,2048]{1,0:T(2,128)S(1)} collective-permute-done((s32[2,2048]{1,0:T(2,128)S(1)}, s32[2,2048]{1,0:T(2,128)S(1)}, u32[]{:S(2)}, u32[]{:S(2)}) %collective-permute-start.21) | collective-permute-done | bytes 16416 | tf_op jit(solution)/shard_map/ppermute | solution.py:484
  248.1 4.2 shard_map.145.refs_2_.hb
  255.3 5.7 %shard_map.146 = (f32[400,2048]{1,0:T(8,128)S(1)}, f32[400,2048]{1,0:T(8,128)S(1)}, f32[5632,128]{1,0:T(8,128)}, f32[400,1408]{1,0:T(8,128)S(1)}, f32[1,1408]{1,0:T(1,128)S(1)}) custom-call(s32[1]{0:T(128)} %bitcast.core_ref.refs_0_, s32[2048]{0:T(1024)S(1)} %bitcast.45, bf16[400,2048]{1,0:T(8,128)(2,1)S(1)} %shard_map.145.refs_2_.hb, ...), custom_call_target="tpu_custom_call" | custom-call | flops 50000000 | tf_op jit(solution)/shard_map/pallas_call | solution.py:528
  261.0 32.8 %collective-permute-done.22 = bf16[400,512]{1,0:T(8,128)(2,1)S(1)} collective-permute-done((bf16[400,512]{1,0:T(8,128)(2,1)S(1)}, bf16[400,512]{1,0:T(8,128)(2,1)S(1)}, u32[]{:S(2)}, u32[]{:S(2)}) %collective-permute-start.22) | collective-permute-done | bytes 409632 | tf_op jit(solution)/shard_map/ppermute | solution.py:484
  295.7 5.4 %shard_map.147 = (f32[1000,2048]{1,0:T(8,128)S(1)}, f32[1,2048]{1,0:T(1,128)S(1)}, f32[1,2048]{1,0:T(1,128)S(1)}) custom-call(s32[1]{0:T(128)} %bitcast.core_ref.refs_0_, f32[400,2048]{1,0:T(8,128)S(1)} %get-tuple-element.198.q, bf16[400,512]{1,0:T(8,128)(2,1)S(1)} %add.95.nfull, bf16[400,512]{1,0:T(8,128)(2,1)S(1)} %collective-permute-done.25.nother), custom_call_target="tpu_custom_call" | custom-call | flops 40000000 | tf_op jit(solution)/shard_map/pallas_call | solution.py:528
  301.1 5.9 %shard_map.148 = (f32[1,128]{1,0:T(1,128)S(1)}, f32[1,2048]{1,0:T(1,128)S(1)}, bf16[1024,2048]{1,0:T(8,128)(2,1)S(1)}, f32[200,1024]{1,0:T(8,128)S(1)}, f32[200,1024]{1,0:T(8,128)S(1)}) custom-call(s32[1]{0:T(128)} %bitcast.core_ref.refs_0_, f32[1,2048]{1,0:T(1,128)S(1)} %get-tuple-element.236.w, f32[400,2048]{1,0:T(8,128)S(1)} %get-tuple-element.198.q, ...), custom_call_target="tpu_custom_call" | custom-call | flops 40000000 | tf_op jit(solution)/shard_map/pallas_call | solution.py:528
  309.5 11.7 %shard_map.149 = (f32[8192,128]{1,0:T(8,128)S(1)}, f32[200,1408]{1,0:T(8,128)S(1)}, f32[200,1408]{1,0:T(8,128)S(1)}) custom-call(s32[1]{0:T(128)} %bitcast.core_ref.refs_0_, s32[2048]{0:T(1024)S(1)} %bitcast.46, bf16[1024,2048]{1,0:T(8,128)(2,1)S(1)} %get-tuple-element.210.ds, f32[1,2048]{1,0:T(1,128)S(1)} %get-tuple-element.211.dp, ...), custom_call_target="tpu_custom_call" | custom-call | flops 60000000 | tf_op jit(solution)/shard_map/pallas_call | solution.py:528
  326.2 58.0 %collective-permute-done.33 = f32[200,1408]{1,0:T(8,128)S(1)} collective-permute-done((f32[200,1408]{1,0:T(8,128)S(1)}, f32[200,1408]{1,0:T(8,128)S(1)}, u32[]{:S(2)}, u32[]{:S(2)}) %collective-permute-start.33) | collective-permute-done | bytes 1126432 | tf_op jit(solution)/shard_map/ppermute | solution.py:484
  385.7 15.6 %collective-permute-done.30.refs_4_ = f32[1,2048]{1,0:T(1,128)S(1)} collective-permute-done((f32[1,2048]{1,0:T(1,128)S(1)}, f32[1,2048]{1,0:T(1,128)S(1)}, u32[]{:S(2)}, u32[]{:S(2)}) %collective-permute-start.30) | collective-permute-done | bytes 8224 | tf_op jit(solution)/shard_map/ppermute | solution.py:484
  402.5 16.4 %shard_map.150.refs_4_ = f32[32800,128]{1,0:T(8,128)S(1)} custom-call(s32[2048]{0:T(1024)S(1)} %bitcast.51, s32[2048]{0:T(1024)S(1)} %bitcast.55, s32[2048]{0:T(1024)S(1)} %bitcast.70, f32[8192,128]{1,0:T(8,128)S(1)} %get-tuple-element.217.refs_3_, f32[1,2048]{1,0:T(1,128)S(1)} %collective-permute-done.30.refs_4_, bf16[400,2048]{1,0:T(8,128)(2,1)} %copy-done.10, ...), custom_call_target="tpu_custom_call" | custom-call | flops 75000000 | tf_op jit(solution)/shard_map/pallas_call | solution.py:528
  418.9 5.7 %copy-done.2 = f32[32800,128]{1,0:T(8,128)} copy-done((f32[32800,128]{1,0:T(8,128)}, f32[32800,128]{1,0:T(8,128)S(1)}, u32[]{:S(2)}) %copy-start.2) | copy-done | bytes 16793624
  427.2 5.8 %copy-done.1 = f32[32800,128]{1,0:T(8,128)S(1)} copy-done((f32[32800,128]{1,0:T(8,128)S(1)}, f32[32800,128]{1,0:T(8,128)}, u32[]{:S(2)}) %copy-start.1) | copy-done | bytes 16793624
  433.0 5.8 %copy-done.3 = f32[32800,128]{1,0:T(8,128)S(1)} copy-done((f32[32800,128]{1,0:T(8,128)S(1)}, f32[32800,128]{1,0:T(8,128)}, u32[]{:S(2)}) %copy-start.3) | copy-done | bytes 16793624
  438.8 16.9 %shard_map.151 = (f32[32800,128]{1,0:T(8,128)S(1)}, f32[400,8192]{1,0:T(8,128)}, f32[64,128]{1,0:T(8,128)}) custom-call(s32[1]{0:T(128)} %bitcast.core_ref.refs_0_, s32[1024]{0:T(1024)S(1)} %bitcast.65, f32[32800,128]{1,0:T(8,128)S(1)} %copy-done.1, f32[64,128]{1,0:T(8,128)S(1)} %get-tuple-element.190.refs_3_, ...), custom_call_target="tpu_custom_call", output_to_operand_aliasing={{0}: (4, {})} | custom-call | flops 150000000 | tf_op jit(solution)/shard_map/pallas_call | solution.py:528
  (133 shorter events, 78.0 us)
Async XLA Ops:
  12.1 2.2 collective-permute-start
  14.4 12.6 %collective-permute-start.1 = (bf16[400,512]{1,0:T(8,128)(2,1)S(1)}, bf16[400,512]{1,0:T(8,128)(2,1)S(1)}, u32[]{:S(2)}, u32[]{:S(2)}) collective-permute-start(bf16[400,512]{1,0:T(8,128)(2,1)S(1)} %add.82), channel_id=1, source_target_pairs={{0,2},{1,3},{2,0},{3,1},{4,6},{5,7},{6,4},{7,5}} | collective-permute-start | bytes 1228808 | tf_op jit(solution)/shard_map/ppermute | solution.py:484
  45.5 2.4 collective-permute-start.3
  60.5 2.8 collective-permute-start.5
  60.7 20.7 %collective-permute-start.4 = (f32[200,1024]{1,0:T(8,128)}, f32[200,1024]{1,0:T(8,128)S(1)}, u32[]{:S(2)}, u32[]{:S(2)}) collective-permute-start(f32[200,1024]{1,0:T(8,128)} %add.84), channel_id=1, source_target_pairs={{0,2},{1,3},{2,0},{3,1},{4,6},{5,7},{6,4},{7,5}} | collective-permute-start | bytes 2457608 | tf_op jit(solution)/shard_map/ppermute | solution.py:484
  82.7 2.4 collective-permute-start.6
  82.7 35.5 %collective-permute-start.10 = (f32[200,1408]{1,0:T(8,128)S(1)}, f32[200,1408]{1,0:T(8,128)S(1)}, u32[]{:S(2)}, u32[]{:S(2)}) collective-permute-start(f32[200,1408]{1,0:T(8,128)S(1)} %add.85), channel_id=1, source_target_pairs={{0,2},{1,3},{2,0},{3,1},{4,6},{5,7},{6,4},{7,5}} | collective-permute-start | bytes 3379208 | tf_op jit(solution)/shard_map/ppermute | solution.py:484
  84.5 25.3 %collective-permute-start.8 = (s32[2,2048]{1,0:T(2,128)S(1)}, s32[2,2048]{1,0:T(2,128)S(1)}, u32[]{:S(2)}, u32[]{:S(2)}) collective-permute-start(s32[2,2048]{1,0:T(2,128)S(1)} %pad_add_fusion), channel_id=1, source_target_pairs={{0,1},{1,2},{2,3},{3,0},{4,5},{5,6},{6,7},{7,4}} | collective-permute-start | bytes 49160 | tf_op jit(solution)/shard_map/ppermute | solution.py:484
  99.9 10.0 %collective-permute-start.7 = (bf16[400,512]{1,0:T(8,128)(2,1)S(1)}, bf16[400,512]{1,0:T(8,128)(2,1)S(1)}, u32[]{:S(2)}, u32[]{:S(2)}) collective-permute-start(bf16[400,512]{1,0:T(8,128)(2,1)S(1)} %get-tuple-element.148), channel_id=1, source_target_pairs={{0,1},{1,0},{2,3},{3,2},{4,5},{5,4},{6,7},{7,6}} | collective-permute-start | bytes 1228808 | tf_op jit(solution)/shard_map/ppermute | solution.py:481
  114.0 36.9 %collective-permute-start.13 = (bf16[400,2048]{1,0:T(8,128)(2,1)S(1)}, bf16[400,2048]{1,0:T(8,128)(2,1)S(1)}, u32[]{:S(2)}, u32[]{:S(2)}) collective-permute-start(bf16[400,2048]{1,0:T(8,128)(2,1)S(1)} %shard_map.136), channel_id=1, source_target_pairs={{0,3},{1,0},{2,1},{3,2},{4,7},{5,4},{6,5},{7,6}} | collective-permute-start | bytes 4915208 | tf_op jit(solution)/shard_map/ppermute | solution.py:484
  118.4 2.9 collective-permute-start.11
  118.9 24.7 %collective-permute-start.9 = (bf16[400,512]{1,0:T(8,128)(2,1)S(1)}, bf16[400,512]{1,0:T(8,128)(2,1)S(1)}, u32[]{:S(2)}, u32[]{:S(2)}) collective-permute-start(bf16[400,512]{1,0:T(8,128)(2,1)S(1)} %add.87), channel_id=1, source_target_pairs={{0,2},{1,3},{2,0},{3,1},{4,6},{5,7},{6,4},{7,5}} | collective-permute-start | bytes 1228808 | tf_op jit(solution)/shard_map/ppermute | solution.py:484
  156.8 2.4 collective-permute-start.14
  156.9 37.9 %collective-permute-start.18 = (bf16[400,2048]{1,0:T(8,128)(2,1)S(1)}, bf16[400,2048]{1,0:T(8,128)(2,1)S(1)}, u32[]{:S(2)}, u32[]{:S(2)}) collective-permute-start(bf16[400,2048]{1,0:T(8,128)(2,1)S(1)} %shard_map.137.refs_2_.hb), channel_id=1, source_target_pairs={{0,1},{1,2},{2,3},{3,0},{4,5},{5,6},{6,7},{7,4}} | collective-permute-start | bytes 4915208 | tf_op jit(solution)/shard_map/ppermute | solution.py:484
  173.9 2.8 collective-permute-start.16
  174.1 40.6 %collective-permute-start.15 = (f32[200,1024]{1,0:T(8,128)}, f32[200,1024]{1,0:T(8,128)S(1)}, u32[]{:S(2)}, u32[]{:S(2)}) collective-permute-start(f32[200,1024]{1,0:T(8,128)} %add.90), channel_id=1, source_target_pairs={{0,2},{1,3},{2,0},{3,1},{4,6},{5,7},{6,4},{7,5}} | collective-permute-start | bytes 2457608 | tf_op jit(solution)/shard_map/ppermute | solution.py:484
  174.3 20.5 %collective-permute-start.17 = (f32[1,2048]{1,0:T(1,128)S(1)}, f32[1,2048]{1,0:T(1,128)S(1)}, u32[]{:S(2)}, u32[]{:S(2)}) collective-permute-start(f32[1,2048]{1,0:T(1,128)S(1)} %get-tuple-element.173.dp), channel_id=1, source_target_pairs={{0,1},{1,2},{2,3},{3,0},{4,5},{5,6},{6,7},{7,4}} | collective-permute-start | bytes 24584 | tf_op jit(solution)/shard_map/ppermute | solution.py:484
  215.9 2.4 collective-permute-start.19
  216.0 36.4 %collective-permute-start.23 = (f32[200,1408]{1,0:T(8,128)S(1)}, f32[200,1408]{1,0:T(8,128)S(1)}, u32[]{:S(2)}, u32[]{:S(2)}) collective-permute-start(f32[200,1408]{1,0:T(8,128)S(1)} %add.91), channel_id=1, source_target_pairs={{0,2},{1,3},{2,0},{3,1},{4,6},{5,7},{6,4},{7,5}} | collective-permute-start | bytes 3379208 | tf_op jit(solution)/shard_map/ppermute | solution.py:484
  216.3 27.2 %collective-permute-start.21 = (s32[2,2048]{1,0:T(2,128)S(1)}, s32[2,2048]{1,0:T(2,128)S(1)}, u32[]{:S(2)}, u32[]{:S(2)}) collective-permute-start(s32[2,2048]{1,0:T(2,128)S(1)} %pad_add_fusion.1), channel_id=1, source_target_pairs={{0,2},{1,3},{2,0},{3,1},{4,6},{5,7},{6,4},{7,5}} | collective-permute-start | bytes 49160 | tf_op jit(solution)/shard_map/ppermute | solution.py:484
  233.1 10.5 %collective-permute-start.20 = (bf16[400,512]{1,0:T(8,128)(2,1)S(1)}, bf16[400,512]{1,0:T(8,128)(2,1)S(1)}, u32[]{:S(2)}, u32[]{:S(2)}) collective-permute-start(bf16[400,512]{1,0:T(8,128)(2,1)S(1)} %get-tuple-element.184), channel_id=1, source_target_pairs={{0,1},{1,0},{2,3},{3,2},{4,5},{5,4},{6,7},{7,6}} | collective-permute-start | bytes 1228808 | tf_op jit(solution)/shard_map/ppermute | solution.py:481
  247.7 53.4 %collective-permute-start.26 = (bf16[400,2048]{1,0:T(8,128)(2,1)S(1)}, bf16[400,2048]{1,0:T(8,128)(2,1)S(1)}, u32[]{:S(2)}, u32[]{:S(2)}) collective-permute-start(bf16[400,2048]{1,0:T(8,128)(2,1)S(1)} %shard_map.144), channel_id=1, source_target_pairs={{0,2},{1,3},{2,0},{3,1},{4,6},{5,7},{6,4},{7,5}} | collective-permute-start | bytes 4915208 | tf_op jit(solution)/shard_map/ppermute | solution.py:484
  252.5 2.8 collective-permute-start.24
  252.5 41.3 %collective-permute-start.22 = (bf16[400,512]{1,0:T(8,128)(2,1)S(1)}, bf16[400,512]{1,0:T(8,128)(2,1)S(1)}, u32[]{:S(2)}, u32[]{:S(2)}) collective-permute-start(bf16[400,512]{1,0:T(8,128)(2,1)S(1)} %add.93), channel_id=1, source_target_pairs={{0,2},{1,3},{2,0},{3,1},{4,6},{5,7},{6,4},{7,5}} | collective-permute-start | bytes 1228808 | tf_op jit(solution)/shard_map/ppermute | solution.py:484
  307.0 2.4 collective-permute-start.27
  321.2 2.8 collective-permute-start.29
  321.4 79.9 %collective-permute-start.31 = (bf16[400,2048]{1,0:T(8,128)(2,1)S(1)}, bf16[400,2048]{1,0:T(8,128)(2,1)S(1)}, u32[]{:S(2)}, u32[]{:S(2)}) collective-permute-start(bf16[400,2048]{1,0:T(8,128)(2,1)S(1)} %shard_map.145.refs_2_.hb), channel_id=1, source_target_pairs={{0,2},{1,3},{2,0},{3,1},{4,6},{5,7},{6,4},{7,5}} | collective-permute-start | bytes 4915208 | tf_op jit(solution)/shard_map/ppermute | solution.py:484
  324.2 60.0 %collective-permute-start.33 = (f32[200,1408]{1,0:T(8,128)S(1)}, f32[200,1408]{1,0:T(8,128)S(1)}, u32[]{:S(2)}, u32[]{:S(2)}) collective-permute-start(f32[200,1408]{1,0:T(8,128)S(1)} %add.97), channel_id=1, source_target_pairs={{0,2},{1,3},{2,0},{3,1},{4,6},{5,7},{6,4},{7,5}} | collective-permute-start | bytes 3379208 | tf_op jit(solution)/shard_map/ppermute | solution.py:484
  324.5 100.1 %collective-permute-start.28 = (f32[200,1024]{1,0:T(8,128)S(1)}, f32[200,1024]{1,0:T(8,128)S(1)}, u32[]{:S(2)}, u32[]{:S(2)}) collective-permute-start(f32[200,1024]{1,0:T(8,128)S(1)} %add.96), channel_id=1, source_target_pairs={{0,2},{1,3},{2,0},{3,1},{4,6},{5,7},{6,4},{7,5}} | collective-permute-start | bytes 2457608 | tf_op jit(solution)/shard_map/ppermute | solution.py:484
  385.3 70.3 %collective-permute-start.34 = (f32[200,1408]{1,0:T(8,128)}, f32[200,1408]{1,0:T(8,128)}, u32[]{:S(2)}, u32[]{:S(2)}) collective-permute-start(f32[200,1408]{1,0:T(8,128)} %add.99), channel_id=1, source_target_pairs={{0,1},{1,0},{2,3},{3,2},{4,5},{5,4},{6,7},{7,6}} | collective-permute-start | bytes 3379208 | tf_op jit(solution)/shard_map/ppermute | solution.py:491
  385.4 16.0 %collective-permute-start.30 = (f32[1,2048]{1,0:T(1,128)S(1)}, f32[1,2048]{1,0:T(1,128)S(1)}, u32[]{:S(2)}, u32[]{:S(2)}) collective-permute-start(f32[1,2048]{1,0:T(1,128)S(1)} %get-tuple-element.211.dp), channel_id=1, source_target_pairs={{0,2},{1,3},{2,0},{3,1},{4,6},{5,7},{6,4},{7,5}} | collective-permute-start | bytes 24584 | tf_op jit(solution)/shard_map/ppermute | solution.py:484
  424.8 2.5 collective-permute-start.32
  (19 other events, 88.3 us)

commit v8 on v7

--- a/solution.py
+++ b/solution.py
@@ -51,8 +51,9 @@
     index = [ids[base + k] for k in range(BATCH)]
     grads = [rows[pl.ds(four(row_base + SLICES * k), SLICES), :] for k in range(BATCH)]
     total = []
+    lanes = [jnp.full((SLICES, LANES), i, jnp.int32) for i in index]
     for k in range(BATCH):
-        repeats = [jnp.where(index[earlier] == index[k], grads[earlier], 0.0) for earlier in range(k)]
+        repeats = [jnp.where(lanes[earlier] == lanes[k], grads[earlier], 0.0) for earlier in range(k)]
         total.append(functools.reduce(jnp.add, repeats, grads[k]))
     total = [acc[pl.ds(four(index[k]), SLICES), :] + total[k] for k in range(BATCH)]
     return index, total
@@ -267,7 +268,7 @@
     zero_rows(racc)
     qs[:, pl.ds(dim, tops - dim), :] = jnp.zeros((2, tops - dim, CHUNK), F32)
 
-    def compute(c, slot):
+    def compute(c):
         cols = pl.ds(pl.multiple_of(c * CHUNK, LANES), CHUNK)
         gq = lax.dot_general(nb[...], ds[:, cols], (((1,), (0,)), ((), ())), preferred_element_type=F32) + dp[:, cols] * tb[:, cols].astype(F32)
         g_re, g_im = gq[:half], gq[half:]
@@ -277,22 +278,26 @@
         for part, (f_re, f_im) in enumerate(((h_re, h_im), (r_re, r_im))):
             qs[part, pl.ds(0, half), :] = g_re * f_re + g_im * f_im
             qs[part, pl.ds(half, half), :] = g_im * f_re - g_re * f_im
-        for b in range(CHUNK // LANES):
-            for j in range(SLICES):
-                place = pl.ds(j * LANES, LANES), pl.ds(b * LANES, LANES)
-                stage[slot, pl.ds(SLICES * b * LANES + j, LANES, stride=SLICES), :] = qs[(0,) + place].T
-                hg[pl.ds(SLICES * (c * CHUNK + b * LANES) + j, LANES, stride=SLICES), :] = qs[(1,) + place].T
-
-    def scatter(c, slot):
-        add_rows([(racc, rel, c * CHUNK, stage.at[slot], 0)], CHUNK)
-
-    compute(0, 0)
+
+    def turn(c, slot, b, j):
+        place = pl.ds(j * LANES, LANES), pl.ds(b * LANES, LANES)
+        stage[slot, pl.ds(SLICES * b * LANES + j, LANES, stride=SLICES), :] = qs[(0,) + place].T
+        hg[pl.ds(SLICES * (c * CHUNK + b * LANES) + j, LANES, stride=SLICES), :] = qs[(1,) + place].T
+
+    blocks = [(b, j) for b in range(CHUNK // LANES) for j in range(SLICES)]
+    share = CHUNK // len(blocks)
+    compute(0)
+    for b, j in blocks:
+        turn(0, 0, b, j)
 
     def step(i, _):
         for slot in range(2):
             c = 2 * i + slot
-            scatter(c, slot)
-            compute(jnp.minimum(c + 1, edges // CHUNK - 1), 1 - slot)
+            after = jnp.minimum(c + 1, edges // CHUNK - 1)
+            compute(after)
+            for k, (b, j) in enumerate(blocks):
+                add_rows([(racc, rel, c * CHUNK + k * share, stage.at[slot], k * share * SLICES)], share)
+                turn(after, 1 - slot, b, j)
         return 0
 
     lax.fori_loop(0, edges // CHUNK // 2, step, 0)
@@ -521,7 +526,7 @@
         def call(kernel, args, kinds, outs, out_kinds, scratch, micros, name, aliases=None):
             places = {'s': smem, 'h': hbm, 'v': vmem, 'V': vmem}
             windows = [a for a, k in zip(list(args) + outs, kinds + out_kinds) if k == 'v']
-            limit = (4 if name == 'grad' else 3) * 2 ** 20 + sum(padded_bytes(a.shape, a.dtype) for a in windows)
+            limit = (4 if name == 'grad' else 2) * 2 ** 20 + sum(padded_bytes(a.shape, a.dtype) for a in windows)
             limit += sum(padded_bytes(a.shape, a.dtype) for a in scratch if getattr(a, 'memory_space', None) == pltpu.VMEM)
             args = [pltpu.with_memory_space_constraint(a, pltpu.VMEM if k == 'V' else pltpu.HBM) if k in 'Vh' else a for a, k in zip(args, kinds)]
             outs = [{'V': pltpu.VMEM, 'h': pltpu.HBM}[k](o.shape, o.dtype) if k in 'Vh' else o for o, k in zip(outs, out_kinds)]

time: 461 us -> 447 us (0.970)
  Pallas kernels: 211 us -> 196 us
  waiting for transfers between devices: 189 us -> 197 us
  local copies, waits for them, and re-layouts: 27.4 us -> 21.9 us
    pallas_call x24, Pallas kernels: 211 us -> 196 us  [call(): pl.pallas_call(kernel, out_shape=outs, in_specs=[places[k]() for k in kin...]
    ppermute x17, waiting for transfers between devices: 167 us -> 176 us  [send(): return lax.ppermute(value, 'ent', pairs)]
    unnamed x33 -> x29, local copies, waits for them, and re-layouts: 26.6 us -> 21.1 us
  transfers between devices with their start and end apart: 35 -> 35, of which waited for: 24 -> 24; matrix products, arithmetic and copies ran while one was open for 1% -> 1% of each run, Pallas kernels for 32% -> 31%
where the time goes in v8:
time: 447 us
  waiting for transfers between devices  197 us (44%)
  Pallas kernels  196 us (44%)
  local copies, waits for them, and re-layouts  21.9 us (5%)
  starting transfers between devices  18.8 us (4%)
  other arithmetic  11.1 us (2%)
    pallas_call x24, Pallas kernels, call(): pl.pallas_call(kernel, out_shape=outs, in_specs=[places[k]() for k in kin...  196 us
    ppermute x17, waiting for transfers between devices, send(): return lax.ppermute(value, 'ent', pairs)  176 us
    unnamed x29, local copies, waits for them, and re-layouts  21.1 us
    ppermute x17, starting transfers between devices, send(): return lax.ppermute(value, 'ent', pairs)  15.9 us
    ppermute x9, waiting for transfers between devices, chip_sum(): return keep + lax.ppermute(send, 'ent', swap)  12.2 us
    ppermute x9, waiting for transfers between devices, finish(): return (mine, lax.ppermute(mine, 'ent', swap))  9.23 us
  transfers between devices with their start and end apart: 35, of which 24 were waited for; matrix products, arithmetic and copies ran while one was open for 1% of the time, Pallas kernels for 31%

profile of v8, /device:TPU:0, one launch (start us, length us, event | category | flops | bytes accessed | tf_op | source)
XLA Modules:
  0.0 446.5 jit_solution(15448404217818144001)
XLA Ops:
  2.2 9.9 %shard_map.128 = (f32[32800,128]{1,0:T(8,128)S(1)}, bf16[400,512]{1,0:T(8,128)(2,1)S(1)}, bf16[400,512]{1,0:T(8,128)(2,1)S(1)}) custom-call(s32[1]{0:T(128)} %bitcast.core_ref.refs_0_, s32[1024]{0:T(1024)S(1)} %bitcast.66, f32[400,8192]{1,0:T(8,128)} %bitcast.75), custom_call_target="tpu_custom_call" | custom-call | flops 100000000 | tf_op jit(solution)/shard_map/pallas_call | solution.py:533
  17.3 7.5 %shard_map.129 = (bf16[400,2048]{1,0:T(8,128)(2,1)S(1)}, bf16[400,2048]{1,0:T(8,128)(2,1)S(1)}) custom-call(s32[2048]{0:T(1024)S(1)} %bitcast.58, s32[2048]{0:T(1024)S(1)} %bitcast.60, f32[32800,128]{1,0:T(8,128)S(1)} %get-tuple-element.120.refs_2_.refs_3_), custom_call_target="tpu_custom_call" | custom-call | flops 55000000 | tf_op jit(solution)/shard_map/pallas_call | solution.py:533
  27.1 5.3 %shard_map.130 = (f32[400,2048]{1,0:T(8,128)S(1)}, f32[400,2048]{1,0:T(8,128)S(1)}) custom-call(s32[1]{0:T(128)} %bitcast.core_ref.refs_0_, s32[2048]{0:T(1024)S(1)} %bitcast.62, bf16[400,2048]{1,0:T(8,128)(2,1)S(1)} %get-tuple-element.126.refs_2_.hb, f32[400,1408]{1,0:T(8,128)S(1)} %pad.13.refs_3_), custom_call_target="tpu_custom_call" | custom-call | flops 50000000 | tf_op jit(solution)/shard_map/pallas_call | solution.py:533
  34.2 5.4 %shard_map.131 = (f32[1000,2048]{1,0:T(8,128)S(1)}, f32[1,2048]{1,0:T(1,128)S(1)}, f32[1,2048]{1,0:T(1,128)S(1)}) custom-call(s32[1]{0:T(128)} %bitcast.core_ref.refs_0_, f32[400,2048]{1,0:T(8,128)S(1)} %get-tuple-element.128.q.refs_4_, bf16[400,512]{1,0:T(8,128)(2,1)S(1)} %add.83.nfull, bf16[400,512]{1,0:T(8,128)(2,1)S(1)} %collective-permute-done.2.nother), custom_call_target="tpu_custom_call" | custom-call | flops 40000000 | tf_op jit(solution)/shard_map/pallas_call | solution.py:533
  39.6 5.9 %shard_map.132 = (f32[1,128]{1,0:T(1,128)S(1)}, f32[1,2048]{1,0:T(1,128)S(1)}, bf16[1024,2048]{1,0:T(8,128)(2,1)S(1)}, f32[200,1024]{1,0:T(8,128)S(1)}, f32[200,1024]{1,0:T(8,128)S(1)}) custom-call(s32[1]{0:T(128)} %bitcast.core_ref.refs_0_, f32[1,2048]{1,0:T(1,128)S(1)} %get-tuple-element.238.w, f32[400,2048]{1,0:T(8,128)S(1)} %get-tuple-element.128.q.refs_4_, ...), custom_call_target="tpu_custom_call" | custom-call | flops 40000000 | tf_op jit(solution)/shard_map/pallas_call | solution.py:533
  48.0 10.2 %shard_map.133 = (f32[8192,128]{1,0:T(8,128)S(1)}, f32[200,1408]{1,0:T(8,128)S(1)}, f32[200,1408]{1,0:T(8,128)S(1)}) custom-call(s32[1]{0:T(128)} %bitcast.core_ref.refs_0_, s32[2048]{0:T(1024)S(1)} %bitcast.63, bf16[1024,2048]{1,0:T(8,128)(2,1)S(1)} %get-tuple-element.138.ds, f32[1,2048]{1,0:T(1,128)S(1)} %get-tuple-element.139.dp.refs_3_, ...), custom_call_target="tpu_custom_call" | custom-call | flops 60000000 | tf_op jit(solution)/shard_map/pallas_call | solution.py:533
  61.1 10.0 %shard_map.134.refs_5_ = f32[32800,128]{1,0:T(8,128)S(1)} custom-call(s32[2048]{0:T(1024)S(1)} %bitcast.61, s32[2048]{0:T(1024)S(1)} %bitcast.59, f32[8192,128]{1,0:T(8,128)S(1)} %get-tuple-element.144.refs_2_, f32[1,2048]{1,0:T(1,128)S(1)} %get-tuple-element.139.dp.refs_3_, f32[400,2048]{1,0:T(8,128)S(1)} %get-tuple-element.128.q.refs_4_), custom_call_target="tpu_custom_call" | custom-call | flops 75000000 | tf_op jit(solution)/shard_map/pallas_call | solution.py:533
  71.1 7.8 %collective-permute-done.4 = f32[200,1024]{1,0:T(8,128)S(1)} collective-permute-done((f32[200,1024]{1,0:T(8,128)S(1)}, f32[200,1024]{1,0:T(8,128)S(1)}, u32[]{:S(2)}, u32[]{:S(2)}) %collective-permute-start.4) | collective-permute-done | bytes 819232 | tf_op jit(solution)/shard_map/ppermute | solution.py:489
  81.3 14.5 %shard_map.135 = (f32[32800,128]{1,0:T(8,128)S(1)}, f32[32800,128]{1,0:T(8,128)S(1)}, f32[64,128]{1,0:T(8,128)S(1)}, bf16[400,512]{1,0:T(8,128)(2,1)S(1)}, bf16[400,512]{1,0:T(8,128)(2,1)S(1)}) custom-call(s32[1]{0:T(128)} %bitcast.core_ref.refs_0_, s32[1024]{0:T(1024)S(1)} %bitcast.67, ...), custom_call_target="tpu_custom_call", output_to_operand_aliasing={{0}: (5, {}), {1}: (3, {}), {2}: (4, {})} | custom-call | flops 150000000 | tf_op jit(solution)/shard_map/pallas_call | solution.py:533
  96.0 10.1 %collective-permute-done.8 = s32[2,2048]{1,0:T(2,128)S(1)} collective-permute-done((s32[2,2048]{1,0:T(2,128)S(1)}, s32[2,2048]{1,0:T(2,128)S(1)}, u32[]{:S(2)}, u32[]{:S(2)}) %collective-permute-start.8) | collective-permute-done | bytes 16416 | tf_op jit(solution)/shard_map/ppermute | solution.py:489
  106.2 4.0 shard_map.136
  117.4 5.9 %shard_map.138 = (f32[400,2048]{1,0:T(8,128)S(1)}, f32[400,2048]{1,0:T(8,128)S(1)}, f32[5632,128]{1,0:T(8,128)}, f32[400,1408]{1,0:T(8,128)S(1)}, f32[1,1408]{1,0:T(1,128)S(1)}) custom-call(s32[1]{0:T(128)} %bitcast.core_ref.refs_0_, s32[2048]{0:T(1024)S(1)} %bitcast.48, bf16[400,2048]{1,0:T(8,128)(2,1)S(1)} %shard_map.137.refs_2_.hb, ...), custom_call_target="tpu_custom_call" | custom-call | flops 50000000 | tf_op jit(solution)/shard_map/pallas_call | solution.py:533
  123.3 16.6 %collective-permute-done.9 = bf16[400,512]{1,0:T(8,128)(2,1)S(1)} collective-permute-done((bf16[400,512]{1,0:T(8,128)(2,1)S(1)}, bf16[400,512]{1,0:T(8,128)(2,1)S(1)}, u32[]{:S(2)}, u32[]{:S(2)}) %collective-permute-start.9) | collective-permute-done | bytes 409632 | tf_op jit(solution)/shard_map/ppermute | solution.py:489
  141.8 5.4 %shard_map.139 = (f32[1000,2048]{1,0:T(8,128)S(1)}, f32[1,2048]{1,0:T(1,128)S(1)}, f32[1,2048]{1,0:T(1,128)S(1)}) custom-call(s32[1]{0:T(128)} %bitcast.core_ref.refs_0_, f32[400,2048]{1,0:T(8,128)S(1)} %get-tuple-element.160.q, bf16[400,512]{1,0:T(8,128)(2,1)S(1)} %add.89.nfull, bf16[400,512]{1,0:T(8,128)(2,1)S(1)} %collective-permute-done.12.nother), custom_call_target="tpu_custom_call" | custom-call | flops 40000000 | tf_op jit(solution)/shard_map/pallas_call | solution.py:533
  147.2 5.9 %shard_map.140 = (f32[1,128]{1,0:T(1,128)S(1)}, f32[1,2048]{1,0:T(1,128)S(1)}, bf16[1024,2048]{1,0:T(8,128)(2,1)S(1)}, f32[200,1024]{1,0:T(8,128)S(1)}, f32[200,1024]{1,0:T(8,128)S(1)}) custom-call(s32[1]{0:T(128)} %bitcast.core_ref.refs_0_, f32[1,2048]{1,0:T(1,128)S(1)} %get-tuple-element.237.w, f32[400,2048]{1,0:T(8,128)S(1)} %get-tuple-element.160.q, ...), custom_call_target="tpu_custom_call" | custom-call | flops 40000000 | tf_op jit(solution)/shard_map/pallas_call | solution.py:533
  156.5 10.2 %shard_map.141 = (f32[8192,128]{1,0:T(8,128)S(1)}, f32[200,1408]{1,0:T(8,128)S(1)}, f32[200,1408]{1,0:T(8,128)S(1)}) custom-call(s32[1]{0:T(128)} %bitcast.core_ref.refs_0_, s32[2048]{0:T(1024)S(1)} %bitcast.49, bf16[1024,2048]{1,0:T(8,128)(2,1)S(1)} %get-tuple-element.172.ds, f32[1,2048]{1,0:T(1,128)S(1)} %get-tuple-element.173.dp, ...), custom_call_target="tpu_custom_call" | custom-call | flops 60000000 | tf_op jit(solution)/shard_map/pallas_call | solution.py:533
  169.6 21.8 %collective-permute-done.17.refs_4_ = f32[1,2048]{1,0:T(1,128)S(1)} collective-permute-done((f32[1,2048]{1,0:T(1,128)S(1)}, f32[1,2048]{1,0:T(1,128)S(1)}, u32[]{:S(2)}, u32[]{:S(2)}) %collective-permute-start.17) | collective-permute-done | bytes 8224 | tf_op jit(solution)/shard_map/ppermute | solution.py:489
  192.6 12.9 %shard_map.142.refs_5_ = f32[32800,128]{1,0:T(8,128)S(1)} custom-call(s32[2048]{0:T(1024)S(1)} %bitcast.53, s32[2048]{0:T(1024)S(1)} %bitcast.57, s32[2048]{0:T(1024)S(1)} %bitcast.71, f32[8192,128]{1,0:T(8,128)S(1)} %get-tuple-element.179.refs_3_, f32[1,2048]{1,0:T(1,128)S(1)} %collective-permute-done.17.refs_4_, bf16[400,2048]{1,0:T(8,128)(2,1)} %copy-done.7, ...), custom_call_target="tpu_custom_call" | custom-call | flops 75000000 | tf_op jit(solution)/shard_map/pallas_call | solution.py:533
  209.2 14.5 %shard_map.143 = (f32[32800,128]{1,0:T(8,128)S(1)}, f32[32800,128]{1,0:T(8,128)S(1)}, f32[64,128]{1,0:T(8,128)S(1)}, bf16[400,512]{1,0:T(8,128)(2,1)S(1)}, bf16[400,512]{1,0:T(8,128)(2,1)S(1)}) custom-call(s32[1]{0:T(128)} %bitcast.core_ref.refs_0_, s32[1024]{0:T(1024)S(1)} %bitcast.69, ...), custom_call_target="tpu_custom_call", output_to_operand_aliasing={{0}: (5, {}), {1}: (3, {}), {2}: (4, {})} | custom-call | flops 150000000 | tf_op jit(solution)/shard_map/pallas_call | solution.py:533
  223.9 10.5 %collective-permute-done.21 = s32[2,2048]{1,0:T(2,128)S(1)} collective-permute-done((s32[2,2048]{1,0:T(2,128)S(1)}, s32[2,2048]{1,0:T(2,128)S(1)}, u32[]{:S(2)}, u32[]{:S(2)}) %collective-permute-start.21) | collective-permute-done | bytes 16416 | tf_op jit(solution)/shard_map/ppermute | solution.py:489
  246.0 5.7 %shard_map.146 = (f32[400,2048]{1,0:T(8,128)S(1)}, f32[400,2048]{1,0:T(8,128)S(1)}, f32[5632,128]{1,0:T(8,128)}, f32[400,1408]{1,0:T(8,128)S(1)}, f32[1,1408]{1,0:T(1,128)S(1)}) custom-call(s32[1]{0:T(128)} %bitcast.core_ref.refs_0_, s32[2048]{0:T(1024)S(1)} %bitcast.45, bf16[400,2048]{1,0:T(8,128)(2,1)S(1)} %shard_map.145.refs_2_.hb, ...), custom_call_target="tpu_custom_call" | custom-call | flops 50000000 | tf_op jit(solution)/shard_map/pallas_call | solution.py:533
  251.7 33.1 %collective-permute-done.22 = bf16[400,512]{1,0:T(8,128)(2,1)S(1)} collective-permute-done((bf16[400,512]{1,0:T(8,128)(2,1)S(1)}, bf16[400,512]{1,0:T(8,128)(2,1)S(1)}, u32[]{:S(2)}, u32[]{:S(2)}) %collective-permute-start.22) | collective-permute-done | bytes 409632 | tf_op jit(solution)/shard_map/ppermute | solution.py:489
  286.6 5.4 %shard_map.147 = (f32[1000,2048]{1,0:T(8,128)S(1)}, f32[1,2048]{1,0:T(1,128)S(1)}, f32[1,2048]{1,0:T(1,128)S(1)}) custom-call(s32[1]{0:T(128)} %bitcast.core_ref.refs_0_, f32[400,2048]{1,0:T(8,128)S(1)} %get-tuple-element.198.q, bf16[400,512]{1,0:T(8,128)(2,1)S(1)} %add.95.nfull, bf16[400,512]{1,0:T(8,128)(2,1)S(1)} %collective-permute-done.25.nother), custom_call_target="tpu_custom_call" | custom-call | flops 40000000 | tf_op jit(solution)/shard_map/pallas_call | solution.py:533
  292.0 5.9 %shard_map.148 = (f32[1,128]{1,0:T(1,128)S(1)}, f32[1,2048]{1,0:T(1,128)S(1)}, bf16[1024,2048]{1,0:T(8,128)(2,1)S(1)}, f32[200,1024]{1,0:T(8,128)S(1)}, f32[200,1024]{1,0:T(8,128)S(1)}) custom-call(s32[1]{0:T(128)} %bitcast.core_ref.refs_0_, f32[1,2048]{1,0:T(1,128)S(1)} %get-tuple-element.236.w, f32[400,2048]{1,0:T(8,128)S(1)} %get-tuple-element.198.q, ...), custom_call_target="tpu_custom_call" | custom-call | flops 40000000 | tf_op jit(solution)/shard_map/pallas_call | solution.py:533
  300.4 10.4 %shard_map.149 = (f32[8192,128]{1,0:T(8,128)S(1)}, f32[200,1408]{1,0:T(8,128)S(1)}, f32[200,1408]{1,0:T(8,128)S(1)}) custom-call(s32[1]{0:T(128)} %bitcast.core_ref.refs_0_, s32[2048]{0:T(1024)S(1)} %bitcast.46, bf16[1024,2048]{1,0:T(8,128)(2,1)S(1)} %get-tuple-element.210.ds, f32[1,2048]{1,0:T(1,128)S(1)} %get-tuple-element.211.dp, ...), custom_call_target="tpu_custom_call" | custom-call | flops 60000000 | tf_op jit(solution)/shard_map/pallas_call | solution.py:533
  315.8 58.0 %collective-permute-done.33 = f32[200,1408]{1,0:T(8,128)S(1)} collective-permute-done((f32[200,1408]{1,0:T(8,128)S(1)}, f32[200,1408]{1,0:T(8,128)S(1)}, u32[]{:S(2)}, u32[]{:S(2)}) %collective-permute-start.33) | collective-permute-done | bytes 1126432 | tf_op jit(solution)/shard_map/ppermute | solution.py:489
  375.3 15.6 %collective-permute-done.30.refs_4_ = f32[1,2048]{1,0:T(1,128)S(1)} collective-permute-done((f32[1,2048]{1,0:T(1,128)S(1)}, f32[1,2048]{1,0:T(1,128)S(1)}, u32[]{:S(2)}, u32[]{:S(2)}) %collective-permute-start.30) | collective-permute-done | bytes 8224 | tf_op jit(solution)/shard_map/ppermute | solution.py:489
  392.1 12.9 %shard_map.150.refs_4_ = f32[32800,128]{1,0:T(8,128)S(1)} custom-call(s32[2048]{0:T(1024)S(1)} %bitcast.51, s32[2048]{0:T(1024)S(1)} %bitcast.55, s32[2048]{0:T(1024)S(1)} %bitcast.70, f32[8192,128]{1,0:T(8,128)S(1)} %get-tuple-element.217.refs_3_, f32[1,2048]{1,0:T(1,128)S(1)} %collective-permute-done.30.refs_4_, bf16[400,2048]{1,0:T(8,128)(2,1)} %copy-done.8, ...), custom_call_target="tpu_custom_call" | custom-call | flops 75000000 | tf_op jit(solution)/shard_map/pallas_call | solution.py:533
  405.0 5.8 %copy-done.2 = f32[32800,128]{1,0:T(8,128)} copy-done((f32[32800,128]{1,0:T(8,128)}, f32[32800,128]{1,0:T(8,128)S(1)}, u32[]{:S(2)}) %copy-start.2) | copy-done | bytes 16793624
  413.4 5.8 %copy-done.1 = f32[32800,128]{1,0:T(8,128)S(1)} copy-done((f32[32800,128]{1,0:T(8,128)S(1)}, f32[32800,128]{1,0:T(8,128)}, u32[]{:S(2)}) %copy-start.1) | copy-done | bytes 16793624
  419.2 5.8 %copy-done.3 = f32[32800,128]{1,0:T(8,128)S(1)} copy-done((f32[32800,128]{1,0:T(8,128)S(1)}, f32[32800,128]{1,0:T(8,128)}, u32[]{:S(2)}) %copy-start.3) | copy-done | bytes 16793624
  425.0 16.6 %shard_map.151 = (f32[32800,128]{1,0:T(8,128)S(1)}, f32[400,8192]{1,0:T(8,128)}, f32[64,128]{1,0:T(8,128)}) custom-call(s32[1]{0:T(128)} %bitcast.core_ref.refs_0_, s32[1024]{0:T(1024)S(1)} %bitcast.65, f32[32800,128]{1,0:T(8,128)S(1)} %copy-done.1, f32[64,128]{1,0:T(8,128)S(1)} %get-tuple-element.190.refs_3_, ...), custom_call_target="tpu_custom_call", output_to_operand_aliasing={{0}: (4, {})} | custom-call | flops 150000000 | tf_op jit(solution)/shard_map/pallas_call | solution.py:533
  (129 shorter events, 70.2 us)
Async XLA Ops:
  12.1 2.2 collective-permute-start
  14.4 12.6 %collective-permute-start.1 = (bf16[400,512]{1,0:T(8,128)(2,1)S(1)}, bf16[400,512]{1,0:T(8,128)(2,1)S(1)}, u32[]{:S(2)}, u32[]{:S(2)}) collective-permute-start(bf16[400,512]{1,0:T(8,128)(2,1)S(1)} %add.82), channel_id=1, source_target_pairs={{0,2},{1,3},{2,0},{3,1},{4,6},{5,7},{6,4},{7,5}} | collective-permute-start | bytes 1228808 | tf_op jit(solution)/shard_map/ppermute | solution.py:489
  45.5 2.4 collective-permute-start.3
  58.2 2.8 collective-permute-start.5
  58.4 20.5 %collective-permute-start.4 = (f32[200,1024]{1,0:T(8,128)S(1)}, f32[200,1024]{1,0:T(8,128)S(1)}, u32[]{:S(2)}, u32[]{:S(2)}) collective-permute-start(f32[200,1024]{1,0:T(8,128)S(1)} %add.84), channel_id=1, source_target_pairs={{0,2},{1,3},{2,0},{3,1},{4,6},{5,7},{6,4},{7,5}} | collective-permute-start | bytes 2457608 | tf_op jit(solution)/shard_map/ppermute | solution.py:489
  79.0 2.4 collective-permute-start.6
  79.0 35.3 %collective-permute-start.10 = (f32[200,1408]{1,0:T(8,128)S(1)}, f32[200,1408]{1,0:T(8,128)S(1)}, u32[]{:S(2)}, u32[]{:S(2)}) collective-permute-start(f32[200,1408]{1,0:T(8,128)S(1)} %add.85), channel_id=1, source_target_pairs={{0,2},{1,3},{2,0},{3,1},{4,6},{5,7},{6,4},{7,5}} | collective-permute-start | bytes 3379208 | tf_op jit(solution)/shard_map/ppermute | solution.py:489
  80.8 25.3 %collective-permute-start.8 = (s32[2,2048]{1,0:T(2,128)S(1)}, s32[2,2048]{1,0:T(2,128)S(1)}, u32[]{:S(2)}, u32[]{:S(2)}) collective-permute-start(s32[2,2048]{1,0:T(2,128)S(1)} %pad_add_fusion), channel_id=1, source_target_pairs={{0,1},{1,2},{2,3},{3,0},{4,5},{5,6},{6,7},{7,4}} | collective-permute-start | bytes 49160 | tf_op jit(solution)/shard_map/ppermute | solution.py:489
  95.8 10.3 %collective-permute-start.7 = (bf16[400,512]{1,0:T(8,128)(2,1)S(1)}, bf16[400,512]{1,0:T(8,128)(2,1)S(1)}, u32[]{:S(2)}, u32[]{:S(2)}) collective-permute-start(bf16[400,512]{1,0:T(8,128)(2,1)S(1)} %get-tuple-element.148), channel_id=1, source_target_pairs={{0,1},{1,0},{2,3},{3,2},{4,5},{5,4},{6,7},{7,6}} | collective-permute-start | bytes 1228808 | tf_op jit(solution)/shard_map/ppermute | solution.py:486
  110.3 36.9 %collective-permute-start.13 = (bf16[400,2048]{1,0:T(8,128)(2,1)S(1)}, bf16[400,2048]{1,0:T(8,128)(2,1)S(1)}, u32[]{:S(2)}, u32[]{:S(2)}) collective-permute-start(bf16[400,2048]{1,0:T(8,128)(2,1)S(1)} %shard_map.136), channel_id=1, source_target_pairs={{0,3},{1,0},{2,1},{3,2},{4,7},{5,4},{6,5},{7,6}} | collective-permute-start | bytes 4915208 | tf_op jit(solution)/shard_map/ppermute | solution.py:489
  114.5 2.9 collective-permute-start.11
  115.0 24.9 %collective-permute-start.9 = (bf16[400,512]{1,0:T(8,128)(2,1)S(1)}, bf16[400,512]{1,0:T(8,128)(2,1)S(1)}, u32[]{:S(2)}, u32[]{:S(2)}) collective-permute-start(bf16[400,512]{1,0:T(8,128)(2,1)S(1)} %add.87), channel_id=1, source_target_pairs={{0,2},{1,3},{2,0},{3,1},{4,6},{5,7},{6,4},{7,5}} | collective-permute-start | bytes 1228808 | tf_op jit(solution)/shard_map/ppermute | solution.py:489
  153.1 2.4 collective-permute-start.14
  153.2 38.2 %collective-permute-start.18 = (bf16[400,2048]{1,0:T(8,128)(2,1)S(1)}, bf16[400,2048]{1,0:T(8,128)(2,1)S(1)}, u32[]{:S(2)}, u32[]{:S(2)}) collective-permute-start(bf16[400,2048]{1,0:T(8,128)(2,1)S(1)} %shard_map.137.refs_2_.hb), channel_id=1, source_target_pairs={{0,1},{1,2},{2,3},{3,0},{4,5},{5,6},{6,7},{7,4}} | collective-permute-start | bytes 4915208 | tf_op jit(solution)/shard_map/ppermute | solution.py:489
  166.7 2.8 collective-permute-start.16
  166.8 38.7 %collective-permute-start.15 = (f32[200,1024]{1,0:T(8,128)}, f32[200,1024]{1,0:T(8,128)S(1)}, u32[]{:S(2)}, u32[]{:S(2)}) collective-permute-start(f32[200,1024]{1,0:T(8,128)} %add.90), channel_id=1, source_target_pairs={{0,2},{1,3},{2,0},{3,1},{4,6},{5,7},{6,4},{7,5}} | collective-permute-start | bytes 2457608 | tf_op jit(solution)/shard_map/ppermute | solution.py:489
  167.1 24.3 %collective-permute-start.17 = (f32[1,2048]{1,0:T(1,128)S(1)}, f32[1,2048]{1,0:T(1,128)S(1)}, u32[]{:S(2)}, u32[]{:S(2)}) collective-permute-start(f32[1,2048]{1,0:T(1,128)S(1)} %get-tuple-element.173.dp), channel_id=1, source_target_pairs={{0,1},{1,2},{2,3},{3,0},{4,5},{5,6},{6,7},{7,4}} | collective-permute-start | bytes 24584 | tf_op jit(solution)/shard_map/ppermute | solution.py:489
  206.8 2.4 collective-permute-start.19
  206.9 36.1 %collective-permute-start.23 = (f32[200,1408]{1,0:T(8,128)S(1)}, f32[200,1408]{1,0:T(8,128)S(1)}, u32[]{:S(2)}, u32[]{:S(2)}) collective-permute-start(f32[200,1408]{1,0:T(8,128)S(1)} %add.91), channel_id=1, source_target_pairs={{0,2},{1,3},{2,0},{3,1},{4,6},{5,7},{6,4},{7,5}} | collective-permute-start | bytes 3379208 | tf_op jit(solution)/shard_map/ppermute | solution.py:489
  207.2 27.2 %collective-permute-start.21 = (s32[2,2048]{1,0:T(2,128)S(1)}, s32[2,2048]{1,0:T(2,128)S(1)}, u32[]{:S(2)}, u32[]{:S(2)}) collective-permute-start(s32[2,2048]{1,0:T(2,128)S(1)} %pad_add_fusion.1), channel_id=1, source_target_pairs={{0,2},{1,3},{2,0},{3,1},{4,6},{5,7},{6,4},{7,5}} | collective-permute-start | bytes 49160 | tf_op jit(solution)/shard_map/ppermute | solution.py:489
  223.7 10.8 %collective-permute-start.20 = (bf16[400,512]{1,0:T(8,128)(2,1)S(1)}, bf16[400,512]{1,0:T(8,128)(2,1)S(1)}, u32[]{:S(2)}, u32[]{:S(2)}) collective-permute-start(bf16[400,512]{1,0:T(8,128)(2,1)S(1)} %get-tuple-element.184), channel_id=1, source_target_pairs={{0,1},{1,0},{2,3},{3,2},{4,5},{5,4},{6,7},{7,6}} | collective-permute-start | bytes 1228808 | tf_op jit(solution)/shard_map/ppermute | solution.py:486
  238.6 53.4 %collective-permute-start.26 = (bf16[400,2048]{1,0:T(8,128)(2,1)S(1)}, bf16[400,2048]{1,0:T(8,128)(2,1)S(1)}, u32[]{:S(2)}, u32[]{:S(2)}) collective-permute-start(bf16[400,2048]{1,0:T(8,128)(2,1)S(1)} %shard_map.144), channel_id=1, source_target_pairs={{0,2},{1,3},{2,0},{3,1},{4,6},{5,7},{6,4},{7,5}} | collective-permute-start | bytes 4915208 | tf_op jit(solution)/shard_map/ppermute | solution.py:489
  243.2 2.8 collective-permute-start.24
  243.2 41.5 %collective-permute-start.22 = (bf16[400,512]{1,0:T(8,128)(2,1)S(1)}, bf16[400,512]{1,0:T(8,128)(2,1)S(1)}, u32[]{:S(2)}, u32[]{:S(2)}) collective-permute-start(bf16[400,512]{1,0:T(8,128)(2,1)S(1)} %add.93), channel_id=1, source_target_pairs={{0,2},{1,3},{2,0},{3,1},{4,6},{5,7},{6,4},{7,5}} | collective-permute-start | bytes 1228808 | tf_op jit(solution)/shard_map/ppermute | solution.py:489
  297.9 2.4 collective-permute-start.27
  310.8 2.8 collective-permute-start.29
  311.0 79.9 %collective-permute-start.31 = (bf16[400,2048]{1,0:T(8,128)(2,1)S(1)}, bf16[400,2048]{1,0:T(8,128)(2,1)S(1)}, u32[]{:S(2)}, u32[]{:S(2)}) collective-permute-start(bf16[400,2048]{1,0:T(8,128)(2,1)S(1)} %shard_map.145.refs_2_.hb), channel_id=1, source_target_pairs={{0,2},{1,3},{2,0},{3,1},{4,6},{5,7},{6,4},{7,5}} | collective-permute-start | bytes 4915208 | tf_op jit(solution)/shard_map/ppermute | solution.py:489
  313.8 60.0 %collective-permute-start.33 = (f32[200,1408]{1,0:T(8,128)S(1)}, f32[200,1408]{1,0:T(8,128)S(1)}, u32[]{:S(2)}, u32[]{:S(2)}) collective-permute-start(f32[200,1408]{1,0:T(8,128)S(1)} %add.97), channel_id=1, source_target_pairs={{0,2},{1,3},{2,0},{3,1},{4,6},{5,7},{6,4},{7,5}} | collective-permute-start | bytes 3379208 | tf_op jit(solution)/shard_map/ppermute | solution.py:489
  314.1 96.7 %collective-permute-start.28 = (f32[200,1024]{1,0:T(8,128)S(1)}, f32[200,1024]{1,0:T(8,128)S(1)}, u32[]{:S(2)}, u32[]{:S(2)}) collective-permute-start(f32[200,1024]{1,0:T(8,128)S(1)} %add.96), channel_id=1, source_target_pairs={{0,2},{1,3},{2,0},{3,1},{4,6},{5,7},{6,4},{7,5}} | collective-permute-start | bytes 2457608 | tf_op jit(solution)/shard_map/ppermute | solution.py:489
  375.0 66.6 %collective-permute-start.34 = (f32[200,1408]{1,0:T(8,128)}, f32[200,1408]{1,0:T(8,128)}, u32[]{:S(2)}, u32[]{:S(2)}) collective-permute-start(f32[200,1408]{1,0:T(8,128)} %add.99), channel_id=1, source_target_pairs={{0,1},{1,0},{2,3},{3,2},{4,5},{5,4},{6,7},{7,6}} | collective-permute-start | bytes 3379208 | tf_op jit(solution)/shard_map/ppermute | solution.py:496
  375.0 15.9 %collective-permute-start.30 = (f32[1,2048]{1,0:T(1,128)S(1)}, f32[1,2048]{1,0:T(1,128)S(1)}, u32[]{:S(2)}, u32[]{:S(2)}) collective-permute-start(f32[1,2048]{1,0:T(1,128)S(1)} %get-tuple-element.211.dp), channel_id=1, source_target_pairs={{0,2},{1,3},{2,0},{3,1},{4,6},{5,7},{6,4},{7,5}} | collective-permute-start | bytes 24584 | tf_op jit(solution)/shard_map/ppermute | solution.py:489
  410.9 2.5 collective-permute-start.32
  (17 other events, 106.9 us)

commit v9 on v8

--- a/solution.py
+++ b/solution.py
@@ -551,6 +551,7 @@
         rel_grads = None
         for s in range(rounds):
             first, last = s == 0, s == rounds - 1
+            even_load = 2 * s == ent_size
             neg_part = chip_sum(nk, ns)
             if first:
                 neg_part, t4 = tie((neg_part, t4))
@@ -561,7 +562,6 @@
                     got = send(jnp.stack([own_tails[later], own_rels[later]]), shift(later))
                     tails.append(got[0])
                     rels.append(got[1])
-                neg_got, hb = tie((neg_got, hb))
             else:
                 neg_part, t4 = tie((neg_part, t4))
                 neg_got = link(neg_part)
@@ -569,6 +569,8 @@
                 tail_cols = send(tb, shift(-s))
                 t4, tb = tie((t4, tb))
                 hb, = gather([heads[s]], t4)
+                if even_load:
+                    head_cols = send(hb, shift(s))
                 rel_got, hb = tie((rel_got, hb))
                 rel_grads = finish(rel_part, rel_got)
             wide = shape((dim, edges))
@@ -595,8 +597,9 @@
                 [pltpu.VMEM((dim, negp), BF16), pltpu.VMEM((negp, dim), BF16), pltpu.VMEM((neg_count, CHUNK), F32)], 8, 'exp')
             if not first:
                 e, tail_cols = tie((e, tail_cols))
-                tail_cols, hb = tie((tail_cols, hb))
-                head_cols = send(hb, shift(s))
+                if not even_load:
+                    tail_cols, hb = tie((tail_cols, hb))
+                    head_cols = send(hb, shift(s))
             loss, dp, ds, gk, gs = call(
                 functools.partial(score_kernel, dim, neg_count, edges), [core, weights[s].reshape(1, edges), q, tail_cols, e, neg_top, neg_total], 'svVVVvv',
                 [shape((1, LANES)), shape((1, edges)), shape((negp, edges), BF16), shape((half, negp)), shape((half, negp))], 'vvVVV',
@@ -649,6 +652,7 @@
         new_r = rfm - LEARN_RATE * rg / jnp.sqrt(new_vr + ADA_EPS)
         return et.T, g.reshape(rows), new_r[:, :num_rel].T, new_vr[0, :num_rel], jnp.stack(losses)[None, :]
 
+
     return jax.shard_map(device_fn, mesh=mesh,
                          in_specs=(row_spec, flat_spec, rel_spec, state_spec, edge_spec, edge_spec, edge_spec, edge_spec, rel_spec),
                          out_specs=(row_spec, flat_spec, rel_spec, state_spec, row_spec), check_vma=False)

time: 447 us -> 442 us (0.989)
    ppermute x17, waiting for transfers between devices: 176 us -> 169 us  [send(): return lax.ppermute(value, 'ent', pairs)]
  transfers between devices with their start and end apart: 35 -> 35, of which waited for: 24 -> 23; matrix products, arithmetic and copies ran while one was open for 1% -> 1% of each run, Pallas kernels for 31% -> 32%
where the time goes in v9:
time: 442 us
  Pallas kernels  196 us (44%)
  waiting for transfers between devices  194 us (44%)
  local copies, waits for them, and re-layouts  20.7 us (5%)
  starting transfers between devices  18.5 us (4%)
  other arithmetic  11.1 us (3%)
    pallas_call x24, Pallas kernels, call(): pl.pallas_call(kernel, out_shape=outs, in_specs=[places[k]() for k in kin...  196 us
    ppermute x17, waiting for transfers between devices, send(): return lax.ppermute(value, 'ent', pairs)  169 us
    unnamed x29, local copies, waits for them, and re-layouts  19.9 us
    ppermute x17, starting transfers between devices, send(): return lax.ppermute(value, 'ent', pairs)  15.6 us
    ppermute x9, waiting for transfers between devices, finish(): return (mine, lax.ppermute(mine, 'ent', swap))  13.6 us
    ppermute x9, waiting for transfers between devices, chip_sum(): return keep + lax.ppermute(send, 'ent', swap)  11.1 us
  transfers between devices with their start and end apart: 35, of which 23 were waited for; matrix products, arithmetic and copies ran while one was open for 1% of the time, Pallas kernels for 32%

profile of v9, /device:TPU:0, one launch (start us, length us, event | category | flops | bytes accessed | tf_op | source)
XLA Modules:
  0.0 441.7 jit_solution(9181004606730746996)
XLA Ops:
  2.2 9.9 %shard_map.128 = (f32[32800,128]{1,0:T(8,128)S(1)}, bf16[400,512]{1,0:T(8,128)(2,1)S(1)}, bf16[400,512]{1,0:T(8,128)(2,1)S(1)}) custom-call(s32[1]{0:T(128)} %bitcast.core_ref.refs_0_, s32[1024]{0:T(1024)S(1)} %bitcast.66, f32[400,8192]{1,0:T(8,128)} %bitcast.75), custom_call_target="tpu_custom_call" | custom-call | flops 100000000 | tf_op jit(solution)/shard_map/pallas_call | solution.py:533
  17.3 7.5 %shard_map.129 = (bf16[400,2048]{1,0:T(8,128)(2,1)S(1)}, bf16[400,2048]{1,0:T(8,128)(2,1)S(1)}) custom-call(s32[2048]{0:T(1024)S(1)} %bitcast.58, s32[2048]{0:T(1024)S(1)} %bitcast.60, f32[32800,128]{1,0:T(8,128)S(1)} %get-tuple-element.116.refs_2_.refs_3_), custom_call_target="tpu_custom_call" | custom-call | flops 55000000 | tf_op jit(solution)/shard_map/pallas_call | solution.py:533
  24.8 5.3 %shard_map.130 = (f32[400,2048]{1,0:T(8,128)S(1)}, f32[400,2048]{1,0:T(8,128)S(1)}) custom-call(s32[1]{0:T(128)} %bitcast.core_ref.refs_0_, s32[2048]{0:T(1024)S(1)} %bitcast.62, bf16[400,2048]{1,0:T(8,128)(2,1)S(1)} %get-tuple-element.120.refs_2_.hb, f32[400,1408]{1,0:T(8,128)S(1)} %pad.13.refs_3_), custom_call_target="tpu_custom_call" | custom-call | flops 50000000 | tf_op jit(solution)/shard_map/pallas_call | solution.py:533
  32.0 5.4 %shard_map.131 = (f32[1000,2048]{1,0:T(8,128)S(1)}, f32[1,2048]{1,0:T(1,128)S(1)}, f32[1,2048]{1,0:T(1,128)S(1)}) custom-call(s32[1]{0:T(128)} %bitcast.core_ref.refs_0_, f32[400,2048]{1,0:T(8,128)S(1)} %get-tuple-element.122.q.refs_4_, bf16[400,512]{1,0:T(8,128)(2,1)S(1)} %add.83.nfull, bf16[400,512]{1,0:T(8,128)(2,1)S(1)} %collective-permute-done.2.nother), custom_call_target="tpu_custom_call" | custom-call | flops 40000000 | tf_op jit(solution)/shard_map/pallas_call | solution.py:533
  37.4 5.9 %shard_map.132 = (f32[1,128]{1,0:T(1,128)S(1)}, f32[1,2048]{1,0:T(1,128)S(1)}, bf16[1024,2048]{1,0:T(8,128)(2,1)S(1)}, f32[200,1024]{1,0:T(8,128)S(1)}, f32[200,1024]{1,0:T(8,128)S(1)}) custom-call(s32[1]{0:T(128)} %bitcast.core_ref.refs_0_, f32[1,2048]{1,0:T(1,128)S(1)} %get-tuple-element.230.w, f32[400,2048]{1,0:T(8,128)S(1)} %get-tuple-element.122.q.refs_4_, ...), custom_call_target="tpu_custom_call" | custom-call | flops 40000000 | tf_op jit(solution)/shard_map/pallas_call | solution.py:533
  45.8 10.2 %shard_map.133 = (f32[8192,128]{1,0:T(8,128)S(1)}, f32[200,1408]{1,0:T(8,128)S(1)}, f32[200,1408]{1,0:T(8,128)S(1)}) custom-call(s32[1]{0:T(128)} %bitcast.core_ref.refs_0_, s32[2048]{0:T(1024)S(1)} %bitcast.63, bf16[1024,2048]{1,0:T(8,128)(2,1)S(1)} %get-tuple-element.132.ds, f32[1,2048]{1,0:T(1,128)S(1)} %get-tuple-element.133.dp.refs_3_, ...), custom_call_target="tpu_custom_call" | custom-call | flops 60000000 | tf_op jit(solution)/shard_map/pallas_call | solution.py:533
  58.9 10.0 %shard_map.134.refs_5_ = f32[32800,128]{1,0:T(8,128)S(1)} custom-call(s32[2048]{0:T(1024)S(1)} %bitcast.61, s32[2048]{0:T(1024)S(1)} %bitcast.59, f32[8192,128]{1,0:T(8,128)S(1)} %get-tuple-element.138.refs_2_, f32[1,2048]{1,0:T(1,128)S(1)} %get-tuple-element.133.dp.refs_3_, f32[400,2048]{1,0:T(8,128)S(1)} %get-tuple-element.122.q.refs_4_), custom_call_target="tpu_custom_call" | custom-call | flops 75000000 | tf_op jit(solution)/shard_map/pallas_call | solution.py:533
  68.9 7.8 %collective-permute-done.4 = f32[200,1024]{1,0:T(8,128)S(1)} collective-permute-done((f32[200,1024]{1,0:T(8,128)S(1)}, f32[200,1024]{1,0:T(8,128)S(1)}, u32[]{:S(2)}, u32[]{:S(2)}) %collective-permute-start.4) | collective-permute-done | bytes 819232 | tf_op jit(solution)/shard_map/ppermute | solution.py:489
  79.1 14.5 %shard_map.135 = (f32[32800,128]{1,0:T(8,128)S(1)}, f32[32800,128]{1,0:T(8,128)S(1)}, f32[64,128]{1,0:T(8,128)S(1)}, bf16[400,512]{1,0:T(8,128)(2,1)S(1)}, bf16[400,512]{1,0:T(8,128)(2,1)S(1)}) custom-call(s32[1]{0:T(128)} %bitcast.core_ref.refs_0_, s32[1024]{0:T(1024)S(1)} %bitcast.67, ...), custom_call_target="tpu_custom_call", output_to_operand_aliasing={{0}: (5, {}), {1}: (3, {}), {2}: (4, {})} | custom-call | flops 150000000 | tf_op jit(solution)/shard_map/pallas_call | solution.py:533
  93.8 10.1 %collective-permute-done.8 = s32[2,2048]{1,0:T(2,128)S(1)} collective-permute-done((s32[2,2048]{1,0:T(2,128)S(1)}, s32[2,2048]{1,0:T(2,128)S(1)}, u32[]{:S(2)}, u32[]{:S(2)}) %collective-permute-start.8) | collective-permute-done | bytes 16416 | tf_op jit(solution)/shard_map/ppermute | solution.py:489
  104.0 4.0 shard_map.136
  115.2 5.9 %shard_map.138 = (f32[400,2048]{1,0:T(8,128)S(1)}, f32[400,2048]{1,0:T(8,128)S(1)}, f32[5632,128]{1,0:T(8,128)}, f32[400,1408]{1,0:T(8,128)S(1)}, f32[1,1408]{1,0:T(1,128)S(1)}) custom-call(s32[1]{0:T(128)} %bitcast.core_ref.refs_0_, s32[2048]{0:T(1024)S(1)} %bitcast.48, bf16[400,2048]{1,0:T(8,128)(2,1)S(1)} %shard_map.137.refs_2_.hb, ...), custom_call_target="tpu_custom_call" | custom-call | flops 50000000 | tf_op jit(solution)/shard_map/pallas_call | solution.py:533
  121.1 15.1 %collective-permute-done.9 = bf16[400,512]{1,0:T(8,128)(2,1)S(1)} collective-permute-done((bf16[400,512]{1,0:T(8,128)(2,1)S(1)}, bf16[400,512]{1,0:T(8,128)(2,1)S(1)}, u32[]{:S(2)}, u32[]{:S(2)}) %collective-permute-start.9) | collective-permute-done | bytes 409632 | tf_op jit(solution)/shard_map/ppermute | solution.py:489
  138.1 5.4 %shard_map.139 = (f32[1000,2048]{1,0:T(8,128)S(1)}, f32[1,2048]{1,0:T(1,128)S(1)}, f32[1,2048]{1,0:T(1,128)S(1)}) custom-call(s32[1]{0:T(128)} %bitcast.core_ref.refs_0_, f32[400,2048]{1,0:T(8,128)S(1)} %get-tuple-element.154.q, bf16[400,512]{1,0:T(8,128)(2,1)S(1)} %add.89.nfull, bf16[400,512]{1,0:T(8,128)(2,1)S(1)} %collective-permute-done.12.nother), custom_call_target="tpu_custom_call" | custom-call | flops 40000000 | tf_op jit(solution)/shard_map/pallas_call | solution.py:533
  143.5 5.9 %shard_map.140 = (f32[1,128]{1,0:T(1,128)S(1)}, f32[1,2048]{1,0:T(1,128)S(1)}, bf16[1024,2048]{1,0:T(8,128)(2,1)S(1)}, f32[200,1024]{1,0:T(8,128)S(1)}, f32[200,1024]{1,0:T(8,128)S(1)}) custom-call(s32[1]{0:T(128)} %bitcast.core_ref.refs_0_, f32[1,2048]{1,0:T(1,128)S(1)} %get-tuple-element.229.w, f32[400,2048]{1,0:T(8,128)S(1)} %get-tuple-element.154.q, ...), custom_call_target="tpu_custom_call" | custom-call | flops 40000000 | tf_op jit(solution)/shard_map/pallas_call | solution.py:533
  152.8 10.2 %shard_map.141 = (f32[8192,128]{1,0:T(8,128)S(1)}, f32[200,1408]{1,0:T(8,128)S(1)}, f32[200,1408]{1,0:T(8,128)S(1)}) custom-call(s32[1]{0:T(128)} %bitcast.core_ref.refs_0_, s32[2048]{0:T(1024)S(1)} %bitcast.49, bf16[1024,2048]{1,0:T(8,128)(2,1)S(1)} %get-tuple-element.166.ds, f32[1,2048]{1,0:T(1,128)S(1)} %get-tuple-element.167.dp, ...), custom_call_target="tpu_custom_call" | custom-call | flops 60000000 | tf_op jit(solution)/shard_map/pallas_call | solution.py:533
  165.9 21.8 %collective-permute-done.17.refs_4_ = f32[1,2048]{1,0:T(1,128)S(1)} collective-permute-done((f32[1,2048]{1,0:T(1,128)S(1)}, f32[1,2048]{1,0:T(1,128)S(1)}, u32[]{:S(2)}, u32[]{:S(2)}) %collective-permute-start.17) | collective-permute-done | bytes 8224 | tf_op jit(solution)/shard_map/ppermute | solution.py:489
  189.0 12.9 %shard_map.142.refs_5_ = f32[32800,128]{1,0:T(8,128)S(1)} custom-call(s32[2048]{0:T(1024)S(1)} %bitcast.53, s32[2048]{0:T(1024)S(1)} %bitcast.57, s32[2048]{0:T(1024)S(1)} %bitcast.71, f32[8192,128]{1,0:T(8,128)S(1)} %get-tuple-element.173.refs_3_, f32[1,2048]{1,0:T(1,128)S(1)} %collective-permute-done.17.refs_4_, bf16[400,2048]{1,0:T(8,128)(2,1)} %copy-done.7, ...), custom_call_target="tpu_custom_call" | custom-call | flops 75000000 | tf_op jit(solution)/shard_map/pallas_call | solution.py:533
  205.5 14.5 %shard_map.143 = (f32[32800,128]{1,0:T(8,128)S(1)}, f32[32800,128]{1,0:T(8,128)S(1)}, f32[64,128]{1,0:T(8,128)S(1)}, bf16[400,512]{1,0:T(8,128)(2,1)S(1)}, bf16[400,512]{1,0:T(8,128)(2,1)S(1)}) custom-call(s32[1]{0:T(128)} %bitcast.core_ref.refs_0_, s32[1024]{0:T(1024)S(1)} %bitcast.69, ...), custom_call_target="tpu_custom_call", output_to_operand_aliasing={{0}: (5, {}), {1}: (3, {}), {2}: (4, {})} | custom-call | flops 150000000 | tf_op jit(solution)/shard_map/pallas_call | solution.py:533
  220.2 10.6 %collective-permute-done.21 = s32[2,2048]{1,0:T(2,128)S(1)} collective-permute-done((s32[2,2048]{1,0:T(2,128)S(1)}, s32[2,2048]{1,0:T(2,128)S(1)}, u32[]{:S(2)}, u32[]{:S(2)}) %collective-permute-start.21) | collective-permute-done | bytes 16416 | tf_op jit(solution)/shard_map/ppermute | solution.py:489
  243.7 5.7 %shard_map.146 = (f32[400,2048]{1,0:T(8,128)S(1)}, f32[400,2048]{1,0:T(8,128)S(1)}, f32[5632,128]{1,0:T(8,128)}, f32[400,1408]{1,0:T(8,128)S(1)}, f32[1,1408]{1,0:T(1,128)S(1)}) custom-call(s32[1]{0:T(128)} %bitcast.core_ref.refs_0_, s32[2048]{0:T(1024)S(1)} %bitcast.45, bf16[400,2048]{1,0:T(8,128)(2,1)S(1)} %shard_map.145.refs_2_.hb, ...), custom_call_target="tpu_custom_call" | custom-call | flops 50000000 | tf_op jit(solution)/shard_map/pallas_call | solution.py:533
  249.5 31.7 %collective-permute-done.22 = bf16[400,512]{1,0:T(8,128)(2,1)S(1)} collective-permute-done((bf16[400,512]{1,0:T(8,128)(2,1)S(1)}, bf16[400,512]{1,0:T(8,128)(2,1)S(1)}, u32[]{:S(2)}, u32[]{:S(2)}) %collective-permute-start.22) | collective-permute-done | bytes 409632 | tf_op jit(solution)/shard_map/ppermute | solution.py:489
  283.0 5.4 %shard_map.147 = (f32[1000,2048]{1,0:T(8,128)S(1)}, f32[1,2048]{1,0:T(1,128)S(1)}, f32[1,2048]{1,0:T(1,128)S(1)}) custom-call(s32[1]{0:T(128)} %bitcast.core_ref.refs_0_, f32[400,2048]{1,0:T(8,128)S(1)} %get-tuple-element.192.q, bf16[400,512]{1,0:T(8,128)(2,1)S(1)} %add.95.nfull, bf16[400,512]{1,0:T(8,128)(2,1)S(1)} %collective-permute-done.25.nother), custom_call_target="tpu_custom_call" | custom-call | flops 40000000 | tf_op jit(solution)/shard_map/pallas_call | solution.py:533
  288.4 5.9 %shard_map.148 = (f32[1,128]{1,0:T(1,128)S(1)}, f32[1,2048]{1,0:T(1,128)S(1)}, bf16[1024,2048]{1,0:T(8,128)(2,1)S(1)}, f32[200,1024]{1,0:T(8,128)S(1)}, f32[200,1024]{1,0:T(8,128)S(1)}) custom-call(s32[1]{0:T(128)} %bitcast.core_ref.refs_0_, f32[1,2048]{1,0:T(1,128)S(1)} %get-tuple-element.228.w, f32[400,2048]{1,0:T(8,128)S(1)} %get-tuple-element.192.q, ...), custom_call_target="tpu_custom_call" | custom-call | flops 40000000 | tf_op jit(solution)/shard_map/pallas_call | solution.py:533
  296.8 10.4 %shard_map.149 = (f32[8192,128]{1,0:T(8,128)S(1)}, f32[200,1408]{1,0:T(8,128)S(1)}, f32[200,1408]{1,0:T(8,128)S(1)}) custom-call(s32[1]{0:T(128)} %bitcast.core_ref.refs_0_, s32[2048]{0:T(1024)S(1)} %bitcast.46, bf16[1024,2048]{1,0:T(8,128)(2,1)S(1)} %get-tuple-element.203.ds, f32[1,2048]{1,0:T(1,128)S(1)} %get-tuple-element.204.dp, ...), custom_call_target="tpu_custom_call" | custom-call | flops 60000000 | tf_op jit(solution)/shard_map/pallas_call | solution.py:533
  312.2 58.0 %collective-permute-done.33 = f32[200,1408]{1,0:T(8,128)S(1)} collective-permute-done((f32[200,1408]{1,0:T(8,128)S(1)}, f32[200,1408]{1,0:T(8,128)S(1)}, u32[]{:S(2)}, u32[]{:S(2)}) %collective-permute-start.33) | collective-permute-done | bytes 1126432 | tf_op jit(solution)/shard_map/ppermute | solution.py:489
  373.1 14.2 %collective-permute-done.30.refs_4_ = f32[1,2048]{1,0:T(1,128)S(1)} collective-permute-done((f32[1,2048]{1,0:T(1,128)S(1)}, f32[1,2048]{1,0:T(1,128)S(1)}, u32[]{:S(2)}, u32[]{:S(2)}) %collective-permute-start.30) | collective-permute-done | bytes 8224 | tf_op jit(solution)/shard_map/ppermute | solution.py:489
  387.3 12.9 %shard_map.150.refs_4_ = f32[32800,128]{1,0:T(8,128)S(1)} custom-call(s32[2048]{0:T(1024)S(1)} %bitcast.51, s32[2048]{0:T(1024)S(1)} %bitcast.55, s32[2048]{0:T(1024)S(1)} %bitcast.70, f32[8192,128]{1,0:T(8,128)S(1)} %get-tuple-element.209.refs_3_, f32[1,2048]{1,0:T(1,128)S(1)} %collective-permute-done.30.refs_4_, bf16[400,2048]{1,0:T(8,128)(2,1)} %copy-done.8, ...), custom_call_target="tpu_custom_call" | custom-call | flops 75000000 | tf_op jit(solution)/shard_map/pallas_call | solution.py:533
  400.2 5.8 %copy-done.2 = f32[32800,128]{1,0:T(8,128)} copy-done((f32[32800,128]{1,0:T(8,128)}, f32[32800,128]{1,0:T(8,128)S(1)}, u32[]{:S(2)}) %copy-start.2) | copy-done | bytes 16793624
  408.6 5.8 %copy-done.1 = f32[32800,128]{1,0:T(8,128)S(1)} copy-done((f32[32800,128]{1,0:T(8,128)S(1)}, f32[32800,128]{1,0:T(8,128)}, u32[]{:S(2)}) %copy-start.1) | copy-done | bytes 16793624
  414.4 5.8 %copy-done.3 = f32[32800,128]{1,0:T(8,128)S(1)} copy-done((f32[32800,128]{1,0:T(8,128)S(1)}, f32[32800,128]{1,0:T(8,128)}, u32[]{:S(2)}) %copy-start.3) | copy-done | bytes 16793624
  420.2 16.6 %shard_map.151 = (f32[32800,128]{1,0:T(8,128)S(1)}, f32[400,8192]{1,0:T(8,128)}, f32[64,128]{1,0:T(8,128)}) custom-call(s32[1]{0:T(128)} %bitcast.core_ref.refs_0_, s32[1024]{0:T(1024)S(1)} %bitcast.65, f32[32800,128]{1,0:T(8,128)S(1)} %copy-done.1, f32[64,128]{1,0:T(8,128)S(1)} %get-tuple-element.184.refs_3_, ...), custom_call_target="tpu_custom_call", output_to_operand_aliasing={{0}: (4, {})} | custom-call | flops 150000000 | tf_op jit(solution)/shard_map/pallas_call | solution.py:533
  (129 shorter events, 69.7 us)
Async XLA Ops:
  12.1 2.2 collective-permute-start
  14.4 15.7 %collective-permute-start.1 = (bf16[400,512]{1,0:T(8,128)(2,1)S(1)}, bf16[400,512]{1,0:T(8,128)(2,1)S(1)}, u32[]{:S(2)}, u32[]{:S(2)}) collective-permute-start(bf16[400,512]{1,0:T(8,128)(2,1)S(1)} %add.82), channel_id=1, source_target_pairs={{0,2},{1,3},{2,0},{3,1},{4,6},{5,7},{6,4},{7,5}} | collective-permute-start | bytes 1228808 | tf_op jit(solution)/shard_map/ppermute | solution.py:489
  43.3 2.4 collective-permute-start.3
  56.0 2.8 collective-permute-start.5
  56.1 20.5 %collective-permute-start.4 = (f32[200,1024]{1,0:T(8,128)S(1)}, f32[200,1024]{1,0:T(8,128)S(1)}, u32[]{:S(2)}, u32[]{:S(2)}) collective-permute-start(f32[200,1024]{1,0:T(8,128)S(1)} %add.84), channel_id=1, source_target_pairs={{0,2},{1,3},{2,0},{3,1},{4,6},{5,7},{6,4},{7,5}} | collective-permute-start | bytes 2457608 | tf_op jit(solution)/shard_map/ppermute | solution.py:489
  76.8 2.4 collective-permute-start.6
  76.8 35.3 %collective-permute-start.10 = (f32[200,1408]{1,0:T(8,128)S(1)}, f32[200,1408]{1,0:T(8,128)S(1)}, u32[]{:S(2)}, u32[]{:S(2)}) collective-permute-start(f32[200,1408]{1,0:T(8,128)S(1)} %add.85), channel_id=1, source_target_pairs={{0,2},{1,3},{2,0},{3,1},{4,6},{5,7},{6,4},{7,5}} | collective-permute-start | bytes 3379208 | tf_op jit(solution)/shard_map/ppermute | solution.py:489
  77.1 26.8 %collective-permute-start.8 = (s32[2,2048]{1,0:T(2,128)S(1)}, s32[2,2048]{1,0:T(2,128)S(1)}, u32[]{:S(2)}, u32[]{:S(2)}) collective-permute-start(s32[2,2048]{1,0:T(2,128)S(1)} %pad_add_fusion), channel_id=1, source_target_pairs={{0,1},{1,2},{2,3},{3,0},{4,5},{5,6},{6,7},{7,4}} | collective-permute-start | bytes 49160 | tf_op jit(solution)/shard_map/ppermute | solution.py:489
  93.6 10.3 %collective-permute-start.7 = (bf16[400,512]{1,0:T(8,128)(2,1)S(1)}, bf16[400,512]{1,0:T(8,128)(2,1)S(1)}, u32[]{:S(2)}, u32[]{:S(2)}) collective-permute-start(bf16[400,512]{1,0:T(8,128)(2,1)S(1)} %get-tuple-element.142), channel_id=1, source_target_pairs={{0,1},{1,0},{2,3},{3,2},{4,5},{5,4},{6,7},{7,6}} | collective-permute-start | bytes 1228808 | tf_op jit(solution)/shard_map/ppermute | solution.py:486
  108.0 35.4 %collective-permute-start.13 = (bf16[400,2048]{1,0:T(8,128)(2,1)S(1)}, bf16[400,2048]{1,0:T(8,128)(2,1)S(1)}, u32[]{:S(2)}, u32[]{:S(2)}) collective-permute-start(bf16[400,2048]{1,0:T(8,128)(2,1)S(1)} %shard_map.136), channel_id=1, source_target_pairs={{0,3},{1,0},{2,1},{3,2},{4,7},{5,4},{6,5},{7,6}} | collective-permute-start | bytes 4915208 | tf_op jit(solution)/shard_map/ppermute | solution.py:489
  112.3 2.9 collective-permute-start.11
  112.8 23.5 %collective-permute-start.9 = (bf16[400,512]{1,0:T(8,128)(2,1)S(1)}, bf16[400,512]{1,0:T(8,128)(2,1)S(1)}, u32[]{:S(2)}, u32[]{:S(2)}) collective-permute-start(bf16[400,512]{1,0:T(8,128)(2,1)S(1)} %add.87), channel_id=1, source_target_pairs={{0,2},{1,3},{2,0},{3,1},{4,6},{5,7},{6,4},{7,5}} | collective-permute-start | bytes 1228808 | tf_op jit(solution)/shard_map/ppermute | solution.py:489
  149.4 2.4 collective-permute-start.14
  149.6 38.2 %collective-permute-start.18 = (bf16[400,2048]{1,0:T(8,128)(2,1)S(1)}, bf16[400,2048]{1,0:T(8,128)(2,1)S(1)}, u32[]{:S(2)}, u32[]{:S(2)}) collective-permute-start(bf16[400,2048]{1,0:T(8,128)(2,1)S(1)} %shard_map.137.refs_2_.hb), channel_id=1, source_target_pairs={{0,1},{1,2},{2,3},{3,0},{4,5},{5,6},{6,7},{7,4}} | collective-permute-start | bytes 4915208 | tf_op jit(solution)/shard_map/ppermute | solution.py:489
  163.0 2.8 collective-permute-start.16
  163.1 38.7 %collective-permute-start.15 = (f32[200,1024]{1,0:T(8,128)}, f32[200,1024]{1,0:T(8,128)S(1)}, u32[]{:S(2)}, u32[]{:S(2)}) collective-permute-start(f32[200,1024]{1,0:T(8,128)} %add.90), channel_id=1, source_target_pairs={{0,2},{1,3},{2,0},{3,1},{4,6},{5,7},{6,4},{7,5}} | collective-permute-start | bytes 2457608 | tf_op jit(solution)/shard_map/ppermute | solution.py:489
  164.9 22.9 %collective-permute-start.17 = (f32[1,2048]{1,0:T(1,128)S(1)}, f32[1,2048]{1,0:T(1,128)S(1)}, u32[]{:S(2)}, u32[]{:S(2)}) collective-permute-start(f32[1,2048]{1,0:T(1,128)S(1)} %get-tuple-element.167.dp), channel_id=1, source_target_pairs={{0,1},{1,2},{2,3},{3,0},{4,5},{5,6},{6,7},{7,4}} | collective-permute-start | bytes 24584 | tf_op jit(solution)/shard_map/ppermute | solution.py:489
  203.2 2.4 collective-permute-start.19
  203.2 37.6 %collective-permute-start.23 = (f32[200,1408]{1,0:T(8,128)S(1)}, f32[200,1408]{1,0:T(8,128)S(1)}, u32[]{:S(2)}, u32[]{:S(2)}) collective-permute-start(f32[200,1408]{1,0:T(8,128)S(1)} %add.91), channel_id=1, source_target_pairs={{0,2},{1,3},{2,0},{3,1},{4,6},{5,7},{6,4},{7,5}} | collective-permute-start | bytes 3379208 | tf_op jit(solution)/shard_map/ppermute | solution.py:489
  205.0 25.8 %collective-permute-start.21 = (s32[2,2048]{1,0:T(2,128)S(1)}, s32[2,2048]{1,0:T(2,128)S(1)}, u32[]{:S(2)}, u32[]{:S(2)}) collective-permute-start(s32[2,2048]{1,0:T(2,128)S(1)} %pad_add_fusion.1), channel_id=1, source_target_pairs={{0,2},{1,3},{2,0},{3,1},{4,6},{5,7},{6,4},{7,5}} | collective-permute-start | bytes 49160 | tf_op jit(solution)/shard_map/ppermute | solution.py:489
  220.0 10.8 %collective-permute-start.20 = (bf16[400,512]{1,0:T(8,128)(2,1)S(1)}, bf16[400,512]{1,0:T(8,128)(2,1)S(1)}, u32[]{:S(2)}, u32[]{:S(2)}) collective-permute-start(bf16[400,512]{1,0:T(8,128)(2,1)S(1)} %get-tuple-element.178), channel_id=1, source_target_pairs={{0,1},{1,0},{2,3},{3,2},{4,5},{5,4},{6,7},{7,6}} | collective-permute-start | bytes 1228808 | tf_op jit(solution)/shard_map/ppermute | solution.py:486
  235.0 53.4 %collective-permute-start.26 = (bf16[400,2048]{1,0:T(8,128)(2,1)S(1)}, bf16[400,2048]{1,0:T(8,128)(2,1)S(1)}, u32[]{:S(2)}, u32[]{:S(2)}) collective-permute-start(bf16[400,2048]{1,0:T(8,128)(2,1)S(1)} %shard_map.144), channel_id=1, source_target_pairs={{0,2},{1,3},{2,0},{3,1},{4,6},{5,7},{6,4},{7,5}} | collective-permute-start | bytes 4915208 | tf_op jit(solution)/shard_map/ppermute | solution.py:489
  240.9 2.8 collective-permute-start.24
  241.0 40.1 %collective-permute-start.22 = (bf16[400,512]{1,0:T(8,128)(2,1)S(1)}, bf16[400,512]{1,0:T(8,128)(2,1)S(1)}, u32[]{:S(2)}, u32[]{:S(2)}) collective-permute-start(bf16[400,512]{1,0:T(8,128)(2,1)S(1)} %add.93), channel_id=1, source_target_pairs={{0,2},{1,3},{2,0},{3,1},{4,6},{5,7},{6,4},{7,5}} | collective-permute-start | bytes 1228808 | tf_op jit(solution)/shard_map/ppermute | solution.py:489
  294.3 2.4 collective-permute-start.27
  307.2 2.8 collective-permute-start.29
  307.4 65.7 %collective-permute-start.31 = (bf16[400,2048]{1,0:T(8,128)(2,1)S(1)}, bf16[400,2048]{1,0:T(8,128)(2,1)S(1)}, u32[]{:S(2)}, u32[]{:S(2)}) collective-permute-start(bf16[400,2048]{1,0:T(8,128)(2,1)S(1)} %shard_map.145.refs_2_.hb), channel_id=1, source_target_pairs={{0,2},{1,3},{2,0},{3,1},{4,6},{5,7},{6,4},{7,5}} | collective-permute-start | bytes 4915208 | tf_op jit(solution)/shard_map/ppermute | solution.py:489
  310.2 60.0 %collective-permute-start.33 = (f32[200,1408]{1,0:T(8,128)S(1)}, f32[200,1408]{1,0:T(8,128)S(1)}, u32[]{:S(2)}, u32[]{:S(2)}) collective-permute-start(f32[200,1408]{1,0:T(8,128)S(1)} %add.97), channel_id=1, source_target_pairs={{0,2},{1,3},{2,0},{3,1},{4,6},{5,7},{6,4},{7,5}} | collective-permute-start | bytes 3379208 | tf_op jit(solution)/shard_map/ppermute | solution.py:489
  311.9 94.1 %collective-permute-start.28 = (f32[200,1024]{1,0:T(8,128)S(1)}, f32[200,1024]{1,0:T(8,128)S(1)}, u32[]{:S(2)}, u32[]{:S(2)}) collective-permute-start(f32[200,1024]{1,0:T(8,128)S(1)} %add.96), channel_id=1, source_target_pairs={{0,2},{1,3},{2,0},{3,1},{4,6},{5,7},{6,4},{7,5}} | collective-permute-start | bytes 2457608 | tf_op jit(solution)/shard_map/ppermute | solution.py:489
  371.3 65.4 %collective-permute-start.34 = (f32[200,1408]{1,0:T(8,128)}, f32[200,1408]{1,0:T(8,128)}, u32[]{:S(2)}, u32[]{:S(2)}) collective-permute-start(f32[200,1408]{1,0:T(8,128)} %add.99), channel_id=1, source_target_pairs={{0,1},{1,0},{2,3},{3,2},{4,5},{5,4},{6,7},{7,6}} | collective-permute-start | bytes 3379208 | tf_op jit(solution)/shard_map/ppermute | solution.py:496
  371.3 16.0 %collective-permute-start.30 = (f32[1,2048]{1,0:T(1,128)S(1)}, f32[1,2048]{1,0:T(1,128)S(1)}, u32[]{:S(2)}, u32[]{:S(2)}) collective-permute-start(f32[1,2048]{1,0:T(1,128)S(1)} %get-tuple-element.204.dp), channel_id=1, source_target_pairs={{0,2},{1,3},{2,0},{3,1},{4,6},{5,7},{6,4},{7,5}} | collective-permute-start | bytes 24584 | tf_op jit(solution)/shard_map/ppermute | solution.py:489
  406.1 2.5 collective-permute-start.32
  (17 other events, 118.5 us)

commit v10 on v9

--- a/solution.py
+++ b/solution.py
@@ -13,6 +13,7 @@
 LANES = 128
 SLICES = 4
 CHUNK = 256
+WIDE = 512
 BATCH = 4
 F32 = jnp.float32
 BF16 = jnp.bfloat16
@@ -205,28 +206,28 @@
     nb[:, pl.ds(pl.multiple_of((1 - core) * nhalf, LANES), nhalf)] = nother[...]
 
 
-def exp_kernel(neg_count, edges, core_ref, q, nfull, nother, e_out, top_out, sum_out, nb, nbt, sc):
+def exp_kernel(neg_count, edges, core_ref, q, nfull, nother, e_out, top_out, sum_out, nb, nbt):
     negp = nb.shape[1]
     place_negs(core_ref[0], nb, nfull, nother)
     for b in range(negp // LANES):
         nbt[pl.ds(b * LANES, LANES), :] = nb[:, pl.ds(b * LANES, LANES)].astype(F32).T.astype(BF16)
 
     def step(c, _):
-        cols = pl.ds(pl.multiple_of(c * CHUNK, LANES), CHUNK)
-        sc[...] = lax.dot_general(nbt[pl.ds(0, neg_count), :], q[:, cols].astype(BF16), (((1,), (0,)), ((), ())), preferred_element_type=F32)
-        top = jnp.max(sc[...], axis=0, keepdims=True)
+        cols = pl.ds(pl.multiple_of(c * WIDE, LANES), WIDE)
+        e_out[:, cols] = lax.dot_general(nbt[pl.ds(0, neg_count), :], q[:, cols].astype(BF16), (((1,), (0,)), ((), ())), preferred_element_type=F32)
+        top = jnp.max(e_out[:, cols], axis=0, keepdims=True)
         top_out[:, cols] = top
-        total = jnp.zeros((1, CHUNK), F32)
+        total = jnp.zeros((1, WIDE), F32)
         part = 200
         for i in range(0, neg_count, part):
             size = min(part, neg_count - i)
-            e = jnp.exp(sc[pl.ds(i, size), :] - top)
+            e = jnp.exp(e_out[pl.ds(i, size), cols] - top)
             e_out[pl.ds(i, size), cols] = e
             total = total + jnp.sum(e, axis=0, keepdims=True)
         sum_out[:, cols] = total
         return 0
 
-    lax.fori_loop(0, edges // CHUNK, step, 0)
+    lax.fori_loop(0, edges // WIDE, step, 0)
 
 
 def score_kernel(dim, neg_count, edges, core_ref, w, q, tb, e, neg_top, neg_sum,
@@ -237,7 +238,7 @@
     ds[pl.ds(neg_count, negp - neg_count), :] = jnp.zeros((negp - neg_count, edges), BF16)
 
     def step(c, loss_row):
-        cols = pl.ds(pl.multiple_of(c * CHUNK, LANES), CHUNK)
+        cols = pl.ds(pl.multiple_of(c * WIDE, LANES), WIDE)
         pos = jnp.sum(q[:, cols] * tb[:, cols].astype(F32), axis=0, keepdims=True)
         top = jnp.maximum(pos, neg_top[:, cols])
         pos_exp = jnp.exp(pos - top)
@@ -250,7 +251,7 @@
         ng[...] += lax.dot_general(ds[:, cols], q[:, cols].astype(BF16), (((1,), (1,)), ((), ())), preferred_element_type=F32)
         return loss_row
 
-    loss_row = lax.fori_loop(0, edges // CHUNK, step, jnp.zeros((1, CHUNK), F32))
+    loss_row = lax.fori_loop(0, edges // WIDE, step, jnp.zeros((1, WIDE), F32))
     loss[...] = jnp.broadcast_to(jnp.sum(loss_row, axis=1, keepdims=True) / edges, loss.shape)
 
     def save(b, _):
@@ -542,7 +543,7 @@
         t4, nk, ns = call(
             functools.partial(entry_kernel, dim, rows), [core, negs[0], ent_emb.T], 'ssh',
             [table_out, neg_half, neg_half], 'VVV',
-            [pltpu.VMEM((4, SLICES * LANES, 4 * LANES), F32), stage_shape, pltpu.VMEM((dim, negp), BF16), pltpu.SemaphoreType.DMA((4,))], 20, 'entry')
+            [pltpu.VMEM((8, SLICES * LANES, 4 * LANES), F32), stage_shape, pltpu.VMEM((dim, negp), BF16), pltpu.SemaphoreType.DMA((8,))], 20, 'entry')
         v = ent_ada.reshape(rows // LANES, LANES)
 
         rfm = jnp.pad(rel_emb.T, ((0, 0), (0, relp - num_rel)))
@@ -594,7 +595,7 @@
             e, neg_top, neg_total = call(
                 functools.partial(exp_kernel, neg_count, edges), [core, q, nmine, nother], 'sVVV',
                 [shape((neg_count, edges)), shape((1, edges)), shape((1, edges))], 'Vvv',
-                [pltpu.VMEM((dim, negp), BF16), pltpu.VMEM((negp, dim), BF16), pltpu.VMEM((neg_count, CHUNK), F32)], 8, 'exp')
+                [pltpu.VMEM((dim, negp), BF16), pltpu.VMEM((negp, dim), BF16)], 8, 'exp')
             if not first:
                 e, tail_cols = tie((e, tail_cols))
                 if not even_load:

time: 442 us -> 437 us (0.989)
  Pallas kernels: 196 us -> 191 us
    pallas_call x24, Pallas kernels: 196 us -> 191 us  [call(): pl.pallas_call(kernel, out_shape=outs, in_specs=[places[k]() for k in kin...]
  transfers between devices with their start and end apart: 35 -> 35, of which waited for: 23 -> 23; matrix products, arithmetic and copies ran while one was open for 1% -> 1% of each run, Pallas kernels for 32% -> 33%
where the time goes in v10:
time: 437 us; the launch traced here: 436 us
  waiting for transfers between devices  194 us (44%)
  Pallas kernels  191 us (44%)
  local copies, waits for them, and re-layouts  20.7 us (5%)
  starting transfers between devices  18.5 us (4%)
  other arithmetic  11 us (3%)
    pallas_call x24, Pallas kernels, call(): pl.pallas_call(kernel, out_shape=outs, in_specs=[places[k]() for k in kin...  191 us
    ppermute x17, waiting for transfers between devices, send(): return lax.ppermute(value, 'ent', pairs)  169 us
    unnamed x29, local copies, waits for them, and re-layouts  19.9 us
    ppermute x17, starting transfers between devices, send(): return lax.ppermute(value, 'ent', pairs)  15.6 us
    ppermute x9, waiting for transfers between devices, finish(): return (mine, lax.ppermute(mine, 'ent', swap))  13.6 us
    ppermute x9, waiting for transfers between devices, chip_sum(): return keep + lax.ppermute(send, 'ent', swap)  11 us
  transfers between devices with their start and end apart: 35, of which 23 were waited for; matrix products, arithmetic and copies ran while one was open for 1% of the time, Pallas kernels for 33%

profile of v10, /device:TPU:0, one launch (start us, length us, event | category | flops | bytes accessed | tf_op | source)
XLA Modules:
  0.0 436.4 jit_solution(12597731751789285855)
XLA Ops:
  2.2 9.1 %shard_map.128 = (f32[32800,128]{1,0:T(8,128)S(1)}, bf16[400,512]{1,0:T(8,128)(2,1)S(1)}, bf16[400,512]{1,0:T(8,128)(2,1)S(1)}) custom-call(s32[1]{0:T(128)} %bitcast.core_ref.refs_0_, s32[1024]{0:T(1024)S(1)} %bitcast.66, f32[400,8192]{1,0:T(8,128)} %bitcast.75), custom_call_target="tpu_custom_call" | custom-call | flops 100000000 | tf_op jit(solution)/shard_map/pallas_call | solution.py:534
  16.5 7.5 %shard_map.129 = (bf16[400,2048]{1,0:T(8,128)(2,1)S(1)}, bf16[400,2048]{1,0:T(8,128)(2,1)S(1)}) custom-call(s32[2048]{0:T(1024)S(1)} %bitcast.58, s32[2048]{0:T(1024)S(1)} %bitcast.60, f32[32800,128]{1,0:T(8,128)S(1)} %get-tuple-element.116.refs_2_.refs_3_), custom_call_target="tpu_custom_call" | custom-call | flops 55000000 | tf_op jit(solution)/shard_map/pallas_call | solution.py:534
  24.0 5.3 %shard_map.130 = (f32[400,2048]{1,0:T(8,128)S(1)}, f32[400,2048]{1,0:T(8,128)S(1)}) custom-call(s32[1]{0:T(128)} %bitcast.core_ref.refs_0_, s32[2048]{0:T(1024)S(1)} %bitcast.62, bf16[400,2048]{1,0:T(8,128)(2,1)S(1)} %get-tuple-element.120.refs_2_.hb, f32[400,1408]{1,0:T(8,128)S(1)} %pad.13.refs_3_), custom_call_target="tpu_custom_call" | custom-call | flops 50000000 | tf_op jit(solution)/shard_map/pallas_call | solution.py:534
  31.2 4.9 %shard_map.131 = (f32[1000,2048]{1,0:T(8,128)S(1)}, f32[1,2048]{1,0:T(1,128)S(1)}, f32[1,2048]{1,0:T(1,128)S(1)}) custom-call(s32[1]{0:T(128)} %bitcast.core_ref.refs_0_, f32[400,2048]{1,0:T(8,128)S(1)} %get-tuple-element.122.q.refs_4_, bf16[400,512]{1,0:T(8,128)(2,1)S(1)} %add.83.nfull, bf16[400,512]{1,0:T(8,128)(2,1)S(1)} %collective-permute-done.2.nother), custom_call_target="tpu_custom_call" | custom-call | flops 40000000 | tf_op jit(solution)/shard_map/pallas_call | solution.py:534
  36.1 5.0 %shard_map.132 = (f32[1,128]{1,0:T(1,128)S(1)}, f32[1,2048]{1,0:T(1,128)S(1)}, bf16[1024,2048]{1,0:T(8,128)(2,1)S(1)}, f32[200,1024]{1,0:T(8,128)S(1)}, f32[200,1024]{1,0:T(8,128)S(1)}) custom-call(s32[1]{0:T(128)} %bitcast.core_ref.refs_0_, f32[1,2048]{1,0:T(1,128)S(1)} %get-tuple-element.230.w, f32[400,2048]{1,0:T(8,128)S(1)} %get-tuple-element.122.q.refs_4_, ...), custom_call_target="tpu_custom_call" | custom-call | flops 40000000 | tf_op jit(solution)/shard_map/pallas_call | solution.py:534
  43.6 10.2 %shard_map.133 = (f32[8192,128]{1,0:T(8,128)S(1)}, f32[200,1408]{1,0:T(8,128)S(1)}, f32[200,1408]{1,0:T(8,128)S(1)}) custom-call(s32[1]{0:T(128)} %bitcast.core_ref.refs_0_, s32[2048]{0:T(1024)S(1)} %bitcast.63, bf16[1024,2048]{1,0:T(8,128)(2,1)S(1)} %get-tuple-element.132.ds, f32[1,2048]{1,0:T(1,128)S(1)} %get-tuple-element.133.dp.refs_3_, ...), custom_call_target="tpu_custom_call" | custom-call | flops 60000000 | tf_op jit(solution)/shard_map/pallas_call | solution.py:534
  56.7 10.0 %shard_map.134.refs_5_ = f32[32800,128]{1,0:T(8,128)S(1)} custom-call(s32[2048]{0:T(1024)S(1)} %bitcast.61, s32[2048]{0:T(1024)S(1)} %bitcast.59, f32[8192,128]{1,0:T(8,128)S(1)} %get-tuple-element.138.refs_2_, f32[1,2048]{1,0:T(1,128)S(1)} %get-tuple-element.133.dp.refs_3_, f32[400,2048]{1,0:T(8,128)S(1)} %get-tuple-element.122.q.refs_4_), custom_call_target="tpu_custom_call" | custom-call | flops 75000000 | tf_op jit(solution)/shard_map/pallas_call | solution.py:534
  66.7 7.8 %collective-permute-done.4 = f32[200,1024]{1,0:T(8,128)S(1)} collective-permute-done((f32[200,1024]{1,0:T(8,128)S(1)}, f32[200,1024]{1,0:T(8,128)S(1)}, u32[]{:S(2)}, u32[]{:S(2)}) %collective-permute-start.4) | collective-permute-done | bytes 819232 | tf_op jit(solution)/shard_map/ppermute | solution.py:490
  76.9 14.5 %shard_map.135 = (f32[32800,128]{1,0:T(8,128)S(1)}, f32[32800,128]{1,0:T(8,128)S(1)}, f32[64,128]{1,0:T(8,128)S(1)}, bf16[400,512]{1,0:T(8,128)(2,1)S(1)}, bf16[400,512]{1,0:T(8,128)(2,1)S(1)}) custom-call(s32[1]{0:T(128)} %bitcast.core_ref.refs_0_, s32[1024]{0:T(1024)S(1)} %bitcast.67, ...), custom_call_target="tpu_custom_call", output_to_operand_aliasing={{0}: (5, {}), {1}: (3, {}), {2}: (4, {})} | custom-call | flops 150000000 | tf_op jit(solution)/shard_map/pallas_call | solution.py:534
  91.6 10.1 %collective-permute-done.8 = s32[2,2048]{1,0:T(2,128)S(1)} collective-permute-done((s32[2,2048]{1,0:T(2,128)S(1)}, s32[2,2048]{1,0:T(2,128)S(1)}, u32[]{:S(2)}, u32[]{:S(2)}) %collective-permute-start.8) | collective-permute-done | bytes 16416 | tf_op jit(solution)/shard_map/ppermute | solution.py:490
  105.9 4.2 shard_map.137.refs_2_.hb
  113.2 5.7 %shard_map.138 = (f32[400,2048]{1,0:T(8,128)S(1)}, f32[400,2048]{1,0:T(8,128)S(1)}, f32[5632,128]{1,0:T(8,128)}, f32[400,1408]{1,0:T(8,128)S(1)}, f32[1,1408]{1,0:T(1,128)S(1)}) custom-call(s32[1]{0:T(128)} %bitcast.core_ref.refs_0_, s32[2048]{0:T(1024)S(1)} %bitcast.48, bf16[400,2048]{1,0:T(8,128)(2,1)S(1)} %shard_map.137.refs_2_.hb, ...), custom_call_target="tpu_custom_call" | custom-call | flops 50000000 | tf_op jit(solution)/shard_map/pallas_call | solution.py:534
  118.9 15.1 %collective-permute-done.9 = bf16[400,512]{1,0:T(8,128)(2,1)S(1)} collective-permute-done((bf16[400,512]{1,0:T(8,128)(2,1)S(1)}, bf16[400,512]{1,0:T(8,128)(2,1)S(1)}, u32[]{:S(2)}, u32[]{:S(2)}) %collective-permute-start.9) | collective-permute-done | bytes 409632 | tf_op jit(solution)/shard_map/ppermute | solution.py:490
  135.9 4.9 %shard_map.139 = (f32[1000,2048]{1,0:T(8,128)S(1)}, f32[1,2048]{1,0:T(1,128)S(1)}, f32[1,2048]{1,0:T(1,128)S(1)}) custom-call(s32[1]{0:T(128)} %bitcast.core_ref.refs_0_, f32[400,2048]{1,0:T(8,128)S(1)} %get-tuple-element.154.q, bf16[400,512]{1,0:T(8,128)(2,1)S(1)} %add.89.nfull, bf16[400,512]{1,0:T(8,128)(2,1)S(1)} %collective-permute-done.12.nother), custom_call_target="tpu_custom_call" | custom-call | flops 40000000 | tf_op jit(solution)/shard_map/pallas_call | solution.py:534
  140.8 5.0 %shard_map.140 = (f32[1,128]{1,0:T(1,128)S(1)}, f32[1,2048]{1,0:T(1,128)S(1)}, bf16[1024,2048]{1,0:T(8,128)(2,1)S(1)}, f32[200,1024]{1,0:T(8,128)S(1)}, f32[200,1024]{1,0:T(8,128)S(1)}) custom-call(s32[1]{0:T(128)} %bitcast.core_ref.refs_0_, f32[1,2048]{1,0:T(1,128)S(1)} %get-tuple-element.229.w, f32[400,2048]{1,0:T(8,128)S(1)} %get-tuple-element.154.q, ...), custom_call_target="tpu_custom_call" | custom-call | flops 40000000 | tf_op jit(solution)/shard_map/pallas_call | solution.py:534
  149.2 10.2 %shard_map.141 = (f32[8192,128]{1,0:T(8,128)S(1)}, f32[200,1408]{1,0:T(8,128)S(1)}, f32[200,1408]{1,0:T(8,128)S(1)}) custom-call(s32[1]{0:T(128)} %bitcast.core_ref.refs_0_, s32[2048]{0:T(1024)S(1)} %bitcast.49, bf16[1024,2048]{1,0:T(8,128)(2,1)S(1)} %get-tuple-element.166.ds, f32[1,2048]{1,0:T(1,128)S(1)} %get-tuple-element.167.dp, ...), custom_call_target="tpu_custom_call" | custom-call | flops 60000000 | tf_op jit(solution)/shard_map/pallas_call | solution.py:534
  162.3 21.8 %collective-permute-done.17.refs_4_ = f32[1,2048]{1,0:T(1,128)S(1)} collective-permute-done((f32[1,2048]{1,0:T(1,128)S(1)}, f32[1,2048]{1,0:T(1,128)S(1)}, u32[]{:S(2)}, u32[]{:S(2)}) %collective-permute-start.17) | collective-permute-done | bytes 8224 | tf_op jit(solution)/shard_map/ppermute | solution.py:490
  185.3 12.9 %shard_map.142.refs_5_ = f32[32800,128]{1,0:T(8,128)S(1)} custom-call(s32[2048]{0:T(1024)S(1)} %bitcast.53, s32[2048]{0:T(1024)S(1)} %bitcast.57, s32[2048]{0:T(1024)S(1)} %bitcast.71, f32[8192,128]{1,0:T(8,128)S(1)} %get-tuple-element.173.refs_3_, f32[1,2048]{1,0:T(1,128)S(1)} %collective-permute-done.17.refs_4_, bf16[400,2048]{1,0:T(8,128)(2,1)} %copy-done.7, ...), custom_call_target="tpu_custom_call" | custom-call | flops 75000000 | tf_op jit(solution)/shard_map/pallas_call | solution.py:534
  201.9 14.5 %shard_map.143 = (f32[32800,128]{1,0:T(8,128)S(1)}, f32[32800,128]{1,0:T(8,128)S(1)}, f32[64,128]{1,0:T(8,128)S(1)}, bf16[400,512]{1,0:T(8,128)(2,1)S(1)}, bf16[400,512]{1,0:T(8,128)(2,1)S(1)}) custom-call(s32[1]{0:T(128)} %bitcast.core_ref.refs_0_, s32[1024]{0:T(1024)S(1)} %bitcast.69, ...), custom_call_target="tpu_custom_call", output_to_operand_aliasing={{0}: (5, {}), {1}: (3, {}), {2}: (4, {})} | custom-call | flops 150000000 | tf_op jit(solution)/shard_map/pallas_call | solution.py:534
  216.6 10.6 %collective-permute-done.21 = s32[2,2048]{1,0:T(2,128)S(1)} collective-permute-done((s32[2,2048]{1,0:T(2,128)S(1)}, s32[2,2048]{1,0:T(2,128)S(1)}, u32[]{:S(2)}, u32[]{:S(2)}) %collective-permute-start.21) | collective-permute-done | bytes 16416 | tf_op jit(solution)/shard_map/ppermute | solution.py:490
  240.1 5.9 %shard_map.146 = (f32[400,2048]{1,0:T(8,128)S(1)}, f32[400,2048]{1,0:T(8,128)S(1)}, f32[5632,128]{1,0:T(8,128)}, f32[400,1408]{1,0:T(8,128)S(1)}, f32[1,1408]{1,0:T(1,128)S(1)}) custom-call(s32[1]{0:T(128)} %bitcast.core_ref.refs_0_, s32[2048]{0:T(1024)S(1)} %bitcast.45, bf16[400,2048]{1,0:T(8,128)(2,1)S(1)} %shard_map.145.refs_2_.hb, ...), custom_call_target="tpu_custom_call" | custom-call | flops 50000000 | tf_op jit(solution)/shard_map/pallas_call | solution.py:534
  246.0 31.5 %collective-permute-done.22 = bf16[400,512]{1,0:T(8,128)(2,1)S(1)} collective-permute-done((bf16[400,512]{1,0:T(8,128)(2,1)S(1)}, bf16[400,512]{1,0:T(8,128)(2,1)S(1)}, u32[]{:S(2)}, u32[]{:S(2)}) %collective-permute-start.22) | collective-permute-done | bytes 409632 | tf_op jit(solution)/shard_map/ppermute | solution.py:490
  279.3 4.9 %shard_map.147 = (f32[1000,2048]{1,0:T(8,128)S(1)}, f32[1,2048]{1,0:T(1,128)S(1)}, f32[1,2048]{1,0:T(1,128)S(1)}) custom-call(s32[1]{0:T(128)} %bitcast.core_ref.refs_0_, f32[400,2048]{1,0:T(8,128)S(1)} %get-tuple-element.192.q, bf16[400,512]{1,0:T(8,128)(2,1)S(1)} %add.95.nfull, bf16[400,512]{1,0:T(8,128)(2,1)S(1)} %collective-permute-done.25.nother), custom_call_target="tpu_custom_call" | custom-call | flops 40000000 | tf_op jit(solution)/shard_map/pallas_call | solution.py:534
  284.2 5.0 %shard_map.148 = (f32[1,128]{1,0:T(1,128)S(1)}, f32[1,2048]{1,0:T(1,128)S(1)}, bf16[1024,2048]{1,0:T(8,128)(2,1)S(1)}, f32[200,1024]{1,0:T(8,128)S(1)}, f32[200,1024]{1,0:T(8,128)S(1)}) custom-call(s32[1]{0:T(128)} %bitcast.core_ref.refs_0_, f32[1,2048]{1,0:T(1,128)S(1)} %get-tuple-element.228.w, f32[400,2048]{1,0:T(8,128)S(1)} %get-tuple-element.192.q, ...), custom_call_target="tpu_custom_call" | custom-call | flops 40000000 | tf_op jit(solution)/shard_map/pallas_call | solution.py:534
  291.6 10.2 %shard_map.149 = (f32[8192,128]{1,0:T(8,128)S(1)}, f32[200,1408]{1,0:T(8,128)S(1)}, f32[200,1408]{1,0:T(8,128)S(1)}) custom-call(s32[1]{0:T(128)} %bitcast.core_ref.refs_0_, s32[2048]{0:T(1024)S(1)} %bitcast.46, bf16[1024,2048]{1,0:T(8,128)(2,1)S(1)} %get-tuple-element.203.ds, f32[1,2048]{1,0:T(1,128)S(1)} %get-tuple-element.204.dp, ...), custom_call_target="tpu_custom_call" | custom-call | flops 60000000 | tf_op jit(solution)/shard_map/pallas_call | solution.py:534
  306.9 58.0 %collective-permute-done.33 = f32[200,1408]{1,0:T(8,128)S(1)} collective-permute-done((f32[200,1408]{1,0:T(8,128)S(1)}, f32[200,1408]{1,0:T(8,128)S(1)}, u32[]{:S(2)}, u32[]{:S(2)}) %collective-permute-start.33) | collective-permute-done | bytes 1126432 | tf_op jit(solution)/shard_map/ppermute | solution.py:490
  367.8 14.2 %collective-permute-done.30.refs_4_ = f32[1,2048]{1,0:T(1,128)S(1)} collective-permute-done((f32[1,2048]{1,0:T(1,128)S(1)}, f32[1,2048]{1,0:T(1,128)S(1)}, u32[]{:S(2)}, u32[]{:S(2)}) %collective-permute-start.30) | collective-permute-done | bytes 8224 | tf_op jit(solution)/shard_map/ppermute | solution.py:490
  382.0 12.9 %shard_map.150.refs_4_ = f32[32800,128]{1,0:T(8,128)S(1)} custom-call(s32[2048]{0:T(1024)S(1)} %bitcast.51, s32[2048]{0:T(1024)S(1)} %bitcast.55, s32[2048]{0:T(1024)S(1)} %bitcast.70, f32[8192,128]{1,0:T(8,128)S(1)} %get-tuple-element.209.refs_3_, f32[1,2048]{1,0:T(1,128)S(1)} %collective-permute-done.30.refs_4_, bf16[400,2048]{1,0:T(8,128)(2,1)} %copy-done.8, ...), custom_call_target="tpu_custom_call" | custom-call | flops 75000000 | tf_op jit(solution)/shard_map/pallas_call | solution.py:534
  394.9 5.8 %copy-done.2 = f32[32800,128]{1,0:T(8,128)} copy-done((f32[32800,128]{1,0:T(8,128)}, f32[32800,128]{1,0:T(8,128)S(1)}, u32[]{:S(2)}) %copy-start.2) | copy-done | bytes 16793624
  403.3 5.8 %copy-done.1 = f32[32800,128]{1,0:T(8,128)S(1)} copy-done((f32[32800,128]{1,0:T(8,128)S(1)}, f32[32800,128]{1,0:T(8,128)}, u32[]{:S(2)}) %copy-start.1) | copy-done | bytes 16793624
  409.1 5.8 %copy-done.3 = f32[32800,128]{1,0:T(8,128)S(1)} copy-done((f32[32800,128]{1,0:T(8,128)S(1)}, f32[32800,128]{1,0:T(8,128)}, u32[]{:S(2)}) %copy-start.3) | copy-done | bytes 16793624
  414.8 16.6 %shard_map.151 = (f32[32800,128]{1,0:T(8,128)S(1)}, f32[400,8192]{1,0:T(8,128)}, f32[64,128]{1,0:T(8,128)}) custom-call(s32[1]{0:T(128)} %bitcast.core_ref.refs_0_, s32[1024]{0:T(1024)S(1)} %bitcast.65, f32[32800,128]{1,0:T(8,128)S(1)} %copy-done.1, f32[64,128]{1,0:T(8,128)S(1)} %get-tuple-element.184.refs_3_, ...), custom_call_target="tpu_custom_call", output_to_operand_aliasing={{0}: (4, {})} | custom-call | flops 150000000 | tf_op jit(solution)/shard_map/pallas_call | solution.py:534
  (129 shorter events, 69.6 us)
Async XLA Ops:
  11.3 2.2 collective-permute-start
  13.6 15.7 %collective-permute-start.1 = (bf16[400,512]{1,0:T(8,128)(2,1)S(1)}, bf16[400,512]{1,0:T(8,128)(2,1)S(1)}, u32[]{:S(2)}, u32[]{:S(2)}) collective-permute-start(bf16[400,512]{1,0:T(8,128)(2,1)S(1)} %add.82), channel_id=1, source_target_pairs={{0,2},{1,3},{2,0},{3,1},{4,6},{5,7},{6,4},{7,5}} | collective-permute-start | bytes 1228808 | tf_op jit(solution)/shard_map/ppermute | solution.py:490
  41.1 2.4 collective-permute-start.3
  53.8 2.8 collective-permute-start.5
  54.0 20.5 %collective-permute-start.4 = (f32[200,1024]{1,0:T(8,128)S(1)}, f32[200,1024]{1,0:T(8,128)S(1)}, u32[]{:S(2)}, u32[]{:S(2)}) collective-permute-start(f32[200,1024]{1,0:T(8,128)S(1)} %add.84), channel_id=1, source_target_pairs={{0,2},{1,3},{2,0},{3,1},{4,6},{5,7},{6,4},{7,5}} | collective-permute-start | bytes 2457608 | tf_op jit(solution)/shard_map/ppermute | solution.py:490
  74.6 2.4 collective-permute-start.6
  74.6 35.5 %collective-permute-start.10 = (f32[200,1408]{1,0:T(8,128)S(1)}, f32[200,1408]{1,0:T(8,128)S(1)}, u32[]{:S(2)}, u32[]{:S(2)}) collective-permute-start(f32[200,1408]{1,0:T(8,128)S(1)} %add.85), channel_id=1, source_target_pairs={{0,2},{1,3},{2,0},{3,1},{4,6},{5,7},{6,4},{7,5}} | collective-permute-start | bytes 3379208 | tf_op jit(solution)/shard_map/ppermute | solution.py:490
  74.9 26.8 %collective-permute-start.8 = (s32[2,2048]{1,0:T(2,128)S(1)}, s32[2,2048]{1,0:T(2,128)S(1)}, u32[]{:S(2)}, u32[]{:S(2)}) collective-permute-start(s32[2,2048]{1,0:T(2,128)S(1)} %pad_add_fusion), channel_id=1, source_target_pairs={{0,1},{1,2},{2,3},{3,0},{4,5},{5,6},{6,7},{7,4}} | collective-permute-start | bytes 49160 | tf_op jit(solution)/shard_map/ppermute | solution.py:490
  91.4 10.3 %collective-permute-start.7 = (bf16[400,512]{1,0:T(8,128)(2,1)S(1)}, bf16[400,512]{1,0:T(8,128)(2,1)S(1)}, u32[]{:S(2)}, u32[]{:S(2)}) collective-permute-start(bf16[400,512]{1,0:T(8,128)(2,1)S(1)} %get-tuple-element.142), channel_id=1, source_target_pairs={{0,1},{1,0},{2,3},{3,2},{4,5},{5,4},{6,7},{7,6}} | collective-permute-start | bytes 1228808 | tf_op jit(solution)/shard_map/ppermute | solution.py:487
  105.9 34.9 %collective-permute-start.13 = (bf16[400,2048]{1,0:T(8,128)(2,1)S(1)}, bf16[400,2048]{1,0:T(8,128)(2,1)S(1)}, u32[]{:S(2)}, u32[]{:S(2)}) collective-permute-start(bf16[400,2048]{1,0:T(8,128)(2,1)S(1)} %shard_map.136), channel_id=1, source_target_pairs={{0,3},{1,0},{2,1},{3,2},{4,7},{5,4},{6,5},{7,6}} | collective-permute-start | bytes 4915208 | tf_op jit(solution)/shard_map/ppermute | solution.py:490
  110.2 2.9 collective-permute-start.11
  110.8 23.3 %collective-permute-start.9 = (bf16[400,512]{1,0:T(8,128)(2,1)S(1)}, bf16[400,512]{1,0:T(8,128)(2,1)S(1)}, u32[]{:S(2)}, u32[]{:S(2)}) collective-permute-start(bf16[400,512]{1,0:T(8,128)(2,1)S(1)} %add.87), channel_id=1, source_target_pairs={{0,2},{1,3},{2,0},{3,1},{4,6},{5,7},{6,4},{7,5}} | collective-permute-start | bytes 1228808 | tf_op jit(solution)/shard_map/ppermute | solution.py:490
  145.8 2.4 collective-permute-start.14
  145.9 38.2 %collective-permute-start.18 = (bf16[400,2048]{1,0:T(8,128)(2,1)S(1)}, bf16[400,2048]{1,0:T(8,128)(2,1)S(1)}, u32[]{:S(2)}, u32[]{:S(2)}) collective-permute-start(bf16[400,2048]{1,0:T(8,128)(2,1)S(1)} %shard_map.137.refs_2_.hb), channel_id=1, source_target_pairs={{0,1},{1,2},{2,3},{3,0},{4,5},{5,6},{6,7},{7,4}} | collective-permute-start | bytes 4915208 | tf_op jit(solution)/shard_map/ppermute | solution.py:490
  159.4 2.8 collective-permute-start.16
  159.5 38.7 %collective-permute-start.15 = (f32[200,1024]{1,0:T(8,128)}, f32[200,1024]{1,0:T(8,128)S(1)}, u32[]{:S(2)}, u32[]{:S(2)}) collective-permute-start(f32[200,1024]{1,0:T(8,128)} %add.90), channel_id=1, source_target_pairs={{0,2},{1,3},{2,0},{3,1},{4,6},{5,7},{6,4},{7,5}} | collective-permute-start | bytes 2457608 | tf_op jit(solution)/shard_map/ppermute | solution.py:490
  161.3 22.9 %collective-permute-start.17 = (f32[1,2048]{1,0:T(1,128)S(1)}, f32[1,2048]{1,0:T(1,128)S(1)}, u32[]{:S(2)}, u32[]{:S(2)}) collective-permute-start(f32[1,2048]{1,0:T(1,128)S(1)} %get-tuple-element.167.dp), channel_id=1, source_target_pairs={{0,1},{1,2},{2,3},{3,0},{4,5},{5,6},{6,7},{7,4}} | collective-permute-start | bytes 24584 | tf_op jit(solution)/shard_map/ppermute | solution.py:490
  199.5 2.4 collective-permute-start.19
  199.6 37.6 %collective-permute-start.23 = (f32[200,1408]{1,0:T(8,128)S(1)}, f32[200,1408]{1,0:T(8,128)S(1)}, u32[]{:S(2)}, u32[]{:S(2)}) collective-permute-start(f32[200,1408]{1,0:T(8,128)S(1)} %add.91), channel_id=1, source_target_pairs={{0,2},{1,3},{2,0},{3,1},{4,6},{5,7},{6,4},{7,5}} | collective-permute-start | bytes 3379208 | tf_op jit(solution)/shard_map/ppermute | solution.py:490
  201.4 25.8 %collective-permute-start.21 = (s32[2,2048]{1,0:T(2,128)S(1)}, s32[2,2048]{1,0:T(2,128)S(1)}, u32[]{:S(2)}, u32[]{:S(2)}) collective-permute-start(s32[2,2048]{1,0:T(2,128)S(1)} %pad_add_fusion.1), channel_id=1, source_target_pairs={{0,2},{1,3},{2,0},{3,1},{4,6},{5,7},{6,4},{7,5}} | collective-permute-start | bytes 49160 | tf_op jit(solution)/shard_map/ppermute | solution.py:490
  216.4 10.8 %collective-permute-start.20 = (bf16[400,512]{1,0:T(8,128)(2,1)S(1)}, bf16[400,512]{1,0:T(8,128)(2,1)S(1)}, u32[]{:S(2)}, u32[]{:S(2)}) collective-permute-start(bf16[400,512]{1,0:T(8,128)(2,1)S(1)} %get-tuple-element.178), channel_id=1, source_target_pairs={{0,1},{1,0},{2,3},{3,2},{4,5},{5,4},{6,7},{7,6}} | collective-permute-start | bytes 1228808 | tf_op jit(solution)/shard_map/ppermute | solution.py:487
  231.3 52.9 %collective-permute-start.26 = (bf16[400,2048]{1,0:T(8,128)(2,1)S(1)}, bf16[400,2048]{1,0:T(8,128)(2,1)S(1)}, u32[]{:S(2)}, u32[]{:S(2)}) collective-permute-start(bf16[400,2048]{1,0:T(8,128)(2,1)S(1)} %shard_map.144), channel_id=1, source_target_pairs={{0,2},{1,3},{2,0},{3,1},{4,6},{5,7},{6,4},{7,5}} | collective-permute-start | bytes 4915208 | tf_op jit(solution)/shard_map/ppermute | solution.py:490
  237.3 2.8 collective-permute-start.24
  237.3 40.2 %collective-permute-start.22 = (bf16[400,512]{1,0:T(8,128)(2,1)S(1)}, bf16[400,512]{1,0:T(8,128)(2,1)S(1)}, u32[]{:S(2)}, u32[]{:S(2)}) collective-permute-start(bf16[400,512]{1,0:T(8,128)(2,1)S(1)} %add.93), channel_id=1, source_target_pairs={{0,2},{1,3},{2,0},{3,1},{4,6},{5,7},{6,4},{7,5}} | collective-permute-start | bytes 1228808 | tf_op jit(solution)/shard_map/ppermute | solution.py:490
  289.2 2.4 collective-permute-start.27
  301.9 2.8 collective-permute-start.29
  302.0 65.7 %collective-permute-start.31 = (bf16[400,2048]{1,0:T(8,128)(2,1)S(1)}, bf16[400,2048]{1,0:T(8,128)(2,1)S(1)}, u32[]{:S(2)}, u32[]{:S(2)}) collective-permute-start(bf16[400,2048]{1,0:T(8,128)(2,1)S(1)} %shard_map.145.refs_2_.hb), channel_id=1, source_target_pairs={{0,2},{1,3},{2,0},{3,1},{4,6},{5,7},{6,4},{7,5}} | collective-permute-start | bytes 4915208 | tf_op jit(solution)/shard_map/ppermute | solution.py:490
  304.8 60.0 %collective-permute-start.33 = (f32[200,1408]{1,0:T(8,128)S(1)}, f32[200,1408]{1,0:T(8,128)S(1)}, u32[]{:S(2)}, u32[]{:S(2)}) collective-permute-start(f32[200,1408]{1,0:T(8,128)S(1)} %add.97), channel_id=1, source_target_pairs={{0,2},{1,3},{2,0},{3,1},{4,6},{5,7},{6,4},{7,5}} | collective-permute-start | bytes 3379208 | tf_op jit(solution)/shard_map/ppermute | solution.py:490
  306.6 94.1 %collective-permute-start.28 = (f32[200,1024]{1,0:T(8,128)S(1)}, f32[200,1024]{1,0:T(8,128)S(1)}, u32[]{:S(2)}, u32[]{:S(2)}) collective-permute-start(f32[200,1024]{1,0:T(8,128)S(1)} %add.96), channel_id=1, source_target_pairs={{0,2},{1,3},{2,0},{3,1},{4,6},{5,7},{6,4},{7,5}} | collective-permute-start | bytes 2457608 | tf_op jit(solution)/shard_map/ppermute | solution.py:490
  366.0 65.4 %collective-permute-start.34 = (f32[200,1408]{1,0:T(8,128)}, f32[200,1408]{1,0:T(8,128)}, u32[]{:S(2)}, u32[]{:S(2)}) collective-permute-start(f32[200,1408]{1,0:T(8,128)} %add.99), channel_id=1, source_target_pairs={{0,1},{1,0},{2,3},{3,2},{4,5},{5,4},{6,7},{7,6}} | collective-permute-start | bytes 3379208 | tf_op jit(solution)/shard_map/ppermute | solution.py:497
  366.0 15.9 %collective-permute-start.30 = (f32[1,2048]{1,0:T(1,128)S(1)}, f32[1,2048]{1,0:T(1,128)S(1)}, u32[]{:S(2)}, u32[]{:S(2)}) collective-permute-start(f32[1,2048]{1,0:T(1,128)S(1)} %get-tuple-element.204.dp), channel_id=1, source_target_pairs={{0,2},{1,3},{2,0},{3,1},{4,6},{5,7},{6,4},{7,5}} | collective-permute-start | bytes 24584 | tf_op jit(solution)/shard_map/ppermute | solution.py:490
  400.8 2.5 collective-permute-start.32
  (17 other events, 115.5 us)

commit v11 on v10

--- a/solution.py
+++ b/solution.py
@@ -95,15 +95,20 @@
 
 
 def gather_out(dim, table, ids, out, stage, count):
-    def body(b, _):
-        gather_rows(table, ids, b * LANES, stage, LANES)
-        cols = pl.ds(pl.multiple_of(b * LANES, LANES), LANES)
-        for j in range(SLICES):
-            size = min(LANES, dim - j * LANES)
-            out[pl.ds(j * LANES, size), cols] = stage_cols(stage, j)[:size].astype(BF16)
-        return 0
-
-    lax.fori_loop(0, count // LANES, body, 0)
+    blocks = count // LANES
+    gather_rows(table, ids, 0, stage.at[0], LANES)
+
+    def body(i, _):
+        for slot in range(2):
+            b = 2 * i + slot
+            gather_rows(table, ids, jnp.minimum(b + 1, blocks - 1) * LANES, stage.at[1 - slot], LANES)
+            cols = pl.ds(pl.multiple_of(b * LANES, LANES), LANES)
+            for j in range(SLICES):
+                size = min(LANES, dim - j * LANES)
+                out[pl.ds(j * LANES, size), cols] = stage_cols(stage.at[slot], j)[:size].astype(BF16)
+        return 0
+
+    lax.fori_loop(0, blocks // 2, body, 0)
 
 
 def gather_negs(dim, core, table, negs, nk, ns, nbuf, stage):
@@ -179,23 +184,27 @@
                 block = fm[pl.ds(j * LANES, LANES), pl.ds(0, LANES)]
             r4[pl.ds(SLICES * b * LANES + j, LANES, stride=SLICES), :] = block.T
 
-    def step(b, _):
-        cols = pl.ds(pl.multiple_of(b * LANES, LANES), LANES)
-        gather_rows(r4, rel, b * LANES, stage, LANES)
-        for j in range(SLICES):
-            size = min(LANES, dim - j * LANES)
-            r_out[pl.ds(j * LANES, size), cols] = stage_cols(stage, j)[:size]
-        h = hb[:, cols].astype(F32)
-        r_re, r_im = r_out[pl.ds(0, half), cols], r_out[pl.ds(half, half), cols]
-        q_out[pl.ds(0, half), cols] = h[:half] * r_re - h[half:] * r_im
-        q_out[pl.ds(half, half), cols] = h[:half] * r_im + h[half:] * r_re
-        return 0
-
-    step(0, 0)
+    blocks = edges // LANES
+    gather_rows(r4, rel, 0, stage.at[0], LANES)
     if not first:
         save = pltpu.make_async_copy(r4, r4_out, out_sem)
         save.start()
-    lax.fori_loop(1, edges // LANES, step, 0)
+
+    def step(i, _):
+        for slot in range(2):
+            b = 2 * i + slot
+            gather_rows(r4, rel, jnp.minimum(b + 1, blocks - 1) * LANES, stage.at[1 - slot], LANES)
+            cols = pl.ds(pl.multiple_of(b * LANES, LANES), LANES)
+            for j in range(SLICES):
+                size = min(LANES, dim - j * LANES)
+                r_out[pl.ds(j * LANES, size), cols] = stage_cols(stage.at[slot], j)[:size]
+            h = hb[:, cols].astype(F32)
+            r_re, r_im = r_out[pl.ds(0, half), cols], r_out[pl.ds(half, half), cols]
+            q_out[pl.ds(0, half), cols] = h[:half] * r_re - h[half:] * r_im
+            q_out[pl.ds(half, half), cols] = h[:half] * r_im + h[half:] * r_re
+        return 0
+
+    lax.fori_loop(0, blocks // 2, step, 0)
     if not first:
         save.wait()
 
@@ -373,8 +382,8 @@
         cols = pl.ds(pl.multiple_of(b * LANES, LANES), LANES)
         rt[pl.ds(pl.multiple_of(core * half, 8), half), :] = nmine[:, cols]
         rt[pl.ds(pl.multiple_of((1 - core) * half, 8), half), :] = nother[:, cols]
-        unstage(rt, stage)
-        add_rows([(acc, negs, b * LANES, stage, 0)], LANES)
+        unstage(rt, stage.at[0])
+        add_rows([(acc, negs, b * LANES, stage.at[0], 0)], LANES)
         return 0
 
     lax.fori_loop(0, nmine.shape[1] // LANES, neg_step, 0)
@@ -519,6 +528,7 @@
 
         wide_rows = (rows + 8) * SLICES
         stage_shape = pltpu.VMEM((SLICES * LANES, LANES), F32)
+        pair_shape = pltpu.VMEM((2, SLICES * LANES, LANES), F32)
         square_shape = pltpu.VMEM((SLICES * LANES, LANES), F32)
         table_out, state_out = shape((wide_rows, LANES)), shape((rows // LANES, LANES))
         cols_bf = shape((dim, edges), BF16)
@@ -527,7 +537,7 @@
         def call(kernel, args, kinds, outs, out_kinds, scratch, micros, name, aliases=None):
             places = {'s': smem, 'h': hbm, 'v': vmem, 'V': vmem}
             windows = [a for a, k in zip(list(args) + outs, kinds + out_kinds) if k == 'v']
-            limit = (4 if name == 'grad' else 2) * 2 ** 20 + sum(padded_bytes(a.shape, a.dtype) for a in windows)
+            limit = int((4 if name == 'grad' else 1.75) * 2 ** 20) + sum(padded_bytes(a.shape, a.dtype) for a in windows)
             limit += sum(padded_bytes(a.shape, a.dtype) for a in scratch if getattr(a, 'memory_space', None) == pltpu.VMEM)
             args = [pltpu.with_memory_space_constraint(a, pltpu.VMEM if k == 'V' else pltpu.HBM) if k in 'Vh' else a for a, k in zip(args, kinds)]
             outs = [{'V': pltpu.VMEM, 'h': pltpu.HBM}[k](o.shape, o.dtype) if k in 'Vh' else o for o, k in zip(outs, out_kinds)]
@@ -538,12 +548,12 @@
 
         def gather(lists, t4):
             return call(functools.partial(gather_kernel, dim, len(lists)), lists + [t4], 's' * len(lists) + 'V',
-                        [cols_bf] * len(lists), 'V' * len(lists), [stage_shape], 1 + 5 * len(lists), 'gather')
+                        [cols_bf] * len(lists), 'V' * len(lists), [pair_shape], 1 + 5 * len(lists), 'gather')
 
         t4, nk, ns = call(
             functools.partial(entry_kernel, dim, rows), [core, negs[0], ent_emb.T], 'ssh',
             [table_out, neg_half, neg_half], 'VVV',
-            [pltpu.VMEM((8, SLICES * LANES, 4 * LANES), F32), stage_shape, pltpu.VMEM((dim, negp), BF16), pltpu.SemaphoreType.DMA((8,))], 20, 'entry')
+            [pltpu.VMEM((8, SLICES * LANES, 4 * LANES), F32), pair_shape, pltpu.VMEM((dim, negp), BF16), pltpu.SemaphoreType.DMA((8,))], 20, 'entry')
         v = ent_ada.reshape(rows // LANES, LANES)
 
         rfm = jnp.pad(rel_emb.T, ((0, 0), (0, relp - num_rel)))
@@ -577,7 +587,7 @@
             wide = shape((dim, edges))
             outs, out_kinds = [wide, wide], 'VV'
             rel_rows = pltpu.VMEM((relp * SLICES, LANES), F32)
-            scratch = [stage_shape, pltpu.VMEM((SLICES * LANES, relp), F32), rel_rows]
+            scratch = [pair_shape, pltpu.VMEM((SLICES * LANES, relp), F32), rel_rows]
             args, kinds = [core, own_rels[s], hb, rfm], 'ssV' + ('v' if first else 'V')
             if not first:
                 outs += [shape((relp * SLICES, LANES)), shape((dim, relp)), shape((1, relp))]
@@ -619,7 +629,7 @@
             rel_part = chip_sum(rk, rs)
             rel_part, hg = tie((rel_part, hg))
             rel_got = link(rel_part)
-            scratch = [stage_shape] + [pltpu.VMEM((2, SLICES * LANES, LANES), F32)] * 2
+            scratch = [stage_shape] + [pair_shape] * 2
             if first:
                 args, kinds = [heads[s], tails[s], hg, dp, q], 'ssVvV'
             else:
@@ -628,7 +638,7 @@
             acc, = call(functools.partial(scatter_kernel, dim, edges, first), args, kinds, [table_out], 'V', scratch, 15, 'scatter')
             neg_got, acc = tie((neg_got, acc))
             gmine, gother = finish(neg_part, neg_got)
-            scratch = [stage_shape, square_shape, pltpu.VMEM((2, 4, LANES, LANES) if last else (2, LANES, LANES), F32)]
+            scratch = [pair_shape, square_shape, pltpu.VMEM((2, 4, LANES, LANES) if last else (2, LANES, LANES), F32)]
             if last:
                 args, kinds = [core, negs[s], t4, v, acc], 'ssVVV'
                 outs, out_kinds = [table_out, shape((dim, rows)), shape((rows // LANES, LANES))], 'Vhv'

time: 437 us -> 433 us (level)
  Pallas kernels: 191 us -> 181 us
  waiting for transfers between devices: 194 us -> 199 us
    pallas_call x24, Pallas kernels: 191 us -> 181 us  [call(): pl.pallas_call(kernel, out_shape=outs, in_specs=[places[k]() for k in kin...]
    ppermute x17, waiting for transfers between devices: 169 us -> 177 us  [send(): return lax.ppermute(value, 'ent', pairs)]
  transfers between devices with their start and end apart: 35 -> 35, of which waited for: 23 -> 23; matrix products, arithmetic and copies ran while one was open for 1% -> 1% of each run, Pallas kernels for 33% -> 31%
where the time goes in v11:
time: 433 us; the launch traced here: 432 us
  waiting for transfers between devices  199 us (46%)
  Pallas kernels  181 us (42%)
  local copies, waits for them, and re-layouts  20.7 us (5%)
  starting transfers between devices  18.8 us (4%)
  other arithmetic  11.1 us (3%)
    pallas_call x24, Pallas kernels, call(): pl.pallas_call(kernel, out_shape=outs, in_specs=[places[k]() for k in kin...  181 us
    ppermute x17, waiting for transfers between devices, send(): return lax.ppermute(value, 'ent', pairs)  177 us
    unnamed x29, local copies, waits for them, and re-layouts  19.9 us
    ppermute x17, starting transfers between devices, send(): return lax.ppermute(value, 'ent', pairs)  15.9 us
    ppermute x9, waiting for transfers between devices, chip_sum(): return keep + lax.ppermute(send, 'ent', swap)  12 us
    ppermute x9, waiting for transfers between devices, finish(): return (mine, lax.ppermute(mine, 'ent', swap))  9.88 us
  transfers between devices with their start and end apart: 35, of which 23 were waited for; matrix products, arithmetic and copies ran while one was open for 1% of the time, Pallas kernels for 31%

profile of v11, /device:TPU:0, one launch (start us, length us, event | category | flops | bytes accessed | tf_op | source)
XLA Modules:
  0.0 432.4 jit_solution(8438493198768106347)
XLA Ops:
  2.2 8.6 %shard_map.128 = (f32[32800,128]{1,0:T(8,128)S(1)}, bf16[400,512]{1,0:T(8,128)(2,1)S(1)}, bf16[400,512]{1,0:T(8,128)(2,1)S(1)}) custom-call(s32[1]{0:T(128)} %bitcast.core_ref.refs_0_, s32[1024]{0:T(1024)S(1)} %bitcast.66, f32[400,8192]{1,0:T(8,128)} %bitcast.75), custom_call_target="tpu_custom_call" | custom-call | flops 100000000 | tf_op jit(solution)/shard_map/pallas_call | solution.py:544
  16.1 5.6 %shard_map.129 = (bf16[400,2048]{1,0:T(8,128)(2,1)S(1)}, bf16[400,2048]{1,0:T(8,128)(2,1)S(1)}) custom-call(s32[2048]{0:T(1024)S(1)} %bitcast.58, s32[2048]{0:T(1024)S(1)} %bitcast.60, f32[32800,128]{1,0:T(8,128)S(1)} %get-tuple-element.116.refs_2_.refs_3_), custom_call_target="tpu_custom_call" | custom-call | flops 55000000 | tf_op jit(solution)/shard_map/pallas_call | solution.py:544
  21.6 4.4 %shard_map.130 = (f32[400,2048]{1,0:T(8,128)S(1)}, f32[400,2048]{1,0:T(8,128)S(1)}) custom-call(s32[1]{0:T(128)} %bitcast.core_ref.refs_0_, s32[2048]{0:T(1024)S(1)} %bitcast.62, bf16[400,2048]{1,0:T(8,128)(2,1)S(1)} %get-tuple-element.120.refs_2_.hb, f32[400,1408]{1,0:T(8,128)S(1)} %pad.13.refs_3_), custom_call_target="tpu_custom_call" | custom-call | flops 50000000 | tf_op jit(solution)/shard_map/pallas_call | solution.py:544
  27.9 4.9 %shard_map.131 = (f32[1000,2048]{1,0:T(8,128)S(1)}, f32[1,2048]{1,0:T(1,128)S(1)}, f32[1,2048]{1,0:T(1,128)S(1)}) custom-call(s32[1]{0:T(128)} %bitcast.core_ref.refs_0_, f32[400,2048]{1,0:T(8,128)S(1)} %get-tuple-element.122.q.refs_4_, bf16[400,512]{1,0:T(8,128)(2,1)S(1)} %add.83.nfull, bf16[400,512]{1,0:T(8,128)(2,1)S(1)} %collective-permute-done.2.nother), custom_call_target="tpu_custom_call" | custom-call | flops 40000000 | tf_op jit(solution)/shard_map/pallas_call | solution.py:544
  32.8 5.0 %shard_map.132 = (f32[1,128]{1,0:T(1,128)S(1)}, f32[1,2048]{1,0:T(1,128)S(1)}, bf16[1024,2048]{1,0:T(8,128)(2,1)S(1)}, f32[200,1024]{1,0:T(8,128)S(1)}, f32[200,1024]{1,0:T(8,128)S(1)}) custom-call(s32[1]{0:T(128)} %bitcast.core_ref.refs_0_, f32[1,2048]{1,0:T(1,128)S(1)} %get-tuple-element.230.w, f32[400,2048]{1,0:T(8,128)S(1)} %get-tuple-element.122.q.refs_4_, ...), custom_call_target="tpu_custom_call" | custom-call | flops 40000000 | tf_op jit(solution)/shard_map/pallas_call | solution.py:544
  40.3 10.2 %shard_map.133 = (f32[8192,128]{1,0:T(8,128)S(1)}, f32[200,1408]{1,0:T(8,128)S(1)}, f32[200,1408]{1,0:T(8,128)S(1)}) custom-call(s32[1]{0:T(128)} %bitcast.core_ref.refs_0_, s32[2048]{0:T(1024)S(1)} %bitcast.63, bf16[1024,2048]{1,0:T(8,128)(2,1)S(1)} %get-tuple-element.132.ds, f32[1,2048]{1,0:T(1,128)S(1)} %get-tuple-element.133.dp.refs_3_, ...), custom_call_target="tpu_custom_call" | custom-call | flops 60000000 | tf_op jit(solution)/shard_map/pallas_call | solution.py:544
  53.4 10.0 %shard_map.134.refs_5_ = f32[32800,128]{1,0:T(8,128)S(1)} custom-call(s32[2048]{0:T(1024)S(1)} %bitcast.61, s32[2048]{0:T(1024)S(1)} %bitcast.59, f32[8192,128]{1,0:T(8,128)S(1)} %get-tuple-element.138.refs_2_, f32[1,2048]{1,0:T(1,128)S(1)} %get-tuple-element.133.dp.refs_3_, f32[400,2048]{1,0:T(8,128)S(1)} %get-tuple-element.122.q.refs_4_), custom_call_target="tpu_custom_call" | custom-call | flops 75000000 | tf_op jit(solution)/shard_map/pallas_call | solution.py:544
  63.4 7.7 %collective-permute-done.4 = f32[200,1024]{1,0:T(8,128)S(1)} collective-permute-done((f32[200,1024]{1,0:T(8,128)S(1)}, f32[200,1024]{1,0:T(8,128)S(1)}, u32[]{:S(2)}, u32[]{:S(2)}) %collective-permute-start.4) | collective-permute-done | bytes 819232 | tf_op jit(solution)/shard_map/ppermute | solution.py:499
  73.6 14.0 %shard_map.135 = (f32[32800,128]{1,0:T(8,128)S(1)}, f32[32800,128]{1,0:T(8,128)S(1)}, f32[64,128]{1,0:T(8,128)S(1)}, bf16[400,512]{1,0:T(8,128)(2,1)S(1)}, bf16[400,512]{1,0:T(8,128)(2,1)S(1)}) custom-call(s32[1]{0:T(128)} %bitcast.core_ref.refs_0_, s32[1024]{0:T(1024)S(1)} %bitcast.67, ...), custom_call_target="tpu_custom_call", output_to_operand_aliasing={{0}: (5, {}), {1}: (3, {}), {2}: (4, {})} | custom-call | flops 150000000 | tf_op jit(solution)/shard_map/pallas_call | solution.py:544
  87.8 10.6 %collective-permute-done.8 = s32[2,2048]{1,0:T(2,128)S(1)} collective-permute-done((s32[2,2048]{1,0:T(2,128)S(1)}, s32[2,2048]{1,0:T(2,128)S(1)}, u32[]{:S(2)}, u32[]{:S(2)}) %collective-permute-start.8) | collective-permute-done | bytes 16416 | tf_op jit(solution)/shard_map/ppermute | solution.py:499
  107.9 4.7 %shard_map.138 = (f32[400,2048]{1,0:T(8,128)S(1)}, f32[400,2048]{1,0:T(8,128)S(1)}, f32[5632,128]{1,0:T(8,128)}, f32[400,1408]{1,0:T(8,128)S(1)}, f32[1,1408]{1,0:T(1,128)S(1)}) custom-call(s32[1]{0:T(128)} %bitcast.core_ref.refs_0_, s32[2048]{0:T(1024)S(1)} %bitcast.48, bf16[400,2048]{1,0:T(8,128)(2,1)S(1)} %shard_map.137.refs_2_.hb, ...), custom_call_target="tpu_custom_call" | custom-call | flops 50000000 | tf_op jit(solution)/shard_map/pallas_call | solution.py:544
  112.7 18.3 %collective-permute-done.9 = bf16[400,512]{1,0:T(8,128)(2,1)S(1)} collective-permute-done((bf16[400,512]{1,0:T(8,128)(2,1)S(1)}, bf16[400,512]{1,0:T(8,128)(2,1)S(1)}, u32[]{:S(2)}, u32[]{:S(2)}) %collective-permute-start.9) | collective-permute-done | bytes 409632 | tf_op jit(solution)/shard_map/ppermute | solution.py:499
  132.9 4.9 %shard_map.139 = (f32[1000,2048]{1,0:T(8,128)S(1)}, f32[1,2048]{1,0:T(1,128)S(1)}, f32[1,2048]{1,0:T(1,128)S(1)}) custom-call(s32[1]{0:T(128)} %bitcast.core_ref.refs_0_, f32[400,2048]{1,0:T(8,128)S(1)} %get-tuple-element.154.q, bf16[400,512]{1,0:T(8,128)(2,1)S(1)} %add.89.nfull, bf16[400,512]{1,0:T(8,128)(2,1)S(1)} %collective-permute-done.12.nother), custom_call_target="tpu_custom_call" | custom-call | flops 40000000 | tf_op jit(solution)/shard_map/pallas_call | solution.py:544
  137.8 5.0 %shard_map.140 = (f32[1,128]{1,0:T(1,128)S(1)}, f32[1,2048]{1,0:T(1,128)S(1)}, bf16[1024,2048]{1,0:T(8,128)(2,1)S(1)}, f32[200,1024]{1,0:T(8,128)S(1)}, f32[200,1024]{1,0:T(8,128)S(1)}) custom-call(s32[1]{0:T(128)} %bitcast.core_ref.refs_0_, f32[1,2048]{1,0:T(1,128)S(1)} %get-tuple-element.229.w, f32[400,2048]{1,0:T(8,128)S(1)} %get-tuple-element.154.q, ...), custom_call_target="tpu_custom_call" | custom-call | flops 40000000 | tf_op jit(solution)/shard_map/pallas_call | solution.py:544
  146.1 10.2 %shard_map.141 = (f32[8192,128]{1,0:T(8,128)S(1)}, f32[200,1408]{1,0:T(8,128)S(1)}, f32[200,1408]{1,0:T(8,128)S(1)}) custom-call(s32[1]{0:T(128)} %bitcast.core_ref.refs_0_, s32[2048]{0:T(1024)S(1)} %bitcast.49, bf16[1024,2048]{1,0:T(8,128)(2,1)S(1)} %get-tuple-element.166.ds, f32[1,2048]{1,0:T(1,128)S(1)} %get-tuple-element.167.dp, ...), custom_call_target="tpu_custom_call" | custom-call | flops 60000000 | tf_op jit(solution)/shard_map/pallas_call | solution.py:544
  159.3 21.8 %collective-permute-done.17.refs_4_ = f32[1,2048]{1,0:T(1,128)S(1)} collective-permute-done((f32[1,2048]{1,0:T(1,128)S(1)}, f32[1,2048]{1,0:T(1,128)S(1)}, u32[]{:S(2)}, u32[]{:S(2)}) %collective-permute-start.17) | collective-permute-done | bytes 8224 | tf_op jit(solution)/shard_map/ppermute | solution.py:499
  182.3 12.9 %shard_map.142.refs_5_ = f32[32800,128]{1,0:T(8,128)S(1)} custom-call(s32[2048]{0:T(1024)S(1)} %bitcast.53, s32[2048]{0:T(1024)S(1)} %bitcast.57, s32[2048]{0:T(1024)S(1)} %bitcast.71, f32[8192,128]{1,0:T(8,128)S(1)} %get-tuple-element.173.refs_3_, f32[1,2048]{1,0:T(1,128)S(1)} %collective-permute-done.17.refs_4_, bf16[400,2048]{1,0:T(8,128)(2,1)} %copy-done.7, ...), custom_call_target="tpu_custom_call" | custom-call | flops 75000000 | tf_op jit(solution)/shard_map/pallas_call | solution.py:544
  198.9 14.0 %shard_map.143 = (f32[32800,128]{1,0:T(8,128)S(1)}, f32[32800,128]{1,0:T(8,128)S(1)}, f32[64,128]{1,0:T(8,128)S(1)}, bf16[400,512]{1,0:T(8,128)(2,1)S(1)}, bf16[400,512]{1,0:T(8,128)(2,1)S(1)}) custom-call(s32[1]{0:T(128)} %bitcast.core_ref.refs_0_, s32[1024]{0:T(1024)S(1)} %bitcast.69, ...), custom_call_target="tpu_custom_call", output_to_operand_aliasing={{0}: (5, {}), {1}: (3, {}), {2}: (4, {})} | custom-call | flops 150000000 | tf_op jit(solution)/shard_map/pallas_call | solution.py:544
  213.1 11.0 %collective-permute-done.21 = s32[2,2048]{1,0:T(2,128)S(1)} collective-permute-done((s32[2,2048]{1,0:T(2,128)S(1)}, s32[2,2048]{1,0:T(2,128)S(1)}, u32[]{:S(2)}, u32[]{:S(2)}) %collective-permute-start.21) | collective-permute-done | bytes 16416 | tf_op jit(solution)/shard_map/ppermute | solution.py:499
  227.9 3.3 shard_map.145.refs_2_.hb
  234.1 4.7 %shard_map.146 = (f32[400,2048]{1,0:T(8,128)S(1)}, f32[400,2048]{1,0:T(8,128)S(1)}, f32[5632,128]{1,0:T(8,128)}, f32[400,1408]{1,0:T(8,128)S(1)}, f32[1,1408]{1,0:T(1,128)S(1)}) custom-call(s32[1]{0:T(128)} %bitcast.core_ref.refs_0_, s32[2048]{0:T(1024)S(1)} %bitcast.45, bf16[400,2048]{1,0:T(8,128)(2,1)S(1)} %shard_map.145.refs_2_.hb, ...), custom_call_target="tpu_custom_call" | custom-call | flops 50000000 | tf_op jit(solution)/shard_map/pallas_call | solution.py:544
  238.9 34.6 %collective-permute-done.22 = bf16[400,512]{1,0:T(8,128)(2,1)S(1)} collective-permute-done((bf16[400,512]{1,0:T(8,128)(2,1)S(1)}, bf16[400,512]{1,0:T(8,128)(2,1)S(1)}, u32[]{:S(2)}, u32[]{:S(2)}) %collective-permute-start.22) | collective-permute-done | bytes 409632 | tf_op jit(solution)/shard_map/ppermute | solution.py:499
  275.3 4.9 %shard_map.147 = (f32[1000,2048]{1,0:T(8,128)S(1)}, f32[1,2048]{1,0:T(1,128)S(1)}, f32[1,2048]{1,0:T(1,128)S(1)}) custom-call(s32[1]{0:T(128)} %bitcast.core_ref.refs_0_, f32[400,2048]{1,0:T(8,128)S(1)} %get-tuple-element.192.q, bf16[400,512]{1,0:T(8,128)(2,1)S(1)} %add.95.nfull, bf16[400,512]{1,0:T(8,128)(2,1)S(1)} %collective-permute-done.25.nother), custom_call_target="tpu_custom_call" | custom-call | flops 40000000 | tf_op jit(solution)/shard_map/pallas_call | solution.py:544
  280.2 5.0 %shard_map.148 = (f32[1,128]{1,0:T(1,128)S(1)}, f32[1,2048]{1,0:T(1,128)S(1)}, bf16[1024,2048]{1,0:T(8,128)(2,1)S(1)}, f32[200,1024]{1,0:T(8,128)S(1)}, f32[200,1024]{1,0:T(8,128)S(1)}) custom-call(s32[1]{0:T(128)} %bitcast.core_ref.refs_0_, f32[1,2048]{1,0:T(1,128)S(1)} %get-tuple-element.228.w, f32[400,2048]{1,0:T(8,128)S(1)} %get-tuple-element.192.q, ...), custom_call_target="tpu_custom_call" | custom-call | flops 40000000 | tf_op jit(solution)/shard_map/pallas_call | solution.py:544
  287.6 10.2 %shard_map.149 = (f32[8192,128]{1,0:T(8,128)S(1)}, f32[200,1408]{1,0:T(8,128)S(1)}, f32[200,1408]{1,0:T(8,128)S(1)}) custom-call(s32[1]{0:T(128)} %bitcast.core_ref.refs_0_, s32[2048]{0:T(1024)S(1)} %bitcast.46, bf16[1024,2048]{1,0:T(8,128)(2,1)S(1)} %get-tuple-element.203.ds, f32[1,2048]{1,0:T(1,128)S(1)} %get-tuple-element.204.dp, ...), custom_call_target="tpu_custom_call" | custom-call | flops 60000000 | tf_op jit(solution)/shard_map/pallas_call | solution.py:544
  302.8 58.0 %collective-permute-done.33 = f32[200,1408]{1,0:T(8,128)S(1)} collective-permute-done((f32[200,1408]{1,0:T(8,128)S(1)}, f32[200,1408]{1,0:T(8,128)S(1)}, u32[]{:S(2)}, u32[]{:S(2)}) %collective-permute-start.33) | collective-permute-done | bytes 1126432 | tf_op jit(solution)/shard_map/ppermute | solution.py:499
  362.6 15.4 %collective-permute-done.30.refs_4_ = f32[1,2048]{1,0:T(1,128)S(1)} collective-permute-done((f32[1,2048]{1,0:T(1,128)S(1)}, f32[1,2048]{1,0:T(1,128)S(1)}, u32[]{:S(2)}, u32[]{:S(2)}) %collective-permute-start.30) | collective-permute-done | bytes 8224 | tf_op jit(solution)/shard_map/ppermute | solution.py:499
  378.0 12.9 %shard_map.150.refs_4_ = f32[32800,128]{1,0:T(8,128)S(1)} custom-call(s32[2048]{0:T(1024)S(1)} %bitcast.51, s32[2048]{0:T(1024)S(1)} %bitcast.55, s32[2048]{0:T(1024)S(1)} %bitcast.70, f32[8192,128]{1,0:T(8,128)S(1)} %get-tuple-element.209.refs_3_, f32[1,2048]{1,0:T(1,128)S(1)} %collective-permute-done.30.refs_4_, bf16[400,2048]{1,0:T(8,128)(2,1)} %copy-done.8, ...), custom_call_target="tpu_custom_call" | custom-call | flops 75000000 | tf_op jit(solution)/shard_map/pallas_call | solution.py:544
  390.9 5.8 %copy-done.2 = f32[32800,128]{1,0:T(8,128)} copy-done((f32[32800,128]{1,0:T(8,128)}, f32[32800,128]{1,0:T(8,128)S(1)}, u32[]{:S(2)}) %copy-start.2) | copy-done | bytes 16793624
  399.3 5.8 %copy-done.1 = f32[32800,128]{1,0:T(8,128)S(1)} copy-done((f32[32800,128]{1,0:T(8,128)S(1)}, f32[32800,128]{1,0:T(8,128)}, u32[]{:S(2)}) %copy-start.1) | copy-done | bytes 16793624
  405.0 5.8 %copy-done.3 = f32[32800,128]{1,0:T(8,128)S(1)} copy-done((f32[32800,128]{1,0:T(8,128)S(1)}, f32[32800,128]{1,0:T(8,128)}, u32[]{:S(2)}) %copy-start.3) | copy-done | bytes 16793624
  410.8 16.6 %shard_map.151 = (f32[32800,128]{1,0:T(8,128)S(1)}, f32[400,8192]{1,0:T(8,128)}, f32[64,128]{1,0:T(8,128)}) custom-call(s32[1]{0:T(128)} %bitcast.core_ref.refs_0_, s32[1024]{0:T(1024)S(1)} %bitcast.65, f32[32800,128]{1,0:T(8,128)S(1)} %copy-done.1, f32[64,128]{1,0:T(8,128)S(1)} %get-tuple-element.184.refs_3_, ...), custom_call_target="tpu_custom_call", output_to_operand_aliasing={{0}: (4, {})} | custom-call | flops 150000000 | tf_op jit(solution)/shard_map/pallas_call | solution.py:544
  (129 shorter events, 64.5 us)
Async XLA Ops:
  10.8 2.2 collective-permute-start
  13.2 12.8 %collective-permute-start.1 = (bf16[400,512]{1,0:T(8,128)(2,1)S(1)}, bf16[400,512]{1,0:T(8,128)(2,1)S(1)}, u32[]{:S(2)}, u32[]{:S(2)}) collective-permute-start(bf16[400,512]{1,0:T(8,128)(2,1)S(1)} %add.82), channel_id=1, source_target_pairs={{0,2},{1,3},{2,0},{3,1},{4,6},{5,7},{6,4},{7,5}} | collective-permute-start | bytes 1228808 | tf_op jit(solution)/shard_map/ppermute | solution.py:499
  37.8 2.4 collective-permute-start.3
  50.5 2.8 collective-permute-start.5
  50.7 20.5 %collective-permute-start.4 = (f32[200,1024]{1,0:T(8,128)S(1)}, f32[200,1024]{1,0:T(8,128)S(1)}, u32[]{:S(2)}, u32[]{:S(2)}) collective-permute-start(f32[200,1024]{1,0:T(8,128)S(1)} %add.84), channel_id=1, source_target_pairs={{0,2},{1,3},{2,0},{3,1},{4,6},{5,7},{6,4},{7,5}} | collective-permute-start | bytes 2457608 | tf_op jit(solution)/shard_map/ppermute | solution.py:499
  71.3 2.4 collective-permute-start.6
  71.3 33.6 %collective-permute-start.10 = (f32[200,1408]{1,0:T(8,128)S(1)}, f32[200,1408]{1,0:T(8,128)S(1)}, u32[]{:S(2)}, u32[]{:S(2)}) collective-permute-start(f32[200,1408]{1,0:T(8,128)S(1)} %add.85), channel_id=1, source_target_pairs={{0,2},{1,3},{2,0},{3,1},{4,6},{5,7},{6,4},{7,5}} | collective-permute-start | bytes 3379208 | tf_op jit(solution)/shard_map/ppermute | solution.py:499
  72.9 25.5 %collective-permute-start.8 = (s32[2,2048]{1,0:T(2,128)S(1)}, s32[2,2048]{1,0:T(2,128)S(1)}, u32[]{:S(2)}, u32[]{:S(2)}) collective-permute-start(s32[2,2048]{1,0:T(2,128)S(1)} %pad_add_fusion), channel_id=1, source_target_pairs={{0,1},{1,2},{2,3},{3,0},{4,5},{5,6},{6,7},{7,4}} | collective-permute-start | bytes 49160 | tf_op jit(solution)/shard_map/ppermute | solution.py:499
  87.6 10.8 %collective-permute-start.7 = (bf16[400,512]{1,0:T(8,128)(2,1)S(1)}, bf16[400,512]{1,0:T(8,128)(2,1)S(1)}, u32[]{:S(2)}, u32[]{:S(2)}) collective-permute-start(bf16[400,512]{1,0:T(8,128)(2,1)S(1)} %get-tuple-element.142), channel_id=1, source_target_pairs={{0,1},{1,0},{2,3},{3,2},{4,5},{5,4},{6,7},{7,6}} | collective-permute-start | bytes 1228808 | tf_op jit(solution)/shard_map/ppermute | solution.py:496
  101.6 36.2 %collective-permute-start.13 = (bf16[400,2048]{1,0:T(8,128)(2,1)S(1)}, bf16[400,2048]{1,0:T(8,128)(2,1)S(1)}, u32[]{:S(2)}, u32[]{:S(2)}) collective-permute-start(bf16[400,2048]{1,0:T(8,128)(2,1)S(1)} %shard_map.136), channel_id=1, source_target_pairs={{0,3},{1,0},{2,1},{3,2},{4,7},{5,4},{6,5},{7,6}} | collective-permute-start | bytes 4915208 | tf_op jit(solution)/shard_map/ppermute | solution.py:499
  105.0 2.9 collective-permute-start.11
  105.5 25.5 %collective-permute-start.9 = (bf16[400,512]{1,0:T(8,128)(2,1)S(1)}, bf16[400,512]{1,0:T(8,128)(2,1)S(1)}, u32[]{:S(2)}, u32[]{:S(2)}) collective-permute-start(bf16[400,512]{1,0:T(8,128)(2,1)S(1)} %add.87), channel_id=1, source_target_pairs={{0,2},{1,3},{2,0},{3,1},{4,6},{5,7},{6,4},{7,5}} | collective-permute-start | bytes 1228808 | tf_op jit(solution)/shard_map/ppermute | solution.py:499
  142.7 2.4 collective-permute-start.14
  142.9 38.2 %collective-permute-start.18 = (bf16[400,2048]{1,0:T(8,128)(2,1)S(1)}, bf16[400,2048]{1,0:T(8,128)(2,1)S(1)}, u32[]{:S(2)}, u32[]{:S(2)}) collective-permute-start(bf16[400,2048]{1,0:T(8,128)(2,1)S(1)} %shard_map.137.refs_2_.hb), channel_id=1, source_target_pairs={{0,1},{1,2},{2,3},{3,0},{4,5},{5,6},{6,7},{7,4}} | collective-permute-start | bytes 4915208 | tf_op jit(solution)/shard_map/ppermute | solution.py:499
  156.4 2.8 collective-permute-start.16
  156.5 38.7 %collective-permute-start.15 = (f32[200,1024]{1,0:T(8,128)}, f32[200,1024]{1,0:T(8,128)S(1)}, u32[]{:S(2)}, u32[]{:S(2)}) collective-permute-start(f32[200,1024]{1,0:T(8,128)} %add.90), channel_id=1, source_target_pairs={{0,2},{1,3},{2,0},{3,1},{4,6},{5,7},{6,4},{7,5}} | collective-permute-start | bytes 2457608 | tf_op jit(solution)/shard_map/ppermute | solution.py:499
  157.0 24.1 %collective-permute-start.17 = (f32[1,2048]{1,0:T(1,128)S(1)}, f32[1,2048]{1,0:T(1,128)S(1)}, u32[]{:S(2)}, u32[]{:S(2)}) collective-permute-start(f32[1,2048]{1,0:T(1,128)S(1)} %get-tuple-element.167.dp), channel_id=1, source_target_pairs={{0,1},{1,2},{2,3},{3,0},{4,5},{5,6},{6,7},{7,4}} | collective-permute-start | bytes 24584 | tf_op jit(solution)/shard_map/ppermute | solution.py:499
  196.5 2.4 collective-permute-start.19
  196.5 34.6 %collective-permute-start.23 = (f32[200,1408]{1,0:T(8,128)S(1)}, f32[200,1408]{1,0:T(8,128)S(1)}, u32[]{:S(2)}, u32[]{:S(2)}) collective-permute-start(f32[200,1408]{1,0:T(8,128)S(1)} %add.91), channel_id=1, source_target_pairs={{0,2},{1,3},{2,0},{3,1},{4,6},{5,7},{6,4},{7,5}} | collective-permute-start | bytes 3379208 | tf_op jit(solution)/shard_map/ppermute | solution.py:499
  197.1 27.0 %collective-permute-start.21 = (s32[2,2048]{1,0:T(2,128)S(1)}, s32[2,2048]{1,0:T(2,128)S(1)}, u32[]{:S(2)}, u32[]{:S(2)}) collective-permute-start(s32[2,2048]{1,0:T(2,128)S(1)} %pad_add_fusion.1), channel_id=1, source_target_pairs={{0,2},{1,3},{2,0},{3,1},{4,6},{5,7},{6,4},{7,5}} | collective-permute-start | bytes 49160 | tf_op jit(solution)/shard_map/ppermute | solution.py:499
  212.9 11.2 %collective-permute-start.20 = (bf16[400,512]{1,0:T(8,128)(2,1)S(1)}, bf16[400,512]{1,0:T(8,128)(2,1)S(1)}, u32[]{:S(2)}, u32[]{:S(2)}) collective-permute-start(bf16[400,512]{1,0:T(8,128)(2,1)S(1)} %get-tuple-element.178), channel_id=1, source_target_pairs={{0,1},{1,0},{2,3},{3,2},{4,5},{5,4},{6,7},{7,6}} | collective-permute-start | bytes 1228808 | tf_op jit(solution)/shard_map/ppermute | solution.py:496
  227.3 52.9 %collective-permute-start.26 = (bf16[400,2048]{1,0:T(8,128)(2,1)S(1)}, bf16[400,2048]{1,0:T(8,128)(2,1)S(1)}, u32[]{:S(2)}, u32[]{:S(2)}) collective-permute-start(bf16[400,2048]{1,0:T(8,128)(2,1)S(1)} %shard_map.144), channel_id=1, source_target_pairs={{0,2},{1,3},{2,0},{3,1},{4,6},{5,7},{6,4},{7,5}} | collective-permute-start | bytes 4915208 | tf_op jit(solution)/shard_map/ppermute | solution.py:499
  231.3 2.8 collective-permute-start.24
  231.4 42.1 %collective-permute-start.22 = (bf16[400,512]{1,0:T(8,128)(2,1)S(1)}, bf16[400,512]{1,0:T(8,128)(2,1)S(1)}, u32[]{:S(2)}, u32[]{:S(2)}) collective-permute-start(bf16[400,512]{1,0:T(8,128)(2,1)S(1)} %add.93), channel_id=1, source_target_pairs={{0,2},{1,3},{2,0},{3,1},{4,6},{5,7},{6,4},{7,5}} | collective-permute-start | bytes 1228808 | tf_op jit(solution)/shard_map/ppermute | solution.py:499
  285.1 2.4 collective-permute-start.27
  297.8 2.8 collective-permute-start.29
  298.0 64.5 %collective-permute-start.31 = (bf16[400,2048]{1,0:T(8,128)(2,1)S(1)}, bf16[400,2048]{1,0:T(8,128)(2,1)S(1)}, u32[]{:S(2)}, u32[]{:S(2)}) collective-permute-start(bf16[400,2048]{1,0:T(8,128)(2,1)S(1)} %shard_map.145.refs_2_.hb), channel_id=1, source_target_pairs={{0,2},{1,3},{2,0},{3,1},{4,6},{5,7},{6,4},{7,5}} | collective-permute-start | bytes 4915208 | tf_op jit(solution)/shard_map/ppermute | solution.py:499
  300.8 60.1 %collective-permute-start.33 = (f32[200,1408]{1,0:T(8,128)S(1)}, f32[200,1408]{1,0:T(8,128)S(1)}, u32[]{:S(2)}, u32[]{:S(2)}) collective-permute-start(f32[200,1408]{1,0:T(8,128)S(1)} %add.97), channel_id=1, source_target_pairs={{0,2},{1,3},{2,0},{3,1},{4,6},{5,7},{6,4},{7,5}} | collective-permute-start | bytes 3379208 | tf_op jit(solution)/shard_map/ppermute | solution.py:499
  301.3 95.3 %collective-permute-start.28 = (f32[200,1024]{1,0:T(8,128)S(1)}, f32[200,1024]{1,0:T(8,128)S(1)}, u32[]{:S(2)}, u32[]{:S(2)}) collective-permute-start(f32[200,1024]{1,0:T(8,128)S(1)} %add.96), channel_id=1, source_target_pairs={{0,2},{1,3},{2,0},{3,1},{4,6},{5,7},{6,4},{7,5}} | collective-permute-start | bytes 2457608 | tf_op jit(solution)/shard_map/ppermute | solution.py:499
  362.0 65.4 %collective-permute-start.34 = (f32[200,1408]{1,0:T(8,128)}, f32[200,1408]{1,0:T(8,128)}, u32[]{:S(2)}, u32[]{:S(2)}) collective-permute-start(f32[200,1408]{1,0:T(8,128)} %add.99), channel_id=1, source_target_pairs={{0,1},{1,0},{2,3},{3,2},{4,5},{5,4},{6,7},{7,6}} | collective-permute-start | bytes 3379208 | tf_op jit(solution)/shard_map/ppermute | solution.py:506
  362.0 15.9 %collective-permute-start.30 = (f32[1,2048]{1,0:T(1,128)S(1)}, f32[1,2048]{1,0:T(1,128)S(1)}, u32[]{:S(2)}, u32[]{:S(2)}) collective-permute-start(f32[1,2048]{1,0:T(1,128)S(1)} %get-tuple-element.204.dp), channel_id=1, source_target_pairs={{0,2},{1,3},{2,0},{3,1},{4,6},{5,7},{6,4},{7,5}} | collective-permute-start | bytes 24584 | tf_op jit(solution)/shard_map/ppermute | solution.py:499
  396.8 2.5 collective-permute-start.32
  (17 other events, 118.0 us)
